TPU v7x, 128 devices: a whole 4x4x4 slice. The times are simulated.
128 devices in a mesh: seq: 32 (over z, y_hi, x), head: 4 (over y_lo, core).
Axes of the slice: x: 4, y: 4 (y_hi: 2, y_lo: 2; y = y_hi * 2 + y_lo), z: 4, core: 2. Of those that a mesh axis runs over, the one named last changes fastest.
Arguments:
- queries: bfloat16 [8192, 3584], P('seq', 'head'), may hold values from -5 to 5
- keys: bfloat16 [8192, 3584], P('seq', 'head'), may hold values from -5 to 5
- values: bfloat16 [8192, 3584], P('seq', 'head'), may hold values from -6 to 6
- attn_grad: bfloat16 [8192, 3584], P('seq', 'head'), may hold values from -6 to 6
- doc_ids: int32 [8192], replicated, may hold values from 0 to 7, never falling along the last dimension, each value on 1 to 4096 neighbouring positions
- conv_input: bfloat16 [8192, 7168], P('seq', 'head'), may hold values from -6 to 6
- conv_weight: float32 [4, 7168], P(None, 'head'), may hold values from -3 to 3
- step_raw: float32 [8192, 112], P('seq', 'head'), may hold values from -4 to 4
- step_bias: float32 [112], P('head'), may hold values from -1.5 to 0
- rate_log: float32 [112], P('head'), may hold values from -13 to -1
- skip_gain: float32 [112], P('head'), may hold values from 0.5 to 1.5
- input_coeff: bfloat16 [8192, 128], P('seq'), may hold values from -0.625 to 0.625
- output_coeff: bfloat16 [8192, 128], P('seq'), may hold values from -0.625 to 0.625
- gate_input: bfloat16 [8192, 7168], P('seq', 'head'), may hold values from -6 to 6
- mix_grad: bfloat16 [8192, 7168], P('seq', 'head'), may hold values from -1.5 to 1.5
Outputs:
- grad_queries: bfloat16 [8192, 3584], P('seq', 'head')
- grad_keys: bfloat16 [8192, 3584], P('seq', 'head')
- grad_values: bfloat16 [8192, 3584], P('seq', 'head')
- grad_conv_input: bfloat16 [8192, 7168], P('seq', 'head')
- grad_gate: bfloat16 [8192, 7168], P('seq', 'head')
- grad_step: float32 [8192, 112], P('seq', 'head')
- grad_input_coeff: float32 [8192, 128], P('seq')
- grad_output_coeff: float32 [8192, 128], P('seq')
- grad_conv_weight: float32 [4, 7168], P(None, 'head')
- grad_step_bias: float32 [112], P('head')
- grad_rate_log: float32 [112], P('head')
- grad_skip: float32 [112], P('head')
Inputs may be any that keep to these rules, and one draw needn't show every extreme that they name: doc_ids never fall along the sequence.
All inputs are finite; a program needn't handle non-finite values.
Results may differ from a plain program's by a relative error of at most 0.012.
Values may be sent and summed in bfloat16 or wider, within the bound.
No kernel may reach another device: no remote copies, remote signals or barrier semaphores. Data moves between devices by JAX's collectives and lax.ppermute only.
A program may use at most 128 MiB of HBM per device.

v0:
```python
import jax
import jax.numpy as jnp
from jax import lax
from jax.experimental import pallas as pl
from jax.experimental.pallas import tpu as pltpu
from jax.sharding import Mesh
from jax.sharding import PartitionSpec as P

HEAD_DIM = 224
WINDOW = 1024
SSM_HEADS = 112
STATE = 64
GROUPS = 2
KERNEL = 4
SEQ = ("seq_0", "seq_1", "seq_2")
SHARDS = 32
T = 256
LOCAL_HEADS = 4
REACH = WINDOW // T
BLK = 256
HEADS_BLK = BLK // 64
COLS = 1792
STEPS = COLS // BLK
NEG = -1e30
F32 = jnp.float32
BF16 = jnp.bfloat16

NN = (((1,), (0,)), ((), ()))
NT = (((1,), (1,)), ((), ()))
TN = (((0,), (0,)), ((), ()))


def dot(a, b, dims=NN):
    return lax.dot_general(a, b, dims, preferred_element_type=F32)


def exact(a, b, dims=NN):
    return lax.dot_general(
        a, b, dims, preferred_element_type=F32, precision=lax.Precision.HIGHEST
    )


def split(a, pieces):
    parts = []
    for _ in range(pieces):
        part = a.astype(BF16)
        parts.append(part)
        a = a - part.astype(F32)
    return parts


def sigmoid(v):
    return 1.0 / (1.0 + jnp.exp(-v))


def iota(shape, dim):
    return lax.broadcasted_iota(jnp.int32, shape, dim)


def columns_of(row):
    return jnp.transpose(jnp.broadcast_to(row, (T, T)))


def token_setup(docs, step_pad, params, cum_s, step_s, mask_s, prev_s, end_s):
    own = columns_of(docs[0:1].astype(F32))
    for lag in range(1, KERNEL):
        lagged = columns_of(docs[4 + lag : 5 + lag].astype(F32))
        mask_s[lag - 1] = jnp.where(own == lagged, 1.0, 0.0)
    before = docs[5:6, 0:1].astype(F32)
    last = docs[0:1, T - 1 : T].astype(F32)
    prev_s[...] = jnp.where(own == before, 0.0, NEG)
    end_s[...] = jnp.where(own == last, 0.0, NEG)
    raw = step_pad + params[0:1]
    step = jnp.maximum(raw, 0.0) + jnp.log1p(jnp.exp(-jnp.abs(raw)))
    decay = -step * jnp.exp(params[1:2])
    lower = jnp.where(iota((T, T), 0) >= iota((T, T), 1), 1.0, 0.0)
    cum = exact(lower, decay)
    for n, part in enumerate(split(cum, 3)):
        cum_s[n] = part
    for n, part in enumerate(split(step, 2)):
        step_s[n] = part
    return raw, step, decay, cum


def spread_of(step_id):
    head = iota((128, BLK), 0)
    owner = step_id * HEADS_BLK + iota((128, BLK), 1) // 64
    return jnp.where(head == owner, 1.0, 0.0).astype(BF16)


def block_gains(step_id, cum_s, step_s, prev_s, end_s):
    spread = spread_of(step_id)
    cum = dot(cum_s[0], spread) + dot(cum_s[1], spread) + dot(cum_s[2], spread)
    step = dot(step_s[0], spread) + dot(step_s[1], spread)
    enter = jnp.exp(cum + prev_s[...])
    to_end = jnp.exp(cum[T - 1 : T] - cum + end_s[...])
    return spread, cum, step, enter, to_end


def conv_pre(x, halo, weight, mask_s):
    extended = jnp.concatenate([halo.astype(F32), x.astype(F32)], axis=0)
    shifted = [extended[8:]]
    summed = weight[0:1] * shifted[0]
    for lag in range(1, KERNEL):
        moved = pltpu.roll(extended, lag, 0)[8:] * mask_s[lag - 1]
        shifted.append(moved)
        summed = summed + weight[lag : lag + 1] * moved
    return summed, shifted


def mixer_first_kernel(
    x_ref, halo_ref, weight_ref, gate_ref, grad_ref, step_ref, par_ref, docs_ref, bc_ref,
    state_ref, through_ref,
    cum_s, step_s, mask_s, prev_s, end_s,
):
    step_id = pl.program_id(0)

    @pl.when(step_id == 0)
    def _():
        cum = token_setup(
            docs_ref[...], step_ref[...], par_ref[...], cum_s, step_s, mask_s, prev_s, end_s
        )[3]
        through = jnp.exp(cum[T - 1 : T] + prev_s[T - 1 : T, 0:1])
        high, low = split(through, 2)
        row = iota((8, 128), 0)
        both = jnp.where(row == 0, high.astype(F32), jnp.where(row == 1, low.astype(F32), 0.0))
        through_ref[...] = both.astype(BF16)

    _, _, step, enter, to_end = block_gains(step_id, cum_s, step_s, prev_s, end_s)
    pre, _ = conv_pre(x_ref[...], halo_ref[...], weight_ref[...], mask_s)
    act = pre * sigmoid(pre)
    gate = gate_ref[...].astype(F32)
    out_grad = grad_ref[...].astype(F32) * gate * sigmoid(gate)
    lane = iota((T, 128), 1)
    bc = bc_ref[...].astype(F32)
    in_half = jnp.where(lane < STATE, bc, 0.0).astype(BF16)
    out_half = jnp.where(lane < STATE, 0.0, bc).astype(BF16)
    ended = (act * step * to_end).astype(BF16)
    entered = (out_grad * enter).astype(BF16)
    state_ref[...] = (dot(ended, in_half, TN) + dot(entered, out_half, TN)).astype(BF16)


def whole(shape):
    return pl.BlockSpec(shape, lambda c: (0,) * len(shape))


def column_block(rows):
    return pl.BlockSpec((rows, BLK), lambda c: (0, c))


TOKEN_SCRATCH = [
    pltpu.VMEM((3, T, 128), BF16),
    pltpu.VMEM((2, T, 128), BF16),
    pltpu.VMEM((KERNEL - 1, T, BLK), F32),
    pltpu.VMEM((T, BLK), F32),
    pltpu.VMEM((T, BLK), F32),
]


def mixer_first(x, halo, weight, gate, grad, step_pad, params, docs, in_out):
    return pl.pallas_call(
        mixer_first_kernel,
        grid=(STEPS,),
        in_specs=[
            column_block(T), column_block(8), column_block(KERNEL), column_block(T),
            column_block(T), whole((T, 128)), whole((8, 128)), whole((8, T)), whole((T, 128)),
        ],
        out_specs=[pl.BlockSpec((BLK, 128), lambda c: (c, 0)), whole((8, 128))],
        out_shape=[
            jax.ShapeDtypeStruct((COLS, 128), BF16),
            jax.ShapeDtypeStruct((8, 128), BF16),
        ],
        scratch_shapes=TOKEN_SCRATCH,
        name="mixer_first",
    )(x, halo, weight, gate, grad, step_pad, params, docs, in_out)


ROWS = COLS // SHARDS


def chain_kernel(slot_ref, parts_ref, out_ref, forward_s):
    slot = slot_ref[0]
    owner = (slot * ROWS + iota((ROWS, 128), 0)) // 64
    choose = jnp.where(owner == iota((ROWS, 128), 1), 1.0, 0.0)
    lane = iota((ROWS, 128), 1)
    through = []
    carry = jnp.zeros((ROWS, 128), F32)
    for shard in range(SHARDS):
        row = parts_ref[shard, ROWS : ROWS + 1].astype(F32)
        row = row + parts_ref[shard, ROWS + 1 : ROWS + 2].astype(F32)
        gain = jnp.sum(choose * row, axis=1, keepdims=True)
        through.append(gain)
        forward_s[shard] = carry
        carry = gain * carry + parts_ref[shard, 0:ROWS].astype(F32)
    carry = jnp.zeros((ROWS, 128), F32)
    for shard in reversed(range(SHARDS)):
        out_ref[shard] = jnp.where(lane < STATE, forward_s[shard], carry).astype(BF16)
        carry = through[shard] * carry + parts_ref[shard, 0:ROWS].astype(F32)


def chain(slot, parts):
    return pl.pallas_call(
        chain_kernel,
        in_specs=[
            pl.BlockSpec(memory_space=pltpu.SMEM),
            pl.BlockSpec(memory_space=pltpu.VMEM),
        ],
        out_specs=pl.BlockSpec(memory_space=pltpu.VMEM),
        out_shape=jax.ShapeDtypeStruct((SHARDS, ROWS, 128), BF16),
        scratch_shapes=[pltpu.VMEM((SHARDS, ROWS, 128), F32)],
        name="chain",
    )(slot, parts)


def mixer_second_kernel(
    x_ref, halo_ref, weight_ref, gate_ref, grad_ref, step_ref, par_ref, docs_ref, cb_ref,
    state_ref,
    dx_ref, tail_ref, spill_ref, dgate_ref, dstep_ref, coeff_ref, dweight_ref, small_ref,
    cum_s, step_s, mask_s, prev_s, end_s,
    cumt_s, pair_s, causal_s, dpair_s, coeff_s, row_s, dt_s, ends_s,
):
    step_id = pl.program_id(0)
    lane = iota((T, 128), 1)
    cb = cb_ref[...].astype(F32)
    out_low = jnp.where(lane < STATE, cb, 0.0).astype(BF16)
    in_high = jnp.where(lane < STATE, 0.0, cb).astype(BF16)

    @pl.when(step_id == 0)
    def _():
        docs = docs_ref[...]
        cum = token_setup(docs, step_ref[...], par_ref[...], cum_s, step_s, mask_s, prev_s, end_s)[3]
        cumt_s[...] = jnp.transpose(cum)
        doc_row = docs[0:1].astype(F32)
        same = columns_of(doc_row) == doc_row
        same = same & (iota((T, T), 0) >= iota((T, T), 1))
        causal_s[...] = jnp.where(same, 0.0, NEG)
        swapped = pltpu.roll(cb, 64, 1)
        in_low = jnp.where(lane < STATE, swapped, 0.0).astype(BF16)
        pair_s[...] = dot(out_low, in_low, NT)
        dpair_s[...] = jnp.zeros((T, T), F32)
        coeff_s[...] = jnp.zeros((T, 128), F32)
        row_s[...] = jnp.zeros((T, 128), F32)
        dt_s[...] = jnp.zeros((T, 128), F32)
        ends_s[...] = jnp.zeros((8, 128), F32)

    spread, cum, step, enter, to_end = block_gains(step_id, cum_s, step_s, prev_s, end_s)
    skip = sum(dot(part, spread) for part in split(par_ref[...], 3))[2:3]
    weight = weight_ref[...]
    pre, shifted = conv_pre(x_ref[...], halo_ref[...], weight, mask_s)
    sig = sigmoid(pre)
    act = pre * sig
    gate = gate_ref[...].astype(F32)
    gate_sig = sigmoid(gate)
    mix_grad = grad_ref[...].astype(F32)
    out_grad = mix_grad * gate * gate_sig
    scaled = act * step
    scaled_half = scaled.astype(BF16)
    grad_half = out_grad.astype(BF16)

    block_head = iota((T, BLK), 1) // 64
    inner = jnp.zeros((T, BLK), F32)
    dscaled = jnp.zeros((T, BLK), F32)
    dpair = dpair_s[...]
    for k in range(HEADS_BLK):
        mine = block_head == k
        cum_col = jnp.broadcast_to(cum[:, 64 * k : 64 * k + 1], (T, T))
        cum_row = cumt_s[pl.ds(step_id * HEADS_BLK + k, 1), :]
        weights = jnp.exp(cum_col - cum_row + causal_s[...])
        mixing = (pair_s[...] * weights).astype(BF16)
        scaled_k = jnp.where(mine, scaled_half, jnp.zeros_like(scaled_half))
        grad_k = jnp.where(mine, grad_half, jnp.zeros_like(grad_half))
        inner = inner + dot(mixing, scaled_k)
        dscaled = dscaled + dot(mixing, grad_k, TN)
        dpair = dpair + dot(grad_k, scaled_half, NT) * weights
    dpair_s[...] = dpair

    state = state_ref[...]
    carried = dot(out_low, state, NT) * enter
    from_end = dot(in_high, state, NT) * to_end
    ssm_out = inner + carried
    dscaled = dscaled + from_end
    mixed_out = ssm_out + skip * act
    dgate_ref[...] = (
        mix_grad * mixed_out * gate_sig * (1.0 + gate * (1.0 - gate_sig))
    ).astype(BF16)

    gave_out = dot((out_grad * enter).astype(BF16), state)
    gave_in = dot((scaled * to_end).astype(BF16), state)
    coeff_s[...] += jnp.where(lane < STATE, gave_out, gave_in)

    grad_round = grad_half.astype(F32)
    scaled_round = scaled_half.astype(F32)
    balance = grad_round * ssm_out - scaled_round * dscaled
    row_s[...] += sum(dot(part, spread, NT) for part in split(balance, 3))
    dt_s[...] += sum(dot(part, spread, NT) for part in split(dscaled * act, 2))

    state_wide = state.astype(F32)
    product = state_wide * pltpu.roll(state_wide, 64, 1)
    through = jnp.sum(jnp.where(iota((BLK, 128), 1) < STATE, product, 0.0), axis=1, keepdims=True)
    through_row = jnp.transpose(jnp.broadcast_to(through, (BLK, BLK)))[0:1]
    end_row = jnp.sum(scaled_round * from_end, axis=0, keepdims=True)
    end_row = end_row + through_row * enter[T - 1 : T]
    skip_row = jnp.sum(out_grad * act, axis=0, keepdims=True)
    row8 = iota((8, BLK), 0)
    both = jnp.where(row8 == 0, end_row, jnp.where(row8 == 1, skip_row, 0.0))
    ends_s[...] += sum(dot(part, spread, NT) for part in split(both, 3))

    dact = step * dscaled + skip * out_grad
    dpre = dact * sig * (1.0 + pre * (1.0 - sig))
    zeros = jnp.zeros((8, BLK), F32)
    dx = weight[0:1] * dpre
    spill = zeros
    dweight_ref[0:1] = jnp.sum(dpre * shifted[0], axis=0, keepdims=True)
    for lag in range(1, KERNEL):
        masked = dpre * mask_s[lag - 1]
        dweight_ref[lag : lag + 1] = jnp.sum(dpre * shifted[lag], axis=0, keepdims=True)
        later = pltpu.roll(jnp.concatenate([masked, zeros], axis=0), T + 8 - lag, 0)[:T]
        dx = dx + weight[lag : lag + 1] * later
        edge = pltpu.roll(jnp.concatenate([zeros, masked[:8]], axis=0), 16 - lag, 0)[:8]
        spill = spill + weight[lag : lag + 1] * edge
    dx_ref[...] = dx.astype(BF16)
    tail_ref[...] = dx[T - 8 :]
    spill_ref[...] = spill

    @pl.when(step_id == STEPS - 1)
    def _():
        params = par_ref[...]
        raw = step_ref[...] + params[0:1]
        step_all = jnp.maximum(raw, 0.0) + jnp.log1p(jnp.exp(-jnp.abs(raw)))
        rate = jnp.exp(params[1:2])
        decay = -step_all * rate
        upper = jnp.where(iota((T, T), 1) >= iota((T, T), 0), 1.0, 0.0)
        ends = ends_s[...]
        ddecay = exact(upper, row_s[...]) + ends[0:1]
        dstep = (dt_s[...] - ddecay * rate) * sigmoid(raw)
        dstep_ref[...] = dstep
        dbias = jnp.sum(dstep, axis=0, keepdims=True)
        drate = jnp.sum(ddecay * decay, axis=0, keepdims=True)
        row = iota((8, 128), 0)
        small = jnp.zeros((8, 128), F32)
        for n, vector in enumerate((dbias, drate, ends[1:2])):
            for m, part in enumerate(split(vector, 2)):
                small = jnp.where(row == 2 * n + m, part.astype(F32), small)
        small_ref[...] = small
        dpair_half = dpair_s[...].astype(BF16)
        swapped = pltpu.roll(cb, 64, 1)
        in_low = jnp.where(lane < STATE, swapped, 0.0).astype(BF16)
        out_high = jnp.where(lane < STATE, 0.0, swapped).astype(BF16)
        total = coeff_s[...] + dot(dpair_half, in_low) + dot(dpair_half, out_high, TN)
        coeff_ref[...] = total.astype(BF16)


def mixer_second(x, halo, weight, gate, grad, step_pad, params, docs, out_in, state):
    return pl.pallas_call(
        mixer_second_kernel,
        grid=(STEPS,),
        in_specs=[
            column_block(T), column_block(8), column_block(KERNEL), column_block(T),
            column_block(T), whole((T, 128)), whole((8, 128)), whole((8, T)), whole((T, 128)),
            pl.BlockSpec((BLK, 128), lambda c: (c, 0)),
        ],
        out_specs=[
            column_block(T), column_block(8), column_block(8), column_block(T),
            whole((T, 128)), whole((T, 128)), column_block(KERNEL), whole((8, 128)),
        ],
        out_shape=[
            jax.ShapeDtypeStruct((T, COLS), BF16),
            jax.ShapeDtypeStruct((8, COLS), F32),
            jax.ShapeDtypeStruct((8, COLS), F32),
            jax.ShapeDtypeStruct((T, COLS), BF16),
            jax.ShapeDtypeStruct((T, 128), F32),
            jax.ShapeDtypeStruct((T, 128), BF16),
            jax.ShapeDtypeStruct((KERNEL, COLS), F32),
            jax.ShapeDtypeStruct((8, 128), F32),
        ],
        scratch_shapes=TOKEN_SCRATCH + [
            pltpu.VMEM((128, T), F32),
            pltpu.VMEM((T, T), F32),
            pltpu.VMEM((T, T), F32),
            pltpu.VMEM((T, T), F32),
            pltpu.VMEM((T, 128), F32),
            pltpu.VMEM((T, 128), F32),
            pltpu.VMEM((T, 128), F32),
            pltpu.VMEM((8, 128), F32),
        ],
        name="mixer_second",
    )(x, halo, weight, gate, grad, step_pad, params, docs, out_in, state)


def attention_kernel(q_ref, g_ref, docs_ref, *refs):
    blocks = REACH + 1
    kv_refs = refs[:blocks]
    dq_ref, own_ref = refs[blocks : blocks + 2]
    back_refs = refs[blocks + 2 : 2 * blocks + 1]
    neg_s = refs[2 * blocks + 1]
    docs = docs_ref[...].astype(F32)
    own = columns_of(docs[0:1])
    for gap in range(blocks):
        same = own == docs[gap : gap + 1]
        if gap == 0:
            same = same & (iota((T, T), 0) >= iota((T, T), 1))
        if gap == REACH:
            same = same & (iota((T, T), 1) > iota((T, T), 0))
        neg_s[gap] = jnp.where(same, 0.0, NEG)
    scale = HEAD_DIM ** (-0.5)
    for head in range(LOCAL_HEADS):
        start, stop = head * HEAD_DIM, (head + 1) * HEAD_DIM
        left, right = start // 128 * 128, -(-stop // 128) * 128
        window = slice(left, right)
        shared = start != left
        column = iota((T, right - left), 1) + left
        mine = (column >= start) & (column < stop)
        q = q_ref[:, window]
        g = g_ref[:, window]
        q = jnp.where(mine, q, jnp.zeros_like(q))
        g = jnp.where(mine, g, jnp.zeros_like(g))
        scores = []
        top = None
        for gap in range(blocks):
            s = dot(q, kv_refs[gap][0:T, window], NT) * scale + neg_s[gap]
            scores.append(s)
            peak = jnp.max(s, axis=1, keepdims=True)
            top = peak if top is None else jnp.maximum(top, peak)
        expos = [jnp.exp(s - top) for s in scores]
        total = sum(jnp.sum(e, axis=1, keepdims=True) for e in expos)
        inverse = 1.0 / jnp.maximum(total, 1.0)
        probs = [e * inverse for e in expos]
        halves = [p.astype(BF16) for p in probs]
        dprobs = [dot(g, kv_refs[gap][T : 2 * T, window], NT) for gap in range(blocks)]
        delta = sum(
            jnp.sum(h.astype(F32) * d, axis=1, keepdims=True) for h, d in zip(halves, dprobs)
        )
        dq = jnp.zeros((T, right - left), F32)

        def put(ref, rows, value):
            value = value.astype(ref.dtype)
            if shared:
                ref[rows, left : left + 128] += value[:, :128]
                ref[rows, left + 128 : right] = value[:, 128:]
            else:
                ref[rows, window] = value

        for gap in range(blocks):
            dscore = (probs[gap] * (dprobs[gap] - delta)).astype(BF16)
            dq = dq + dot(dscore, kv_refs[gap][0:T, window])
            ref = own_ref if gap == 0 else back_refs[gap - 1]
            put(ref, slice(0, T), dot(dscore, q, TN))
            put(ref, slice(T, 2 * T), dot(halves[gap], g, TN))
        put(dq_ref, slice(0, T), jnp.where(mine, dq * scale, 0.0))


def attention(queries, grads, docs, key_values):
    width = queries.shape[1]
    vmem = pl.BlockSpec(memory_space=pltpu.VMEM)
    both = jax.ShapeDtypeStruct((2 * T, width), BF16)
    return pl.pallas_call(
        attention_kernel,
        in_specs=[vmem] * (3 + REACH + 1),
        out_specs=[vmem] * (2 + REACH),
        out_shape=[
            jax.ShapeDtypeStruct((T, width), BF16),
            jax.ShapeDtypeStruct((2 * T, width), F32),
        ] + [both] * REACH,
        scratch_shapes=[pltpu.VMEM((REACH + 1, T, T), F32)],
        name="attention",
    )(queries, grads, docs, *key_values)


def passed_along(value, axis, steps):
    count = lax.axis_size(axis)
    initial, last = (max(0, -steps), min(count, count - steps))
    return lax.ppermute(value, axis, [(source, source + steps) for source in range(initial, last)])


def exchange(array, axis):
    return lax.all_to_all(array, axis, split_axis=0, concat_axis=0, tiled=True)


def from_everyone(array, axis):
    return exchange(jnp.broadcast_to(array, (lax.axis_size(axis), *array.shape)), axis)


def local(
    queries, keys, values, attn_grad, doc_ids, conv_input, conv_weight, step_raw, step_bias,
    rate_log, skip_gain, input_coeff, output_coeff, gate_input, mix_grad,
):
    heads = step_raw.shape[1]
    shard = lax.axis_index(SEQ)
    halo = passed_along(conv_input[T - 8 :], SEQ, 1)
    own = jnp.concatenate([keys, values], axis=0)
    key_values = [own] + [passed_along(own, SEQ, gap) for gap in range(1, REACH + 1)]

    doc_pad = jnp.concatenate([jnp.full((WINDOW,), -1, jnp.int32), doc_ids])
    doc_near = lax.dynamic_slice_in_dim(doc_pad, shard * T, WINDOW + T)
    docs = jnp.stack(
        [doc_near[WINDOW - T * gap : WINDOW - T * gap + T] for gap in range(REACH + 1)]
        + [doc_near[WINDOW - lag : WINDOW - lag + T] for lag in range(1, KERNEL)]
    )
    step_pad = jnp.pad(step_raw, ((0, 0), (0, 128 - heads)))
    params = jnp.pad(jnp.stack([step_bias, rate_log, skip_gain]), ((0, 5), (0, 128 - heads)))
    first = lax.axis_index("head") * heads < SSM_HEADS // GROUPS
    group_in = jnp.where(first, input_coeff[:, :STATE], input_coeff[:, STATE:])
    group_out = jnp.where(first, output_coeff[:, :STATE], output_coeff[:, STATE:])
    in_out = jnp.concatenate([group_in, group_out], axis=1)
    out_in = jnp.concatenate([group_out, group_in], axis=1)

    parts, through = mixer_first(
        conv_input, halo, conv_weight, gate_input, mix_grad, step_pad, params, docs, in_out
    )
    parts = jnp.concatenate(
        [
            parts.reshape(SHARDS, ROWS, 128),
            jnp.broadcast_to(through[None], (SHARDS, 8, 128)),
        ],
        axis=1,
    )
    slot = jnp.reshape(shard, (1,)).astype(jnp.int32)
    entering = exchange(chain(slot, exchange(parts, SEQ)), SEQ).reshape(COLS, 128)
    dx, tail, spill, dgate, dstep, coeff, dweight, small = mixer_second(
        conv_input, halo, conv_weight, gate_input, mix_grad, step_pad, params, docs, out_in,
        entering,
    )
    spilled = passed_along(spill, SEQ, -1)

    dq, own_grad, *back = attention(queries, attn_grad, docs, key_values)
    returned = [passed_along(piece, SEQ, -gap) for gap, piece in enumerate(back, 1)]

    coeffs = from_everyone(coeff, "head").astype(F32)
    low, high = coeffs[0] + coeffs[1], coeffs[2] + coeffs[3]
    sum_in = jnp.concatenate([low[:, STATE:], high[:, STATE:]], axis=1)
    sum_out = jnp.concatenate([low[:, :STATE], high[:, :STATE]], axis=1)

    bundle = jnp.concatenate([dweight.reshape(-1, 128).astype(BF16), small.astype(BF16)], axis=0)
    totals = jnp.sum(from_everyone(bundle, SEQ).astype(F32), axis=0)
    rows = KERNEL * COLS // 128
    grad_weight = totals[:rows].reshape(KERNEL, COLS)
    grad_bias, grad_rate, grad_skip = (
        totals[rows + 2 * n, :heads] + totals[rows + 2 * n + 1, :heads] for n in range(3)
    )

    tail = (tail + spilled).astype(BF16)
    grad_conv = lax.dynamic_update_slice_in_dim(dx, tail, T - 8, 0)

    total = own_grad
    for piece in returned:
        total = total + piece.astype(F32)
    grad_keys = (total[:T] * HEAD_DIM ** (-0.5)).astype(BF16)
    grad_values = total[T:].astype(BF16)
    return (
        dq, grad_keys, grad_values, grad_conv, dgate, dstep[:, :heads], sum_in, sum_out,
        grad_weight, grad_bias, grad_rate, grad_skip,
    )


def solution(mesh):
    finer = Mesh(
        mesh.devices.reshape(4, 2, 4, mesh.shape["head"]), ("seq_0", "seq_1", "seq_2", "head")
    )
    wide = P(SEQ, "head")
    return jax.shard_map(
        local,
        mesh=finer,
        in_specs=(
            wide, wide, wide, wide, P(), wide, P(None, "head"), wide, P("head"), P("head"),
            P("head"), P(SEQ, None), P(SEQ, None), wide, wide,
        ),
        out_specs=(
            wide, wide, wide, wide, wide, wide, P(SEQ, None), P(SEQ, None), P(None, "head"),
            P("head"), P("head"), P("head"),
        ),
        check_vma=False,
    )
```

profile of v0, /device:TPU:0, one launch (start us, length us, event | category | flops | bytes accessed | tf_op | source)
XLA Modules:
  0.0 225.7 jit_solution(1070335703021553433)
XLA Ops:
  1.4 3.5 %collective-permute-start.8 = (bf16[8,1792]{1,0:T(8,128)(2,1)S(1)}, bf16[8,1792]{1,0:T(8,128)(2,1)S(1)}, u32[]{:S(2)}, u32[]{:S(2)}) collective-permute-start(bf16[8,1792]{1,0:T(8,128)(2,1)S(1)} %slice.104), channel_id=1, source_target_pairs={{0,4},{4,8},{8,12},{12,16},{16,20},{20,24},{24,28},{28,32},{32,36}... | collective-permute-start | bytes 86024 | tf_op jit(solution)/shard_map/ppermute | solution.py:472
  4.9 1.1 constant_dynamic-update-slice_fusion.1
  6.0 1.0 slice_select_fusion
  8.7 1.3 select_maximum_fusion.par_ref
  12.8 8.9 %mixer_first.1 = (bf16[1792,128]{1,0:T(8,128)(2,1)}, bf16[8,128]{1,0:T(8,128)(2,1)}) custom-call(bf16[256,1792]{1,0:T(8,128)(2,1)} %x_ref.3, bf16[8,1792]{1,0:T(8,128)(2,1)} %copy-done.7, f32[4,1792]{1,0:T(4,128)} %weight_ref.3, bf16[256,1792]{1,0:T(8,128)(2,1)} %gate_ref.3, bf16[256,1792]{1,0:T(8,128)(2,1)} %grad_ref.3, f32[256,128]{1,0:T(8,128)} %pad.9.step_ref, ...), custom_call_target="tpu_custom_call" | custom-call | tf_op jit(solution)/shard_map/mixer_first/pallas_call | solution.py:161
  22.4 1.9 pad_maximum_fusion
  24.3 10.6 %all-to-all-start = ((bf16[32,64,128]{2,1,0:T(8,128)(2,1)}), bf16[32,64,128]{2,1,0:T(8,128)(2,1)S(1)}, u32[]{:S(2)}, u32[]{:S(2)}) async-start(bf16[32,64,128]{2,1,0:T(8,128)(2,1)} %pad_maximum_fusion), calls=%async_computation | async-start | bytes 1048576 | tf_op jit(solution)/shard_map/all_to_all | solution.py:476
  34.9 3.8 %collective-permute-start = (bf16[512,896]{1,0:T(8,128)(2,1)S(1)}, bf16[512,896]{1,0:T(8,128)(2,1)S(1)}, u32[]{:S(2)}, u32[]{:S(2)}) collective-permute-start(bf16[512,896]{1,0:T(8,128)(2,1)S(1)} %constant_dynamic-update-slice_fusion.refs_0_), channel_id=1, source_target_pairs={{0,4},{4,8},{8,12},{12,16},{16,20},{20,24},{24,28},{28,32},{32,36}... | collective-permute-start | bytes 2752520 | tf_op jit(solution)/shard_map/ppermute | solution.py:472
  38.7 4.6 %collective-permute-start.1 = (bf16[512,896]{1,0:T(8,128)(2,1)S(1)}, bf16[512,896]{1,0:T(8,128)(2,1)S(1)}, u32[]{:S(2)}, u32[]{:S(2)}) collective-permute-start(bf16[512,896]{1,0:T(8,128)(2,1)S(1)} %constant_dynamic-update-slice_fusion.refs_0_), channel_id=1, source_target_pairs={{0,8},{4,12},{8,16},{12,20},{16,24},{20,28},{24,32},{28,36},{32,40... | collective-permute-start | bytes 2752520 | tf_op jit(solution)/shard_map/ppermute | solution.py:472
  43.3 6.6 %collective-permute-start.2 = (bf16[512,896]{1,0:T(8,128)(2,1)S(1)}, bf16[512,896]{1,0:T(8,128)(2,1)}, u32[]{:S(2)}, u32[]{:S(2)}) collective-permute-start(bf16[512,896]{1,0:T(8,128)(2,1)S(1)} %constant_dynamic-update-slice_fusion.refs_0_), channel_id=1, source_target_pairs={{0,12},{4,16},{8,20},{12,24},{16,28},{20,32},{24,36},{28,40},{32,4... | collective-permute-start | bytes 2752520 | tf_op jit(solution)/shard_map/ppermute | solution.py:472
  49.9 3.5 %collective-permute-start.3 = (bf16[512,896]{1,0:T(8,128)(2,1)S(1)}, bf16[512,896]{1,0:T(8,128)(2,1)}, u32[]{:S(2)}, u32[]{:S(2)}) collective-permute-start(bf16[512,896]{1,0:T(8,128)(2,1)S(1)} %constant_dynamic-update-slice_fusion.refs_0_), channel_id=1, source_target_pairs={{0,16},{4,20},{8,24},{12,28},{16,32},{20,36},{24,40},{28,44},{32,4... | collective-permute-start | bytes 2752520 | tf_op jit(solution)/shard_map/ppermute | solution.py:472
  54.2 2.3 %chain.1 = bf16[32,56,128]{2,1,0:T(8,128)(2,1)} custom-call(s32[1]{0:T(128)} %bitcast.11.slot_ref, bf16[32,64,128]{2,1,0:T(8,128)(2,1)} %copy-done), custom_call_target="tpu_custom_call" | custom-call | tf_op jit(solution)/shard_map/chain/pallas_call | solution.py:202
  56.5 5.8 %all-to-all-start.1 = ((bf16[32,56,128]{2,1,0:T(8,128)(2,1)}), bf16[32,56,128]{2,1,0:T(8,128)(2,1)S(1)}, u32[]{:S(2)}, u32[]{:S(2)}) async-start(bf16[32,56,128]{2,1,0:T(8,128)(2,1)} %chain.1), calls=%async_computation.1 | async-start | bytes 917504 | tf_op jit(solution)/shard_map/all_to_all | solution.py:476
  62.4 18.5 %collective-permute-done.1.refs_2_ = bf16[512,896]{1,0:T(8,128)(2,1)S(1)} collective-permute-done((bf16[512,896]{1,0:T(8,128)(2,1)S(1)}, bf16[512,896]{1,0:T(8,128)(2,1)S(1)}, u32[]{:S(2)}, u32[]{:S(2)}) %collective-permute-start.1) | collective-permute-done | bytes 917536 | tf_op jit(solution)/shard_map/ppermute | solution.py:472
  80.9 2.4 %collective-permute-done.2.refs_3_ = bf16[512,896]{1,0:T(8,128)(2,1)} collective-permute-done((bf16[512,896]{1,0:T(8,128)(2,1)S(1)}, bf16[512,896]{1,0:T(8,128)(2,1)}, u32[]{:S(2)}, u32[]{:S(2)}) %collective-permute-start.2) | collective-permute-done | bytes 917536 | tf_op jit(solution)/shard_map/ppermute | solution.py:472
  83.3 41.6 %collective-permute-done.3.refs_4_ = bf16[512,896]{1,0:T(8,128)(2,1)} collective-permute-done((bf16[512,896]{1,0:T(8,128)(2,1)S(1)}, bf16[512,896]{1,0:T(8,128)(2,1)}, u32[]{:S(2)}, u32[]{:S(2)}) %collective-permute-start.3) | collective-permute-done | bytes 917536 | tf_op jit(solution)/shard_map/ppermute | solution.py:472
  124.8 12.3 %attention.1 = (bf16[256,896]{1,0:T(8,128)(2,1)}, f32[512,896]{1,0:T(8,128)}, bf16[512,896]{1,0:T(8,128)(2,1)}, bf16[512,896]{1,0:T(8,128)(2,1)}, bf16[512,896]{1,0:T(8,128)(2,1)}, /*index=5*/bf16[512,896]{1,0:T(8,128)(2,1)}) custom-call(bf16[256,896]{1,0:T(8,128)(2,1)} %q_ref.1, bf16[256,896]{1,0:T(8,128)(2,1)} %g_ref.1, s32[8,256]{1,0:T(8,128)} %stack.47.docs_ref, ...), custom_call_target="tpu_custom_call" | custom-call | tf_op jit(solution)/shard_map/attention/pallas_call | solution.py:456
  137.1 1.3 collective-permute-start.7
  138.4 1.3 collective-permute-start.6
  139.7 1.3 collective-permute-start.5
  141.0 1.5 collective-permute-start.4
  143.3 18.6 %mixer_second.1 = (bf16[256,1792]{1,0:T(8,128)(2,1)}, f32[8,1792]{1,0:T(8,128)}, f32[8,1792]{1,0:T(8,128)}, bf16[256,1792]{1,0:T(8,128)(2,1)}, f32[256,128]{1,0:...) custom-call(bf16[256,1792]{1,0:T(8,128)(2,1)} %x_ref.3, bf16[8,1792]{1,0:T(8,128)(2,1)} %copy-done.7, ...), custom_call_target="tpu_custom_call" | custom-call | tf_op jit(solution)/shard_map/mixer_second/pallas_call | solution.py:354
  161.9 1.3 collective-permute-start.9
  163.2 1.6 copy.30
  164.8 1.6 broadcast_in_dim.14
  166.4 3.4 %all-to-all-start.2 = ((bf16[4,256,128]{2,1,0:T(8,128)(2,1)}), bf16[4,256,128]{2,1,0:T(8,128)(2,1)S(1)}, u32[]{:S(2)}, u32[]{:S(2)}) async-start(bf16[4,256,128]{2,1,0:T(8,128)(2,1)} %broadcast_in_dim.14), calls=%async_computation.2 | async-start | bytes 524288 | tf_op jit(solution)/shard_map/all_to_all | solution.py:476
  171.3 1.4 fusion.3
  172.7 3.1 %all-to-all-done.2 = bf16[4,256,128]{2,1,0:T(8,128)(2,1)S(1)} async-done(((bf16[4,256,128]{2,1,0:T(8,128)(2,1)}), bf16[4,256,128]{2,1,0:T(8,128)(2,1)S(1)}, u32[]{:S(2)}, u32[]{:S(2)}) %all-to-all-start.2) | async-done | bytes 262176 | tf_op jit(solution)/shard_map/all_to_all | solution.py:476
  175.8 1.0 broadcast_in_dim.15
  176.7 30.5 %all-to-all-start.3 = ((bf16[32,64,128]{2,1,0:T(8,128)(2,1)}), bf16[32,64,128]{2,1,0:T(8,128)(2,1)S(1)}, u32[]{:S(2)}, u32[]{:S(2)}) async-start(bf16[32,64,128]{2,1,0:T(8,128)(2,1)} %broadcast_in_dim.15), calls=%async_computation.3 | async-start | bytes 1048576 | tf_op jit(solution)/shard_map/all_to_all | solution.py:476
  209.1 11.5 %all-to-all-done.3 = bf16[32,64,128]{2,1,0:T(8,128)(2,1)S(1)} async-done(((bf16[32,64,128]{2,1,0:T(8,128)(2,1)}), bf16[32,64,128]{2,1,0:T(8,128)(2,1)S(1)}, u32[]{:S(2)}, u32[]{:S(2)}) %all-to-all-start.3) | async-done | bytes 524320 | tf_op jit(solution)/shard_map/all_to_all | solution.py:476
  221.8 2.2 convert_add_fusion
  (49 shorter events, 13.7 us)
Async XLA Ops:
  1.4 10.8 %collective-permute-start.8 = (bf16[8,1792]{1,0:T(8,128)(2,1)S(1)}, bf16[8,1792]{1,0:T(8,128)(2,1)S(1)}, u32[]{:S(2)}, u32[]{:S(2)}) collective-permute-start(bf16[8,1792]{1,0:T(8,128)(2,1)S(1)} %slice.104), channel_id=1, source_target_pairs={{0,4},{4,8},{8,12},{12,16},{16,20},{20,24},{24,28},{28,32},{32,36}... | collective-permute-start | bytes 86024 | tf_op jit(solution)/shard_map/ppermute | solution.py:472
  12.2 0.6 copy-start.7
  21.7 13.2 %copy-start.6 = (bf16[256,896]{1,0:T(8,128)(2,1)S(1)}, bf16[256,896]{1,0:T(8,128)(2,1)}, u32[]{:S(2)}) copy-start(bf16[256,896]{1,0:T(8,128)(2,1)} %param.17) | copy-start | bytes 1376260
  24.3 29.1 %all-to-all-start = ((bf16[32,64,128]{2,1,0:T(8,128)(2,1)}), bf16[32,64,128]{2,1,0:T(8,128)(2,1)S(1)}, u32[]{:S(2)}, u32[]{:S(2)}) async-start(bf16[32,64,128]{2,1,0:T(8,128)(2,1)} %pad_maximum_fusion), calls=%async_computation | async-start | bytes 1048576 | tf_op jit(solution)/shard_map/all_to_all | solution.py:476
  34.9 89.9 %copy-start.1 = (bf16[512,896]{1,0:T(8,128)(2,1)}, bf16[512,896]{1,0:T(8,128)(2,1)S(1)}, u32[]{:S(2)}) copy-start(bf16[512,896]{1,0:T(8,128)(2,1)S(1)} %constant_dynamic-update-slice_fusion.refs_0_) | copy-start | bytes 2752516
  34.9 27.4 %collective-permute-start = (bf16[512,896]{1,0:T(8,128)(2,1)S(1)}, bf16[512,896]{1,0:T(8,128)(2,1)S(1)}, u32[]{:S(2)}, u32[]{:S(2)}) collective-permute-start(bf16[512,896]{1,0:T(8,128)(2,1)S(1)} %constant_dynamic-update-slice_fusion.refs_0_), channel_id=1, source_target_pairs={{0,4},{4,8},{8,12},{12,16},{16,20},{20,24},{24,28},{28,32},{32,36}... | collective-permute-start | bytes 2752520 | tf_op jit(solution)/shard_map/ppermute | solution.py:472
  38.7 42.2 %collective-permute-start.1 = (bf16[512,896]{1,0:T(8,128)(2,1)S(1)}, bf16[512,896]{1,0:T(8,128)(2,1)S(1)}, u32[]{:S(2)}, u32[]{:S(2)}) collective-permute-start(bf16[512,896]{1,0:T(8,128)(2,1)S(1)} %constant_dynamic-update-slice_fusion.refs_0_), channel_id=1, source_target_pairs={{0,8},{4,12},{8,16},{12,20},{16,24},{20,28},{24,32},{28,36},{32,40... | collective-permute-start | bytes 2752520 | tf_op jit(solution)/shard_map/ppermute | solution.py:472
  43.3 40.0 %collective-permute-start.2 = (bf16[512,896]{1,0:T(8,128)(2,1)S(1)}, bf16[512,896]{1,0:T(8,128)(2,1)}, u32[]{:S(2)}, u32[]{:S(2)}) collective-permute-start(bf16[512,896]{1,0:T(8,128)(2,1)S(1)} %constant_dynamic-update-slice_fusion.refs_0_), channel_id=1, source_target_pairs={{0,12},{4,16},{8,20},{12,24},{16,28},{20,32},{24,36},{28,40},{32,4... | collective-permute-start | bytes 2752520 | tf_op jit(solution)/shard_map/ppermute | solution.py:472
  49.9 74.9 %collective-permute-start.3 = (bf16[512,896]{1,0:T(8,128)(2,1)S(1)}, bf16[512,896]{1,0:T(8,128)(2,1)}, u32[]{:S(2)}, u32[]{:S(2)}) collective-permute-start(bf16[512,896]{1,0:T(8,128)(2,1)S(1)} %constant_dynamic-update-slice_fusion.refs_0_), channel_id=1, source_target_pairs={{0,16},{4,20},{8,24},{12,28},{16,32},{20,36},{24,40},{28,44},{32,4... | collective-permute-start | bytes 2752520 | tf_op jit(solution)/shard_map/ppermute | solution.py:472
  53.4 0.8 copy-start
  56.5 86.0 %all-to-all-start.1 = ((bf16[32,56,128]{2,1,0:T(8,128)(2,1)}), bf16[32,56,128]{2,1,0:T(8,128)(2,1)S(1)}, u32[]{:S(2)}, u32[]{:S(2)}) async-start(bf16[32,56,128]{2,1,0:T(8,128)(2,1)} %chain.1), calls=%async_computation.1 | async-start | bytes 917504 | tf_op jit(solution)/shard_map/all_to_all | solution.py:476
  62.4 62.5 %copy-start.4 = (bf16[512,896]{1,0:T(8,128)(2,1)}, bf16[512,896]{1,0:T(8,128)(2,1)S(1)}, u32[]{:S(2)}) copy-start(bf16[512,896]{1,0:T(8,128)(2,1)S(1)} %collective-permute-done.refs_1_) | copy-start | bytes 2752516
  80.9 43.9 %copy-start.5 = (bf16[512,896]{1,0:T(8,128)(2,1)}, bf16[512,896]{1,0:T(8,128)(2,1)S(1)}, u32[]{:S(2)}) copy-start(bf16[512,896]{1,0:T(8,128)(2,1)S(1)} %collective-permute-done.1.refs_2_) | copy-start | bytes 2752516
  137.1 84.7 %collective-permute-start.7 = (bf16[512,896]{1,0:T(8,128)(2,1)}, bf16[512,896]{1,0:T(8,128)(2,1)S(1)}, u32[]{:S(2)}, u32[]{:S(2)}) collective-permute-start(bf16[512,896]{1,0:T(8,128)(2,1)} %get-tuple-element.33), channel_id=1, source_target_pairs={{16,0},{20,4},{24,8},{28,12},{32,16},{36,20},{40,24},{44,28},{48,3... | collective-permute-start | bytes 2752520 | tf_op jit(solution)/shard_map/ppermute | solution.py:472
  138.4 83.4 %collective-permute-start.6 = (bf16[512,896]{1,0:T(8,128)(2,1)}, bf16[512,896]{1,0:T(8,128)(2,1)}, u32[]{:S(2)}, u32[]{:S(2)}) collective-permute-start(bf16[512,896]{1,0:T(8,128)(2,1)} %get-tuple-element.32), channel_id=1, source_target_pairs={{12,0},{16,4},{20,8},{24,12},{28,16},{32,20},{36,24},{40,28},{44,3... | collective-permute-start | bytes 2752520 | tf_op jit(solution)/shard_map/ppermute | solution.py:472
  139.7 82.1 %collective-permute-start.5 = (bf16[512,896]{1,0:T(8,128)(2,1)}, bf16[512,896]{1,0:T(8,128)(2,1)}, u32[]{:S(2)}, u32[]{:S(2)}) collective-permute-start(bf16[512,896]{1,0:T(8,128)(2,1)} %get-tuple-element.31), channel_id=1, source_target_pairs={{8,0},{12,4},{16,8},{20,12},{24,16},{28,20},{32,24},{36,28},{40,32... | collective-permute-start | bytes 2752520 | tf_op jit(solution)/shard_map/ppermute | solution.py:472
  141.0 80.8 %collective-permute-start.4 = (bf16[512,896]{1,0:T(8,128)(2,1)}, bf16[512,896]{1,0:T(8,128)(2,1)}, u32[]{:S(2)}, u32[]{:S(2)}) collective-permute-start(bf16[512,896]{1,0:T(8,128)(2,1)} %get-tuple-element.30), channel_id=1, source_target_pairs={{4,0},{8,4},{12,8},{16,12},{20,16},{24,20},{28,24},{32,28},{36,32}... | collective-permute-start | bytes 2752520 | tf_op jit(solution)/shard_map/ppermute | solution.py:472
  142.5 0.8 copy-start.3
  161.9 9.4 %collective-permute-start.9 = (f32[8,1792]{1,0:T(8,128)}, f32[8,1792]{1,0:T(8,128)S(1)}, u32[]{:S(2)}, u32[]{:S(2)}) collective-permute-start(f32[8,1792]{1,0:T(8,128)} %get-tuple-element.38), channel_id=1, source_target_pairs={{4,0},{8,4},{12,8},{16,12},{20,16},{24,20},{28,24},{32,28},{36,32}... | collective-permute-start | bytes 172040 | tf_op jit(solution)/shard_map/ppermute | solution.py:472
  166.4 9.4 %all-to-all-start.2 = ((bf16[4,256,128]{2,1,0:T(8,128)(2,1)}), bf16[4,256,128]{2,1,0:T(8,128)(2,1)S(1)}, u32[]{:S(2)}, u32[]{:S(2)}) async-start(bf16[4,256,128]{2,1,0:T(8,128)(2,1)} %broadcast_in_dim.14), calls=%async_computation.2 | async-start | bytes 524288 | tf_op jit(solution)/shard_map/all_to_all | solution.py:476
  176.7 43.8 %all-to-all-start.3 = ((bf16[32,64,128]{2,1,0:T(8,128)(2,1)}), bf16[32,64,128]{2,1,0:T(8,128)(2,1)S(1)}, u32[]{:S(2)}, u32[]{:S(2)}) async-start(bf16[32,64,128]{2,1,0:T(8,128)(2,1)} %broadcast_in_dim.15), calls=%async_computation.3 | async-start | bytes 1048576 | tf_op jit(solution)/shard_map/all_to_all | solution.py:476
  207.3 14.5 %copy-start.2 = (f32[512,896]{1,0:T(8,128)S(1)}, f32[512,896]{1,0:T(8,128)}, u32[]{:S(2)}) copy-start(f32[512,896]{1,0:T(8,128)} %get-tuple-element.29) | copy-start | bytes 5505028
where the time goes:
time: 227 us; the launch traced here: 226 us
  starting transfers between devices  78.9 us (35%)
  waiting for transfers between devices  77 us (34%)
  Pallas kernels  42.1 us (19%)
  local copies, waits for them, and re-layouts  13.7 us (6%)
  other arithmetic  13.1 us (6%)
    ppermute x10, waiting for transfers between devices, passed_along(): lax.ppermute(value, axis, [(source, source + steps) for source in range(i...  62.5 us
    all_to_all x4, starting transfers between devices, exchange(): return lax.all_to_all(array, axis, split_axis=0, concat_axis=0, tiled=True)  50.3 us
    ppermute x10, starting transfers between devices, passed_along(): lax.ppermute(value, axis, [(source, source + steps) for source in range(i...  28.6 us
    pallas_call x1, Pallas kernels, mixer_second(): pl.pallas_call(mixer_second_kernel, grid=(STEPS,), in_specs=[column_block...  18.6 us
    all_to_all x4, waiting for transfers between devices, exchange(): return lax.all_to_all(array, axis, split_axis=0, concat_axis=0, tiled=True)  14.5 us
    pallas_call x1, Pallas kernels, attention(): pl.pallas_call(attention_kernel, in_specs=[vmem] * (3 + REACH + 1), out_s...  12.3 us
    pallas_call x1, Pallas kernels, mixer_first(): pl.pallas_call(mixer_first_kernel, grid=(STEPS,), in_specs=[column_block(...  8.88 us
    unnamed x19, local copies, waits for them, and re-layouts  5.72 us
  transfers between devices with their start and end apart: 14, of which 5 were waited for; matrix products, arithmetic and copies ran while one was open for 8% of the time, Pallas kernels for 15%

commit v1 on v0

v1 whole, which is shorter than its diff:
```python
import jax
import jax.numpy as jnp
from jax import lax
from jax.experimental import pallas as pl
from jax.experimental.pallas import tpu as pltpu
from jax.sharding import Mesh
from jax.sharding import PartitionSpec as P

HEAD_DIM = 224
WINDOW = 1024
SSM_HEADS = 112
STATE = 64
GROUPS = 2
KERNEL = 4
SEQ = ("seq_0", "seq_1", "seq_2")
SHARDS = 32
T = 256
LOCAL_HEADS = 4
REACH = WINDOW // T
BLK = 256
HEADS_BLK = BLK // 64
COLS = 1792
STEPS = COLS // BLK
NEG = -1e30
F32 = jnp.float32
BF16 = jnp.bfloat16

NN = (((1,), (0,)), ((), ()))
NT = (((1,), (1,)), ((), ()))
TN = (((0,), (0,)), ((), ()))


def dot(a, b, dims=NN):
    return lax.dot_general(a, b, dims, preferred_element_type=F32)


def exact(a, b, dims=NN):
    return lax.dot_general(
        a, b, dims, preferred_element_type=F32, precision=lax.Precision.HIGHEST
    )


def split(a, pieces):
    parts = []
    for _ in range(pieces):
        part = a.astype(BF16)
        parts.append(part)
        a = a - part.astype(F32)
    return parts


def sigmoid(v):
    return 1.0 / (1.0 + jnp.exp(-v))


def iota(shape, dim):
    return lax.broadcasted_iota(jnp.int32, shape, dim)


def columns_of(row):
    return jnp.transpose(jnp.broadcast_to(row, (T, T)))


def whole(shape):
    return pl.BlockSpec(shape, lambda c: (0,) * len(shape))


def column_block(rows):
    return pl.BlockSpec((rows, BLK), lambda c: (0, c))


IN_SMEM = pl.BlockSpec(memory_space=pltpu.SMEM)
IN_VMEM = pl.BlockSpec(memory_space=pltpu.VMEM)


PARAM_ROWS = 3


def doc_rows(where_ref, docs_ref):
    shard = where_ref[0]
    own = docs_ref[pl.ds(shard, 1), :].astype(F32)
    before = docs_ref[pl.ds(jnp.maximum(shard - 1, 0), 1), :].astype(F32)
    return own, jnp.where(shard == 0, -1.0, before)


def group_halves(where_ref, coeff_ref):
    coeff = coeff_ref[...].astype(F32)
    turned = pltpu.roll(coeff, STATE, 1)
    first = where_ref[1] == 0
    low = iota((T, 128), 1) < STATE
    mine_low = jnp.where(low, jnp.where(first, coeff, turned), 0.0)
    mine_high = jnp.where(low, 0.0, jnp.where(first, turned, coeff))
    return mine_low.astype(BF16), mine_high.astype(BF16)


def padded_params(bias_ref, rate_ref, skip_ref, params_s):
    heads = bias_ref.shape[1]
    params_s[...] = jnp.zeros((8, 128), F32)
    for n, ref in enumerate((bias_ref, rate_ref, skip_ref)):
        params_s[n : n + 1, 0:heads] = ref[...]
    return params_s[...]


def raw_steps(step_ref):
    rows = step_ref.shape[0]
    filled = jnp.concatenate([step_ref[...], jnp.zeros((128 - rows, T), F32)], axis=0)
    return jnp.transpose(filled)


def step_and_decay(raw, params):
    step = jnp.maximum(raw, 0.0) + jnp.log1p(jnp.exp(-jnp.abs(raw)))
    return step, -step * jnp.exp(params[1:2])


def token_setup(where_ref, docs_ref, step_ref, params, cum_s, step_s, mask_s, prev_s, end_s):
    own_row, before_row = doc_rows(where_ref, docs_ref)
    own = columns_of(own_row)
    lane = iota((8, T), 1)
    own8 = jnp.broadcast_to(own_row, (8, T))
    before8 = jnp.broadcast_to(before_row, (8, T))
    for lag in range(1, KERNEL):
        lagged = jnp.where(lane < lag, pltpu.roll(before8, lag, 1), pltpu.roll(own8, lag, 1))
        mask_s[lag - 1] = jnp.where(own == columns_of(lagged[0:1]), 1.0, 0.0)
    prev_s[...] = jnp.where(own == before_row[:, T - 1 : T], 0.0, NEG)
    end_s[...] = jnp.where(own == own_row[:, T - 1 : T], 0.0, NEG)
    raw = raw_steps(step_ref) + params[0:1]
    step, decay = step_and_decay(raw, params)
    lower = jnp.where(iota((T, T), 0) >= iota((T, T), 1), 1.0, 0.0)
    cum = exact(lower, decay)
    for n, part in enumerate(split(cum, 3)):
        cum_s[n] = part
    for n, part in enumerate(split(step, 2)):
        step_s[n] = part
    return own, own_row, cum


def spread_of(step_id):
    head = iota((128, BLK), 0)
    owner = step_id * HEADS_BLK + iota((128, BLK), 1) // 64
    return jnp.where(head == owner, 1.0, 0.0).astype(BF16)


def block_gains(step_id, cum_s, step_s, prev_s, end_s):
    spread = spread_of(step_id)
    cum = dot(cum_s[0], spread) + dot(cum_s[1], spread) + dot(cum_s[2], spread)
    step = dot(step_s[0], spread) + dot(step_s[1], spread)
    enter = jnp.exp(cum + prev_s[...])
    to_end = jnp.exp(cum[T - 1 : T] - cum + end_s[...])
    return spread, cum, step, enter, to_end


def conv_pre(x, halo, weight, mask_s):
    extended = jnp.concatenate([halo.astype(F32), x.astype(F32)], axis=0)
    shifted = [extended[8:]]
    summed = weight[0:1] * shifted[0]
    for lag in range(1, KERNEL):
        moved = pltpu.roll(extended, lag, 0)[8:] * mask_s[lag - 1]
        shifted.append(moved)
        summed = summed + weight[lag : lag + 1] * moved
    return summed, shifted


ROWS = COLS // SHARDS
GROUPS8 = ROWS // 8
SLOT = ROWS + 8


def mixer_first_kernel(
    where_ref, x_ref, halo_ref, weight_ref, gate_ref, grad_ref, step_ref, bias_ref, rate_ref,
    skip_ref, docs_ref, in_ref, out_ref,
    parts_ref,
    cum_s, step_s, mask_s, prev_s, end_s, params_s, state_s, in_s, out_s,
):
    step_id = pl.program_id(0)

    @pl.when(step_id == 0)
    def _():
        params = padded_params(bias_ref, rate_ref, skip_ref, params_s)
        cum = token_setup(
            where_ref, docs_ref, step_ref, params, cum_s, step_s, mask_s, prev_s, end_s
        )[2]
        through = jnp.exp(cum[T - 1 : T] + prev_s[T - 1 : T, 0:1])
        high, low = split(through, 2)
        row = iota((8, 128), 0)
        both = jnp.where(row == 0, high.astype(F32), jnp.where(row == 1, low.astype(F32), 0.0))
        for shard in range(SHARDS):
            state_s[SLOT * shard + ROWS : SLOT * (shard + 1)] = both
        in_s[...] = group_halves(where_ref, in_ref)[0]
        out_s[...] = group_halves(where_ref, out_ref)[1]

    _, _, step, enter, to_end = block_gains(step_id, cum_s, step_s, prev_s, end_s)
    pre, _ = conv_pre(x_ref[...], halo_ref[...], weight_ref[...], mask_s)
    act = pre * sigmoid(pre)
    gate = gate_ref[...].astype(F32)
    out_grad = grad_ref[...].astype(F32) * gate * sigmoid(gate)
    ended = (act * step * to_end).astype(BF16)
    entered = (out_grad * enter).astype(BF16)
    state = dot(ended, in_s[...], TN) + dot(entered, out_s[...], TN)
    for part in range(BLK // 8):
        place = step_id * (BLK // 8) + part
        target = lax.div(place, GROUPS8)
        offset = SLOT * target + 8 * (place - GROUPS8 * target)
        state_s[pl.ds(pl.multiple_of(offset, 8), 8), :] = state[8 * part : 8 * part + 8]

    @pl.when(step_id == STEPS - 1)
    def _():
        parts_ref[...] = state_s[...].astype(BF16)


TOKEN_SCRATCH = [
    pltpu.VMEM((3, T, 128), BF16),
    pltpu.VMEM((2, T, 128), BF16),
    pltpu.VMEM((KERNEL - 1, T, BLK), F32),
    pltpu.VMEM((T, BLK), F32),
    pltpu.VMEM((T, BLK), F32),
    pltpu.VMEM((8, 128), F32),
]


def mixer_specs(heads):
    return [
        IN_SMEM, column_block(T), column_block(8), column_block(KERNEL), column_block(T),
        column_block(T), whole((heads, T)), whole((1, heads)), whole((1, heads)),
        whole((1, heads)), whole((SHARDS, T)), whole((T, 128)), whole((T, 128)),
    ]


def mixer_first(*arrays):
    heads = arrays[6].shape[0]
    return pl.pallas_call(
        mixer_first_kernel,
        grid=(STEPS,),
        in_specs=mixer_specs(heads),
        out_specs=whole((SHARDS * SLOT, 128)),
        out_shape=jax.ShapeDtypeStruct((SHARDS * SLOT, 128), BF16),
        scratch_shapes=TOKEN_SCRATCH + [
            pltpu.VMEM((SHARDS * SLOT, 128), F32),
            pltpu.VMEM((T, 128), BF16),
            pltpu.VMEM((T, 128), BF16),
        ],
        cost_estimate=pl.CostEstimate(flops=8 * 10**9, bytes_accessed=4 * 10**6, transcendentals=0),
        name="mixer_first",
    )(*arrays)


def chain_kernel(where_ref, parts_ref, out_ref, forward_s):
    slot = where_ref[0]
    owner = (slot * ROWS + iota((ROWS, 128), 0)) // 64
    choose = jnp.where(owner == iota((ROWS, 128), 1), 1.0, 0.0)
    lane = iota((ROWS, 128), 1)
    through = []
    carry = jnp.zeros((ROWS, 128), F32)
    for shard in range(SHARDS):
        row = parts_ref[shard, ROWS : ROWS + 1].astype(F32)
        row = row + parts_ref[shard, ROWS + 1 : ROWS + 2].astype(F32)
        gain = jnp.sum(choose * row, axis=1, keepdims=True)
        through.append(gain)
        forward_s[shard] = carry
        carry = gain * carry + parts_ref[shard, 0:ROWS].astype(F32)
    carry = jnp.zeros((ROWS, 128), F32)
    for shard in reversed(range(SHARDS)):
        out_ref[shard] = jnp.where(lane < STATE, forward_s[shard], carry).astype(BF16)
        carry = through[shard] * carry + parts_ref[shard, 0:ROWS].astype(F32)


def chain(where, parts):
    return pl.pallas_call(
        chain_kernel,
        in_specs=[IN_SMEM, IN_VMEM],
        out_specs=IN_VMEM,
        out_shape=jax.ShapeDtypeStruct((SHARDS, ROWS, 128), BF16),
        scratch_shapes=[pltpu.VMEM((SHARDS, ROWS, 128), F32)],
        cost_estimate=pl.CostEstimate(flops=2 * 10**9, bytes_accessed=10**6, transcendentals=0),
        name="chain",
    )(where, parts)


BUNDLE = KERNEL * COLS // 128
LANES_BLK = BLK // 128


def mixer_second_kernel(
    where_ref, x_ref, halo_ref, weight_ref, gate_ref, grad_ref, step_ref, bias_ref, rate_ref,
    skip_ref, docs_ref, in_ref, out_ref, state_ref,
    dx_ref, tail_ref, spill_ref, dgate_ref, dstep_ref, coeff_ref, bundle_ref,
    cum_s, step_s, mask_s, prev_s, end_s, params_s,
    cumt_s, pair_s, causal_s, dpair_s, coeff_s, row_s, dt_s, ends_s, bundle_s,
    in_low_s, in_high_s, out_low_s, out_high_s,
):
    step_id = pl.program_id(0)
    lane = iota((T, 128), 1)

    @pl.when(step_id == 0)
    def _():
        params = padded_params(bias_ref, rate_ref, skip_ref, params_s)
        own, own_row, cum = token_setup(
            where_ref, docs_ref, step_ref, params, cum_s, step_s, mask_s, prev_s, end_s
        )
        cumt_s[...] = jnp.transpose(cum)
        same = (own == own_row) & (iota((T, T), 0) >= iota((T, T), 1))
        causal_s[...] = jnp.where(same, 0.0, NEG)
        in_low_s[...], in_high_s[...] = group_halves(where_ref, in_ref)
        out_low_s[...], out_high_s[...] = group_halves(where_ref, out_ref)
        pair_s[...] = dot(out_low_s[...], in_low_s[...], NT)
        dpair_s[...] = jnp.zeros((T, T), F32)
        coeff_s[...] = jnp.zeros((T, 128), F32)
        row_s[...] = jnp.zeros((T, 128), F32)
        dt_s[...] = jnp.zeros((T, 128), F32)
        ends_s[...] = jnp.zeros((8, 128), F32)

    out_low = out_low_s[...]
    in_high = in_high_s[...]
    spread, cum, step, enter, to_end = block_gains(step_id, cum_s, step_s, prev_s, end_s)
    skip = sum(dot(part, spread) for part in split(params_s[...], 3))[2:3]
    weight = weight_ref[...]
    pre, shifted = conv_pre(x_ref[...], halo_ref[...], weight, mask_s)
    sig = sigmoid(pre)
    act = pre * sig
    gate = gate_ref[...].astype(F32)
    gate_sig = sigmoid(gate)
    mix_grad = grad_ref[...].astype(F32)
    out_grad = mix_grad * gate * gate_sig
    scaled = act * step
    scaled_half = scaled.astype(BF16)
    grad_half = out_grad.astype(BF16)

    block_head = iota((T, BLK), 1) // 64
    inner = jnp.zeros((T, BLK), F32)
    dscaled = jnp.zeros((T, BLK), F32)
    dpair = dpair_s[...]
    for k in range(HEADS_BLK):
        mine = block_head == k
        cum_col = jnp.broadcast_to(cum[:, 64 * k : 64 * k + 1], (T, T))
        cum_row = cumt_s[pl.ds(step_id * HEADS_BLK + k, 1), :]
        weights = jnp.exp(cum_col - cum_row + causal_s[...])
        mixing = (pair_s[...] * weights).astype(BF16)
        scaled_k = jnp.where(mine, scaled_half, jnp.zeros_like(scaled_half))
        grad_k = jnp.where(mine, grad_half, jnp.zeros_like(grad_half))
        inner = inner + dot(mixing, scaled_k)
        dscaled = dscaled + dot(mixing, grad_k, TN)
        dpair = dpair + dot(grad_k, scaled_half, NT) * weights
    dpair_s[...] = dpair

    state = state_ref[...]
    carried = dot(out_low, state, NT) * enter
    from_end = dot(in_high, state, NT) * to_end
    ssm_out = inner + carried
    dscaled = dscaled + from_end
    mixed_out = ssm_out + skip * act
    dgate_ref[...] = (
        mix_grad * mixed_out * gate_sig * (1.0 + gate * (1.0 - gate_sig))
    ).astype(BF16)

    gave_out = dot((out_grad * enter).astype(BF16), state)
    gave_in = dot((scaled * to_end).astype(BF16), state)
    coeff_s[...] += jnp.where(lane < STATE, gave_out, gave_in)

    grad_round = grad_half.astype(F32)
    scaled_round = scaled_half.astype(F32)
    balance = grad_round * ssm_out - scaled_round * dscaled
    row_s[...] += sum(dot(part, spread, NT) for part in split(balance, 3))
    dt_s[...] += sum(dot(part, spread, NT) for part in split(dscaled * act, 2))

    state_wide = state.astype(F32)
    product = state_wide * pltpu.roll(state_wide, STATE, 1)
    through = jnp.sum(jnp.where(iota((BLK, 128), 1) < STATE, product, 0.0), axis=1, keepdims=True)
    through_row = jnp.transpose(jnp.broadcast_to(through, (BLK, BLK)))[0:1]
    end_row = jnp.sum(scaled_round * from_end, axis=0, keepdims=True)
    end_row = end_row + through_row * enter[T - 1 : T]
    skip_row = jnp.sum(out_grad * act, axis=0, keepdims=True)
    row8 = iota((8, BLK), 0)
    both = jnp.where(row8 == 0, end_row, jnp.where(row8 == 1, skip_row, 0.0))
    ends_s[...] += sum(dot(part, spread, NT) for part in split(both, 3))

    dact = step * dscaled + skip * out_grad
    dpre = dact * sig * (1.0 + pre * (1.0 - sig))
    zeros = jnp.zeros((8, BLK), F32)
    dx = weight[0:1] * dpre
    spill = zeros
    for lag in range(KERNEL):
        tap = jnp.sum(dpre * shifted[lag], axis=0, keepdims=True)
        for m in range(LANES_BLK):
            place = lag * (COLS // 128) + step_id * LANES_BLK + m
            bundle_s[pl.ds(place, 1), :] = tap[:, 128 * m : 128 * (m + 1)]
        if lag == 0:
            continue
        masked = dpre * mask_s[lag - 1]
        later = pltpu.roll(jnp.concatenate([masked, zeros], axis=0), T + 8 - lag, 0)[:T]
        dx = dx + weight[lag : lag + 1] * later
        edge = pltpu.roll(jnp.concatenate([zeros, masked[:8]], axis=0), 16 - lag, 0)[:8]
        spill = spill + weight[lag : lag + 1] * edge
    dx_ref[...] = dx.astype(BF16)
    tail_ref[...] = dx[T - 8 :]
    spill_ref[...] = spill

    @pl.when(step_id == STEPS - 1)
    def _():
        params = params_s[...]
        raw = raw_steps(step_ref) + params[0:1]
        rate = jnp.exp(params[1:2])
        decay = step_and_decay(raw, params)[1]
        upper = jnp.where(iota((T, T), 1) >= iota((T, T), 0), 1.0, 0.0)
        ends = ends_s[...]
        ddecay = exact(upper, row_s[...]) + ends[0:1]
        dstep = (dt_s[...] - ddecay * rate) * sigmoid(raw)
        dstep_ref[...] = jnp.transpose(dstep)[: dstep_ref.shape[0]]
        dbias = jnp.sum(dstep, axis=0, keepdims=True)
        drate = jnp.sum(ddecay * decay, axis=0, keepdims=True)
        row = iota((8, 128), 0)
        small = jnp.zeros((8, 128), F32)
        for n, vector in enumerate((dbias, drate, ends[1:2])):
            for m, part in enumerate(split(vector, 2)):
                small = jnp.where(row == 2 * n + m, part.astype(F32), small)
        bundle_s[BUNDLE : BUNDLE + 8] = small
        bundle = bundle_s[...].astype(BF16)
        for shard in range(SHARDS):
            bundle_ref[shard] = bundle
        dpair_half = dpair.astype(BF16)
        total = coeff_s[...] + dot(dpair_half, in_low_s[...])
        total = (total + dot(dpair_half, out_high_s[...], TN)).astype(BF16)
        for peer in range(coeff_ref.shape[0]):
            coeff_ref[peer] = total


def mixer_second(*arrays):
    heads = arrays[6].shape[0]
    half = pltpu.VMEM((T, 128), BF16)
    return pl.pallas_call(
        mixer_second_kernel,
        grid=(STEPS,),
        in_specs=mixer_specs(heads) + [pl.BlockSpec((BLK, 128), lambda c: (c, 0))],
        out_specs=[
            column_block(T), column_block(8), column_block(8), column_block(T),
            whole((heads, T)), whole((LOCAL_HEADS, T, 128)), whole((SHARDS, BUNDLE + 8, 128)),
        ],
        out_shape=[
            jax.ShapeDtypeStruct((T, COLS), BF16),
            jax.ShapeDtypeStruct((8, COLS), F32),
            jax.ShapeDtypeStruct((8, COLS), F32),
            jax.ShapeDtypeStruct((T, COLS), BF16),
            jax.ShapeDtypeStruct((heads, T), F32),
            jax.ShapeDtypeStruct((LOCAL_HEADS, T, 128), BF16),
            jax.ShapeDtypeStruct((SHARDS, BUNDLE + 8, 128), BF16),
        ],
        scratch_shapes=TOKEN_SCRATCH + [
            pltpu.VMEM((128, T), F32),
            pltpu.VMEM((T, T), F32),
            pltpu.VMEM((T, T), F32),
            pltpu.VMEM((T, T), F32),
            pltpu.VMEM((T, 128), F32),
            pltpu.VMEM((T, 128), F32),
            pltpu.VMEM((T, 128), F32),
            pltpu.VMEM((8, 128), F32),
            pltpu.VMEM((BUNDLE + 8, 128), F32),
            half, half, half, half,
        ],
        cost_estimate=pl.CostEstimate(flops=18 * 10**9, bytes_accessed=8 * 10**6, transcendentals=0),
        name="mixer_second",
    )(*arrays)


def finish_kernel(bundle_ref, coeff_ref, weight_ref, bias_ref, rate_ref, skip_ref, in_ref, out_ref):
    total = bundle_ref[0].astype(F32)
    for shard in range(1, SHARDS):
        total = total + bundle_ref[shard].astype(F32)
    tiles = COLS // 128
    for lag in range(KERNEL):
        for m in range(tiles):
            weight_ref[lag : lag + 1, 128 * m : 128 * (m + 1)] = total[
                lag * tiles + m : lag * tiles + m + 1
            ]
    for n, ref in enumerate((bias_ref, rate_ref, skip_ref)):
        row = BUNDLE + 2 * n
        ref[...] = (total[row : row + 1] + total[row + 1 : row + 2])[:, : ref.shape[1]]
    low = coeff_ref[0].astype(F32) + coeff_ref[1].astype(F32)
    high = coeff_ref[2].astype(F32) + coeff_ref[3].astype(F32)
    left = iota((T, 128), 1) < STATE
    out_ref[...] = jnp.where(left, low, pltpu.roll(high, STATE, 1))
    in_ref[...] = jnp.where(left, pltpu.roll(low, STATE, 1), high)


def finish(bundle, coeff, heads):
    small = jax.ShapeDtypeStruct((1, heads), F32)
    wide = jax.ShapeDtypeStruct((T, 128), F32)
    return pl.pallas_call(
        finish_kernel,
        in_specs=[IN_VMEM] * 2,
        out_specs=[IN_VMEM] * 6,
        out_shape=[jax.ShapeDtypeStruct((KERNEL, COLS), F32), small, small, small, wide, wide],
        name="finish",
    )(bundle, coeff)


ROW = 4
K_AT, V_AT, Q_AT, G_AT = (slice(n * HEAD_DIM, (n + 1) * HEAD_DIM) for n in range(4))
KV_AT = slice(0, 2 * HEAD_DIM)


def pack_kernel(k_ref, v_ref, q_ref, g_ref, out_ref):
    for ref, place in ((k_ref, K_AT), (v_ref, V_AT), (q_ref, Q_AT), (g_ref, G_AT)):
        turned = jnp.transpose(ref[...])
        for head in range(LOCAL_HEADS):
            out_ref[head, place] = turned[head * HEAD_DIM : (head + 1) * HEAD_DIM]


def pack(keys, values, queries, grads):
    return pl.pallas_call(
        pack_kernel,
        in_specs=[IN_VMEM] * 4,
        out_specs=IN_VMEM,
        out_shape=jax.ShapeDtypeStruct((LOCAL_HEADS, 4 * HEAD_DIM, T), BF16),
        name="pack",
    )(keys, values, queries, grads)


def attention_kernel(
    where_ref, docs_ref, own_ref, far_ref, dq_ref, dkv_ref, back_ref, far_s
):
    first_block = where_ref[2] * ROW
    later = iota((T, T), 1) > iota((T, T), 0)
    scale = HEAD_DIM ** (-0.5)

    def doc_row(block):
        place = first_block + block
        row = docs_ref[pl.ds(jnp.maximum(place, 0), 1), :].astype(F32)
        return row if block >= 0 else jnp.where(place < 0, -1.0, row)

    rows = {block: doc_row(block) for block in range(-ROW, ROW)}
    for i in range(ROW):
        own_doc = columns_of(rows[i])
        qt, gt = own_ref[i, Q_AT], own_ref[i, G_AT]
        q, g = jnp.transpose(qt), jnp.transpose(gt)

        def part(gap, place):
            block = i - gap
            return own_ref[block, place] if block >= 0 else far_ref[block + ROW, place]

        scores = []
        top = None
        for gap in range(ROW + 1):
            same = own_doc == rows[i - gap]
            if gap == 0:
                same = same & jnp.logical_not(later)
            if gap == ROW:
                same = same & later
            s = jnp.where(same, dot(q, part(gap, K_AT)) * scale, NEG)
            scores.append(s)
            top = s if top is None else jnp.maximum(top, s)
        top = jnp.max(top, axis=1, keepdims=True)
        expos = [jnp.exp(s - top) for s in scores]
        total = jnp.sum(sum(expos), axis=1, keepdims=True)
        inverse = 1.0 / jnp.maximum(total, 1.0)
        probs = [e * inverse for e in expos]
        halves = [p.astype(BF16) for p in probs]
        dprobs = [dot(g, part(gap, V_AT)) for gap in range(ROW + 1)]
        delta = sum(h.astype(F32) * d for h, d in zip(halves, dprobs))
        delta = jnp.sum(delta, axis=1, keepdims=True)
        dq = jnp.zeros((HEAD_DIM, T), F32)
        for gap in range(ROW + 1):
            dscore = (probs[gap] * (dprobs[gap] - delta)).astype(BF16)
            dq = dq + dot(part(gap, K_AT), dscore, NT)
            block = i - gap
            ref, index = (dkv_ref, block) if block >= 0 else (far_s, block + ROW)
            dk, dv = dot(qt, dscore), dot(gt, halves[gap])
            if gap == 0 or (block < 0 and i == 0):
                ref[index, K_AT] = dk
                ref[index, V_AT] = dv
            else:
                ref[index, K_AT] += dk
                ref[index, V_AT] += dv
            if gap == ROW:
                back_ref[index] = far_s[index].astype(BF16)
        dq_ref[i] = (dq * scale).astype(BF16)


def attention(where, docs, own, far):
    pair = (ROW, 2 * HEAD_DIM, T)
    return pl.pallas_call(
        attention_kernel,
        in_specs=[IN_SMEM] + [IN_VMEM] * 3,
        out_specs=[IN_VMEM] * 3,
        out_shape=[
            jax.ShapeDtypeStruct((ROW, HEAD_DIM, T), BF16),
            jax.ShapeDtypeStruct(pair, F32),
            jax.ShapeDtypeStruct(pair, BF16),
        ],
        scratch_shapes=[pltpu.VMEM(pair, F32)],
        cost_estimate=pl.CostEstimate(flops=12 * 10**9, bytes_accessed=8 * 10**6, transcendentals=0),
        name="attention",
    )(where, docs, own, far)


def merge_kernel(dq_ref, dkv_ref, back_ref, out_ref):
    scale = HEAD_DIM ** (-0.5)
    total = dkv_ref[0] + back_ref[0].astype(F32)
    out_ref[0, K_AT] = (total[K_AT] * scale).astype(BF16)
    out_ref[0, V_AT] = total[V_AT].astype(BF16)
    out_ref[0, Q_AT] = dq_ref[0]


def merge(dq, dkv, back):
    def block(rows):
        return pl.BlockSpec((1, rows, T), lambda n: (n, 0, 0))

    return pl.pallas_call(
        merge_kernel,
        grid=(ROW,),
        in_specs=[block(HEAD_DIM), block(2 * HEAD_DIM), block(2 * HEAD_DIM)],
        out_specs=block(3 * HEAD_DIM),
        out_shape=jax.ShapeDtypeStruct((ROW, 3 * HEAD_DIM, T), BF16),
        name="merge",
    )(dq, dkv, back)


def unpack_kernel(parts_ref, dq_ref, dk_ref, dv_ref):
    for ref, place in ((dk_ref, K_AT), (dv_ref, V_AT), (dq_ref, Q_AT)):
        stacked = jnp.concatenate([parts_ref[h, place] for h in range(LOCAL_HEADS)], axis=0)
        ref[...] = jnp.transpose(stacked)


def unpack(parts):
    wide = jax.ShapeDtypeStruct((T, LOCAL_HEADS * HEAD_DIM), BF16)
    return pl.pallas_call(
        unpack_kernel,
        in_specs=[IN_VMEM],
        out_specs=[IN_VMEM] * 3,
        out_shape=[wide] * 3,
        name="unpack",
    )(parts)


def passed_along(value, axis, steps):
    count = lax.axis_size(axis)
    initial, last = (max(0, -steps), min(count, count - steps))
    return lax.ppermute(value, axis, [(source, source + steps) for source in range(initial, last)])


def exchange(array, axis):
    return lax.all_to_all(array, axis, split_axis=0, concat_axis=0, tiled=True)


def local(
    queries, keys, values, attn_grad, doc_ids, conv_input, conv_weight, step_raw, step_bias,
    rate_log, skip_gain, input_coeff, output_coeff, gate_input, mix_grad,
):
    heads = step_raw.shape[1]
    shard = lax.axis_index(SEQ)
    group = lax.axis_index("head") * heads // (SSM_HEADS // GROUPS)
    where = jnp.stack([shard, group, shard // ROW]).astype(jnp.int32)
    docs = doc_ids.reshape(SHARDS, T)
    halo = passed_along(conv_input[T - 8 :], SEQ, 1)

    own = exchange(pack(keys, values, queries, attn_grad), "seq_2")
    far = passed_along(own[:, KV_AT], SEQ, ROW)

    mixer_args = (
        where, conv_input, halo, conv_weight, gate_input, mix_grad, step_raw.T,
        step_bias.reshape(1, heads), rate_log.reshape(1, heads), skip_gain.reshape(1, heads),
        docs, input_coeff, output_coeff,
    )
    parts = mixer_first(*mixer_args).reshape(SHARDS, SLOT, 128)
    entering = exchange(chain(where, exchange(parts, SEQ)), SEQ).reshape(COLS, 128)

    dq, dkv, back = attention(where, docs, own, far)
    returned = passed_along(back, SEQ, -ROW)

    dx, tail, spill, dgate, dstep, coeff, bundle = mixer_second(*mixer_args, entering)
    spilled = passed_along(spill, SEQ, -1)

    dq, dk, dv = unpack(exchange(merge(dq, dkv, returned), "seq_2"))

    grad_weight, grad_bias, grad_rate, grad_skip, sum_in, sum_out = finish(
        exchange(bundle, SEQ), exchange(coeff, "head"), heads
    )
    tail = (tail + spilled).astype(BF16)
    grad_conv = lax.dynamic_update_slice_in_dim(dx, tail, T - 8, 0)
    return (
        dq, dk, dv, grad_conv, dgate, dstep.T, sum_in, sum_out, grad_weight,
        grad_bias.reshape(heads), grad_rate.reshape(heads), grad_skip.reshape(heads),
    )


def solution(mesh):
    finer = Mesh(
        mesh.devices.reshape(4, 2, 4, mesh.shape["head"]), ("seq_0", "seq_1", "seq_2", "head")
    )
    wide = P(SEQ, "head")
    return jax.shard_map(
        local,
        mesh=finer,
        in_specs=(
            wide, wide, wide, wide, P(), wide, P(None, "head"), wide, P("head"), P("head"),
            P("head"), P(SEQ, None), P(SEQ, None), wide, wide,
        ),
        out_specs=(
            wide, wide, wide, wide, wide, wide, P(SEQ, None), P(SEQ, None), P(None, "head"),
            P("head"), P("head"), P("head"),
        ),
        check_vma=False,
    )
```

time: 227 us -> 166 us (0.73)
  starting transfers between devices: 78.9 us -> 36.5 us
  waiting for transfers between devices: 77 us -> 41.6 us
  blocking collectives: 0 us -> 28.4 us
  other arithmetic: 13.1 us -> 1.23 us
  Pallas kernels: 42.1 us -> 51.5 us
  local copies, waits for them, and re-layouts: 13.7 us -> 4.84 us
    ppermute x10 -> x4, waiting for transfers between devices: 62.5 us -> 15.1 us  [passed_along(): lax.ppermute(value, axis, [(source, source + steps) for source in range(i...]
    all_to_all x0 -> x2, blocking collectives: none -> 28.4 us  [exchange(): return lax.all_to_all(array, axis, split_axis=0, concat_axis=0, tiled=True)]
    all_to_all x4, starting transfers between devices: 50.3 us -> 23.8 us  [exchange(): return lax.all_to_all(array, axis, split_axis=0, concat_axis=0, tiled=True)]
    ppermute x10 -> x4, starting transfers between devices: 28.6 us -> 12.7 us  [passed_along(): lax.ppermute(value, axis, [(source, source + steps) for source in range(i...]
    all_to_all x4, waiting for transfers between devices: 14.5 us -> 26.6 us  [exchange(): return lax.all_to_all(array, axis, split_axis=0, concat_axis=0, tiled=True)]
    pallas_call x4 -> x8, Pallas kernels: 42.1 us -> 51.5 us  [the longest x1 19.1 us: mixer_second(): pl.pallas_call(mixer_second_kernel, grid=(STEPS,), in_specs=mixer_specs(h...]
    concatenate x5 -> x0, other arithmetic: 4.18 us -> none  [the longest x1 1.88 us: local(): jnp.concatenate([parts.reshape(SHARDS, ROWS, 128), jnp.broadcast_to(throu...]
    broadcast_in_dim x3 -> x0, local copies, waits for them, and re-layouts: 3.3 us -> none  [the longest x2 2.55 us: from_everyone(): jnp.broadcast_to(array, (lax.axis_size(axis), *array.shape))]
  transfers between devices with their start and end apart: 14 -> 8, of which waited for: 5 -> 4; matrix products, arithmetic and copies ran while one was open for 8% -> 2% of each run, Pallas kernels for 15% -> 28%
where the time goes in v1:
time: 166 us; the launch traced here: 165 us
  Pallas kernels  51.5 us (31%)
  waiting for transfers between devices  41.6 us (25%)
  starting transfers between devices  36.5 us (22%)
  blocking collectives  28.4 us (17%)
  local copies, waits for them, and re-layouts  4.84 us (3%)
    all_to_all x2, blocking collectives, exchange(): return lax.all_to_all(array, axis, split_axis=0, concat_axis=0, tiled=True)  28.4 us
    all_to_all x4, waiting for transfers between devices, exchange(): return lax.all_to_all(array, axis, split_axis=0, concat_axis=0, tiled=True)  26.6 us
    all_to_all x4, starting transfers between devices, exchange(): return lax.all_to_all(array, axis, split_axis=0, concat_axis=0, tiled=True)  23.8 us
    pallas_call x1, Pallas kernels, mixer_second(): pl.pallas_call(mixer_second_kernel, grid=(STEPS,), in_specs=mixer_specs(h...  19.1 us
    ppermute x4, waiting for transfers between devices, passed_along(): lax.ppermute(value, axis, [(source, source + steps) for source in range(i...  15.1 us
    ppermute x4, starting transfers between devices, passed_along(): lax.ppermute(value, axis, [(source, source + steps) for source in range(i...  12.7 us
    pallas_call x1, Pallas kernels, attention(): pl.pallas_call(attention_kernel, in_specs=[IN_SMEM] + [IN_VMEM] * 3, out_...  9.27 us
    pallas_call x1, Pallas kernels, mixer_first(): pl.pallas_call(mixer_first_kernel, grid=(STEPS,), in_specs=mixer_specs(he...  9.22 us
  transfers between devices with their start and end apart: 8, of which 4 were waited for; matrix products, arithmetic and copies ran while one was open for 2% of the time, Pallas kernels for 28%

profile of v1, /device:TPU:0, one launch (start us, length us, event | category | flops | bytes accessed | tf_op | source)
XLA Modules:
  0.0 164.8 jit_solution(5937159761311798659)
XLA Ops:
  0.6 3.2 %pack.1 = bf16[4,896,256]{2,1,0:T(8,128)(2,1)} custom-call(bf16[256,896]{1,0:T(8,128)(2,1)} %k_ref.1, bf16[256,896]{1,0:T(8,128)(2,1)} %v_ref.1, bf16[256,896]{1,0:T(8,128)(2,1)} %q_ref.1, bf16[256,896]{1,0:T(8,128)(2,1)} %g_ref.1), custom_call_target="tpu_custom_call" | custom-call | tf_op jit(solution)/shard_map/pack/pallas_call | solution.py:507
  3.9 4.5 %all-to-all-start = ((bf16[4,896,256]{2,1,0:T(8,128)(2,1)}), bf16[4,896,256]{2,1,0:T(8,128)(2,1)S(1)}, u32[]{:S(2)}, u32[]{:S(2)}) async-start(bf16[4,896,256]{2,1,0:T(8,128)(2,1)} %pack.1), calls=%async_computation | async-start | bytes 3670016 | tf_op jit(solution)/shard_map/all_to_all | solution.py:639
  8.4 0.8 slice.7
  9.2 3.9 %collective-permute-start.2 = (bf16[8,1792]{1,0:T(8,128)(2,1)S(1)}, bf16[8,1792]{1,0:T(8,128)(2,1)S(1)}, u32[]{:S(2)}, u32[]{:S(2)}) collective-permute-start(bf16[8,1792]{1,0:T(8,128)(2,1)S(1)} %slice.7), channel_id=1, source_target_pairs={{0,4},{4,8},{8,12},{12,16},{16,20},{20,24},{24,28},{28,32},{32,36}... | collective-permute-start | bytes 86024 | tf_op jit(solution)/shard_map/ppermute | solution.py:635
  13.1 0.6 pad_add_fusion.where_ref
  13.7 0.6 reshape.51.docs_ref
  14.4 17.9 %all-to-all-done.own_ref = bf16[4,896,256]{2,1,0:T(8,128)(2,1)S(1)} async-done(((bf16[4,896,256]{2,1,0:T(8,128)(2,1)}), bf16[4,896,256]{2,1,0:T(8,128)(2,1)S(1)}, u32[]{:S(2)}, u32[]{:S(2)}) %all-to-all-start) | async-done | bytes 1835040 | tf_op jit(solution)/shard_map/all_to_all | solution.py:639
  32.3 0.1 slice.8
  32.4 6.1 %collective-permute-start = (bf16[4,448,256]{2,1,0:T(8,128)(2,1)S(1)}, bf16[4,448,256]{2,1,0:T(8,128)(2,1)}, u32[]{:S(2)}, u32[]{:S(2)}) collective-permute-start(bf16[4,448,256]{2,1,0:T(8,128)(2,1)S(1)} %slice.8), channel_id=1, source_target_pairs={{0,16},{4,20},{8,24},{12,28},{16,32},{20,36},{24,40},{28,44},{32,4... | collective-permute-start | bytes 2752520 | tf_op jit(solution)/shard_map/ppermute | solution.py:635
  38.4 0.6 copy-done.8
  39.0 9.2 %mixer_first.1 = bf16[2048,128]{1,0:T(8,128)(2,1)} custom-call(s32[3]{0:T(128)} %pad_add_fusion.where_ref, bf16[256,1792]{1,0:T(8,128)(2,1)} %x_ref.3, bf16[8,1792]{1,0:T(8,128)(2,1)} %copy-done.8, f32[4,1792]{1,0:T(4,128)} %weight_ref.3, bf16[256,1792]{1,0:T(8,128)(2,1)} %gate_ref.3, bf16[256,1792]{1,0:T(8,128)(2,1)} %grad_ref.3, f32[28,256]{1,0:T(8,128)} %bitcast.15, ...), custom_call_target="tpu_custom_call" | custom-call | flops 8000000000 | bytes 4000000 | tf_op jit(solution)/shard_map/mixer_first/pallas_call | solution.py:230
  48.2 18.3 %all_to_all.30.parts_ref = bf16[32,64,128]{2,1,0:T(8,128)(2,1)} all-to-all(bf16[32,64,128]{2,1,0:T(8,128)(2,1)} %bitcast.13), channel_id=1, replica_groups=mesh['seq_0'=4,'seq_1'=2,'seq_2'=4,'head'=4] {'seq_0','seq_1','seq_2'}, dimensions={0} | all-to-all | bytes 1048576 | tf_op jit(solution)/shard_map/all_to_all | solution.py:639
  66.5 2.3 %chain.1 = bf16[32,56,128]{2,1,0:T(8,128)(2,1)} custom-call(s32[3]{0:T(128)} %pad_add_fusion.where_ref, bf16[32,64,128]{2,1,0:T(8,128)(2,1)} %all_to_all.30.parts_ref), custom_call_target="tpu_custom_call" | custom-call | flops 2000000000 | bytes 1000000 | tf_op jit(solution)/shard_map/chain/pallas_call | solution.py:267
  68.8 5.4 %all-to-all-start.3 = ((bf16[32,56,128]{2,1,0:T(8,128)(2,1)}), bf16[32,56,128]{2,1,0:T(8,128)(2,1)S(1)}, u32[]{:S(2)}, u32[]{:S(2)}) async-start(bf16[32,56,128]{2,1,0:T(8,128)(2,1)} %chain.1), calls=%async_computation.3 | async-start | bytes 917504 | tf_op jit(solution)/shard_map/all_to_all | solution.py:639
  74.2 0.0 collective-permute-done.far_ref
  74.2 9.3 %attention.1 = (bf16[4,224,256]{2,1,0:T(8,128)(2,1)}, f32[4,448,256]{2,1,0:T(8,128)}, bf16[4,448,256]{2,1,0:T(8,128)(2,1)}) custom-call(s32[3]{0:T(128)} %pad_add_fusion.where_ref, s32[32,256]{1,0:T(8,128)} %reshape.51.docs_ref, bf16[4,896,256]{2,1,0:T(8,128)(2,1)} %copy-done.1, bf16[4,448,256]{2,1,0:T(8,128)(2,1)} %collective-permute-done.far_ref), custom_call_target="tpu_custom_call" | custom-call | flops 12000000000 | bytes 8000000 | tf_op jit(solution)/shard_map/attention/pallas_call | solution.py:578
  83.5 1.5 collective-permute-start.1
  85.0 0.7 all-to-all-done.3
  85.7 0.8 copy-done.4
  86.5 19.1 %mixer_second.1 = (bf16[256,1792]{1,0:T(8,128)(2,1)}, f32[8,1792]{1,0:T(8,128)}, f32[8,1792]{1,0:T(8,128)}, bf16[256,1792]{1,0:T(8,128)(2,1)}, f32[28,256]{1,0:T...) custom-call(s32[3]{0:T(128)} %pad_add_fusion.where_ref, bf16[256,1792]{1,0:T(8,128)(2,1)} %x_ref.3, ...), custom_call_target="tpu_custom_call" | custom-call | flops 17999998976 | bytes 8000000 | tf_op jit(solution)/shard_map/mixer_second/pallas_call | solution.py:428
  105.5 10.1 %all_to_all.31.coeff_ref = bf16[4,256,128]{2,1,0:T(8,128)(2,1)} all-to-all(bf16[4,256,128]{2,1,0:T(8,128)(2,1)} %get-tuple-element.43), channel_id=1, replica_groups=mesh['seq_0'=4,'seq_1'=2,'seq_2'=4,'head'=4] {'head'}, dimensions={0} | all-to-all | bytes 524288 | tf_op jit(solution)/shard_map/all_to_all | solution.py:639
  115.7 10.3 %all-to-all-start.4 = ((bf16[32,64,128]{2,1,0:T(8,128)(2,1)}), bf16[32,64,128]{2,1,0:T(8,128)(2,1)S(1)}, u32[]{:S(2)}, u32[]{:S(2)}) async-start(bf16[32,64,128]{2,1,0:T(8,128)(2,1)} %get-tuple-element.42), calls=%async_computation.4 | async-start | bytes 1048576 | tf_op jit(solution)/shard_map/all_to_all | solution.py:639
  126.0 0.9 copy-done.3
  126.9 3.9 %merge.1 = bf16[4,672,256]{2,1,0:T(8,128)(2,1)} custom-call(bf16[4,224,256]{2,1,0:T(8,128)(2,1)} %get-tuple-element.31.dq_ref, f32[4,448,256]{2,1,0:T(8,128)} %get-tuple-element.32.dkv_ref, bf16[4,448,256]{2,1,0:T(8,128)(2,1)} %copy-done.3), custom_call_target="tpu_custom_call" | custom-call | tf_op jit(solution)/shard_map/merge/pallas_call | solution.py:605
  130.8 7.9 %all-to-all-done.4.bundle_ref = bf16[32,64,128]{2,1,0:T(8,128)(2,1)S(1)} async-done(((bf16[32,64,128]{2,1,0:T(8,128)(2,1)}), bf16[32,64,128]{2,1,0:T(8,128)(2,1)S(1)}, u32[]{:S(2)}, u32[]{:S(2)}) %all-to-all-start.4) | async-done | bytes 524320 | tf_op jit(solution)/shard_map/all_to_all | solution.py:639
  138.7 3.5 %all-to-all-start.1 = ((bf16[4,672,256]{2,1,0:T(8,128)(2,1)}), bf16[4,672,256]{2,1,0:T(8,128)(2,1)S(1)}, u32[]{:S(2)}, u32[]{:S(2)}) async-start(bf16[4,672,256]{2,1,0:T(8,128)(2,1)} %merge.1), calls=%async_computation.1 | async-start | bytes 2752512 | tf_op jit(solution)/shard_map/all_to_all | solution.py:639
  142.3 1.3 collective-permute-start.3
  143.6 15.0 %collective-permute-done.3 = f32[8,1792]{1,0:T(8,128)S(1)} collective-permute-done((f32[8,1792]{1,0:T(8,128)S(1)}, f32[8,1792]{1,0:T(8,128)S(1)}, u32[]{:S(2)}, u32[]{:S(2)}) %collective-permute-start.3) | collective-permute-done | bytes 57376 | tf_op jit(solution)/shard_map/ppermute | solution.py:635
  158.6 0.6 fusion
  159.2 1.9 %finish.1 = (f32[4,1792]{1,0:T(4,128)}, f32[1,28]{1,0:T(1,128)}, f32[1,28]{1,0:T(1,128)}, f32[1,28]{1,0:T(1,128)}, f32[256,128]{1,0:T(8,128)}, /*index=5*/f32[256,128]{1,0:T(8,128)}) custom-call(bf16[32,64,128]{2,1,0:T(8,128)(2,1)} %copy-done.2, bf16[4,256,128]{2,1,0:T(8,128)(2,1)} %all_to_all.31.coeff_ref), custom_call_target="tpu_custom_call" | custom-call | tf_op jit(solution)/shard_map/finish/pallas_call | solution.py:485
  161.2 1.1 copy-done
  162.2 2.6 %unpack.1 = (bf16[256,896]{1,0:T(8,128)(2,1)}, bf16[256,896]{1,0:T(8,128)(2,1)}, bf16[256,896]{1,0:T(8,128)(2,1)}) custom-call(bf16[4,672,256]{2,1,0:T(8,128)(2,1)} %copy-done), custom_call_target="tpu_custom_call" | custom-call | tf_op jit(solution)/shard_map/unpack/pallas_call | solution.py:623
  (17 shorter events, 0.0 us)
Async XLA Ops:
  3.9 9.9 %copy-start.6 = (s32[8192]{0:T(1024)S(1)}, s32[8192]{0:T(1024)}, u32[]{:S(2)}) copy-start(s32[8192]{0:T(1024)} %param.19) | copy-start | bytes 98308
  3.9 28.4 %all-to-all-start = ((bf16[4,896,256]{2,1,0:T(8,128)(2,1)}), bf16[4,896,256]{2,1,0:T(8,128)(2,1)S(1)}, u32[]{:S(2)}, u32[]{:S(2)}) async-start(bf16[4,896,256]{2,1,0:T(8,128)(2,1)} %pack.1), calls=%async_computation | async-start | bytes 3670016 | tf_op jit(solution)/shard_map/all_to_all | solution.py:639
  9.2 29.2 %collective-permute-start.2 = (bf16[8,1792]{1,0:T(8,128)(2,1)S(1)}, bf16[8,1792]{1,0:T(8,128)(2,1)S(1)}, u32[]{:S(2)}, u32[]{:S(2)}) collective-permute-start(bf16[8,1792]{1,0:T(8,128)(2,1)S(1)} %slice.7), channel_id=1, source_target_pairs={{0,4},{4,8},{8,12},{12,16},{16,20},{20,24},{24,28},{28,32},{32,36}... | collective-permute-start | bytes 86024 | tf_op jit(solution)/shard_map/ppermute | solution.py:635
  32.3 15.9 %copy-start.1 = (bf16[4,896,256]{2,1,0:T(8,128)(2,1)}, bf16[4,896,256]{2,1,0:T(8,128)(2,1)S(1)}, u32[]{:S(2)}) copy-start(bf16[4,896,256]{2,1,0:T(8,128)(2,1)S(1)} %all-to-all-done.own_ref) | copy-start | bytes 5505028
  32.4 41.9 %collective-permute-start = (bf16[4,448,256]{2,1,0:T(8,128)(2,1)S(1)}, bf16[4,448,256]{2,1,0:T(8,128)(2,1)}, u32[]{:S(2)}, u32[]{:S(2)}) collective-permute-start(bf16[4,448,256]{2,1,0:T(8,128)(2,1)S(1)} %slice.8), channel_id=1, source_target_pairs={{0,16},{4,20},{8,24},{12,28},{16,32},{20,36},{24,40},{28,44},{32,4... | collective-permute-start | bytes 2752520 | tf_op jit(solution)/shard_map/ppermute | solution.py:635
  38.4 0.6 copy-start.8
  68.8 16.9 %all-to-all-start.3 = ((bf16[32,56,128]{2,1,0:T(8,128)(2,1)}), bf16[32,56,128]{2,1,0:T(8,128)(2,1)S(1)}, u32[]{:S(2)}, u32[]{:S(2)}) async-start(bf16[32,56,128]{2,1,0:T(8,128)(2,1)} %chain.1), calls=%async_computation.3 | async-start | bytes 917504 | tf_op jit(solution)/shard_map/all_to_all | solution.py:639
  83.5 42.5 %collective-permute-start.1 = (bf16[4,448,256]{2,1,0:T(8,128)(2,1)}, bf16[4,448,256]{2,1,0:T(8,128)(2,1)S(1)}, u32[]{:S(2)}, u32[]{:S(2)}) collective-permute-start(bf16[4,448,256]{2,1,0:T(8,128)(2,1)} %get-tuple-element.33), channel_id=1, source_target_pairs={{16,0},{20,4},{24,8},{28,12},{32,16},{36,20},{40,24},{44,28},{48,3... | collective-permute-start | bytes 2752520 | tf_op jit(solution)/shard_map/ppermute | solution.py:635
  85.7 0.8 copy-start.4
  115.7 23.0 %all-to-all-start.4 = ((bf16[32,64,128]{2,1,0:T(8,128)(2,1)}), bf16[32,64,128]{2,1,0:T(8,128)(2,1)S(1)}, u32[]{:S(2)}, u32[]{:S(2)}) async-start(bf16[32,64,128]{2,1,0:T(8,128)(2,1)} %get-tuple-element.42), calls=%async_computation.4 | async-start | bytes 1048576 | tf_op jit(solution)/shard_map/all_to_all | solution.py:639
  126.0 0.9 copy-start.3
  130.8 11.5 %copy-start.7 = (f32[8,1792]{1,0:T(8,128)S(1)}, f32[8,1792]{1,0:T(8,128)}, u32[]{:S(2)}) copy-start(f32[8,1792]{1,0:T(8,128)} %get-tuple-element.39) | copy-start | bytes 172036
  130.8 27.8 %copy-start.5 = (f32[8,1792]{1,0:T(8,128)S(1)}, f32[8,1792]{1,0:T(8,128)}, u32[]{:S(2)}) copy-start(f32[8,1792]{1,0:T(8,128)} %get-tuple-element.38) | copy-start | bytes 172036
  138.7 20.5 %copy-start.2 = (bf16[32,64,128]{2,1,0:T(8,128)(2,1)}, bf16[32,64,128]{2,1,0:T(8,128)(2,1)S(1)}, u32[]{:S(2)}) copy-start(bf16[32,64,128]{2,1,0:T(8,128)(2,1)S(1)} %all-to-all-done.4.bundle_ref) | copy-start | bytes 1572868
  138.7 22.5 %all-to-all-start.1 = ((bf16[4,672,256]{2,1,0:T(8,128)(2,1)}), bf16[4,672,256]{2,1,0:T(8,128)(2,1)S(1)}, u32[]{:S(2)}, u32[]{:S(2)}) async-start(bf16[4,672,256]{2,1,0:T(8,128)(2,1)} %merge.1), calls=%async_computation.1 | async-start | bytes 2752512 | tf_op jit(solution)/shard_map/all_to_all | solution.py:639
  142.3 16.3 %collective-permute-start.3 = (f32[8,1792]{1,0:T(8,128)S(1)}, f32[8,1792]{1,0:T(8,128)S(1)}, u32[]{:S(2)}, u32[]{:S(2)}) collective-permute-start(f32[8,1792]{1,0:T(8,128)S(1)} %copy-done.7), channel_id=1, source_target_pairs={{4,0},{8,4},{12,8},{16,12},{20,16},{24,20},{28,24},{32,28},{36,32}... | collective-permute-start | bytes 172040 | tf_op jit(solution)/shard_map/ppermute | solution.py:635
  161.1 1.1 copy-start

commit v2 on v1

--- a/solution.py
+++ b/solution.py
@@ -6,8 +6,8 @@
 from jax.sharding import Mesh
 from jax.sharding import PartitionSpec as P
 
+
 HEAD_DIM = 224
-WINDOW = 1024
 SSM_HEADS = 112
 STATE = 64
 GROUPS = 2
@@ -16,7 +16,6 @@
 SHARDS = 32
 T = 256
 LOCAL_HEADS = 4
-REACH = WINDOW // T
 BLK = 256
 HEADS_BLK = BLK // 64
 COLS = 1792
@@ -71,9 +70,6 @@
 
 IN_SMEM = pl.BlockSpec(memory_space=pltpu.SMEM)
 IN_VMEM = pl.BlockSpec(memory_space=pltpu.VMEM)
-
-
-PARAM_ROWS = 3
 
 
 def doc_rows(where_ref, docs_ref):
@@ -590,49 +586,61 @@
     )(where, docs, own, far)
 
 
-def merge_kernel(dq_ref, dkv_ref, back_ref, out_ref):
+def merge_kernel(where_ref, dq_ref, dkv_ref, back_ref, *out_refs):
     scale = HEAD_DIM ** (-0.5)
-    total = dkv_ref[0] + back_ref[0].astype(F32)
-    out_ref[0, K_AT] = (total[K_AT] * scale).astype(BF16)
-    out_ref[0, V_AT] = total[V_AT].astype(BF16)
-    out_ref[0, Q_AT] = dq_ref[0]
-
-
-def merge(dq, dkv, back):
-    def block(rows):
-        return pl.BlockSpec((1, rows, T), lambda n: (n, 0, 0))
-
+    place = where_ref[3]
+    for turn, out_ref in enumerate(out_refs):
+        block = lax.rem(place + turn, ROW)
+        total = dkv_ref[block] + back_ref[block].astype(F32)
+        out_ref[K_AT] = (total[K_AT] * scale).astype(BF16)
+        out_ref[V_AT] = total[V_AT].astype(BF16)
+        out_ref[Q_AT] = dq_ref[block]
+
+
+def merge(where, dq, dkv, back):
     return pl.pallas_call(
         merge_kernel,
-        grid=(ROW,),
-        in_specs=[block(HEAD_DIM), block(2 * HEAD_DIM), block(2 * HEAD_DIM)],
-        out_specs=block(3 * HEAD_DIM),
-        out_shape=jax.ShapeDtypeStruct((ROW, 3 * HEAD_DIM, T), BF16),
+        in_specs=[IN_SMEM] + [IN_VMEM] * 3,
+        out_specs=[IN_VMEM] * ROW,
+        out_shape=[jax.ShapeDtypeStruct((3 * HEAD_DIM, T), BF16)] * ROW,
+        cost_estimate=pl.CostEstimate(flops=3 * 10**9, bytes_accessed=4 * 10**6, transcendentals=0),
         name="merge",
-    )(dq, dkv, back)
-
-
-def unpack_kernel(parts_ref, dq_ref, dk_ref, dv_ref):
-    for ref, place in ((dk_ref, K_AT), (dv_ref, V_AT), (dq_ref, Q_AT)):
-        stacked = jnp.concatenate([parts_ref[h, place] for h in range(LOCAL_HEADS)], axis=0)
+    )(where, dq, dkv, back)
+
+
+def unpack_kernel(where_ref, *refs):
+    parts, outs, stacked_s = refs[:ROW], refs[ROW : ROW + 3], refs[ROW + 3]
+    place = where_ref[3]
+    for turn, part in enumerate(parts):
+        source = lax.rem(place - turn + ROW, ROW)
+        for n, at in enumerate((Q_AT, K_AT, V_AT)):
+            stacked_s[n, source] = part[at]
+    for n, ref in enumerate(outs):
+        stacked = jnp.concatenate([stacked_s[n, h] for h in range(LOCAL_HEADS)], axis=0)
         ref[...] = jnp.transpose(stacked)
 
 
-def unpack(parts):
+def unpack(where, parts):
     wide = jax.ShapeDtypeStruct((T, LOCAL_HEADS * HEAD_DIM), BF16)
     return pl.pallas_call(
         unpack_kernel,
-        in_specs=[IN_VMEM],
+        in_specs=[IN_SMEM] + [IN_VMEM] * ROW,
         out_specs=[IN_VMEM] * 3,
         out_shape=[wide] * 3,
+        scratch_shapes=[pltpu.VMEM((3, LOCAL_HEADS, HEAD_DIM, T), BF16)],
         name="unpack",
-    )(parts)
+    )(where, *parts)
 
 
 def passed_along(value, axis, steps):
     count = lax.axis_size(axis)
     initial, last = (max(0, -steps), min(count, count - steps))
     return lax.ppermute(value, axis, [(source, source + steps) for source in range(initial, last)])
+
+
+def turned(value, axis, steps):
+    count = lax.axis_size(axis)
+    return lax.ppermute(value, axis, [(n, (n + steps) % count) for n in range(count)])
 
 
 def exchange(array, axis):
@@ -646,12 +654,13 @@
     heads = step_raw.shape[1]
     shard = lax.axis_index(SEQ)
     group = lax.axis_index("head") * heads // (SSM_HEADS // GROUPS)
-    where = jnp.stack([shard, group, shard // ROW]).astype(jnp.int32)
+    where = jnp.stack([shard, group, shard // ROW, lax.axis_index("seq_2")]).astype(jnp.int32)
     docs = doc_ids.reshape(SHARDS, T)
     halo = passed_along(conv_input[T - 8 :], SEQ, 1)
-
-    own = exchange(pack(keys, values, queries, attn_grad), "seq_2")
-    far = passed_along(own[:, KV_AT], SEQ, ROW)
+    packed = pack(keys, values, queries, attn_grad)
+    own = exchange(packed, "seq_2")
+    borrowed = own[:, KV_AT]
+    far = passed_along(borrowed, SEQ, ROW)
 
     mixer_args = (
         where, conv_input, halo, conv_weight, gate_input, mix_grad, step_raw.T,
@@ -659,19 +668,19 @@
         docs, input_coeff, output_coeff,
     )
     parts = mixer_first(*mixer_args).reshape(SHARDS, SLOT, 128)
-    entering = exchange(chain(where, exchange(parts, SEQ)), SEQ).reshape(COLS, 128)
-
+    gathered = exchange(parts, SEQ)
+    scanned = chain(where, gathered)
+    entering = exchange(scanned, SEQ).reshape(COLS, 128)
     dq, dkv, back = attention(where, docs, own, far)
     returned = passed_along(back, SEQ, -ROW)
-
     dx, tail, spill, dgate, dstep, coeff, bundle = mixer_second(*mixer_args, entering)
     spilled = passed_along(spill, SEQ, -1)
-
-    dq, dk, dv = unpack(exchange(merge(dq, dkv, returned), "seq_2"))
-
-    grad_weight, grad_bias, grad_rate, grad_skip, sum_in, sum_out = finish(
-        exchange(bundle, SEQ), exchange(coeff, "head"), heads
-    )
+    bundles = exchange(bundle, SEQ)
+    coeffs = exchange(coeff, "head")
+    kept, *leaving = merge(where, dq, dkv, returned)
+    swapped = [kept] + [turned(part, "seq_2", n) for n, part in enumerate(leaving, 1)]
+    grad_weight, grad_bias, grad_rate, grad_skip, sum_in, sum_out = finish(bundles, coeffs, heads)
+    dq, dk, dv = unpack(where, swapped)
     tail = (tail + spilled).astype(BF16)
     grad_conv = lax.dynamic_update_slice_in_dim(dx, tail, T - 8, 0)
     return (

time: 166 us -> 153 us (0.922)
  blocking collectives: 28.4 us -> 18.3 us
  waiting for transfers between devices: 41.6 us -> 33.5 us
  starting transfers between devices: 36.5 us -> 42.3 us
    ppermute x4, waiting for transfers between devices: 15.1 us -> 0.01 us  [passed_along(): lax.ppermute(value, axis, [(source, source + steps) for source in range(i...]
    all_to_all x2 -> x1, blocking collectives: 28.4 us -> 18.3 us  [exchange(): return lax.all_to_all(array, axis, split_axis=0, concat_axis=0, tiled=True)]
    ppermute x0 -> x3, waiting for transfers between devices: none -> 8.04 us  [turned(): lax.ppermute(value, axis, [(n, (n + steps) % count) for n in range(count)])]
    ppermute x0 -> x3, starting transfers between devices: none -> 5.93 us  [turned(): lax.ppermute(value, axis, [(n, (n + steps) % count) for n in range(count)])]
    unnamed x18 -> x22, local copies, waits for them, and re-layouts: 3.41 us -> 4.02 us
  transfers between devices with their start and end apart: 8 -> 11, of which waited for: 4 -> 6; matrix products, arithmetic and copies ran while one was open for 2% -> 2% of each run, Pallas kernels for 28% -> 29%
where the time goes in v2:
time: 153 us; the launch traced here: 152 us
  Pallas kernels  50.8 us (33%)
  starting transfers between devices  42.3 us (28%)
  waiting for transfers between devices  33.5 us (22%)
  blocking collectives  18.3 us (12%)
  local copies, waits for them, and re-layouts  5.45 us (4%)
    all_to_all x4, waiting for transfers between devices, exchange(): return lax.all_to_all(array, axis, split_axis=0, concat_axis=0, tiled=True)  25.5 us
    all_to_all x4, starting transfers between devices, exchange(): return lax.all_to_all(array, axis, split_axis=0, concat_axis=0, tiled=True)  23.7 us
    pallas_call x1, Pallas kernels, mixer_second(): pl.pallas_call(mixer_second_kernel, grid=(STEPS,), in_specs=mixer_specs(h...  19.1 us
    all_to_all x1, blocking collectives, exchange(): return lax.all_to_all(array, axis, split_axis=0, concat_axis=0, tiled=True)  18.3 us
    ppermute x4, starting transfers between devices, passed_along(): lax.ppermute(value, axis, [(source, source + steps) for source in range(i...  12.7 us
    pallas_call x1, Pallas kernels, attention(): pl.pallas_call(attention_kernel, in_specs=[IN_SMEM] + [IN_VMEM] * 3, out_...  9.27 us
    pallas_call x1, Pallas kernels, mixer_first(): pl.pallas_call(mixer_first_kernel, grid=(STEPS,), in_specs=mixer_specs(he...  9.21 us
    ppermute x3, waiting for transfers between devices, turned(): lax.ppermute(value, axis, [(n, (n + steps) % count) for n in range(count)])  8.04 us
  transfers between devices with their start and end apart: 11, of which 6 were waited for; matrix products, arithmetic and copies ran while one was open for 2% of the time, Pallas kernels for 29%

profile of v2, /device:TPU:0, one launch (start us, length us, event | category | flops | bytes accessed | tf_op | source)
XLA Modules:
  0.0 152.3 jit_solution(12424216907974691083)
XLA Ops:
  0.6 3.2 %pack.1 = bf16[4,896,256]{2,1,0:T(8,128)(2,1)} custom-call(bf16[256,896]{1,0:T(8,128)(2,1)} %k_ref.1, bf16[256,896]{1,0:T(8,128)(2,1)} %v_ref.1, bf16[256,896]{1,0:T(8,128)(2,1)} %q_ref.1, bf16[256,896]{1,0:T(8,128)(2,1)} %g_ref.1), custom_call_target="tpu_custom_call" | custom-call | tf_op jit(solution)/shard_map/pack/pallas_call | solution.py:503
  3.9 4.5 %all-to-all-start = ((bf16[4,896,256]{2,1,0:T(8,128)(2,1)}), bf16[4,896,256]{2,1,0:T(8,128)(2,1)S(1)}, u32[]{:S(2)}, u32[]{:S(2)}) async-start(bf16[4,896,256]{2,1,0:T(8,128)(2,1)} %pack.1), calls=%async_computation | async-start | bytes 3670016 | tf_op jit(solution)/shard_map/all_to_all | solution.py:647
  8.4 0.8 slice.7
  9.2 3.9 %collective-permute-start.5 = (bf16[8,1792]{1,0:T(8,128)(2,1)S(1)}, bf16[8,1792]{1,0:T(8,128)(2,1)S(1)}, u32[]{:S(2)}, u32[]{:S(2)}) collective-permute-start(bf16[8,1792]{1,0:T(8,128)(2,1)S(1)} %slice.7), channel_id=1, source_target_pairs={{0,4},{4,8},{8,12},{12,16},{16,20},{20,24},{24,28},{28,32},{32,36}... | collective-permute-start | bytes 86024 | tf_op jit(solution)/shard_map/ppermute | solution.py:638
  13.7 0.6 reshape.51.docs_ref
  14.4 17.9 %all-to-all-done.own_ref = bf16[4,896,256]{2,1,0:T(8,128)(2,1)S(1)} async-done(((bf16[4,896,256]{2,1,0:T(8,128)(2,1)}), bf16[4,896,256]{2,1,0:T(8,128)(2,1)S(1)}, u32[]{:S(2)}, u32[]{:S(2)}) %all-to-all-start) | async-done | bytes 1835040 | tf_op jit(solution)/shard_map/all_to_all | solution.py:647
  32.3 6.1 %collective-permute-start = (bf16[4,448,256]{2,1,0:T(8,128)(2,1)S(1)}, bf16[4,448,256]{2,1,0:T(8,128)(2,1)}, u32[]{:S(2)}, u32[]{:S(2)}) collective-permute-start(bf16[4,448,256]{2,1,0:T(8,128)(2,1)S(1)} %slice.8), channel_id=1, source_target_pairs={{0,16},{4,20},{8,24},{12,28},{16,32},{20,36},{24,40},{28,44},{32,4... | collective-permute-start | bytes 2752520 | tf_op jit(solution)/shard_map/ppermute | solution.py:638
  39.0 9.2 %mixer_first.1 = bf16[2048,128]{1,0:T(8,128)(2,1)} custom-call(s32[4]{0:T(128)} %pad_add_fusion.where_ref, bf16[256,1792]{1,0:T(8,128)(2,1)} %x_ref.3, bf16[8,1792]{1,0:T(8,128)(2,1)} %copy-done.10, f32[4,1792]{1,0:T(4,128)} %weight_ref.3, bf16[256,1792]{1,0:T(8,128)(2,1)} %gate_ref.3, bf16[256,1792]{1,0:T(8,128)(2,1)} %grad_ref.3, f32[28,256]{1,0:T(8,128)} %bitcast.16, ...), custom_call_target="tpu_custom_call" | custom-call | flops 8000000000 | bytes 4000000 | tf_op jit(solution)/shard_map/mixer_first/pallas_call | solution.py:226
  48.2 18.3 %all_to_all.25.parts_ref = bf16[32,64,128]{2,1,0:T(8,128)(2,1)} all-to-all(bf16[32,64,128]{2,1,0:T(8,128)(2,1)} %bitcast.14), channel_id=1, replica_groups=mesh['seq_0'=4,'seq_1'=2,'seq_2'=4,'head'=4] {'seq_0','seq_1','seq_2'}, dimensions={0} | all-to-all | bytes 1048576 | tf_op jit(solution)/shard_map/all_to_all | solution.py:647
  66.5 2.3 %chain.1 = bf16[32,56,128]{2,1,0:T(8,128)(2,1)} custom-call(s32[4]{0:T(128)} %pad_add_fusion.where_ref, bf16[32,64,128]{2,1,0:T(8,128)(2,1)} %all_to_all.25.parts_ref), custom_call_target="tpu_custom_call" | custom-call | flops 2000000000 | bytes 1000000 | tf_op jit(solution)/shard_map/chain/pallas_call | solution.py:263
  68.8 5.4 %all-to-all-start.2 = ((bf16[32,56,128]{2,1,0:T(8,128)(2,1)}), bf16[32,56,128]{2,1,0:T(8,128)(2,1)S(1)}, u32[]{:S(2)}, u32[]{:S(2)}) async-start(bf16[32,56,128]{2,1,0:T(8,128)(2,1)} %chain.1), calls=%async_computation.2 | async-start | bytes 917504 | tf_op jit(solution)/shard_map/all_to_all | solution.py:647
  74.2 9.3 %attention.1 = (bf16[4,224,256]{2,1,0:T(8,128)(2,1)}, f32[4,448,256]{2,1,0:T(8,128)}, bf16[4,448,256]{2,1,0:T(8,128)(2,1)}) custom-call(s32[4]{0:T(128)} %pad_add_fusion.where_ref, s32[32,256]{1,0:T(8,128)} %reshape.51.docs_ref, bf16[4,896,256]{2,1,0:T(8,128)(2,1)} %copy-done, bf16[4,448,256]{2,1,0:T(8,128)(2,1)} %collective-permute-done.far_ref), custom_call_target="tpu_custom_call" | custom-call | flops 12000000000 | bytes 8000000 | tf_op jit(solution)/shard_map/attention/pallas_call | solution.py:574
  83.5 1.5 collective-permute-start.1
  85.0 0.7 all-to-all-done.2
  85.7 0.8 copy-done.3
  86.5 19.1 %mixer_second.1 = (bf16[256,1792]{1,0:T(8,128)(2,1)}, f32[8,1792]{1,0:T(8,128)}, f32[8,1792]{1,0:T(8,128)}, bf16[256,1792]{1,0:T(8,128)(2,1)}, f32[28,256]{1,0:T...) custom-call(s32[4]{0:T(128)} %pad_add_fusion.where_ref, bf16[256,1792]{1,0:T(8,128)(2,1)} %x_ref.3, ...), custom_call_target="tpu_custom_call" | custom-call | flops 17999998976 | bytes 8000000 | tf_op jit(solution)/shard_map/mixer_second/pallas_call | solution.py:424
  105.5 3.4 %all-to-all-start.4 = ((bf16[4,256,128]{2,1,0:T(8,128)(2,1)}), bf16[4,256,128]{2,1,0:T(8,128)(2,1)S(1)}, u32[]{:S(2)}, u32[]{:S(2)}) async-start(bf16[4,256,128]{2,1,0:T(8,128)(2,1)} %get-tuple-element.51), calls=%async_computation.4 | async-start | bytes 524288 | tf_op jit(solution)/shard_map/all_to_all | solution.py:647
  109.0 1.3 collective-permute-start.6
  110.3 4.7 %all-to-all-done.4.coeff_ref = bf16[4,256,128]{2,1,0:T(8,128)(2,1)S(1)} async-done(((bf16[4,256,128]{2,1,0:T(8,128)(2,1)}), bf16[4,256,128]{2,1,0:T(8,128)(2,1)S(1)}, u32[]{:S(2)}, u32[]{:S(2)}) %all-to-all-start.4) | async-done | bytes 262176 | tf_op jit(solution)/shard_map/all_to_all | solution.py:647
  114.9 10.3 %all-to-all-start.3 = ((bf16[32,64,128]{2,1,0:T(8,128)(2,1)}), bf16[32,64,128]{2,1,0:T(8,128)(2,1)S(1)}, u32[]{:S(2)}, u32[]{:S(2)}) async-start(bf16[32,64,128]{2,1,0:T(8,128)(2,1)} %get-tuple-element.50), calls=%async_computation.3 | async-start | bytes 1048576 | tf_op jit(solution)/shard_map/all_to_all | solution.py:647
  125.2 0.9 copy-done.9
  126.2 3.1 %merge.1 = (bf16[672,256]{1,0:T(8,128)(2,1)}, bf16[672,256]{1,0:T(8,128)(2,1)}, bf16[672,256]{1,0:T(8,128)(2,1)}, bf16[672,256]{1,0:T(8,128)(2,1)}) custom-call(s32[4]{0:T(128)} %pad_add_fusion.where_ref, bf16[4,224,256]{2,1,0:T(8,128)(2,1)} %get-tuple-element.35.dq_ref, f32[4,448,256]{2,1,0:T(8,128)} %get-tuple-element.36.dkv_ref, ...), custom_call_target="tpu_custom_call" | custom-call | flops 3000000000 | bytes 4000000 | tf_op jit(solution)/shard_map/merge/pallas_call | solution.py:601
  129.3 1.8 %collective-permute-start.2 = (bf16[672,256]{1,0:T(8,128)(2,1)}, bf16[672,256]{1,0:T(8,128)(2,1)S(1)}, u32[]{:S(2)}, u32[]{:S(2)}) collective-permute-start(bf16[672,256]{1,0:T(8,128)(2,1)} %get-tuple-element.39), channel_id=1, source_target_pairs={{0,4},{4,8},{8,12},{12,0},{1,5},{5,9},{9,13},{13,1},{2,6},{6,10},{... | collective-permute-start | bytes 1032200 | tf_op jit(solution)/shard_map/ppermute | solution.py:643
  131.1 2.7 %collective-permute-start.3 = (bf16[672,256]{1,0:T(8,128)(2,1)}, bf16[672,256]{1,0:T(8,128)(2,1)S(1)}, u32[]{:S(2)}, u32[]{:S(2)}) collective-permute-start(bf16[672,256]{1,0:T(8,128)(2,1)} %get-tuple-element.40), channel_id=1, source_target_pairs={{0,8},{4,12},{8,0},{12,4},{1,9},{5,13},{9,1},{13,5},{2,10},{6,14},... | collective-permute-start | bytes 1032200 | tf_op jit(solution)/shard_map/ppermute | solution.py:643
  133.8 1.5 collective-permute-start.4
  135.8 2.2 %all-to-all-done.3.bundle_ref = bf16[32,64,128]{2,1,0:T(8,128)(2,1)S(1)} async-done(((bf16[32,64,128]{2,1,0:T(8,128)(2,1)}), bf16[32,64,128]{2,1,0:T(8,128)(2,1)S(1)}, u32[]{:S(2)}, u32[]{:S(2)}) %all-to-all-start.3) | async-done | bytes 524320 | tf_op jit(solution)/shard_map/all_to_all | solution.py:647
  138.0 0.8 copy-done.1
  138.8 1.9 %finish.1 = (f32[4,1792]{1,0:T(4,128)}, f32[1,28]{1,0:T(1,128)}, f32[1,28]{1,0:T(1,128)}, f32[1,28]{1,0:T(1,128)}, f32[256,128]{1,0:T(8,128)}, /*index=5*/f32[256,128]{1,0:T(8,128)}) custom-call(bf16[32,64,128]{2,1,0:T(8,128)(2,1)} %copy-done.1, bf16[4,256,128]{2,1,0:T(8,128)(2,1)} %copy-done.2), custom_call_target="tpu_custom_call" | custom-call | tf_op jit(solution)/shard_map/finish/pallas_call | solution.py:481
  140.8 1.5 %collective-permute-done.2.refs_1_ = bf16[672,256]{1,0:T(8,128)(2,1)S(1)} collective-permute-done((bf16[672,256]{1,0:T(8,128)(2,1)}, bf16[672,256]{1,0:T(8,128)(2,1)S(1)}, u32[]{:S(2)}, u32[]{:S(2)}) %collective-permute-start.2) | collective-permute-done | bytes 344096 | tf_op jit(solution)/shard_map/ppermute | solution.py:643
  142.3 6.5 %collective-permute-done.3.refs_2_ = bf16[672,256]{1,0:T(8,128)(2,1)S(1)} collective-permute-done((bf16[672,256]{1,0:T(8,128)(2,1)}, bf16[672,256]{1,0:T(8,128)(2,1)S(1)}, u32[]{:S(2)}, u32[]{:S(2)}) %collective-permute-start.3) | collective-permute-done | bytes 344096 | tf_op jit(solution)/shard_map/ppermute | solution.py:643
  148.8 0.7 copy-done.5
  149.7 2.7 %unpack.1 = (bf16[256,896]{1,0:T(8,128)(2,1)}, bf16[256,896]{1,0:T(8,128)(2,1)}, bf16[256,896]{1,0:T(8,128)(2,1)}) custom-call(s32[4]{0:T(128)} %pad_add_fusion.where_ref, bf16[672,256]{1,0:T(8,128)(2,1)} %get-tuple-element.38.refs_0_, bf16[672,256]{1,0:T(8,128)(2,1)} %copy-done.4, bf16[672,256]{1,0:T(8,128)(2,1)} %copy-done.5, bf16[672,256]{1,0:T(8,128)(2,1)} %copy-done.6), custom_call_target="tpu_custom_call" | custom-call | tf_op jit(solution)/shard_map/unpack/pallas_call | solution.py:625
  (26 shorter events, 2.1 us)
Async XLA Ops:
  3.9 9.9 %copy-start.8 = (s32[8192]{0:T(1024)S(1)}, s32[8192]{0:T(1024)}, u32[]{:S(2)}) copy-start(s32[8192]{0:T(1024)} %param.19) | copy-start | bytes 98308
  3.9 28.4 %all-to-all-start = ((bf16[4,896,256]{2,1,0:T(8,128)(2,1)}), bf16[4,896,256]{2,1,0:T(8,128)(2,1)S(1)}, u32[]{:S(2)}, u32[]{:S(2)}) async-start(bf16[4,896,256]{2,1,0:T(8,128)(2,1)} %pack.1), calls=%async_computation | async-start | bytes 3670016 | tf_op jit(solution)/shard_map/all_to_all | solution.py:647
  9.2 29.3 %collective-permute-start.5 = (bf16[8,1792]{1,0:T(8,128)(2,1)S(1)}, bf16[8,1792]{1,0:T(8,128)(2,1)S(1)}, u32[]{:S(2)}, u32[]{:S(2)}) collective-permute-start(bf16[8,1792]{1,0:T(8,128)(2,1)S(1)} %slice.7), channel_id=1, source_target_pairs={{0,4},{4,8},{8,12},{12,16},{16,20},{20,24},{24,28},{28,32},{32,36}... | collective-permute-start | bytes 86024 | tf_op jit(solution)/shard_map/ppermute | solution.py:638
  32.3 16.0 %copy-start = (bf16[4,896,256]{2,1,0:T(8,128)(2,1)}, bf16[4,896,256]{2,1,0:T(8,128)(2,1)S(1)}, u32[]{:S(2)}) copy-start(bf16[4,896,256]{2,1,0:T(8,128)(2,1)S(1)} %all-to-all-done.own_ref) | copy-start | bytes 5505028
  32.3 41.9 %collective-permute-start = (bf16[4,448,256]{2,1,0:T(8,128)(2,1)S(1)}, bf16[4,448,256]{2,1,0:T(8,128)(2,1)}, u32[]{:S(2)}, u32[]{:S(2)}) collective-permute-start(bf16[4,448,256]{2,1,0:T(8,128)(2,1)S(1)} %slice.8), channel_id=1, source_target_pairs={{0,16},{4,20},{8,24},{12,28},{16,32},{20,36},{24,40},{28,44},{32,4... | collective-permute-start | bytes 2752520 | tf_op jit(solution)/shard_map/ppermute | solution.py:638
  38.4 0.6 copy-start.10
  68.8 16.9 %all-to-all-start.2 = ((bf16[32,56,128]{2,1,0:T(8,128)(2,1)}), bf16[32,56,128]{2,1,0:T(8,128)(2,1)S(1)}, u32[]{:S(2)}, u32[]{:S(2)}) async-start(bf16[32,56,128]{2,1,0:T(8,128)(2,1)} %chain.1), calls=%async_computation.2 | async-start | bytes 917504 | tf_op jit(solution)/shard_map/all_to_all | solution.py:647
  83.5 41.7 %collective-permute-start.1 = (bf16[4,448,256]{2,1,0:T(8,128)(2,1)}, bf16[4,448,256]{2,1,0:T(8,128)(2,1)S(1)}, u32[]{:S(2)}, u32[]{:S(2)}) collective-permute-start(bf16[4,448,256]{2,1,0:T(8,128)(2,1)} %get-tuple-element.37), channel_id=1, source_target_pairs={{16,0},{20,4},{24,8},{28,12},{32,16},{36,20},{40,24},{44,28},{48,3... | collective-permute-start | bytes 2752520 | tf_op jit(solution)/shard_map/ppermute | solution.py:638
  85.7 0.8 copy-start.3
  105.5 9.4 %all-to-all-start.4 = ((bf16[4,256,128]{2,1,0:T(8,128)(2,1)}), bf16[4,256,128]{2,1,0:T(8,128)(2,1)S(1)}, u32[]{:S(2)}, u32[]{:S(2)}) async-start(bf16[4,256,128]{2,1,0:T(8,128)(2,1)} %get-tuple-element.51), calls=%async_computation.4 | async-start | bytes 524288 | tf_op jit(solution)/shard_map/all_to_all | solution.py:647
  109.0 26.3 %collective-permute-start.6 = (f32[8,1792]{1,0:T(8,128)}, f32[8,1792]{1,0:T(8,128)S(1)}, u32[]{:S(2)}, u32[]{:S(2)}) collective-permute-start(f32[8,1792]{1,0:T(8,128)} %get-tuple-element.47), channel_id=1, source_target_pairs={{4,0},{8,4},{12,8},{16,12},{20,16},{24,20},{28,24},{32,28},{36,32}... | collective-permute-start | bytes 172040 | tf_op jit(solution)/shard_map/ppermute | solution.py:638
  114.9 14.4 %copy-start.2 = (bf16[4,256,128]{2,1,0:T(8,128)(2,1)}, bf16[4,256,128]{2,1,0:T(8,128)(2,1)S(1)}, u32[]{:S(2)}) copy-start(bf16[4,256,128]{2,1,0:T(8,128)(2,1)S(1)} %all-to-all-done.4.coeff_ref) | copy-start | bytes 786436
  114.9 23.1 %all-to-all-start.3 = ((bf16[32,64,128]{2,1,0:T(8,128)(2,1)}), bf16[32,64,128]{2,1,0:T(8,128)(2,1)S(1)}, u32[]{:S(2)}, u32[]{:S(2)}) async-start(bf16[32,64,128]{2,1,0:T(8,128)(2,1)} %get-tuple-element.50), calls=%async_computation.3 | async-start | bytes 1048576 | tf_op jit(solution)/shard_map/all_to_all | solution.py:647
  125.2 0.9 copy-start.9
  126.2 9.1 %copy-start.7 = (f32[8,1792]{1,0:T(8,128)S(1)}, f32[8,1792]{1,0:T(8,128)}, u32[]{:S(2)}) copy-start(f32[8,1792]{1,0:T(8,128)} %get-tuple-element.46) | copy-start | bytes 172036
  129.3 13.0 %collective-permute-start.2 = (bf16[672,256]{1,0:T(8,128)(2,1)}, bf16[672,256]{1,0:T(8,128)(2,1)S(1)}, u32[]{:S(2)}, u32[]{:S(2)}) collective-permute-start(bf16[672,256]{1,0:T(8,128)(2,1)} %get-tuple-element.39), channel_id=1, source_target_pairs={{0,4},{4,8},{8,12},{12,0},{1,5},{5,9},{9,13},{13,1},{2,6},{6,10},{... | collective-permute-start | bytes 1032200 | tf_op jit(solution)/shard_map/ppermute | solution.py:643
  131.1 17.7 %collective-permute-start.3 = (bf16[672,256]{1,0:T(8,128)(2,1)}, bf16[672,256]{1,0:T(8,128)(2,1)S(1)}, u32[]{:S(2)}, u32[]{:S(2)}) collective-permute-start(bf16[672,256]{1,0:T(8,128)(2,1)} %get-tuple-element.40), channel_id=1, source_target_pairs={{0,8},{4,12},{8,0},{12,4},{1,9},{5,13},{9,1},{13,5},{2,10},{6,14},... | collective-permute-start | bytes 1032200 | tf_op jit(solution)/shard_map/ppermute | solution.py:643
  133.8 15.0 %collective-permute-start.4 = (bf16[672,256]{1,0:T(8,128)(2,1)}, bf16[672,256]{1,0:T(8,128)(2,1)S(1)}, u32[]{:S(2)}, u32[]{:S(2)}) collective-permute-start(bf16[672,256]{1,0:T(8,128)(2,1)} %get-tuple-element.41), channel_id=1, source_target_pairs={{0,12},{4,0},{8,4},{12,8},{1,13},{5,1},{9,5},{13,9},{2,14},{6,2},{... | collective-permute-start | bytes 1032200 | tf_op jit(solution)/shard_map/ppermute | solution.py:643
  138.0 0.8 copy-start.1
  142.3 6.5 %copy-start.4 = (bf16[672,256]{1,0:T(8,128)(2,1)}, bf16[672,256]{1,0:T(8,128)(2,1)S(1)}, u32[]{:S(2)}) copy-start(bf16[672,256]{1,0:T(8,128)(2,1)S(1)} %collective-permute-done.2.refs_1_) | copy-start | bytes 1032196
  148.8 0.7 copy-start.5
  148.8 0.9 copy-start.6

commit v3 on v2

--- a/solution.py
+++ b/solution.py
@@ -17,10 +17,12 @@
 T = 256
 LOCAL_HEADS = 4
 BLK = 256
+HALF = T // 2
 HEADS_BLK = BLK // 64
 COLS = 1792
 STEPS = COLS // BLK
 NEG = -1e30
+LOG2E = 1.4426950408889634
 F32 = jnp.float32
 BF16 = jnp.bfloat16
 
@@ -49,7 +51,7 @@
 
 
 def sigmoid(v):
-    return 1.0 / (1.0 + jnp.exp(-v))
+    return 0.5 + 0.5 * jnp.tanh(0.5 * v)
 
 
 def iota(shape, dim):
@@ -122,7 +124,7 @@
     raw = raw_steps(step_ref) + params[0:1]
     step, decay = step_and_decay(raw, params)
     lower = jnp.where(iota((T, T), 0) >= iota((T, T), 1), 1.0, 0.0)
-    cum = exact(lower, decay)
+    cum = exact(lower, decay) * LOG2E
     for n, part in enumerate(split(cum, 3)):
         cum_s[n] = part
     for n, part in enumerate(split(step, 2)):
@@ -140,8 +142,8 @@
     spread = spread_of(step_id)
     cum = dot(cum_s[0], spread) + dot(cum_s[1], spread) + dot(cum_s[2], spread)
     step = dot(step_s[0], spread) + dot(step_s[1], spread)
-    enter = jnp.exp(cum + prev_s[...])
-    to_end = jnp.exp(cum[T - 1 : T] - cum + end_s[...])
+    enter = jnp.exp2(cum + prev_s[...])
+    to_end = jnp.exp2(cum[T - 1 : T] - cum + end_s[...])
     return spread, cum, step, enter, to_end
 
 
@@ -175,7 +177,7 @@
         cum = token_setup(
             where_ref, docs_ref, step_ref, params, cum_s, step_s, mask_s, prev_s, end_s
         )[2]
-        through = jnp.exp(cum[T - 1 : T] + prev_s[T - 1 : T, 0:1])
+        through = jnp.exp2(cum[T - 1 : T] + prev_s[T - 1 : T, 0:1])
         high, low = split(through, 2)
         row = iota((8, 128), 0)
         both = jnp.where(row == 0, high.astype(F32), jnp.where(row == 1, low.astype(F32), 0.0))
@@ -280,7 +282,7 @@
     skip_ref, docs_ref, in_ref, out_ref, state_ref,
     dx_ref, tail_ref, spill_ref, dgate_ref, dstep_ref, coeff_ref, bundle_ref,
     cum_s, step_s, mask_s, prev_s, end_s, params_s,
-    cumt_s, pair_s, causal_s, dpair_s, coeff_s, row_s, dt_s, ends_s, bundle_s,
+    cumt_s, pair_s, causal_s, dtop_s, dbottom_s, coeff_s, row_s, dt_s, ends_s, bundle_s,
     in_low_s, in_high_s, out_low_s, out_high_s,
 ):
     step_id = pl.program_id(0)
@@ -298,7 +300,8 @@
         in_low_s[...], in_high_s[...] = group_halves(where_ref, in_ref)
         out_low_s[...], out_high_s[...] = group_halves(where_ref, out_ref)
         pair_s[...] = dot(out_low_s[...], in_low_s[...], NT)
-        dpair_s[...] = jnp.zeros((T, T), F32)
+        dtop_s[...] = jnp.zeros((HALF, HALF), F32)
+        dbottom_s[...] = jnp.zeros((HALF, T), F32)
         coeff_s[...] = jnp.zeros((T, 128), F32)
         row_s[...] = jnp.zeros((T, 128), F32)
         dt_s[...] = jnp.zeros((T, 128), F32)
@@ -321,21 +324,40 @@
     grad_half = out_grad.astype(BF16)
 
     block_head = iota((T, BLK), 1) // 64
-    inner = jnp.zeros((T, BLK), F32)
-    dscaled = jnp.zeros((T, BLK), F32)
-    dpair = dpair_s[...]
+    tops, bottoms, scaled_parts, grad_parts = [], [], [], []
+    dtop, dbottom = dtop_s[...], dbottom_s[...]
     for k in range(HEADS_BLK):
         mine = block_head == k
-        cum_col = jnp.broadcast_to(cum[:, 64 * k : 64 * k + 1], (T, T))
+        cum_col = cum[:, 64 * k : 64 * k + 1]
         cum_row = cumt_s[pl.ds(step_id * HEADS_BLK + k, 1), :]
-        weights = jnp.exp(cum_col - cum_row + causal_s[...])
-        mixing = (pair_s[...] * weights).astype(BF16)
+        top = jnp.exp2(
+            jnp.broadcast_to(cum_col[:HALF], (HALF, HALF)) - cum_row[:, :HALF]
+            + causal_s[:HALF, :HALF]
+        )
+        bottom = jnp.exp2(
+            jnp.broadcast_to(cum_col[HALF:], (HALF, T)) - cum_row + causal_s[HALF:, :]
+        )
+        tops.append((pair_s[:HALF, :HALF] * top).astype(BF16))
+        bottoms.append((pair_s[HALF:, :] * bottom).astype(BF16))
         scaled_k = jnp.where(mine, scaled_half, jnp.zeros_like(scaled_half))
         grad_k = jnp.where(mine, grad_half, jnp.zeros_like(grad_half))
-        inner = inner + dot(mixing, scaled_k)
-        dscaled = dscaled + dot(mixing, grad_k, TN)
-        dpair = dpair + dot(grad_k, scaled_half, NT) * weights
-    dpair_s[...] = dpair
+        scaled_parts.append(scaled_k)
+        grad_parts.append(grad_k)
+        dtop = dtop + dot(grad_k[:HALF], scaled_half[:HALF], NT) * top
+        dbottom = dbottom + dot(grad_k[HALF:], scaled_half, NT) * bottom
+    dtop_s[...] = dtop
+    dbottom_s[...] = dbottom
+    join = jnp.concatenate
+    inner = join(
+        [
+            dot(join(tops, axis=1), join([v[:HALF] for v in scaled_parts], axis=0)),
+            dot(join(bottoms, axis=1), join(scaled_parts, axis=0)),
+        ],
+        axis=0,
+    )
+    upper_part = dot(join(tops, axis=0), join([v[:HALF] for v in grad_parts], axis=0), TN)
+    dscaled = dot(join(bottoms, axis=0), join([v[HALF:] for v in grad_parts], axis=0), TN)
+    dscaled = join([dscaled[:HALF] + upper_part, dscaled[HALF:]], axis=0)
 
     state = state_ref[...]
     carried = dot(out_low, state, NT) * enter
@@ -354,8 +376,8 @@
     grad_round = grad_half.astype(F32)
     scaled_round = scaled_half.astype(F32)
     balance = grad_round * ssm_out - scaled_round * dscaled
-    row_s[...] += sum(dot(part, spread, NT) for part in split(balance, 3))
-    dt_s[...] += sum(dot(part, spread, NT) for part in split(dscaled * act, 2))
+    row_s[...] += sum(dot(part, spread, NT) for part in split(balance, 2))
+    dt_s[...] += dot((dscaled * act).astype(BF16), spread, NT)
 
     state_wide = state.astype(F32)
     product = state_wide * pltpu.roll(state_wide, STATE, 1)
@@ -411,11 +433,14 @@
         bundle = bundle_s[...].astype(BF16)
         for shard in range(SHARDS):
             bundle_ref[shard] = bundle
-        dpair_half = dpair.astype(BF16)
-        total = coeff_s[...] + dot(dpair_half, in_low_s[...])
-        total = (total + dot(dpair_half, out_high_s[...], TN)).astype(BF16)
-        for peer in range(coeff_ref.shape[0]):
-            coeff_ref[peer] = total
+        top_half, bottom_half = dtop.astype(BF16), dbottom.astype(BF16)
+        in_low, out_high = in_low_s[...], out_high_s[...]
+        out_part = join([dot(top_half, in_low[:HALF]), dot(bottom_half, in_low)], axis=0)
+        in_part = dot(bottom_half, out_high[HALF:], TN)
+        in_part = join(
+            [in_part[:HALF] + dot(top_half, out_high[:HALF], TN), in_part[HALF:]], axis=0
+        )
+        coeff_ref[...] = (coeff_s[...] + out_part + in_part).astype(BF16)
 
 
 def mixer_second(*arrays):
@@ -427,7 +452,7 @@
         in_specs=mixer_specs(heads) + [pl.BlockSpec((BLK, 128), lambda c: (c, 0))],
         out_specs=[
             column_block(T), column_block(8), column_block(8), column_block(T),
-            whole((heads, T)), whole((LOCAL_HEADS, T, 128)), whole((SHARDS, BUNDLE + 8, 128)),
+            whole((heads, T)), whole((T, 128)), whole((SHARDS, BUNDLE + 8, 128)),
         ],
         out_shape=[
             jax.ShapeDtypeStruct((T, COLS), BF16),
@@ -435,14 +460,15 @@
             jax.ShapeDtypeStruct((8, COLS), F32),
             jax.ShapeDtypeStruct((T, COLS), BF16),
             jax.ShapeDtypeStruct((heads, T), F32),
-            jax.ShapeDtypeStruct((LOCAL_HEADS, T, 128), BF16),
+            jax.ShapeDtypeStruct((T, 128), BF16),
             jax.ShapeDtypeStruct((SHARDS, BUNDLE + 8, 128), BF16),
         ],
         scratch_shapes=TOKEN_SCRATCH + [
             pltpu.VMEM((128, T), F32),
             pltpu.VMEM((T, T), F32),
             pltpu.VMEM((T, T), F32),
-            pltpu.VMEM((T, T), F32),
+            pltpu.VMEM((HALF, HALF), F32),
+            pltpu.VMEM((HALF, T), F32),
             pltpu.VMEM((T, 128), F32),
             pltpu.VMEM((T, 128), F32),
             pltpu.VMEM((T, 128), F32),
@@ -455,7 +481,13 @@
     )(*arrays)
 
 
-def finish_kernel(bundle_ref, coeff_ref, weight_ref, bias_ref, rate_ref, skip_ref, in_ref, out_ref):
+def finish_kernel(
+    where_ref, bundle_ref, *refs
+):
+    coeff_refs = refs[:LOCAL_HEADS]
+    weight_ref, bias_ref, rate_ref, skip_ref, in_ref, out_ref, coeff_s = refs[LOCAL_HEADS:]
+    for turn, ref in enumerate(coeff_refs):
+        coeff_s[lax.rem(where_ref[4] - turn + LOCAL_HEADS, LOCAL_HEADS)] = ref[...].astype(F32)
     total = bundle_ref[0].astype(F32)
     for shard in range(1, SHARDS):
         total = total + bundle_ref[shard].astype(F32)
@@ -468,50 +500,61 @@
     for n, ref in enumerate((bias_ref, rate_ref, skip_ref)):
         row = BUNDLE + 2 * n
         ref[...] = (total[row : row + 1] + total[row + 1 : row + 2])[:, : ref.shape[1]]
-    low = coeff_ref[0].astype(F32) + coeff_ref[1].astype(F32)
-    high = coeff_ref[2].astype(F32) + coeff_ref[3].astype(F32)
+    low, high = coeff_s[0] + coeff_s[1], coeff_s[2] + coeff_s[3]
     left = iota((T, 128), 1) < STATE
     out_ref[...] = jnp.where(left, low, pltpu.roll(high, STATE, 1))
     in_ref[...] = jnp.where(left, pltpu.roll(low, STATE, 1), high)
 
 
-def finish(bundle, coeff, heads):
+def finish(where, bundle, coeffs, heads):
     small = jax.ShapeDtypeStruct((1, heads), F32)
     wide = jax.ShapeDtypeStruct((T, 128), F32)
     return pl.pallas_call(
         finish_kernel,
-        in_specs=[IN_VMEM] * 2,
+        in_specs=[IN_SMEM] + [IN_VMEM] * (1 + LOCAL_HEADS),
         out_specs=[IN_VMEM] * 6,
         out_shape=[jax.ShapeDtypeStruct((KERNEL, COLS), F32), small, small, small, wide, wide],
+        scratch_shapes=[pltpu.VMEM((LOCAL_HEADS, T, 128), F32)],
         name="finish",
-    )(bundle, coeff)
+    )(where, bundle, *coeffs)
 
 
 ROW = 4
-K_AT, V_AT, Q_AT, G_AT = (slice(n * HEAD_DIM, (n + 1) * HEAD_DIM) for n in range(4))
-KV_AT = slice(0, 2 * HEAD_DIM)
-
-
-def pack_kernel(k_ref, v_ref, q_ref, g_ref, out_ref):
-    for ref, place in ((k_ref, K_AT), (v_ref, V_AT), (q_ref, Q_AT), (g_ref, G_AT)):
-        turned = jnp.transpose(ref[...])
+K_AT, V_AT, Q_AT = (slice(n * HEAD_DIM, (n + 1) * HEAD_DIM) for n in range(3))
+
+
+def pack_kernel(where_ref, k_ref, v_ref, q_ref, g_ref, *refs):
+    out_refs, turned_s = refs[: 2 * ROW], refs[2 * ROW]
+    for n, ref in enumerate((k_ref, v_ref, q_ref, g_ref)):
+        half = slice((n % 2) * HEAD_DIM, (n % 2 + 1) * HEAD_DIM)
+        turned_part = jnp.transpose(ref[...])
         for head in range(LOCAL_HEADS):
-            out_ref[head, place] = turned[head * HEAD_DIM : (head + 1) * HEAD_DIM]
-
-
-def pack(keys, values, queries, grads):
-    return pl.pallas_call(
+            turned_s[n // 2, head, half] = turned_part[head * HEAD_DIM : (head + 1) * HEAD_DIM]
+    for turn in range(ROW):
+        head = lax.rem(where_ref[3] + turn, ROW)
+        out_refs[turn][...] = turned_s[0, head]
+        out_refs[ROW + turn][...] = turned_s[1, head]
+
+
+def pack(where, keys, values, queries, grads):
+    outs = pl.pallas_call(
         pack_kernel,
-        in_specs=[IN_VMEM] * 4,
-        out_specs=IN_VMEM,
-        out_shape=jax.ShapeDtypeStruct((LOCAL_HEADS, 4 * HEAD_DIM, T), BF16),
+        in_specs=[IN_SMEM] + [IN_VMEM] * 4,
+        out_specs=[IN_VMEM] * (2 * ROW),
+        out_shape=[jax.ShapeDtypeStruct((2 * HEAD_DIM, T), BF16)] * (2 * ROW),
+        scratch_shapes=[pltpu.VMEM((2, LOCAL_HEADS, 2 * HEAD_DIM, T), BF16)],
         name="pack",
-    )(keys, values, queries, grads)
-
-
-def attention_kernel(
-    where_ref, docs_ref, own_ref, far_ref, dq_ref, dkv_ref, back_ref, far_s
-):
+    )(where, keys, values, queries, grads)
+    return outs[:ROW], outs[ROW:]
+
+
+def attention_kernel(where_ref, docs_ref, *refs):
+    arrived, (dq_ref, dkv_ref, back_ref, far_s, kv_s, qg_s) = refs[: 3 * ROW], refs[3 * ROW :]
+    for turn in range(ROW):
+        block = lax.rem(where_ref[3] - turn + ROW, ROW)
+        qg_s[block] = arrived[turn][...]
+        kv_s[ROW + block] = arrived[ROW + turn][...]
+        kv_s[block] = arrived[2 * ROW + turn][...]
     first_block = where_ref[2] * ROW
     later = iota((T, T), 1) > iota((T, T), 0)
     scale = HEAD_DIM ** (-0.5)
@@ -524,12 +567,11 @@
     rows = {block: doc_row(block) for block in range(-ROW, ROW)}
     for i in range(ROW):
         own_doc = columns_of(rows[i])
-        qt, gt = own_ref[i, Q_AT], own_ref[i, G_AT]
+        qt, gt = qg_s[i, K_AT], qg_s[i, V_AT]
         q, g = jnp.transpose(qt), jnp.transpose(gt)
 
         def part(gap, place):
-            block = i - gap
-            return own_ref[block, place] if block >= 0 else far_ref[block + ROW, place]
+            return kv_s[ROW + i - gap, place]
 
         scores = []
         top = None
@@ -539,11 +581,11 @@
                 same = same & jnp.logical_not(later)
             if gap == ROW:
                 same = same & later
-            s = jnp.where(same, dot(q, part(gap, K_AT)) * scale, NEG)
+            s = jnp.where(same, dot(q, part(gap, K_AT)) * (scale * LOG2E), NEG)
             scores.append(s)
             top = s if top is None else jnp.maximum(top, s)
         top = jnp.max(top, axis=1, keepdims=True)
-        expos = [jnp.exp(s - top) for s in scores]
+        expos = [jnp.exp2(s - top) for s in scores]
         total = jnp.sum(sum(expos), axis=1, keepdims=True)
         inverse = 1.0 / jnp.maximum(total, 1.0)
         probs = [e * inverse for e in expos]
@@ -569,21 +611,25 @@
         dq_ref[i] = (dq * scale).astype(BF16)
 
 
-def attention(where, docs, own, far):
+def attention(where, docs, qg, kv, far):
     pair = (ROW, 2 * HEAD_DIM, T)
     return pl.pallas_call(
         attention_kernel,
-        in_specs=[IN_SMEM] + [IN_VMEM] * 3,
+        in_specs=[IN_SMEM] + [IN_VMEM] * (1 + 3 * ROW),
         out_specs=[IN_VMEM] * 3,
         out_shape=[
             jax.ShapeDtypeStruct((ROW, HEAD_DIM, T), BF16),
             jax.ShapeDtypeStruct(pair, F32),
             jax.ShapeDtypeStruct(pair, BF16),
         ],
-        scratch_shapes=[pltpu.VMEM(pair, F32)],
+        scratch_shapes=[
+            pltpu.VMEM(pair, F32),
+            pltpu.VMEM((2 * ROW, 2 * HEAD_DIM, T), BF16),
+            pltpu.VMEM(pair, BF16),
+        ],
         cost_estimate=pl.CostEstimate(flops=12 * 10**9, bytes_accessed=8 * 10**6, transcendentals=0),
         name="attention",
-    )(where, docs, own, far)
+    )(where, docs, *qg, *kv, *far)
 
 
 def merge_kernel(where_ref, dq_ref, dkv_ref, back_ref, *out_refs):
@@ -638,9 +684,12 @@
     return lax.ppermute(value, axis, [(source, source + steps) for source in range(initial, last)])
 
 
-def turned(value, axis, steps):
+def turns(parts, axis):
     count = lax.axis_size(axis)
-    return lax.ppermute(value, axis, [(n, (n + steps) % count) for n in range(count)])
+    return [parts[0]] + [
+        lax.ppermute(part, axis, [(n, (n + turn) % count) for n in range(count)])
+        for turn, part in enumerate(parts[1:], 1)
+    ]
 
 
 def exchange(array, axis):
@@ -654,13 +703,14 @@
     heads = step_raw.shape[1]
     shard = lax.axis_index(SEQ)
     group = lax.axis_index("head") * heads // (SSM_HEADS // GROUPS)
-    where = jnp.stack([shard, group, shard // ROW, lax.axis_index("seq_2")]).astype(jnp.int32)
+    where = jnp.stack([shard, group, shard // ROW, lax.axis_index("seq_2"), lax.axis_index("head")]).astype(jnp.int32)
     docs = doc_ids.reshape(SHARDS, T)
     halo = passed_along(conv_input[T - 8 :], SEQ, 1)
-    packed = pack(keys, values, queries, attn_grad)
-    own = exchange(packed, "seq_2")
-    borrowed = own[:, KV_AT]
-    far = passed_along(borrowed, SEQ, ROW)
+    kv_parts, qg_parts = pack(where, keys, values, queries, attn_grad)
+    kv = turns(kv_parts, "seq_2")
+    qg = turns(qg_parts, "seq_2")
+    far = [passed_along(kv[0], SEQ, ROW)]
+    far = far + [passed_along(part, SEQ, ROW) for part in kv[1:]]
 
     mixer_args = (
         where, conv_input, halo, conv_weight, gate_input, mix_grad, step_raw.T,
@@ -671,15 +721,17 @@
     gathered = exchange(parts, SEQ)
     scanned = chain(where, gathered)
     entering = exchange(scanned, SEQ).reshape(COLS, 128)
-    dq, dkv, back = attention(where, docs, own, far)
+    dq, dkv, back = attention(where, docs, qg, kv, far)
     returned = passed_along(back, SEQ, -ROW)
     dx, tail, spill, dgate, dstep, coeff, bundle = mixer_second(*mixer_args, entering)
     spilled = passed_along(spill, SEQ, -1)
     bundles = exchange(bundle, SEQ)
-    coeffs = exchange(coeff, "head")
-    kept, *leaving = merge(where, dq, dkv, returned)
-    swapped = [kept] + [turned(part, "seq_2", n) for n, part in enumerate(leaving, 1)]
-    grad_weight, grad_bias, grad_rate, grad_skip, sum_in, sum_out = finish(bundles, coeffs, heads)
+    coeffs = turns([coeff] * LOCAL_HEADS, "head")
+    leaving = merge(where, dq, dkv, returned)
+    swapped = turns(leaving, "seq_2")
+    grad_weight, grad_bias, grad_rate, grad_skip, sum_in, sum_out = finish(
+        where, bundles, coeffs, heads
+    )
     dq, dk, dv = unpack(where, swapped)
     tail = (tail + spilled).astype(BF16)
     grad_conv = lax.dynamic_update_slice_in_dim(dx, tail, T - 8, 0)

time: 153 us -> 150 us (0.980)
  starting transfers between devices: 42.3 us -> 71.9 us
  blocking collectives: 18.3 us -> 0 us
  waiting for transfers between devices: 33.5 us -> 18.5 us
  local copies, waits for them, and re-layouts: 5.45 us -> 8.48 us
  Pallas kernels: 50.8 us -> 48 us
    all_to_all x4 -> x3, waiting for transfers between devices: 25.5 us -> 2.02 us  [exchange(): return lax.all_to_all(array, axis, split_axis=0, concat_axis=0, tiled=True)]
    all_to_all x1 -> x0, blocking collectives: 18.3 us -> none  [exchange(): return lax.all_to_all(array, axis, split_axis=0, concat_axis=0, tiled=True)]
    ppermute x4 -> x7, starting transfers between devices: 12.7 us -> 23.4 us  [passed_along(): lax.ppermute(value, axis, [(source, source + steps) for source in range(i...]
    ppermute x3 -> x12, starting transfers between devices: 5.93 us -> 16.1 us  [turns(): lax.ppermute(part, axis, [(n, (n + turn) % count) for n in range(count)])]
    all_to_all x4 -> x3, starting transfers between devices: 23.7 us -> 32.4 us  [exchange(): return lax.all_to_all(array, axis, split_axis=0, concat_axis=0, tiled=True)]
    ppermute x3 -> x12, waiting for transfers between devices: 8.04 us -> 16.4 us  [turns(): lax.ppermute(part, axis, [(n, (n + turn) % count) for n in range(count)])]
    pallas_call x1, Pallas kernels: 19.1 us -> 16.3 us  [mixer_second(): pl.pallas_call(mixer_second_kernel, grid=(STEPS,), in_specs=mixer_specs(h...]
    unnamed x22 -> x44, local copies, waits for them, and re-layouts: 4.02 us -> 5.67 us
  transfers between devices with their start and end apart: 11 -> 22, of which waited for: 6 -> 5; matrix products, arithmetic and copies ran while one was open for 2% -> 2% of each run, Pallas kernels for 29% -> 24%
where the time goes in v3:
time: 150 us; the launch traced here: 149 us
  starting transfers between devices  71.9 us (48%)
  Pallas kernels  48 us (32%)
  waiting for transfers between devices  18.5 us (12%)
  local copies, waits for them, and re-layouts  8.48 us (6%)
    all_to_all x3, starting transfers between devices, exchange(): return lax.all_to_all(array, axis, split_axis=0, concat_axis=0, tiled=True)  32.4 us
    ppermute x7, starting transfers between devices, passed_along(): lax.ppermute(value, axis, [(source, source + steps) for source in range(i...  23.4 us
    ppermute x12, waiting for transfers between devices, turns(): lax.ppermute(part, axis, [(n, (n + turn) % count) for n in range(count)])  16.4 us
    pallas_call x1, Pallas kernels, mixer_second(): pl.pallas_call(mixer_second_kernel, grid=(STEPS,), in_specs=mixer_specs(h...  16.3 us
    ppermute x12, starting transfers between devices, turns(): lax.ppermute(part, axis, [(n, (n + turn) % count) for n in range(count)])  16.1 us
    pallas_call x1, Pallas kernels, attention(): pl.pallas_call(attention_kernel, in_specs=[IN_SMEM] + [IN_VMEM] * (1 + 3...  9.58 us
    pallas_call x1, Pallas kernels, mixer_first(): pl.pallas_call(mixer_first_kernel, grid=(STEPS,), in_specs=mixer_specs(he...  9.06 us
    unnamed x44, local copies, waits for them, and re-layouts  5.67 us
  transfers between devices with their start and end apart: 22, of which 5 were waited for; matrix products, arithmetic and copies ran while one was open for 2% of the time, Pallas kernels for 24%

profile of v3, /device:TPU:0, one launch (start us, length us, event | category | flops | bytes accessed | tf_op | source)
XLA Modules:
  0.0 148.6 jit_solution(9905441287855241489)
XLA Ops:
  1.4 3.5 %collective-permute-start.14 = (bf16[8,1792]{1,0:T(8,128)(2,1)S(1)}, bf16[8,1792]{1,0:T(8,128)(2,1)S(1)}, u32[]{:S(2)}, u32[]{:S(2)}) collective-permute-start(bf16[8,1792]{1,0:T(8,128)(2,1)S(1)} %slice.3), channel_id=1, source_target_pairs={{0,4},{4,8},{8,12},{12,16},{16,20},{20,24},{24,28},{28,32},{32,36}... | collective-permute-start | bytes 86024 | tf_op jit(solution)/shard_map/ppermute | solution.py:684
  4.9 1.4 reshape.51.docs_ref
  7.6 9.1 %mixer_first.1 = bf16[2048,128]{1,0:T(8,128)(2,1)} custom-call(s32[5]{0:T(128)} %stack.23.where_ref, bf16[256,1792]{1,0:T(8,128)(2,1)} %x_ref.3, bf16[8,1792]{1,0:T(8,128)(2,1)} %copy-done.21, f32[4,1792]{1,0:T(4,128)} %weight_ref.3, bf16[256,1792]{1,0:T(8,128)(2,1)} %gate_ref.3, bf16[256,1792]{1,0:T(8,128)(2,1)} %grad_ref.3, f32[28,256]{1,0:T(8,128)} %bitcast.17, ...), custom_call_target="tpu_custom_call" | custom-call | flops 8000000000 | bytes 4000000 | tf_op jit(solution)/shard_map/mixer_first/pallas_call | solution.py:228
  16.7 12.2 %all-to-all-start = ((bf16[32,64,128]{2,1,0:T(8,128)(2,1)}), bf16[32,64,128]{2,1,0:T(8,128)(2,1)S(1)}, u32[]{:S(2)}, u32[]{:S(2)}) async-start(bf16[32,64,128]{2,1,0:T(8,128)(2,1)} %bitcast.15), calls=%async_computation | async-start | bytes 1048576 | tf_op jit(solution)/shard_map/all_to_all | solution.py:696
  28.9 3.0 %pack.1 = (bf16[448,256]{1,0:T(8,128)(2,1)}, bf16[448,256]{1,0:T(8,128)(2,1)}, bf16[448,256]{1,0:T(8,128)(2,1)}, bf16[448,256]{1,0:T(8,128)(2,1)}, bf16[448,256]...) custom-call(s32[5]{0:T(128)} %stack.23.where_ref, ...), custom_call_target="tpu_custom_call" | custom-call | tf_op jit(solution)/shard_map/pack/pallas_call | solution.py:540
  31.9 1.8 %collective-permute-start = (bf16[448,256]{1,0:T(8,128)(2,1)}, bf16[448,256]{1,0:T(8,128)(2,1)S(1)}, u32[]{:S(2)}, u32[]{:S(2)}) collective-permute-start(bf16[448,256]{1,0:T(8,128)(2,1)} %get-tuple-element.44), channel_id=1, source_target_pairs={{0,4},{4,8},{8,12},{12,0},{1,5},{5,9},{9,13},{13,1},{2,6},{6,10},{... | collective-permute-start | bytes 688136 | tf_op jit(solution)/shard_map/ppermute | solution.py:690
  33.7 2.7 %collective-permute-start.1 = (bf16[448,256]{1,0:T(8,128)(2,1)}, bf16[448,256]{1,0:T(8,128)(2,1)S(1)}, u32[]{:S(2)}, u32[]{:S(2)}) collective-permute-start(bf16[448,256]{1,0:T(8,128)(2,1)} %get-tuple-element.45), channel_id=1, source_target_pairs={{0,8},{4,12},{8,0},{12,4},{1,9},{5,13},{9,1},{13,5},{2,10},{6,14},... | collective-permute-start | bytes 688136 | tf_op jit(solution)/shard_map/ppermute | solution.py:690
  36.4 2.9 %collective-permute-start.4 = (bf16[448,256]{1,0:T(8,128)(2,1)}, bf16[448,256]{1,0:T(8,128)(2,1)S(1)}, u32[]{:S(2)}, u32[]{:S(2)}) collective-permute-start(bf16[448,256]{1,0:T(8,128)(2,1)} %get-tuple-element.49), channel_id=1, source_target_pairs={{0,8},{4,12},{8,0},{12,4},{1,9},{5,13},{9,1},{13,5},{2,10},{6,14},... | collective-permute-start | bytes 688136 | tf_op jit(solution)/shard_map/ppermute | solution.py:690
  39.9 6.5 %collective-permute-done.refs_1_ = bf16[448,256]{1,0:T(8,128)(2,1)S(1)} collective-permute-done((bf16[448,256]{1,0:T(8,128)(2,1)}, bf16[448,256]{1,0:T(8,128)(2,1)S(1)}, u32[]{:S(2)}, u32[]{:S(2)}) %collective-permute-start) | collective-permute-done | bytes 229408 | tf_op jit(solution)/shard_map/ppermute | solution.py:690
  46.4 2.0 %collective-permute-done.1.refs_2_ = bf16[448,256]{1,0:T(8,128)(2,1)S(1)} collective-permute-done((bf16[448,256]{1,0:T(8,128)(2,1)}, bf16[448,256]{1,0:T(8,128)(2,1)S(1)}, u32[]{:S(2)}, u32[]{:S(2)}) %collective-permute-start.1) | collective-permute-done | bytes 229408 | tf_op jit(solution)/shard_map/ppermute | solution.py:690
  48.3 4.9 %collective-permute-start.6 = (bf16[448,256]{1,0:T(8,128)(2,1)}, bf16[448,256]{1,0:T(8,128)(2,1)S(1)}, u32[]{:S(2)}, u32[]{:S(2)}) collective-permute-start(bf16[448,256]{1,0:T(8,128)(2,1)} %get-tuple-element.47.refs_4_), channel_id=1, source_target_pairs={{0,16},{4,20},{8,24},{12,28},{16,32},{20,36},{24,40},{28,44},{32,4... | collective-permute-start | bytes 688136 | tf_op jit(solution)/shard_map/ppermute | solution.py:684
  53.2 4.2 %collective-permute-start.7 = (bf16[448,256]{1,0:T(8,128)(2,1)S(1)}, bf16[448,256]{1,0:T(8,128)(2,1)S(1)}, u32[]{:S(2)}, u32[]{:S(2)}) collective-permute-start(bf16[448,256]{1,0:T(8,128)(2,1)S(1)} %collective-permute-done.3.refs_5_), channel_id=1, source_target_pairs={{0,16},{4,20},{8,24},{12,28},{16,32},{20,36},{24,40},{28,44},{32,4... | collective-permute-start | bytes 688136 | tf_op jit(solution)/shard_map/ppermute | solution.py:684
  57.5 4.0 %collective-permute-start.8 = (bf16[448,256]{1,0:T(8,128)(2,1)S(1)}, bf16[448,256]{1,0:T(8,128)(2,1)S(1)}, u32[]{:S(2)}, u32[]{:S(2)}) collective-permute-start(bf16[448,256]{1,0:T(8,128)(2,1)S(1)} %collective-permute-done.4.refs_6_), channel_id=1, source_target_pairs={{0,16},{4,20},{8,24},{12,28},{16,32},{20,36},{24,40},{28,44},{32,4... | collective-permute-start | bytes 688136 | tf_op jit(solution)/shard_map/ppermute | solution.py:684
  61.5 4.2 %collective-permute-start.9 = (bf16[448,256]{1,0:T(8,128)(2,1)S(1)}, bf16[448,256]{1,0:T(8,128)(2,1)S(1)}, u32[]{:S(2)}, u32[]{:S(2)}) collective-permute-start(bf16[448,256]{1,0:T(8,128)(2,1)S(1)} %collective-permute-done.5.refs_7_), channel_id=1, source_target_pairs={{0,16},{4,20},{8,24},{12,28},{16,32},{20,36},{24,40},{28,44},{32,4... | collective-permute-start | bytes 688136 | tf_op jit(solution)/shard_map/ppermute | solution.py:684
  66.5 2.3 %chain.1 = bf16[32,56,128]{2,1,0:T(8,128)(2,1)} custom-call(s32[5]{0:T(128)} %stack.23.where_ref, bf16[32,64,128]{2,1,0:T(8,128)(2,1)} %copy-done.1), custom_call_target="tpu_custom_call" | custom-call | flops 2000000000 | bytes 1000000 | tf_op jit(solution)/shard_map/chain/pallas_call | solution.py:265
  68.9 6.1 %all-to-all-start.1 = ((bf16[32,56,128]{2,1,0:T(8,128)(2,1)}), bf16[32,56,128]{2,1,0:T(8,128)(2,1)S(1)}, u32[]{:S(2)}, u32[]{:S(2)}) async-start(bf16[32,56,128]{2,1,0:T(8,128)(2,1)} %chain.1), calls=%async_computation.1 | async-start | bytes 917504 | tf_op jit(solution)/shard_map/all_to_all | solution.py:696
  76.0 9.6 %attention.1 = (bf16[4,224,256]{2,1,0:T(8,128)(2,1)}, f32[4,448,256]{2,1,0:T(8,128)}, bf16[4,448,256]{2,1,0:T(8,128)(2,1)}) custom-call(s32[5]{0:T(128)} %stack.23.where_ref, s32[32,256]{1,0:T(8,128)} %reshape.51.docs_ref, bf16[448,256]{1,0:T(8,128)(2,1)} %get-tuple-element.43.refs_0_, bf16[448,256]{1,0:T(8,128)(2,1)} %copy-done.11, ...), custom_call_target="tpu_custom_call" | custom-call | flops 12000000000 | bytes 8000000 | tf_op jit(solution)/shard_map/attention/pallas_call | solution.py:616
  85.6 1.3 collective-permute-start.10
  87.6 16.3 %mixer_second.1 = (bf16[256,1792]{1,0:T(8,128)(2,1)}, f32[8,1792]{1,0:T(8,128)}, f32[8,1792]{1,0:T(8,128)}, bf16[256,1792]{1,0:T(8,128)(2,1)}, f32[28,256]{1,0:T...) custom-call(s32[5]{0:T(128)} %stack.23.where_ref, bf16[256,1792]{1,0:T(8,128)(2,1)} %x_ref.3, ...), custom_call_target="tpu_custom_call" | custom-call | flops 17999998976 | bytes 8000000 | tf_op jit(solution)/shard_map/mixer_second/pallas_call | solution.py:449
  104.8 1.4 collective-permute-start.18
  106.1 1.3 collective-permute-start.15
  107.4 14.1 %all-to-all-start.2 = ((bf16[32,64,128]{2,1,0:T(8,128)(2,1)}), bf16[32,64,128]{2,1,0:T(8,128)(2,1)S(1)}, u32[]{:S(2)}, u32[]{:S(2)}) async-start(bf16[32,64,128]{2,1,0:T(8,128)(2,1)} %get-tuple-element.66), calls=%async_computation.2 | async-start | bytes 1048576 | tf_op jit(solution)/shard_map/all_to_all | solution.py:696
  121.6 0.9 copy-done.10
  122.5 3.1 %merge.1 = (bf16[672,256]{1,0:T(8,128)(2,1)}, bf16[672,256]{1,0:T(8,128)(2,1)}, bf16[672,256]{1,0:T(8,128)(2,1)}, bf16[672,256]{1,0:T(8,128)(2,1)}) custom-call(s32[5]{0:T(128)} %stack.23.where_ref, bf16[4,224,256]{2,1,0:T(8,128)(2,1)} %get-tuple-element.51.dq_ref, f32[4,448,256]{2,1,0:T(8,128)} %get-tuple-element.52.dkv_ref, bf16[4,448,256]{2,1,0:T(8,128)(2,1)} %copy-done.10), custom_call_target="tpu_custom_call" | custom-call | flops 3000000000 | bytes 4000000 | tf_op jit(solution)/shard_map/merge/pallas_call | solution.py:647
  125.6 1.8 %collective-permute-start.11 = (bf16[672,256]{1,0:T(8,128)(2,1)}, bf16[672,256]{1,0:T(8,128)(2,1)S(1)}, u32[]{:S(2)}, u32[]{:S(2)}) collective-permute-start(bf16[672,256]{1,0:T(8,128)(2,1)} %get-tuple-element.55), channel_id=1, source_target_pairs={{0,4},{4,8},{8,12},{12,0},{1,5},{5,9},{9,13},{13,1},{2,6},{6,10},{... | collective-permute-start | bytes 1032200 | tf_op jit(solution)/shard_map/ppermute | solution.py:690
  127.4 2.7 %collective-permute-start.12 = (bf16[672,256]{1,0:T(8,128)(2,1)}, bf16[672,256]{1,0:T(8,128)(2,1)S(1)}, u32[]{:S(2)}, u32[]{:S(2)}) collective-permute-start(bf16[672,256]{1,0:T(8,128)(2,1)} %get-tuple-element.56), channel_id=1, source_target_pairs={{0,8},{4,12},{8,0},{12,4},{1,9},{5,13},{9,1},{13,5},{2,10},{6,14},... | collective-permute-start | bytes 1032200 | tf_op jit(solution)/shard_map/ppermute | solution.py:690
  130.1 1.5 collective-permute-start.13
  132.2 2.0 %all-to-all-done.2.bundle_ref = bf16[32,64,128]{2,1,0:T(8,128)(2,1)S(1)} async-done(((bf16[32,64,128]{2,1,0:T(8,128)(2,1)}), bf16[32,64,128]{2,1,0:T(8,128)(2,1)S(1)}, u32[]{:S(2)}, u32[]{:S(2)}) %all-to-all-start.2) | async-done | bytes 524320 | tf_op jit(solution)/shard_map/all_to_all | solution.py:696
  135.0 2.0 %finish.1 = (f32[4,1792]{1,0:T(4,128)}, f32[1,28]{1,0:T(1,128)}, f32[1,28]{1,0:T(1,128)}, f32[1,28]{1,0:T(1,128)}, f32[256,128]{1,0:T(8,128)}, /*index=5*/f32[256,128]{1,0:T(8,128)}) custom-call(s32[5]{0:T(128)} %stack.23.where_ref, bf16[32,64,128]{2,1,0:T(8,128)(2,1)} %copy-done, bf16[256,128]{1,0:T(8,128)(2,1)} %get-tuple-element.67.refs_0_, ...), custom_call_target="tpu_custom_call" | custom-call | tf_op jit(solution)/shard_map/finish/pallas_call | solution.py:512
  137.1 1.6 %collective-permute-done.11.refs_1_ = bf16[672,256]{1,0:T(8,128)(2,1)S(1)} collective-permute-done((bf16[672,256]{1,0:T(8,128)(2,1)}, bf16[672,256]{1,0:T(8,128)(2,1)S(1)}, u32[]{:S(2)}, u32[]{:S(2)}) %collective-permute-start.11) | collective-permute-done | bytes 344096 | tf_op jit(solution)/shard_map/ppermute | solution.py:690
  138.6 6.4 %collective-permute-done.12.refs_2_ = bf16[672,256]{1,0:T(8,128)(2,1)S(1)} collective-permute-done((bf16[672,256]{1,0:T(8,128)(2,1)}, bf16[672,256]{1,0:T(8,128)(2,1)S(1)}, u32[]{:S(2)}, u32[]{:S(2)}) %collective-permute-start.12) | collective-permute-done | bytes 344096 | tf_op jit(solution)/shard_map/ppermute | solution.py:690
  145.9 2.7 %unpack.1 = (bf16[256,896]{1,0:T(8,128)(2,1)}, bf16[256,896]{1,0:T(8,128)(2,1)}, bf16[256,896]{1,0:T(8,128)(2,1)}) custom-call(s32[5]{0:T(128)} %stack.23.where_ref, bf16[672,256]{1,0:T(8,128)(2,1)} %get-tuple-element.54.refs_0_, bf16[672,256]{1,0:T(8,128)(2,1)} %copy-done.3, bf16[672,256]{1,0:T(8,128)(2,1)} %copy-done.4, bf16[672,256]{1,0:T(8,128)(2,1)} %copy-done.5), custom_call_target="tpu_custom_call" | custom-call | tf_op jit(solution)/shard_map/unpack/pallas_call | solution.py:671
  (68 shorter events, 8.2 us)
Async XLA Ops:
  1.4 5.6 %collective-permute-start.14 = (bf16[8,1792]{1,0:T(8,128)(2,1)S(1)}, bf16[8,1792]{1,0:T(8,128)(2,1)S(1)}, u32[]{:S(2)}, u32[]{:S(2)}) collective-permute-start(bf16[8,1792]{1,0:T(8,128)(2,1)S(1)} %slice.3), channel_id=1, source_target_pairs={{0,4},{4,8},{8,12},{12,16},{16,20},{20,24},{24,28},{28,32},{32,36}... | collective-permute-start | bytes 86024 | tf_op jit(solution)/shard_map/ppermute | solution.py:684
  16.7 49.1 %all-to-all-start = ((bf16[32,64,128]{2,1,0:T(8,128)(2,1)}), bf16[32,64,128]{2,1,0:T(8,128)(2,1)S(1)}, u32[]{:S(2)}, u32[]{:S(2)}) async-start(bf16[32,64,128]{2,1,0:T(8,128)(2,1)} %bitcast.15), calls=%async_computation | async-start | bytes 1048576 | tf_op jit(solution)/shard_map/all_to_all | solution.py:696
  31.9 14.4 %collective-permute-start = (bf16[448,256]{1,0:T(8,128)(2,1)}, bf16[448,256]{1,0:T(8,128)(2,1)S(1)}, u32[]{:S(2)}, u32[]{:S(2)}) collective-permute-start(bf16[448,256]{1,0:T(8,128)(2,1)} %get-tuple-element.44), channel_id=1, source_target_pairs={{0,4},{4,8},{8,12},{12,0},{1,5},{5,9},{9,13},{13,1},{2,6},{6,10},{... | collective-permute-start | bytes 688136 | tf_op jit(solution)/shard_map/ppermute | solution.py:690
  33.7 14.6 %collective-permute-start.1 = (bf16[448,256]{1,0:T(8,128)(2,1)}, bf16[448,256]{1,0:T(8,128)(2,1)S(1)}, u32[]{:S(2)}, u32[]{:S(2)}) collective-permute-start(bf16[448,256]{1,0:T(8,128)(2,1)} %get-tuple-element.45), channel_id=1, source_target_pairs={{0,8},{4,12},{8,0},{12,4},{1,9},{5,13},{9,1},{13,5},{2,10},{6,14},... | collective-permute-start | bytes 688136 | tf_op jit(solution)/shard_map/ppermute | solution.py:690
  36.4 16.8 %collective-permute-start.3 = (bf16[448,256]{1,0:T(8,128)(2,1)}, bf16[448,256]{1,0:T(8,128)(2,1)S(1)}, u32[]{:S(2)}, u32[]{:S(2)}) collective-permute-start(bf16[448,256]{1,0:T(8,128)(2,1)} %get-tuple-element.48), channel_id=1, source_target_pairs={{0,4},{4,8},{8,12},{12,0},{1,5},{5,9},{9,13},{13,1},{2,6},{6,10},{... | collective-permute-start | bytes 688136 | tf_op jit(solution)/shard_map/ppermute | solution.py:690
  36.4 21.0 %collective-permute-start.4 = (bf16[448,256]{1,0:T(8,128)(2,1)}, bf16[448,256]{1,0:T(8,128)(2,1)S(1)}, u32[]{:S(2)}, u32[]{:S(2)}) collective-permute-start(bf16[448,256]{1,0:T(8,128)(2,1)} %get-tuple-element.49), channel_id=1, source_target_pairs={{0,8},{4,12},{8,0},{12,4},{1,9},{5,13},{9,1},{13,5},{2,10},{6,14},... | collective-permute-start | bytes 688136 | tf_op jit(solution)/shard_map/ppermute | solution.py:690
  39.3 22.2 %collective-permute-start.5 = (bf16[448,256]{1,0:T(8,128)(2,1)}, bf16[448,256]{1,0:T(8,128)(2,1)S(1)}, u32[]{:S(2)}, u32[]{:S(2)}) collective-permute-start(bf16[448,256]{1,0:T(8,128)(2,1)} %get-tuple-element.50), channel_id=1, source_target_pairs={{0,12},{4,0},{8,4},{12,8},{1,13},{5,1},{9,5},{13,9},{2,14},{6,2},{... | collective-permute-start | bytes 688136 | tf_op jit(solution)/shard_map/ppermute | solution.py:690
  46.4 28.7 %copy-start.11 = (bf16[448,256]{1,0:T(8,128)(2,1)}, bf16[448,256]{1,0:T(8,128)(2,1)S(1)}, u32[]{:S(2)}) copy-start(bf16[448,256]{1,0:T(8,128)(2,1)S(1)} %collective-permute-done.refs_1_) | copy-start | bytes 688132
  46.4 28.6 %collective-permute-start.2 = (bf16[448,256]{1,0:T(8,128)(2,1)}, bf16[448,256]{1,0:T(8,128)(2,1)S(1)}, u32[]{:S(2)}, u32[]{:S(2)}) collective-permute-start(bf16[448,256]{1,0:T(8,128)(2,1)} %get-tuple-element.46), channel_id=1, source_target_pairs={{0,12},{4,0},{8,4},{12,8},{1,13},{5,1},{9,5},{13,9},{2,14},{6,2},{... | collective-permute-start | bytes 688136 | tf_op jit(solution)/shard_map/ppermute | solution.py:690
  48.3 26.8 %copy-start.12 = (bf16[448,256]{1,0:T(8,128)(2,1)}, bf16[448,256]{1,0:T(8,128)(2,1)S(1)}, u32[]{:S(2)}) copy-start(bf16[448,256]{1,0:T(8,128)(2,1)S(1)} %collective-permute-done.1.refs_2_) | copy-start | bytes 688132
  48.3 26.7 %collective-permute-start.6 = (bf16[448,256]{1,0:T(8,128)(2,1)}, bf16[448,256]{1,0:T(8,128)(2,1)S(1)}, u32[]{:S(2)}, u32[]{:S(2)}) collective-permute-start(bf16[448,256]{1,0:T(8,128)(2,1)} %get-tuple-element.47.refs_4_), channel_id=1, source_target_pairs={{0,16},{4,20},{8,24},{12,28},{16,32},{20,36},{24,40},{28,44},{32,4... | collective-permute-start | bytes 688136 | tf_op jit(solution)/shard_map/ppermute | solution.py:684
  53.2 21.9 %copy-start.13 = (bf16[448,256]{1,0:T(8,128)(2,1)}, bf16[448,256]{1,0:T(8,128)(2,1)S(1)}, u32[]{:S(2)}) copy-start(bf16[448,256]{1,0:T(8,128)(2,1)S(1)} %collective-permute-done.3.refs_5_) | copy-start | bytes 688132
  53.2 21.8 %collective-permute-start.7 = (bf16[448,256]{1,0:T(8,128)(2,1)S(1)}, bf16[448,256]{1,0:T(8,128)(2,1)S(1)}, u32[]{:S(2)}, u32[]{:S(2)}) collective-permute-start(bf16[448,256]{1,0:T(8,128)(2,1)S(1)} %collective-permute-done.3.refs_5_), channel_id=1, source_target_pairs={{0,16},{4,20},{8,24},{12,28},{16,32},{20,36},{24,40},{28,44},{32,4... | collective-permute-start | bytes 688136 | tf_op jit(solution)/shard_map/ppermute | solution.py:684
  57.4 17.7 %copy-start.14 = (bf16[448,256]{1,0:T(8,128)(2,1)}, bf16[448,256]{1,0:T(8,128)(2,1)S(1)}, u32[]{:S(2)}) copy-start(bf16[448,256]{1,0:T(8,128)(2,1)S(1)} %collective-permute-done.4.refs_6_) | copy-start | bytes 688132
  57.5 17.6 %collective-permute-start.8 = (bf16[448,256]{1,0:T(8,128)(2,1)S(1)}, bf16[448,256]{1,0:T(8,128)(2,1)S(1)}, u32[]{:S(2)}, u32[]{:S(2)}) collective-permute-start(bf16[448,256]{1,0:T(8,128)(2,1)S(1)} %collective-permute-done.4.refs_6_), channel_id=1, source_target_pairs={{0,16},{4,20},{8,24},{12,28},{16,32},{20,36},{24,40},{28,44},{32,4... | collective-permute-start | bytes 688136 | tf_op jit(solution)/shard_map/ppermute | solution.py:684
  61.5 13.6 %copy-start.15 = (bf16[448,256]{1,0:T(8,128)(2,1)}, bf16[448,256]{1,0:T(8,128)(2,1)S(1)}, u32[]{:S(2)}) copy-start(bf16[448,256]{1,0:T(8,128)(2,1)S(1)} %collective-permute-done.5.refs_7_) | copy-start | bytes 688132
  61.5 13.5 %collective-permute-start.9 = (bf16[448,256]{1,0:T(8,128)(2,1)S(1)}, bf16[448,256]{1,0:T(8,128)(2,1)S(1)}, u32[]{:S(2)}, u32[]{:S(2)}) collective-permute-start(bf16[448,256]{1,0:T(8,128)(2,1)S(1)} %collective-permute-done.5.refs_7_), channel_id=1, source_target_pairs={{0,16},{4,20},{8,24},{12,28},{16,32},{20,36},{24,40},{28,44},{32,4... | collective-permute-start | bytes 688136 | tf_op jit(solution)/shard_map/ppermute | solution.py:684
  68.9 18.0 %all-to-all-start.1 = ((bf16[32,56,128]{2,1,0:T(8,128)(2,1)}), bf16[32,56,128]{2,1,0:T(8,128)(2,1)S(1)}, u32[]{:S(2)}, u32[]{:S(2)}) async-start(bf16[32,56,128]{2,1,0:T(8,128)(2,1)} %chain.1), calls=%async_computation.1 | async-start | bytes 917504 | tf_op jit(solution)/shard_map/all_to_all | solution.py:696
  85.6 36.0 %collective-permute-start.10 = (bf16[4,448,256]{2,1,0:T(8,128)(2,1)}, bf16[4,448,256]{2,1,0:T(8,128)(2,1)S(1)}, u32[]{:S(2)}, u32[]{:S(2)}) collective-permute-start(bf16[4,448,256]{2,1,0:T(8,128)(2,1)} %get-tuple-element.53), channel_id=1, source_target_pairs={{16,0},{20,4},{24,8},{28,12},{32,16},{36,20},{40,24},{44,28},{48,3... | collective-permute-start | bytes 2752520 | tf_op jit(solution)/shard_map/ppermute | solution.py:684
  103.9 26.2 %collective-permute-start.16 = (bf16[256,128]{1,0:T(8,128)(2,1)}, bf16[256,128]{1,0:T(8,128)(2,1)S(1)}, u32[]{:S(2)}, u32[]{:S(2)}) collective-permute-start(bf16[256,128]{1,0:T(8,128)(2,1)} %get-tuple-element.67.refs_0_), channel_id=1, source_target_pairs={{0,1},{1,2},{2,3},{3,0},{4,5},{5,6},{6,7},{7,4},{8,9},{9,10},{10,1... | collective-permute-start | bytes 196616 | tf_op jit(solution)/shard_map/ppermute | solution.py:690
  104.0 28.2 %collective-permute-start.17 = (bf16[256,128]{1,0:T(8,128)(2,1)}, bf16[256,128]{1,0:T(8,128)(2,1)S(1)}, u32[]{:S(2)}, u32[]{:S(2)}) collective-permute-start(bf16[256,128]{1,0:T(8,128)(2,1)} %get-tuple-element.67.refs_0_), channel_id=1, source_target_pairs={{0,2},{1,3},{2,0},{3,1},{4,6},{5,7},{6,4},{7,5},{8,10},{9,11},{10,... | collective-permute-start | bytes 196616 | tf_op jit(solution)/shard_map/ppermute | solution.py:690
  104.8 27.4 %collective-permute-start.18 = (bf16[256,128]{1,0:T(8,128)(2,1)}, bf16[256,128]{1,0:T(8,128)(2,1)S(1)}, u32[]{:S(2)}, u32[]{:S(2)}) collective-permute-start(bf16[256,128]{1,0:T(8,128)(2,1)} %get-tuple-element.67.refs_0_), channel_id=1, source_target_pairs={{0,3},{1,0},{2,1},{3,2},{4,7},{5,4},{6,5},{7,6},{8,11},{9,8},{10,9... | collective-permute-start | bytes 196616 | tf_op jit(solution)/shard_map/ppermute | solution.py:690
  106.1 21.3 %collective-permute-start.15 = (f32[8,1792]{1,0:T(8,128)}, f32[8,1792]{1,0:T(8,128)S(1)}, u32[]{:S(2)}, u32[]{:S(2)}) collective-permute-start(f32[8,1792]{1,0:T(8,128)} %get-tuple-element.63), channel_id=1, source_target_pairs={{4,0},{8,4},{12,8},{16,12},{20,16},{24,20},{28,24},{32,28},{36,32}... | collective-permute-start | bytes 172040 | tf_op jit(solution)/shard_map/ppermute | solution.py:684
  107.4 26.8 %all-to-all-start.2 = ((bf16[32,64,128]{2,1,0:T(8,128)(2,1)}), bf16[32,64,128]{2,1,0:T(8,128)(2,1)S(1)}, u32[]{:S(2)}, u32[]{:S(2)}) async-start(bf16[32,64,128]{2,1,0:T(8,128)(2,1)} %get-tuple-element.66), calls=%async_computation.2 | async-start | bytes 1048576 | tf_op jit(solution)/shard_map/all_to_all | solution.py:696
  122.5 9.1 %copy-start.9 = (f32[8,1792]{1,0:T(8,128)S(1)}, f32[8,1792]{1,0:T(8,128)}, u32[]{:S(2)}) copy-start(f32[8,1792]{1,0:T(8,128)} %get-tuple-element.62) | copy-start | bytes 172036
  125.6 13.0 %collective-permute-start.11 = (bf16[672,256]{1,0:T(8,128)(2,1)}, bf16[672,256]{1,0:T(8,128)(2,1)S(1)}, u32[]{:S(2)}, u32[]{:S(2)}) collective-permute-start(bf16[672,256]{1,0:T(8,128)(2,1)} %get-tuple-element.55), channel_id=1, source_target_pairs={{0,4},{4,8},{8,12},{12,0},{1,5},{5,9},{9,13},{13,1},{2,6},{6,10},{... | collective-permute-start | bytes 1032200 | tf_op jit(solution)/shard_map/ppermute | solution.py:690
  127.4 17.6 %collective-permute-start.12 = (bf16[672,256]{1,0:T(8,128)(2,1)}, bf16[672,256]{1,0:T(8,128)(2,1)S(1)}, u32[]{:S(2)}, u32[]{:S(2)}) collective-permute-start(bf16[672,256]{1,0:T(8,128)(2,1)} %get-tuple-element.56), channel_id=1, source_target_pairs={{0,8},{4,12},{8,0},{12,4},{1,9},{5,13},{9,1},{13,5},{2,10},{6,14},... | collective-permute-start | bytes 1032200 | tf_op jit(solution)/shard_map/ppermute | solution.py:690
  130.1 4.1 %copy-start.6 = (bf16[256,128]{1,0:T(8,128)(2,1)}, bf16[256,128]{1,0:T(8,128)(2,1)S(1)}, u32[]{:S(2)}) copy-start(bf16[256,128]{1,0:T(8,128)(2,1)S(1)} %collective-permute-done.16.refs_1_) | copy-start | bytes 196612
  130.1 14.9 %collective-permute-start.13 = (bf16[672,256]{1,0:T(8,128)(2,1)}, bf16[672,256]{1,0:T(8,128)(2,1)S(1)}, u32[]{:S(2)}, u32[]{:S(2)}) collective-permute-start(bf16[672,256]{1,0:T(8,128)(2,1)} %get-tuple-element.57), channel_id=1, source_target_pairs={{0,12},{4,0},{8,4},{12,8},{1,13},{5,1},{9,5},{13,9},{2,14},{6,2},{... | collective-permute-start | bytes 1032200 | tf_op jit(solution)/shard_map/ppermute | solution.py:690
  132.2 2.0 %copy-start.7 = (bf16[256,128]{1,0:T(8,128)(2,1)}, bf16[256,128]{1,0:T(8,128)(2,1)S(1)}, u32[]{:S(2)}) copy-start(bf16[256,128]{1,0:T(8,128)(2,1)S(1)} %collective-permute-done.17.refs_2_) | copy-start | bytes 196612
  132.2 2.0 %copy-start.8 = (bf16[256,128]{1,0:T(8,128)(2,1)}, bf16[256,128]{1,0:T(8,128)(2,1)S(1)}, u32[]{:S(2)}) copy-start(bf16[256,128]{1,0:T(8,128)(2,1)S(1)} %collective-permute-done.18.refs_3_) | copy-start | bytes 196612
  138.6 6.4 %copy-start.3 = (bf16[672,256]{1,0:T(8,128)(2,1)}, bf16[672,256]{1,0:T(8,128)(2,1)S(1)}, u32[]{:S(2)}) copy-start(bf16[672,256]{1,0:T(8,128)(2,1)S(1)} %collective-permute-done.11.refs_1_) | copy-start | bytes 1032196
  (12 other events, 9.6 us)

commit v4 on v3

--- a/solution.py
+++ b/solution.py
@@ -8,9 +8,7 @@
 
 
 HEAD_DIM = 224
-SSM_HEADS = 112
 STATE = 64
-GROUPS = 2
 KERNEL = 4
 SEQ = ("seq_0", "seq_1", "seq_2")
 SHARDS = 32
@@ -74,17 +72,34 @@
 IN_VMEM = pl.BlockSpec(memory_space=pltpu.VMEM)
 
 
-def doc_rows(where_ref, docs_ref):
-    shard = where_ref[0]
-    own = docs_ref[pl.ds(shard, 1), :].astype(F32)
-    before = docs_ref[pl.ds(jnp.maximum(shard - 1, 0), 1), :].astype(F32)
+def seq_index():
+    index = 0
+    for axis in SEQ:
+        index = index * lax.axis_size(axis) + lax.axis_index(axis)
+    return index
+
+
+def row_place():
+    return lax.axis_index(SEQ[-1])
+
+
+def doc_row_of(docs_ref, shard):
+    return jnp.concatenate(
+        [docs_ref[pl.ds(2 * shard + part, 1), :] for part in range(2)], axis=1
+    ).astype(F32)
+
+
+def doc_rows(docs_ref):
+    shard = seq_index()
+    own = doc_row_of(docs_ref, shard)
+    before = doc_row_of(docs_ref, jnp.maximum(shard - 1, 0))
     return own, jnp.where(shard == 0, -1.0, before)
 
 
-def group_halves(where_ref, coeff_ref):
+def group_halves(coeff_ref):
     coeff = coeff_ref[...].astype(F32)
     turned = pltpu.roll(coeff, STATE, 1)
-    first = where_ref[1] == 0
+    first = lax.axis_index("head") < 2
     low = iota((T, 128), 1) < STATE
     mine_low = jnp.where(low, jnp.where(first, coeff, turned), 0.0)
     mine_high = jnp.where(low, 0.0, jnp.where(first, turned, coeff))
@@ -110,8 +125,8 @@
     return step, -step * jnp.exp(params[1:2])
 
 
-def token_setup(where_ref, docs_ref, step_ref, params, cum_s, step_s, mask_s, prev_s, end_s):
-    own_row, before_row = doc_rows(where_ref, docs_ref)
+def token_setup(docs_ref, step_ref, params, cum_s, step_s, mask_s, prev_s, end_s):
+    own_row, before_row = doc_rows(docs_ref)
     own = columns_of(own_row)
     lane = iota((8, T), 1)
     own8 = jnp.broadcast_to(own_row, (8, T))
@@ -164,7 +179,7 @@
 
 
 def mixer_first_kernel(
-    where_ref, x_ref, halo_ref, weight_ref, gate_ref, grad_ref, step_ref, bias_ref, rate_ref,
+    x_ref, halo_ref, weight_ref, gate_ref, grad_ref, step_ref, bias_ref, rate_ref,
     skip_ref, docs_ref, in_ref, out_ref,
     parts_ref,
     cum_s, step_s, mask_s, prev_s, end_s, params_s, state_s, in_s, out_s,
@@ -175,7 +190,7 @@
     def _():
         params = padded_params(bias_ref, rate_ref, skip_ref, params_s)
         cum = token_setup(
-            where_ref, docs_ref, step_ref, params, cum_s, step_s, mask_s, prev_s, end_s
+            docs_ref, step_ref, params, cum_s, step_s, mask_s, prev_s, end_s
         )[2]
         through = jnp.exp2(cum[T - 1 : T] + prev_s[T - 1 : T, 0:1])
         high, low = split(through, 2)
@@ -183,8 +198,8 @@
         both = jnp.where(row == 0, high.astype(F32), jnp.where(row == 1, low.astype(F32), 0.0))
         for shard in range(SHARDS):
             state_s[SLOT * shard + ROWS : SLOT * (shard + 1)] = both
-        in_s[...] = group_halves(where_ref, in_ref)[0]
-        out_s[...] = group_halves(where_ref, out_ref)[1]
+        in_s[...] = group_halves(in_ref)[0]
+        out_s[...] = group_halves(out_ref)[1]
 
     _, _, step, enter, to_end = block_gains(step_id, cum_s, step_s, prev_s, end_s)
     pre, _ = conv_pre(x_ref[...], halo_ref[...], weight_ref[...], mask_s)
@@ -217,14 +232,14 @@
 
 def mixer_specs(heads):
     return [
-        IN_SMEM, column_block(T), column_block(8), column_block(KERNEL), column_block(T),
+        column_block(T), column_block(8), column_block(KERNEL), column_block(T),
         column_block(T), whole((heads, T)), whole((1, heads)), whole((1, heads)),
-        whole((1, heads)), whole((SHARDS, T)), whole((T, 128)), whole((T, 128)),
+        whole((1, heads)), whole((SHARDS * T // 128, 128)), whole((T, 128)), whole((T, 128)),
     ]
 
 
 def mixer_first(*arrays):
-    heads = arrays[6].shape[0]
+    heads = arrays[5].shape[0]
     return pl.pallas_call(
         mixer_first_kernel,
         grid=(STEPS,),
@@ -241,8 +256,8 @@
     )(*arrays)
 
 
-def chain_kernel(where_ref, parts_ref, out_ref, forward_s):
-    slot = where_ref[0]
+def chain_kernel(parts_ref, out_ref, forward_s):
+    slot = seq_index()
     owner = (slot * ROWS + iota((ROWS, 128), 0)) // 64
     choose = jnp.where(owner == iota((ROWS, 128), 1), 1.0, 0.0)
     lane = iota((ROWS, 128), 1)
@@ -261,16 +276,16 @@
         carry = through[shard] * carry + parts_ref[shard, 0:ROWS].astype(F32)
 
 
-def chain(where, parts):
+def chain(parts):
     return pl.pallas_call(
         chain_kernel,
-        in_specs=[IN_SMEM, IN_VMEM],
+        in_specs=[IN_VMEM],
         out_specs=IN_VMEM,
         out_shape=jax.ShapeDtypeStruct((SHARDS, ROWS, 128), BF16),
         scratch_shapes=[pltpu.VMEM((SHARDS, ROWS, 128), F32)],
         cost_estimate=pl.CostEstimate(flops=2 * 10**9, bytes_accessed=10**6, transcendentals=0),
         name="chain",
-    )(where, parts)
+    )(parts)
 
 
 BUNDLE = KERNEL * COLS // 128
@@ -278,7 +293,7 @@
 
 
 def mixer_second_kernel(
-    where_ref, x_ref, halo_ref, weight_ref, gate_ref, grad_ref, step_ref, bias_ref, rate_ref,
+    x_ref, halo_ref, weight_ref, gate_ref, grad_ref, step_ref, bias_ref, rate_ref,
     skip_ref, docs_ref, in_ref, out_ref, state_ref,
     dx_ref, tail_ref, spill_ref, dgate_ref, dstep_ref, coeff_ref, bundle_ref,
     cum_s, step_s, mask_s, prev_s, end_s, params_s,
@@ -292,13 +307,13 @@
     def _():
         params = padded_params(bias_ref, rate_ref, skip_ref, params_s)
         own, own_row, cum = token_setup(
-            where_ref, docs_ref, step_ref, params, cum_s, step_s, mask_s, prev_s, end_s
+            docs_ref, step_ref, params, cum_s, step_s, mask_s, prev_s, end_s
         )
         cumt_s[...] = jnp.transpose(cum)
         same = (own == own_row) & (iota((T, T), 0) >= iota((T, T), 1))
         causal_s[...] = jnp.where(same, 0.0, NEG)
-        in_low_s[...], in_high_s[...] = group_halves(where_ref, in_ref)
-        out_low_s[...], out_high_s[...] = group_halves(where_ref, out_ref)
+        in_low_s[...], in_high_s[...] = group_halves(in_ref)
+        out_low_s[...], out_high_s[...] = group_halves(out_ref)
         pair_s[...] = dot(out_low_s[...], in_low_s[...], NT)
         dtop_s[...] = jnp.zeros((HALF, HALF), F32)
         dbottom_s[...] = jnp.zeros((HALF, T), F32)
@@ -444,7 +459,7 @@
 
 
 def mixer_second(*arrays):
-    heads = arrays[6].shape[0]
+    heads = arrays[5].shape[0]
     half = pltpu.VMEM((T, 128), BF16)
     return pl.pallas_call(
         mixer_second_kernel,
@@ -481,13 +496,11 @@
     )(*arrays)
 
 
-def finish_kernel(
-    where_ref, bundle_ref, *refs
-):
+def finish_kernel(bundle_ref, *refs):
     coeff_refs = refs[:LOCAL_HEADS]
     weight_ref, bias_ref, rate_ref, skip_ref, in_ref, out_ref, coeff_s = refs[LOCAL_HEADS:]
     for turn, ref in enumerate(coeff_refs):
-        coeff_s[lax.rem(where_ref[4] - turn + LOCAL_HEADS, LOCAL_HEADS)] = ref[...].astype(F32)
+        coeff_s[lax.rem(lax.axis_index("head") - turn + LOCAL_HEADS, LOCAL_HEADS)] = ref[...].astype(F32)
     total = bundle_ref[0].astype(F32)
     for shard in range(1, SHARDS):
         total = total + bundle_ref[shard].astype(F32)
@@ -506,62 +519,64 @@
     in_ref[...] = jnp.where(left, pltpu.roll(low, STATE, 1), high)
 
 
-def finish(where, bundle, coeffs, heads):
+def finish(bundle, coeffs, heads):
     small = jax.ShapeDtypeStruct((1, heads), F32)
     wide = jax.ShapeDtypeStruct((T, 128), F32)
     return pl.pallas_call(
         finish_kernel,
-        in_specs=[IN_SMEM] + [IN_VMEM] * (1 + LOCAL_HEADS),
+        in_specs=[IN_VMEM] * (1 + LOCAL_HEADS),
         out_specs=[IN_VMEM] * 6,
         out_shape=[jax.ShapeDtypeStruct((KERNEL, COLS), F32), small, small, small, wide, wide],
         scratch_shapes=[pltpu.VMEM((LOCAL_HEADS, T, 128), F32)],
         name="finish",
-    )(where, bundle, *coeffs)
+    )(bundle, *coeffs)
 
 
 ROW = 4
-K_AT, V_AT, Q_AT = (slice(n * HEAD_DIM, (n + 1) * HEAD_DIM) for n in range(3))
-
-
-def pack_kernel(where_ref, k_ref, v_ref, q_ref, g_ref, *refs):
-    out_refs, turned_s = refs[: 2 * ROW], refs[2 * ROW]
-    for n, ref in enumerate((k_ref, v_ref, q_ref, g_ref)):
-        half = slice((n % 2) * HEAD_DIM, (n % 2 + 1) * HEAD_DIM)
+K_AT, V_AT, Q_AT, G_AT = (slice(n * HEAD_DIM, (n + 1) * HEAD_DIM) for n in range(4))
+PAIR = (2 * HEAD_DIM, T)
+
+
+def pack_kernel(k_ref, v_ref, q_ref, g_ref, *refs):
+    own_refs, far_refs, turned_s = refs[:ROW], refs[ROW : 2 * ROW], refs[2 * ROW]
+    for ref, place in ((k_ref, K_AT), (v_ref, V_AT), (q_ref, Q_AT), (g_ref, G_AT)):
         turned_part = jnp.transpose(ref[...])
         for head in range(LOCAL_HEADS):
-            turned_s[n // 2, head, half] = turned_part[head * HEAD_DIM : (head + 1) * HEAD_DIM]
+            turned_s[head, place] = turned_part[head * HEAD_DIM : (head + 1) * HEAD_DIM]
     for turn in range(ROW):
-        head = lax.rem(where_ref[3] + turn, ROW)
-        out_refs[turn][...] = turned_s[0, head]
-        out_refs[ROW + turn][...] = turned_s[1, head]
-
-
-def pack(where, keys, values, queries, grads):
+        head = lax.rem(row_place() + turn, ROW)
+        own_refs[turn][...] = turned_s[head]
+        far_refs[turn][...] = turned_s[head, : PAIR[0]]
+
+
+def pack(keys, values, queries, grads):
     outs = pl.pallas_call(
         pack_kernel,
-        in_specs=[IN_SMEM] + [IN_VMEM] * 4,
+        in_specs=[IN_VMEM] * 4,
         out_specs=[IN_VMEM] * (2 * ROW),
-        out_shape=[jax.ShapeDtypeStruct((2 * HEAD_DIM, T), BF16)] * (2 * ROW),
-        scratch_shapes=[pltpu.VMEM((2, LOCAL_HEADS, 2 * HEAD_DIM, T), BF16)],
+        out_shape=[jax.ShapeDtypeStruct((4 * HEAD_DIM, T), BF16)] * ROW
+        + [jax.ShapeDtypeStruct(PAIR, BF16)] * ROW,
+        scratch_shapes=[pltpu.VMEM((LOCAL_HEADS, 4 * HEAD_DIM, T), BF16)],
         name="pack",
-    )(where, keys, values, queries, grads)
+    )(keys, values, queries, grads)
     return outs[:ROW], outs[ROW:]
 
 
-def attention_kernel(where_ref, docs_ref, *refs):
-    arrived, (dq_ref, dkv_ref, back_ref, far_s, kv_s, qg_s) = refs[: 3 * ROW], refs[3 * ROW :]
+def attention_kernel(docs_ref, *refs):
+    arrived, outs = refs[: 2 * ROW], refs[2 * ROW :]
+    out_ref, back_refs, (own_s, far_s, qg_s, kv_s) = outs[0], outs[1 : ROW + 1], outs[ROW + 1 :]
     for turn in range(ROW):
-        block = lax.rem(where_ref[3] - turn + ROW, ROW)
-        qg_s[block] = arrived[turn][...]
-        kv_s[ROW + block] = arrived[ROW + turn][...]
-        kv_s[block] = arrived[2 * ROW + turn][...]
-    first_block = where_ref[2] * ROW
+        block = lax.rem(row_place() - turn + ROW, ROW)
+        kv_s[ROW + block] = arrived[turn][: PAIR[0]]
+        qg_s[block] = arrived[turn][PAIR[0] :]
+        kv_s[block] = arrived[ROW + turn][...]
+    first_block = lax.div(seq_index(), ROW) * ROW
     later = iota((T, T), 1) > iota((T, T), 0)
     scale = HEAD_DIM ** (-0.5)
 
     def doc_row(block):
         place = first_block + block
-        row = docs_ref[pl.ds(jnp.maximum(place, 0), 1), :].astype(F32)
+        row = doc_row_of(docs_ref, jnp.maximum(place, 0))
         return row if block >= 0 else jnp.where(place < 0, -1.0, row)
 
     rows = {block: doc_row(block) for block in range(-ROW, ROW)}
@@ -598,7 +613,7 @@
             dscore = (probs[gap] * (dprobs[gap] - delta)).astype(BF16)
             dq = dq + dot(part(gap, K_AT), dscore, NT)
             block = i - gap
-            ref, index = (dkv_ref, block) if block >= 0 else (far_s, block + ROW)
+            ref, index = (own_s, block) if block >= 0 else (far_s, block + ROW)
             dk, dv = dot(qt, dscore), dot(gt, halves[gap])
             if gap == 0 or (block < 0 and i == 0):
                 ref[index, K_AT] = dk
@@ -606,76 +621,57 @@
             else:
                 ref[index, K_AT] += dk
                 ref[index, V_AT] += dv
-            if gap == ROW:
-                back_ref[index] = far_s[index].astype(BF16)
-        dq_ref[i] = (dq * scale).astype(BF16)
-
-
-def attention(where, docs, qg, kv, far):
-    pair = (ROW, 2 * HEAD_DIM, T)
-    return pl.pallas_call(
+        out_ref[i, Q_AT] = (dq * scale).astype(BF16)
+    for block in range(ROW):
+        out_ref[block, : PAIR[0]] = own_s[block].astype(BF16)
+    for turn in range(ROW):
+        block = lax.rem(row_place() + turn, ROW)
+        back_refs[turn][...] = far_s[block].astype(BF16)
+
+
+def attention(docs, own, far):
+    outs = pl.pallas_call(
         attention_kernel,
-        in_specs=[IN_SMEM] + [IN_VMEM] * (1 + 3 * ROW),
-        out_specs=[IN_VMEM] * 3,
-        out_shape=[
-            jax.ShapeDtypeStruct((ROW, HEAD_DIM, T), BF16),
-            jax.ShapeDtypeStruct(pair, F32),
-            jax.ShapeDtypeStruct(pair, BF16),
-        ],
+        in_specs=[IN_VMEM] * (1 + 2 * ROW),
+        out_specs=[IN_VMEM] * (1 + ROW),
+        out_shape=[jax.ShapeDtypeStruct((ROW, 3 * HEAD_DIM, T), BF16)]
+        + [jax.ShapeDtypeStruct(PAIR, BF16)] * ROW,
         scratch_shapes=[
-            pltpu.VMEM(pair, F32),
-            pltpu.VMEM((2 * ROW, 2 * HEAD_DIM, T), BF16),
-            pltpu.VMEM(pair, BF16),
+            pltpu.VMEM((ROW, *PAIR), F32),
+            pltpu.VMEM((ROW, *PAIR), F32),
+            pltpu.VMEM((ROW, *PAIR), BF16),
+            pltpu.VMEM((2 * ROW, *PAIR), BF16),
         ],
         cost_estimate=pl.CostEstimate(flops=12 * 10**9, bytes_accessed=8 * 10**6, transcendentals=0),
         name="attention",
-    )(where, docs, *qg, *kv, *far)
-
-
-def merge_kernel(where_ref, dq_ref, dkv_ref, back_ref, *out_refs):
-    scale = HEAD_DIM ** (-0.5)
-    place = where_ref[3]
-    for turn, out_ref in enumerate(out_refs):
-        block = lax.rem(place + turn, ROW)
-        total = dkv_ref[block] + back_ref[block].astype(F32)
-        out_ref[K_AT] = (total[K_AT] * scale).astype(BF16)
-        out_ref[V_AT] = total[V_AT].astype(BF16)
-        out_ref[Q_AT] = dq_ref[block]
-
-
-def merge(where, dq, dkv, back):
-    return pl.pallas_call(
-        merge_kernel,
-        in_specs=[IN_SMEM] + [IN_VMEM] * 3,
-        out_specs=[IN_VMEM] * ROW,
-        out_shape=[jax.ShapeDtypeStruct((3 * HEAD_DIM, T), BF16)] * ROW,
-        cost_estimate=pl.CostEstimate(flops=3 * 10**9, bytes_accessed=4 * 10**6, transcendentals=0),
-        name="merge",
-    )(where, dq, dkv, back)
-
-
-def unpack_kernel(where_ref, *refs):
-    parts, outs, stacked_s = refs[:ROW], refs[ROW : ROW + 3], refs[ROW + 3]
-    place = where_ref[3]
-    for turn, part in enumerate(parts):
-        source = lax.rem(place - turn + ROW, ROW)
-        for n, at in enumerate((Q_AT, K_AT, V_AT)):
-            stacked_s[n, source] = part[at]
-    for n, ref in enumerate(outs):
-        stacked = jnp.concatenate([stacked_s[n, h] for h in range(LOCAL_HEADS)], axis=0)
-        ref[...] = jnp.transpose(stacked)
-
-
-def unpack(where, parts):
+    )(docs, *own, *far)
+    return outs[0], outs[1:]
+
+
+def unpack_kernel(own_ref, *refs):
+    back_refs, (dq_ref, dk_ref, dv_ref, back_s) = refs[:ROW], refs[ROW:]
+    for turn, ref in enumerate(back_refs):
+        back_s[lax.rem(row_place() - turn + ROW, ROW)] = ref[...]
+    join = jnp.concatenate
+    heads = range(LOCAL_HEADS)
+    dq_ref[...] = jnp.transpose(join([own_ref[h, Q_AT] for h in heads], axis=0))
+    for ref, place, scale in ((dk_ref, K_AT, HEAD_DIM ** (-0.5)), (dv_ref, V_AT, 1.0)):
+        own = join([own_ref[h, place] for h in heads], axis=0).astype(F32)
+        back = join([back_s[h, place] for h in heads], axis=0).astype(F32)
+        ref[...] = jnp.transpose(((own + back) * scale).astype(BF16))
+
+
+def unpack(own, back):
     wide = jax.ShapeDtypeStruct((T, LOCAL_HEADS * HEAD_DIM), BF16)
     return pl.pallas_call(
         unpack_kernel,
-        in_specs=[IN_SMEM] + [IN_VMEM] * ROW,
+        in_specs=[IN_VMEM] * (1 + ROW),
         out_specs=[IN_VMEM] * 3,
         out_shape=[wide] * 3,
-        scratch_shapes=[pltpu.VMEM((3, LOCAL_HEADS, HEAD_DIM, T), BF16)],
+        scratch_shapes=[pltpu.VMEM((ROW, *PAIR), BF16)],
+        cost_estimate=pl.CostEstimate(flops=2 * 10**9, bytes_accessed=4 * 10**6, transcendentals=0),
         name="unpack",
-    )(where, *parts)
+    )(own, *back)
 
 
 def passed_along(value, axis, steps):
@@ -692,6 +688,15 @@
     ]
 
 
+def to_row(part, rows, turn):
+    pairs = []
+    for shard in range(SHARDS):
+        row, place = shard // ROW + rows, (shard + turn) % ROW
+        if 0 <= row < SHARDS // ROW:
+            pairs.append((shard, row * ROW + place))
+    return lax.ppermute(part, SEQ, pairs)
+
+
 def exchange(array, axis):
     return lax.all_to_all(array, axis, split_axis=0, concat_axis=0, tiled=True)
 
@@ -701,38 +706,30 @@
     rate_log, skip_gain, input_coeff, output_coeff, gate_input, mix_grad,
 ):
     heads = step_raw.shape[1]
-    shard = lax.axis_index(SEQ)
-    group = lax.axis_index("head") * heads // (SSM_HEADS // GROUPS)
-    where = jnp.stack([shard, group, shard // ROW, lax.axis_index("seq_2"), lax.axis_index("head")]).astype(jnp.int32)
-    docs = doc_ids.reshape(SHARDS, T)
+    docs = doc_ids.reshape(SHARDS * T // 128, 128)
     halo = passed_along(conv_input[T - 8 :], SEQ, 1)
-    kv_parts, qg_parts = pack(where, keys, values, queries, attn_grad)
-    kv = turns(kv_parts, "seq_2")
-    qg = turns(qg_parts, "seq_2")
-    far = [passed_along(kv[0], SEQ, ROW)]
-    far = far + [passed_along(part, SEQ, ROW) for part in kv[1:]]
+    own_parts, far_parts = pack(keys, values, queries, attn_grad)
+    own = turns(own_parts, "seq_2")
+    far = [to_row(part, 1, turn) for turn, part in enumerate(far_parts)]
 
     mixer_args = (
-        where, conv_input, halo, conv_weight, gate_input, mix_grad, step_raw.T,
+        conv_input, halo, conv_weight, gate_input, mix_grad, step_raw.T,
         step_bias.reshape(1, heads), rate_log.reshape(1, heads), skip_gain.reshape(1, heads),
         docs, input_coeff, output_coeff,
     )
     parts = mixer_first(*mixer_args).reshape(SHARDS, SLOT, 128)
     gathered = exchange(parts, SEQ)
-    scanned = chain(where, gathered)
+    scanned = chain(gathered)
     entering = exchange(scanned, SEQ).reshape(COLS, 128)
-    dq, dkv, back = attention(where, docs, qg, kv, far)
-    returned = passed_along(back, SEQ, -ROW)
+    out, back = attention(docs, own, far)
+    swapped = exchange(out, "seq_2")
+    returned = [to_row(part, -1, turn) for turn, part in enumerate(back)]
     dx, tail, spill, dgate, dstep, coeff, bundle = mixer_second(*mixer_args, entering)
     spilled = passed_along(spill, SEQ, -1)
     bundles = exchange(bundle, SEQ)
     coeffs = turns([coeff] * LOCAL_HEADS, "head")
-    leaving = merge(where, dq, dkv, returned)
-    swapped = turns(leaving, "seq_2")
-    grad_weight, grad_bias, grad_rate, grad_skip, sum_in, sum_out = finish(
-        where, bundles, coeffs, heads
-    )
-    dq, dk, dv = unpack(where, swapped)
+    dq, dk, dv = unpack(swapped, returned)
+    grad_weight, grad_bias, grad_rate, grad_skip, sum_in, sum_out = finish(bundles, coeffs, heads)
     tail = (tail + spilled).astype(BF16)
     grad_conv = lax.dynamic_update_slice_in_dim(dx, tail, T - 8, 0)
     return (

time: 150 us -> 158 us (1.053)
  the two profiles are of different devices: /device:TPU:0 before, /device:TPU:65 now
where the time goes in v4:
time: 158 us; the launch traced here: 157 us
  starting transfers between devices  72.5 us (46%)
  Pallas kernels  45.2 us (29%)
  blocking collectives  15.8 us (10%)
  waiting for transfers between devices  15.3 us (10%)
  local copies, waits for them, and re-layouts  6.68 us (4%)
    ppermute x8, starting transfers between devices, to_row(): return lax.ppermute(part, SEQ, pairs)  30.8 us
    all_to_all x3, starting transfers between devices, exchange(): return lax.all_to_all(array, axis, split_axis=0, concat_axis=0, tiled=True)  18.2 us
    pallas_call x1, Pallas kernels, mixer_second(): pl.pallas_call(mixer_second_kernel, grid=(STEPS,), in_specs=mixer_specs(h...  16.2 us
    all_to_all x1, blocking collectives, exchange(): return lax.all_to_all(array, axis, split_axis=0, concat_axis=0, tiled=True)  15.8 us
    ppermute x6, starting transfers between devices, turns(): lax.ppermute(part, axis, [(n, (n + turn) % count) for n in range(count)])  13.1 us
    ppermute x2, starting transfers between devices, passed_along(): lax.ppermute(value, axis, [(source, source + steps) for source in range(i...  10.4 us
    ppermute x6, waiting for transfers between devices, turns(): lax.ppermute(part, axis, [(n, (n + turn) % count) for n in range(count)])  9.3 us
    pallas_call x1, Pallas kernels, attention(): pl.pallas_call(attention_kernel, in_specs=[IN_VMEM] * (1 + 2 * ROW), out_...  9.27 us
  transfers between devices with their start and end apart: 19, of which 2 were waited for; matrix products, arithmetic and copies ran while one was open for 0% of the time, Pallas kernels for 20%

profile of v4, /device:TPU:65, one launch (start us, length us, event | category | flops | bytes accessed | tf_op | source)
XLA Modules:
  0.0 157.2 jit_solution(435441205572027252)
XLA Ops:
  0.6 0.8 slice.3
  1.4 3.1 %collective-permute-start.11 = (bf16[8,1792]{1,0:T(8,128)(2,1)S(1)}, bf16[8,1792]{1,0:T(8,128)(2,1)S(1)}, u32[]{:S(2)}, u32[]{:S(2)}) collective-permute-start(bf16[8,1792]{1,0:T(8,128)(2,1)S(1)} %slice.3), channel_id=1, source_target_pairs={{0,4},{4,8},{8,12},{12,16},{16,20},{20,24},{24,28},{28,32},{32,36}... | collective-permute-start | bytes 86024 | tf_op jit(solution)/shard_map/ppermute | solution.py:680
  4.5 6.0 %collective-permute-done.11.halo_ref = bf16[8,1792]{1,0:T(8,128)(2,1)S(1)} collective-permute-done((bf16[8,1792]{1,0:T(8,128)(2,1)S(1)}, bf16[8,1792]{1,0:T(8,128)(2,1)S(1)}, u32[]{:S(2)}, u32[]{:S(2)}) %collective-permute-start.11) | collective-permute-done | bytes 28704 | tf_op jit(solution)/shard_map/ppermute | solution.py:680
  11.1 9.0 %mixer_first.1 = bf16[2048,128]{1,0:T(8,128)(2,1)} custom-call(bf16[256,1792]{1,0:T(8,128)(2,1)} %x_ref.3, bf16[8,1792]{1,0:T(8,128)(2,1)} %copy-done.23, f32[4,1792]{1,0:T(4,128)} %weight_ref.3, bf16[256,1792]{1,0:T(8,128)(2,1)} %gate_ref.3, bf16[256,1792]{1,0:T(8,128)(2,1)} %grad_ref.3, f32[28,256]{1,0:T(8,128)} %bitcast.13, f32[1,28]{1,0:T(1,128)} %bitcast.18, ...), custom_call_target="tpu_custom_call" | custom-call | flops 8000000000 | bytes 4000000 | tf_op jit(solution)/shard_map/mixer_first/pallas_call | solution.py:243
  20.1 15.8 %all_to_all.20.parts_ref = bf16[32,64,128]{2,1,0:T(8,128)(2,1)} all-to-all(bf16[32,64,128]{2,1,0:T(8,128)(2,1)} %bitcast.11), channel_id=1, replica_groups=mesh['seq_0'=4,'seq_1'=2,'seq_2'=4,'head'=4] {'seq_0','seq_1','seq_2'}, dimensions={0} | all-to-all | bytes 1048576 | tf_op jit(solution)/shard_map/all_to_all | solution.py:701
  36.0 2.3 %chain.1 = bf16[32,56,128]{2,1,0:T(8,128)(2,1)} custom-call(bf16[32,64,128]{2,1,0:T(8,128)(2,1)} %all_to_all.20.parts_ref), custom_call_target="tpu_custom_call" | custom-call | flops 2000000000 | bytes 1000000 | tf_op jit(solution)/shard_map/chain/pallas_call | solution.py:280
  38.3 5.6 %all-to-all-start.2 = ((bf16[32,56,128]{2,1,0:T(8,128)(2,1)}), bf16[32,56,128]{2,1,0:T(8,128)(2,1)S(1)}, u32[]{:S(2)}, u32[]{:S(2)}) async-start(bf16[32,56,128]{2,1,0:T(8,128)(2,1)} %chain.1), calls=%async_computation.2 | async-start | bytes 917504 | tf_op jit(solution)/shard_map/all_to_all | solution.py:701
  43.9 3.4 %pack.1 = (bf16[896,256]{1,0:T(8,128)(2,1)}, bf16[896,256]{1,0:T(8,128)(2,1)}, bf16[896,256]{1,0:T(8,128)(2,1)}, bf16[896,256]{1,0:T(8,128)(2,1)}, bf16[448,256]...) custom-call(bf16[256,896]{1,0:T(8,128)(2,1)} %k_ref.1, ...), custom_call_target="tpu_custom_call" | custom-call | tf_op jit(solution)/shard_map/pack/pallas_call | solution.py:553
  47.3 4.6 %collective-permute-start.3 = (bf16[448,256]{1,0:T(8,128)(2,1)}, bf16[448,256]{1,0:T(8,128)(2,1)S(1)}, u32[]{:S(2)}, u32[]{:S(2)}) collective-permute-start(bf16[448,256]{1,0:T(8,128)(2,1)} %get-tuple-element.45), channel_id=1, source_target_pairs={{0,16},{4,20},{8,24},{12,28},{16,32},{20,36},{24,40},{28,44},{32,4... | collective-permute-start | bytes 688136 | tf_op jit(solution)/shard_map/ppermute | solution.py:697
  51.9 3.7 %collective-permute-start.4 = (bf16[448,256]{1,0:T(8,128)(2,1)}, bf16[448,256]{1,0:T(8,128)(2,1)S(1)}, u32[]{:S(2)}, u32[]{:S(2)}) collective-permute-start(bf16[448,256]{1,0:T(8,128)(2,1)} %get-tuple-element.46), channel_id=1, source_target_pairs={{0,20},{4,24},{8,28},{12,16},{16,36},{20,40},{24,44},{28,32},{32,5... | collective-permute-start | bytes 688136 | tf_op jit(solution)/shard_map/ppermute | solution.py:697
  55.6 1.3 collective-permute-start
  56.9 1.5 collective-permute-start.1
  58.4 1.8 %collective-permute-start.2 = (bf16[896,256]{1,0:T(8,128)(2,1)}, bf16[896,256]{1,0:T(8,128)(2,1)S(1)}, u32[]{:S(2)}, u32[]{:S(2)}) collective-permute-start(bf16[896,256]{1,0:T(8,128)(2,1)} %get-tuple-element.44), channel_id=1, source_target_pairs={{0,12},{4,0},{8,4},{12,8},{1,13},{5,1},{9,5},{13,9},{2,14},{6,2},{... | collective-permute-start | bytes 1376264 | tf_op jit(solution)/shard_map/ppermute | solution.py:686
  60.2 4.9 %collective-permute-start.5 = (bf16[448,256]{1,0:T(8,128)(2,1)}, bf16[448,256]{1,0:T(8,128)(2,1)S(1)}, u32[]{:S(2)}, u32[]{:S(2)}) collective-permute-start(bf16[448,256]{1,0:T(8,128)(2,1)} %get-tuple-element.47), channel_id=1, source_target_pairs={{0,24},{4,28},{8,16},{12,20},{16,40},{20,44},{24,32},{28,36},{32,5... | collective-permute-start | bytes 688136 | tf_op jit(solution)/shard_map/ppermute | solution.py:697
  65.1 3.1 %collective-permute-start.6 = (bf16[448,256]{1,0:T(8,128)(2,1)}, bf16[448,256]{1,0:T(8,128)(2,1)S(1)}, u32[]{:S(2)}, u32[]{:S(2)}) collective-permute-start(bf16[448,256]{1,0:T(8,128)(2,1)} %get-tuple-element.48), channel_id=1, source_target_pairs={{0,28},{4,16},{8,20},{12,24},{16,44},{20,32},{24,36},{28,40},{32,6... | collective-permute-start | bytes 688136 | tf_op jit(solution)/shard_map/ppermute | solution.py:697
  68.3 0.8 copy-done.2
  69.1 16.2 %mixer_second.1 = (bf16[256,1792]{1,0:T(8,128)(2,1)}, f32[8,1792]{1,0:T(8,128)}, f32[8,1792]{1,0:T(8,128)}, bf16[256,1792]{1,0:T(8,128)(2,1)}, f32[28,256]{1,0:T...) custom-call(bf16[256,1792]{1,0:T(8,128)(2,1)} %x_ref.3, bf16[8,1792]{1,0:T(8,128)(2,1)} %copy-done.23, ...), custom_call_target="tpu_custom_call" | custom-call | flops 17999998976 | bytes 8000000 | tf_op jit(solution)/shard_map/mixer_second/pallas_call | solution.py:464
  85.3 8.6 %all-to-all-start.3 = ((bf16[32,64,128]{2,1,0:T(8,128)(2,1)}), bf16[32,64,128]{2,1,0:T(8,128)(2,1)S(1)}, u32[]{:S(2)}, u32[]{:S(2)}) async-start(bf16[32,64,128]{2,1,0:T(8,128)(2,1)} %get-tuple-element.62), calls=%async_computation.3 | async-start | bytes 1048576 | tf_op jit(solution)/shard_map/all_to_all | solution.py:701
  95.2 9.3 %attention.1 = (bf16[4,672,256]{2,1,0:T(8,128)(2,1)}, bf16[448,256]{1,0:T(8,128)(2,1)}, bf16[448,256]{1,0:T(8,128)(2,1)}, bf16[448,256]{1,0:T(8,128)(2,1)}, bf16[448,256]{1,0:T(8,128)(2,1)}) custom-call(s32[64,128]{1,0:T(8,128)} %bitcast.17, bf16[896,256]{1,0:T(8,128)(2,1)} %get-tuple-element.41.refs_0_, bf16[896,256]{1,0:T(8,128)(2,1)} %copy-done.8, ...), custom_call_target="tpu_custom_call" | custom-call | flops 12000000000 | bytes 8000000 | tf_op jit(solution)/shard_map/attention/pallas_call | solution.py:633
  105.3 4.0 %all-to-all-start = ((bf16[4,672,256]{2,1,0:T(8,128)(2,1)}), bf16[4,672,256]{2,1,0:T(8,128)(2,1)S(1)}, u32[]{:S(2)}, u32[]{:S(2)}) async-start(bf16[4,672,256]{2,1,0:T(8,128)(2,1)} %get-tuple-element.49), calls=%async_computation | async-start | bytes 2752512 | tf_op jit(solution)/shard_map/all_to_all | solution.py:701
  109.3 6.2 %collective-permute-start.13 = (bf16[256,128]{1,0:T(8,128)(2,1)S(1)}, bf16[256,128]{1,0:T(8,128)(2,1)S(1)}, u32[]{:S(2)}, u32[]{:S(2)}) collective-permute-start(bf16[256,128]{1,0:T(8,128)(2,1)S(1)} %copy-done.3), channel_id=1, source_target_pairs={{0,1},{1,2},{2,3},{3,0},{4,5},{5,6},{6,7},{7,4},{8,9},{9,10},{10,1... | collective-permute-start | bytes 196616 | tf_op jit(solution)/shard_map/ppermute | solution.py:686
  115.4 1.1 collective-permute-start.14
  116.5 7.3 %collective-permute-start.12 = (f32[8,1792]{1,0:T(8,128)S(1)}, f32[8,1792]{1,0:T(8,128)S(1)}, u32[]{:S(2)}, u32[]{:S(2)}) collective-permute-start(f32[8,1792]{1,0:T(8,128)S(1)} %copy-done.22), channel_id=1, source_target_pairs={{4,0},{8,4},{12,8},{16,12},{20,16},{24,20},{28,24},{32,28},{36,32}... | collective-permute-start | bytes 172040 | tf_op jit(solution)/shard_map/ppermute | solution.py:680
  123.8 2.2 %collective-permute-start.7 = (bf16[448,256]{1,0:T(8,128)(2,1)S(1)}, bf16[448,256]{1,0:T(8,128)(2,1)S(1)}, u32[]{:S(2)}, u32[]{:S(2)}) collective-permute-start(bf16[448,256]{1,0:T(8,128)(2,1)S(1)} %copy-done.14), channel_id=1, source_target_pairs={{16,0},{20,4},{24,8},{28,12},{32,16},{36,20},{40,24},{44,28},{48,3... | collective-permute-start | bytes 688136 | tf_op jit(solution)/shard_map/ppermute | solution.py:697
  126.0 1.9 %collective-permute-start.8 = (bf16[448,256]{1,0:T(8,128)(2,1)S(1)}, bf16[448,256]{1,0:T(8,128)(2,1)S(1)}, u32[]{:S(2)}, u32[]{:S(2)}) collective-permute-start(bf16[448,256]{1,0:T(8,128)(2,1)S(1)} %copy-done.13), channel_id=1, source_target_pairs={{16,4},{20,8},{24,12},{28,0},{32,20},{36,24},{40,28},{44,16},{48,3... | collective-permute-start | bytes 688136 | tf_op jit(solution)/shard_map/ppermute | solution.py:697
  127.9 6.1 %collective-permute-start.9 = (bf16[448,256]{1,0:T(8,128)(2,1)S(1)}, bf16[448,256]{1,0:T(8,128)(2,1)S(1)}, u32[]{:S(2)}, u32[]{:S(2)}) collective-permute-start(bf16[448,256]{1,0:T(8,128)(2,1)S(1)} %copy-done.12), channel_id=1, source_target_pairs={{16,8},{20,12},{24,0},{28,4},{32,24},{36,28},{40,16},{44,20},{48,4... | collective-permute-start | bytes 688136 | tf_op jit(solution)/shard_map/ppermute | solution.py:697
  134.0 4.2 %collective-permute-start.10 = (bf16[448,256]{1,0:T(8,128)(2,1)S(1)}, bf16[448,256]{1,0:T(8,128)(2,1)}, u32[]{:S(2)}, u32[]{:S(2)}) collective-permute-start(bf16[448,256]{1,0:T(8,128)(2,1)S(1)} %copy-done.11), channel_id=1, source_target_pairs={{16,12},{20,0},{24,4},{28,8},{32,28},{36,16},{40,20},{44,24},{48,4... | collective-permute-start | bytes 688136 | tf_op jit(solution)/shard_map/ppermute | solution.py:697
  138.3 1.3 collective-permute-start.15
  140.3 9.3 %collective-permute-done.15.refs_3_ = bf16[256,128]{1,0:T(8,128)(2,1)S(1)} collective-permute-done((bf16[256,128]{1,0:T(8,128)(2,1)S(1)}, bf16[256,128]{1,0:T(8,128)(2,1)S(1)}, u32[]{:S(2)}, u32[]{:S(2)}) %collective-permute-start.15) | collective-permute-done | bytes 65568 | tf_op jit(solution)/shard_map/ppermute | solution.py:686
  150.2 2.0 %finish.1 = (f32[4,1792]{1,0:T(4,128)}, f32[1,28]{1,0:T(1,128)}, f32[1,28]{1,0:T(1,128)}, f32[1,28]{1,0:T(1,128)}, f32[256,128]{1,0:T(8,128)}, /*index=5*/f32[256,128]{1,0:T(8,128)}) custom-call(bf16[32,64,128]{2,1,0:T(8,128)(2,1)} %copy-done, bf16[256,128]{1,0:T(8,128)(2,1)} %get-tuple-element.63.refs_0_, bf16[256,128]{1,0:T(8,128)(2,1)} %copy-done.4, ...), custom_call_target="tpu_custom_call" | custom-call | tf_op jit(solution)/shard_map/finish/pallas_call | solution.py:525
  153.1 1.1 copy-done.1
  154.2 3.0 %unpack.1 = (bf16[256,896]{1,0:T(8,128)(2,1)}, bf16[256,896]{1,0:T(8,128)(2,1)}, bf16[256,896]{1,0:T(8,128)(2,1)}) custom-call(bf16[4,672,256]{2,1,0:T(8,128)(2,1)} %copy-done.1, bf16[448,256]{1,0:T(8,128)(2,1)} %copy-done.17, bf16[448,256]{1,0:T(8,128)(2,1)} %copy-done.18, bf16[448,256]{1,0:T(8,128)(2,1)} %copy-done.19, ...), custom_call_target="tpu_custom_call" | custom-call | flops 2000000000 | bytes 4000000 | tf_op jit(solution)/shard_map/unpack/pallas_call | solution.py:666
  (64 shorter events, 4.7 us)
Async XLA Ops:
  1.4 9.1 %collective-permute-start.11 = (bf16[8,1792]{1,0:T(8,128)(2,1)S(1)}, bf16[8,1792]{1,0:T(8,128)(2,1)S(1)}, u32[]{:S(2)}, u32[]{:S(2)}) collective-permute-start(bf16[8,1792]{1,0:T(8,128)(2,1)S(1)} %slice.3), channel_id=1, source_target_pairs={{0,4},{4,8},{8,12},{12,16},{16,20},{20,24},{24,28},{28,32},{32,36}... | collective-permute-start | bytes 86024 | tf_op jit(solution)/shard_map/ppermute | solution.py:680
  38.3 30.0 %all-to-all-start.2 = ((bf16[32,56,128]{2,1,0:T(8,128)(2,1)}), bf16[32,56,128]{2,1,0:T(8,128)(2,1)S(1)}, u32[]{:S(2)}, u32[]{:S(2)}) async-start(bf16[32,56,128]{2,1,0:T(8,128)(2,1)} %chain.1), calls=%async_computation.2 | async-start | bytes 917504 | tf_op jit(solution)/shard_map/all_to_all | solution.py:701
  47.3 12.9 %collective-permute-start.3 = (bf16[448,256]{1,0:T(8,128)(2,1)}, bf16[448,256]{1,0:T(8,128)(2,1)S(1)}, u32[]{:S(2)}, u32[]{:S(2)}) collective-permute-start(bf16[448,256]{1,0:T(8,128)(2,1)} %get-tuple-element.45), channel_id=1, source_target_pairs={{0,16},{4,20},{8,24},{12,28},{16,32},{20,36},{24,40},{28,44},{32,4... | collective-permute-start | bytes 688136 | tf_op jit(solution)/shard_map/ppermute | solution.py:697
  51.9 13.2 %collective-permute-start.4 = (bf16[448,256]{1,0:T(8,128)(2,1)}, bf16[448,256]{1,0:T(8,128)(2,1)S(1)}, u32[]{:S(2)}, u32[]{:S(2)}) collective-permute-start(bf16[448,256]{1,0:T(8,128)(2,1)} %get-tuple-element.46), channel_id=1, source_target_pairs={{0,20},{4,24},{8,28},{12,16},{16,36},{20,40},{24,44},{28,32},{32,5... | collective-permute-start | bytes 688136 | tf_op jit(solution)/shard_map/ppermute | solution.py:697
  55.6 38.4 %collective-permute-start = (bf16[896,256]{1,0:T(8,128)(2,1)}, bf16[896,256]{1,0:T(8,128)(2,1)S(1)}, u32[]{:S(2)}, u32[]{:S(2)}) collective-permute-start(bf16[896,256]{1,0:T(8,128)(2,1)} %get-tuple-element.42), channel_id=1, source_target_pairs={{0,4},{4,8},{8,12},{12,0},{1,5},{5,9},{9,13},{13,1},{2,6},{6,10},{... | collective-permute-start | bytes 1376264 | tf_op jit(solution)/shard_map/ppermute | solution.py:686
  56.9 37.1 %collective-permute-start.1 = (bf16[896,256]{1,0:T(8,128)(2,1)}, bf16[896,256]{1,0:T(8,128)(2,1)S(1)}, u32[]{:S(2)}, u32[]{:S(2)}) collective-permute-start(bf16[896,256]{1,0:T(8,128)(2,1)} %get-tuple-element.43), channel_id=1, source_target_pairs={{0,8},{4,12},{8,0},{12,4},{1,9},{5,13},{9,1},{13,5},{2,10},{6,14},... | collective-permute-start | bytes 1376264 | tf_op jit(solution)/shard_map/ppermute | solution.py:686
  58.4 35.7 %collective-permute-start.2 = (bf16[896,256]{1,0:T(8,128)(2,1)}, bf16[896,256]{1,0:T(8,128)(2,1)S(1)}, u32[]{:S(2)}, u32[]{:S(2)}) collective-permute-start(bf16[896,256]{1,0:T(8,128)(2,1)} %get-tuple-element.44), channel_id=1, source_target_pairs={{0,12},{4,0},{8,4},{12,8},{1,13},{5,1},{9,5},{13,9},{2,14},{6,2},{... | collective-permute-start | bytes 1376264 | tf_op jit(solution)/shard_map/ppermute | solution.py:686
  60.2 25.1 %copy-start.15 = (bf16[448,256]{1,0:T(8,128)(2,1)}, bf16[448,256]{1,0:T(8,128)(2,1)S(1)}, u32[]{:S(2)}) copy-start(bf16[448,256]{1,0:T(8,128)(2,1)S(1)} %collective-permute-done.3.refs_4_) | copy-start | bytes 688132
  60.2 33.8 %collective-permute-start.5 = (bf16[448,256]{1,0:T(8,128)(2,1)}, bf16[448,256]{1,0:T(8,128)(2,1)S(1)}, u32[]{:S(2)}, u32[]{:S(2)}) collective-permute-start(bf16[448,256]{1,0:T(8,128)(2,1)} %get-tuple-element.47), channel_id=1, source_target_pairs={{0,24},{4,28},{8,16},{12,20},{16,40},{20,44},{24,32},{28,36},{32,5... | collective-permute-start | bytes 688136 | tf_op jit(solution)/shard_map/ppermute | solution.py:697
  65.1 20.2 %copy-start.16 = (bf16[448,256]{1,0:T(8,128)(2,1)}, bf16[448,256]{1,0:T(8,128)(2,1)S(1)}, u32[]{:S(2)}) copy-start(bf16[448,256]{1,0:T(8,128)(2,1)S(1)} %collective-permute-done.4.refs_5_) | copy-start | bytes 688132
  65.1 28.9 %collective-permute-start.6 = (bf16[448,256]{1,0:T(8,128)(2,1)}, bf16[448,256]{1,0:T(8,128)(2,1)S(1)}, u32[]{:S(2)}, u32[]{:S(2)}) collective-permute-start(bf16[448,256]{1,0:T(8,128)(2,1)} %get-tuple-element.48), channel_id=1, source_target_pairs={{0,28},{4,16},{8,20},{12,24},{16,44},{20,32},{24,36},{28,40},{32,6... | collective-permute-start | bytes 688136 | tf_op jit(solution)/shard_map/ppermute | solution.py:697
  85.3 19.2 %all-to-all-start.3 = ((bf16[32,64,128]{2,1,0:T(8,128)(2,1)}), bf16[32,64,128]{2,1,0:T(8,128)(2,1)S(1)}, u32[]{:S(2)}, u32[]{:S(2)}) async-start(bf16[32,64,128]{2,1,0:T(8,128)(2,1)} %get-tuple-element.62), calls=%async_computation.3 | async-start | bytes 1048576 | tf_op jit(solution)/shard_map/all_to_all | solution.py:701
  94.1 1.1 copy-start.10
  104.5 4.8 %copy-start.3 = (bf16[256,128]{1,0:T(8,128)(2,1)S(1)}, bf16[256,128]{1,0:T(8,128)(2,1)}, u32[]{:S(2)}) copy-start(bf16[256,128]{1,0:T(8,128)(2,1)} %get-tuple-element.63.refs_0_) | copy-start | bytes 196612
  104.5 12.0 %copy-start.22 = (f32[8,1792]{1,0:T(8,128)S(1)}, f32[8,1792]{1,0:T(8,128)}, u32[]{:S(2)}) copy-start(f32[8,1792]{1,0:T(8,128)} %get-tuple-element.59) | copy-start | bytes 172036
  104.5 19.2 %copy-start.14 = (bf16[448,256]{1,0:T(8,128)(2,1)S(1)}, bf16[448,256]{1,0:T(8,128)(2,1)}, u32[]{:S(2)}) copy-start(bf16[448,256]{1,0:T(8,128)(2,1)} %get-tuple-element.50) | copy-start | bytes 688132
  104.5 21.4 %copy-start.13 = (bf16[448,256]{1,0:T(8,128)(2,1)S(1)}, bf16[448,256]{1,0:T(8,128)(2,1)}, u32[]{:S(2)}) copy-start(bf16[448,256]{1,0:T(8,128)(2,1)} %get-tuple-element.51) | copy-start | bytes 688132
  104.5 23.4 %copy-start.12 = (bf16[448,256]{1,0:T(8,128)(2,1)S(1)}, bf16[448,256]{1,0:T(8,128)(2,1)}, u32[]{:S(2)}) copy-start(bf16[448,256]{1,0:T(8,128)(2,1)} %get-tuple-element.52) | copy-start | bytes 688132
  104.6 29.5 %copy-start.11 = (bf16[448,256]{1,0:T(8,128)(2,1)S(1)}, bf16[448,256]{1,0:T(8,128)(2,1)}, u32[]{:S(2)}) copy-start(bf16[448,256]{1,0:T(8,128)(2,1)} %get-tuple-element.53) | copy-start | bytes 688132
  104.6 35.1 %copy-start.7 = (f32[8,1792]{1,0:T(8,128)S(1)}, f32[8,1792]{1,0:T(8,128)}, u32[]{:S(2)}) copy-start(f32[8,1792]{1,0:T(8,128)} %get-tuple-element.58) | copy-start | bytes 172036
  105.3 46.9 %all-to-all-start = ((bf16[4,672,256]{2,1,0:T(8,128)(2,1)}), bf16[4,672,256]{2,1,0:T(8,128)(2,1)S(1)}, u32[]{:S(2)}, u32[]{:S(2)}) async-start(bf16[4,672,256]{2,1,0:T(8,128)(2,1)} %get-tuple-element.49), calls=%async_computation | async-start | bytes 2752512 | tf_op jit(solution)/shard_map/all_to_all | solution.py:701
  109.3 24.7 %collective-permute-start.13 = (bf16[256,128]{1,0:T(8,128)(2,1)S(1)}, bf16[256,128]{1,0:T(8,128)(2,1)S(1)}, u32[]{:S(2)}, u32[]{:S(2)}) collective-permute-start(bf16[256,128]{1,0:T(8,128)(2,1)S(1)} %copy-done.3), channel_id=1, source_target_pairs={{0,1},{1,2},{2,3},{3,0},{4,5},{5,6},{6,7},{7,4},{8,9},{9,10},{10,1... | collective-permute-start | bytes 196616 | tf_op jit(solution)/shard_map/ppermute | solution.py:686
  115.4 22.9 %collective-permute-start.14 = (bf16[256,128]{1,0:T(8,128)(2,1)S(1)}, bf16[256,128]{1,0:T(8,128)(2,1)S(1)}, u32[]{:S(2)}, u32[]{:S(2)}) collective-permute-start(bf16[256,128]{1,0:T(8,128)(2,1)S(1)} %copy-done.3), channel_id=1, source_target_pairs={{0,2},{1,3},{2,0},{3,1},{4,6},{5,7},{6,4},{7,5},{8,10},{9,11},{10,... | collective-permute-start | bytes 196616 | tf_op jit(solution)/shard_map/ppermute | solution.py:686
  116.5 11.4 %collective-permute-start.12 = (f32[8,1792]{1,0:T(8,128)S(1)}, f32[8,1792]{1,0:T(8,128)S(1)}, u32[]{:S(2)}, u32[]{:S(2)}) collective-permute-start(f32[8,1792]{1,0:T(8,128)S(1)} %copy-done.22), channel_id=1, source_target_pairs={{4,0},{8,4},{12,8},{16,12},{20,16},{24,20},{28,24},{32,28},{36,32}... | collective-permute-start | bytes 172040 | tf_op jit(solution)/shard_map/ppermute | solution.py:680
  123.8 28.4 %collective-permute-start.7 = (bf16[448,256]{1,0:T(8,128)(2,1)S(1)}, bf16[448,256]{1,0:T(8,128)(2,1)S(1)}, u32[]{:S(2)}, u32[]{:S(2)}) collective-permute-start(bf16[448,256]{1,0:T(8,128)(2,1)S(1)} %copy-done.14), channel_id=1, source_target_pairs={{16,0},{20,4},{24,8},{28,12},{32,16},{36,20},{40,24},{44,28},{48,3... | collective-permute-start | bytes 688136 | tf_op jit(solution)/shard_map/ppermute | solution.py:697
  126.0 26.2 %collective-permute-start.8 = (bf16[448,256]{1,0:T(8,128)(2,1)S(1)}, bf16[448,256]{1,0:T(8,128)(2,1)S(1)}, u32[]{:S(2)}, u32[]{:S(2)}) collective-permute-start(bf16[448,256]{1,0:T(8,128)(2,1)S(1)} %copy-done.13), channel_id=1, source_target_pairs={{16,4},{20,8},{24,12},{28,0},{32,20},{36,24},{40,28},{44,16},{48,3... | collective-permute-start | bytes 688136 | tf_op jit(solution)/shard_map/ppermute | solution.py:697
  127.9 24.3 %collective-permute-start.9 = (bf16[448,256]{1,0:T(8,128)(2,1)S(1)}, bf16[448,256]{1,0:T(8,128)(2,1)S(1)}, u32[]{:S(2)}, u32[]{:S(2)}) collective-permute-start(bf16[448,256]{1,0:T(8,128)(2,1)S(1)} %copy-done.12), channel_id=1, source_target_pairs={{16,8},{20,12},{24,0},{28,4},{32,24},{36,28},{40,16},{44,20},{48,4... | collective-permute-start | bytes 688136 | tf_op jit(solution)/shard_map/ppermute | solution.py:697
  134.0 15.5 %copy-start.4 = (bf16[256,128]{1,0:T(8,128)(2,1)}, bf16[256,128]{1,0:T(8,128)(2,1)S(1)}, u32[]{:S(2)}) copy-start(bf16[256,128]{1,0:T(8,128)(2,1)S(1)} %collective-permute-done.13.refs_1_) | copy-start | bytes 196612
  134.0 18.2 %collective-permute-start.10 = (bf16[448,256]{1,0:T(8,128)(2,1)S(1)}, bf16[448,256]{1,0:T(8,128)(2,1)}, u32[]{:S(2)}, u32[]{:S(2)}) collective-permute-start(bf16[448,256]{1,0:T(8,128)(2,1)S(1)} %copy-done.11), channel_id=1, source_target_pairs={{16,12},{20,0},{24,4},{28,8},{32,28},{36,16},{40,20},{44,24},{48,4... | collective-permute-start | bytes 688136 | tf_op jit(solution)/shard_map/ppermute | solution.py:697
  138.3 11.3 %copy-start.5 = (bf16[256,128]{1,0:T(8,128)(2,1)}, bf16[256,128]{1,0:T(8,128)(2,1)S(1)}, u32[]{:S(2)}) copy-start(bf16[256,128]{1,0:T(8,128)(2,1)S(1)} %collective-permute-done.14.refs_2_) | copy-start | bytes 196612
  138.3 11.2 %collective-permute-start.15 = (bf16[256,128]{1,0:T(8,128)(2,1)S(1)}, bf16[256,128]{1,0:T(8,128)(2,1)S(1)}, u32[]{:S(2)}, u32[]{:S(2)}) collective-permute-start(bf16[256,128]{1,0:T(8,128)(2,1)S(1)} %copy-done.3), channel_id=1, source_target_pairs={{0,3},{1,0},{2,1},{3,2},{4,7},{5,4},{6,5},{7,6},{8,11},{9,8},{10,9... | collective-permute-start | bytes 196616 | tf_op jit(solution)/shard_map/ppermute | solution.py:686
  153.1 1.1 copy-start.1
  (11 other events, 8.5 us)

commit v5 on v4

--- a/solution.py
+++ b/solution.py
@@ -538,38 +538,48 @@
 
 
 def pack_kernel(k_ref, v_ref, q_ref, g_ref, *refs):
-    own_refs, far_refs, turned_s = refs[:ROW], refs[ROW : 2 * ROW], refs[2 * ROW]
+    out_refs, turned_s = refs[:ROW], refs[ROW]
     for ref, place in ((k_ref, K_AT), (v_ref, V_AT), (q_ref, Q_AT), (g_ref, G_AT)):
         turned_part = jnp.transpose(ref[...])
         for head in range(LOCAL_HEADS):
             turned_s[head, place] = turned_part[head * HEAD_DIM : (head + 1) * HEAD_DIM]
     for turn in range(ROW):
-        head = lax.rem(row_place() + turn, ROW)
-        own_refs[turn][...] = turned_s[head]
-        far_refs[turn][...] = turned_s[head, : PAIR[0]]
+        out_refs[turn][...] = turned_s[lax.rem(row_place() + turn, ROW)]
 
 
 def pack(keys, values, queries, grads):
-    outs = pl.pallas_call(
+    return pl.pallas_call(
         pack_kernel,
         in_specs=[IN_VMEM] * 4,
-        out_specs=[IN_VMEM] * (2 * ROW),
-        out_shape=[jax.ShapeDtypeStruct((4 * HEAD_DIM, T), BF16)] * ROW
-        + [jax.ShapeDtypeStruct(PAIR, BF16)] * ROW,
+        out_specs=[IN_VMEM] * ROW,
+        out_shape=[jax.ShapeDtypeStruct((4 * HEAD_DIM, T), BF16)] * ROW,
         scratch_shapes=[pltpu.VMEM((LOCAL_HEADS, 4 * HEAD_DIM, T), BF16)],
         name="pack",
     )(keys, values, queries, grads)
-    return outs[:ROW], outs[ROW:]
-
-
-def attention_kernel(docs_ref, *refs):
-    arrived, outs = refs[: 2 * ROW], refs[2 * ROW :]
-    out_ref, back_refs, (own_s, far_s, qg_s, kv_s) = outs[0], outs[1 : ROW + 1], outs[ROW + 1 :]
+
+
+def lend_kernel(*refs):
+    for turn, ref in enumerate(refs[:ROW]):
+        refs[ROW][turn * PAIR[0] : (turn + 1) * PAIR[0]] = ref[: PAIR[0]]
+
+
+def lend(own):
+    return pl.pallas_call(
+        lend_kernel,
+        in_specs=[IN_VMEM] * ROW,
+        out_specs=IN_VMEM,
+        out_shape=jax.ShapeDtypeStruct((ROW * PAIR[0], T), BF16),
+        name="lend",
+    )(*own)
+
+
+def attention_kernel(docs_ref, far_ref, *refs):
+    arrived, (dq_ref, own_ref, back_ref, far_s, qg_s, kv_s) = refs[:ROW], refs[ROW:]
     for turn in range(ROW):
         block = lax.rem(row_place() - turn + ROW, ROW)
         kv_s[ROW + block] = arrived[turn][: PAIR[0]]
         qg_s[block] = arrived[turn][PAIR[0] :]
-        kv_s[block] = arrived[ROW + turn][...]
+        kv_s[block] = far_ref[turn * PAIR[0] : (turn + 1) * PAIR[0]]
     first_block = lax.div(seq_index(), ROW) * ROW
     later = iota((T, T), 1) > iota((T, T), 0)
     scale = HEAD_DIM ** (-0.5)
@@ -613,7 +623,7 @@
             dscore = (probs[gap] * (dprobs[gap] - delta)).astype(BF16)
             dq = dq + dot(part(gap, K_AT), dscore, NT)
             block = i - gap
-            ref, index = (own_s, block) if block >= 0 else (far_s, block + ROW)
+            ref, index = (own_ref, block) if block >= 0 else (far_s, block + ROW)
             dk, dv = dot(qt, dscore), dot(gt, halves[gap])
             if gap == 0 or (block < 0 and i == 0):
                 ref[index, K_AT] = dk
@@ -621,57 +631,77 @@
             else:
                 ref[index, K_AT] += dk
                 ref[index, V_AT] += dv
-        out_ref[i, Q_AT] = (dq * scale).astype(BF16)
-    for block in range(ROW):
-        out_ref[block, : PAIR[0]] = own_s[block].astype(BF16)
-    for turn in range(ROW):
-        block = lax.rem(row_place() + turn, ROW)
-        back_refs[turn][...] = far_s[block].astype(BF16)
-
-
-def attention(docs, own, far):
-    outs = pl.pallas_call(
+            if gap == ROW:
+                back_ref[index] = far_s[index].astype(BF16)
+        dq_ref[i] = (dq * scale).astype(BF16)
+
+
+def attention(docs, far, own):
+    pairs = (ROW, *PAIR)
+    return pl.pallas_call(
         attention_kernel,
-        in_specs=[IN_VMEM] * (1 + 2 * ROW),
-        out_specs=[IN_VMEM] * (1 + ROW),
-        out_shape=[jax.ShapeDtypeStruct((ROW, 3 * HEAD_DIM, T), BF16)]
-        + [jax.ShapeDtypeStruct(PAIR, BF16)] * ROW,
+        in_specs=[IN_VMEM] * (2 + ROW),
+        out_specs=[IN_VMEM] * 3,
+        out_shape=[
+            jax.ShapeDtypeStruct((ROW, HEAD_DIM, T), BF16),
+            jax.ShapeDtypeStruct(pairs, F32),
+            jax.ShapeDtypeStruct(pairs, BF16),
+        ],
         scratch_shapes=[
-            pltpu.VMEM((ROW, *PAIR), F32),
-            pltpu.VMEM((ROW, *PAIR), F32),
-            pltpu.VMEM((ROW, *PAIR), BF16),
+            pltpu.VMEM(pairs, F32),
+            pltpu.VMEM(pairs, BF16),
             pltpu.VMEM((2 * ROW, *PAIR), BF16),
         ],
         cost_estimate=pl.CostEstimate(flops=12 * 10**9, bytes_accessed=8 * 10**6, transcendentals=0),
         name="attention",
-    )(docs, *own, *far)
-    return outs[0], outs[1:]
-
-
-def unpack_kernel(own_ref, *refs):
-    back_refs, (dq_ref, dk_ref, dv_ref, back_s) = refs[:ROW], refs[ROW:]
-    for turn, ref in enumerate(back_refs):
-        back_s[lax.rem(row_place() - turn + ROW, ROW)] = ref[...]
-    join = jnp.concatenate
-    heads = range(LOCAL_HEADS)
-    dq_ref[...] = jnp.transpose(join([own_ref[h, Q_AT] for h in heads], axis=0))
-    for ref, place, scale in ((dk_ref, K_AT, HEAD_DIM ** (-0.5)), (dv_ref, V_AT, 1.0)):
-        own = join([own_ref[h, place] for h in heads], axis=0).astype(F32)
-        back = join([back_s[h, place] for h in heads], axis=0).astype(F32)
-        ref[...] = jnp.transpose(((own + back) * scale).astype(BF16))
-
-
-def unpack(own, back):
+    )(docs, far, *own)
+
+
+def merge_kernel(dq_ref, dkv_ref, back_ref, *out_refs):
+    scale = HEAD_DIM ** (-0.5)
+    place = row_place()
+    for turn, out_ref in enumerate(out_refs):
+        block = lax.rem(place + turn, ROW)
+        total = dkv_ref[block] + back_ref[block].astype(F32)
+        out_ref[K_AT] = (total[K_AT] * scale).astype(BF16)
+        out_ref[V_AT] = total[V_AT].astype(BF16)
+        out_ref[Q_AT] = dq_ref[block]
+
+
+def merge(dq, dkv, back):
+    return pl.pallas_call(
+        merge_kernel,
+        in_specs=[IN_VMEM] * 3,
+        out_specs=[IN_VMEM] * ROW,
+        out_shape=[jax.ShapeDtypeStruct((3 * HEAD_DIM, T), BF16)] * ROW,
+        cost_estimate=pl.CostEstimate(flops=3 * 10**9, bytes_accessed=4 * 10**6, transcendentals=0),
+        name="merge",
+    )(dq, dkv, back)
+
+
+def unpack_kernel(*refs):
+    parts, outs, stacked_s = refs[:ROW], refs[ROW : ROW + 3], refs[ROW + 3]
+    place = row_place()
+    for turn, part in enumerate(parts):
+        source = lax.rem(place - turn + ROW, ROW)
+        for n, at in enumerate((Q_AT, K_AT, V_AT)):
+            stacked_s[n, source] = part[at]
+    for n, ref in enumerate(outs):
+        stacked = jnp.concatenate([stacked_s[n, h] for h in range(LOCAL_HEADS)], axis=0)
+        ref[...] = jnp.transpose(stacked)
+
+
+def unpack(parts):
     wide = jax.ShapeDtypeStruct((T, LOCAL_HEADS * HEAD_DIM), BF16)
     return pl.pallas_call(
         unpack_kernel,
-        in_specs=[IN_VMEM] * (1 + ROW),
+        in_specs=[IN_VMEM] * ROW,
         out_specs=[IN_VMEM] * 3,
         out_shape=[wide] * 3,
-        scratch_shapes=[pltpu.VMEM((ROW, *PAIR), BF16)],
-        cost_estimate=pl.CostEstimate(flops=2 * 10**9, bytes_accessed=4 * 10**6, transcendentals=0),
+        scratch_shapes=[pltpu.VMEM((3, LOCAL_HEADS, HEAD_DIM, T), BF16)],
+        cost_estimate=pl.CostEstimate(flops=2 * 10**9, bytes_accessed=3 * 10**6, transcendentals=0),
         name="unpack",
-    )(own, *back)
+    )(*parts)
 
 
 def passed_along(value, axis, steps):
@@ -688,13 +718,8 @@
     ]
 
 
-def to_row(part, rows, turn):
-    pairs = []
-    for shard in range(SHARDS):
-        row, place = shard // ROW + rows, (shard + turn) % ROW
-        if 0 <= row < SHARDS // ROW:
-            pairs.append((shard, row * ROW + place))
-    return lax.ppermute(part, SEQ, pairs)
+def near(array):
+    return pltpu.with_memory_space_constraint(array, pltpu.VMEM)
 
 
 def exchange(array, axis):
@@ -708,9 +733,10 @@
     heads = step_raw.shape[1]
     docs = doc_ids.reshape(SHARDS * T // 128, 128)
     halo = passed_along(conv_input[T - 8 :], SEQ, 1)
-    own_parts, far_parts = pack(keys, values, queries, attn_grad)
-    own = turns(own_parts, "seq_2")
-    far = [to_row(part, 1, turn) for turn, part in enumerate(far_parts)]
+    parts = pack(keys, values, queries, attn_grad)
+    own = [near(v) for v in turns(parts, "seq_2")]
+    lent = lend(own)
+    far = passed_along(lent, SEQ, ROW)
 
     mixer_args = (
         conv_input, halo, conv_weight, gate_input, mix_grad, step_raw.T,
@@ -719,17 +745,20 @@
     )
     parts = mixer_first(*mixer_args).reshape(SHARDS, SLOT, 128)
     gathered = exchange(parts, SEQ)
-    scanned = chain(gathered)
+    scanned = chain(near(gathered))
     entering = exchange(scanned, SEQ).reshape(COLS, 128)
-    out, back = attention(docs, own, far)
-    swapped = exchange(out, "seq_2")
-    returned = [to_row(part, -1, turn) for turn, part in enumerate(back)]
+    dq, dkv, back = attention(docs, near(far), own)
+    returned = passed_along(back, SEQ, -ROW)
     dx, tail, spill, dgate, dstep, coeff, bundle = mixer_second(*mixer_args, entering)
+    leaving = merge(dq, dkv, near(returned))
+    swapped = turns(leaving, "seq_2")
     spilled = passed_along(spill, SEQ, -1)
     bundles = exchange(bundle, SEQ)
     coeffs = turns([coeff] * LOCAL_HEADS, "head")
-    dq, dk, dv = unpack(swapped, returned)
-    grad_weight, grad_bias, grad_rate, grad_skip, sum_in, sum_out = finish(bundles, coeffs, heads)
+    dq, dk, dv = unpack([near(v) for v in swapped])
+    grad_weight, grad_bias, grad_rate, grad_skip, sum_in, sum_out = finish(
+        near(bundles), [near(v) for v in coeffs], heads
+    )
     tail = (tail + spilled).astype(BF16)
     grad_conv = lax.dynamic_update_slice_in_dim(dx, tail, T - 8, 0)
     return (

time: 158 us -> 147 us (0.930)
  the two profiles are of different devices: /device:TPU:65 before, /device:TPU:0 now
where the time goes in v5:
time: 147 us
  starting transfers between devices  45.9 us (31%)
  Pallas kernels  44.9 us (31%)
  waiting for transfers between devices  29.1 us (20%)
  blocking collectives  19.7 us (13%)
  local copies, waits for them, and re-layouts  5.5 us (4%)
    ppermute x9, waiting for transfers between devices, turns(): lax.ppermute(part, axis, [(n, (n + turn) % count) for n in range(count)])  25.1 us
    all_to_all x2, starting transfers between devices, exchange(): return lax.all_to_all(array, axis, split_axis=0, concat_axis=0, tiled=True)  20.8 us
    all_to_all x1, blocking collectives, exchange(): return lax.all_to_all(array, axis, split_axis=0, concat_axis=0, tiled=True)  19.7 us
    pallas_call x1, Pallas kernels, mixer_second(): pl.pallas_call(mixer_second_kernel, grid=(STEPS,), in_specs=mixer_specs(h...  16.2 us
    ppermute x9, starting transfers between devices, turns(): lax.ppermute(part, axis, [(n, (n + turn) % count) for n in range(count)])  13.9 us
    ppermute x4, starting transfers between devices, passed_along(): lax.ppermute(value, axis, [(source, source + steps) for source in range(i...  11.2 us
    pallas_call x1, Pallas kernels, mixer_first(): pl.pallas_call(mixer_first_kernel, grid=(STEPS,), in_specs=mixer_specs(he...  9.02 us
    pallas_call x1, Pallas kernels, attention(): pl.pallas_call(attention_kernel, in_specs=[IN_VMEM] * (2 + ROW), out_spec...  8.91 us
  transfers between devices with their start and end apart: 15, of which 6 were waited for; matrix products, arithmetic and copies ran while one was open for 1% of the time, Pallas kernels for 27%

profile of v5, /device:TPU:0, one launch (start us, length us, event | category | flops | bytes accessed | tf_op | source)
XLA Modules:
  0.0 146.6 jit_solution(2155025436864586459)
XLA Ops:
  0.6 3.3 %pack.1 = (bf16[896,256]{1,0:T(8,128)(2,1)}, bf16[896,256]{1,0:T(8,128)(2,1)}, bf16[896,256]{1,0:T(8,128)(2,1)}, bf16[896,256]{1,0:T(8,128)(2,1)}) custom-call(bf16[256,896]{1,0:T(8,128)(2,1)} %k_ref.1, bf16[256,896]{1,0:T(8,128)(2,1)} %v_ref.1, bf16[256,896]{1,0:T(8,128)(2,1)} %q_ref.1, bf16[256,896]{1,0:T(8,128)(2,1)} %g_ref.1), custom_call_target="tpu_custom_call" | custom-call | tf_op jit(solution)/shard_map/pack/pallas_call | solution.py:551
  4.0 1.6 %collective-permute-start = (bf16[896,256]{1,0:T(8,128)(2,1)}, bf16[896,256]{1,0:T(8,128)(2,1)S(1)}, u32[]{:S(2)}, u32[]{:S(2)}) collective-permute-start(bf16[896,256]{1,0:T(8,128)(2,1)} %get-tuple-element.40), channel_id=1, source_target_pairs={{0,4},{4,8},{8,12},{12,0},{1,5},{5,9},{9,13},{13,1},{2,6},{6,10},{... | collective-permute-start | bytes 1376264 | tf_op jit(solution)/shard_map/ppermute | solution.py:716
  5.6 2.7 %collective-permute-start.1 = (bf16[896,256]{1,0:T(8,128)(2,1)}, bf16[896,256]{1,0:T(8,128)(2,1)S(1)}, u32[]{:S(2)}, u32[]{:S(2)}) collective-permute-start(bf16[896,256]{1,0:T(8,128)(2,1)} %get-tuple-element.41), channel_id=1, source_target_pairs={{0,8},{4,12},{8,0},{12,4},{1,9},{5,13},{9,1},{13,5},{2,10},{6,14},... | collective-permute-start | bytes 1376264 | tf_op jit(solution)/shard_map/ppermute | solution.py:716
  8.3 1.4 collective-permute-start.2
  10.5 2.5 %collective-permute-start.8 = (bf16[8,1792]{1,0:T(8,128)(2,1)S(1)}, bf16[8,1792]{1,0:T(8,128)(2,1)S(1)}, u32[]{:S(2)}, u32[]{:S(2)}) collective-permute-start(bf16[8,1792]{1,0:T(8,128)(2,1)S(1)} %slice.3), channel_id=1, source_target_pairs={{0,4},{4,8},{8,12},{12,16},{16,20},{20,24},{24,28},{28,32},{32,36}... | collective-permute-start | bytes 86024 | tf_op jit(solution)/shard_map/ppermute | solution.py:710
  13.0 4.6 %collective-permute-done.refs_1_ = bf16[896,256]{1,0:T(8,128)(2,1)S(1)} collective-permute-done((bf16[896,256]{1,0:T(8,128)(2,1)}, bf16[896,256]{1,0:T(8,128)(2,1)S(1)}, u32[]{:S(2)}, u32[]{:S(2)}) %collective-permute-start) | collective-permute-done | bytes 458784 | tf_op jit(solution)/shard_map/ppermute | solution.py:716
  17.6 11.4 %collective-permute-done.1.refs_2_ = bf16[896,256]{1,0:T(8,128)(2,1)S(1)} collective-permute-done((bf16[896,256]{1,0:T(8,128)(2,1)}, bf16[896,256]{1,0:T(8,128)(2,1)S(1)}, u32[]{:S(2)}, u32[]{:S(2)}) %collective-permute-start.1) | collective-permute-done | bytes 458784 | tf_op jit(solution)/shard_map/ppermute | solution.py:716
  28.9 1.3 copy-done
  30.3 1.0 lend.1
  31.3 6.0 %collective-permute-start.3 = (bf16[1792,256]{1,0:T(8,128)(2,1)}, bf16[1792,256]{1,0:T(8,128)(2,1)}, u32[]{:S(2)}, u32[]{:S(2)}) collective-permute-start(bf16[1792,256]{1,0:T(8,128)(2,1)} %lend.1), channel_id=1, source_target_pairs={{0,16},{4,20},{8,24},{12,28},{16,32},{20,36},{24,40},{28,44},{32,4... | collective-permute-start | bytes 2752520 | tf_op jit(solution)/shard_map/ppermute | solution.py:710
  37.9 9.0 %mixer_first.1 = bf16[2048,128]{1,0:T(8,128)(2,1)} custom-call(bf16[256,1792]{1,0:T(8,128)(2,1)} %x_ref.3, bf16[8,1792]{1,0:T(8,128)(2,1)} %copy-done.12, f32[4,1792]{1,0:T(4,128)} %weight_ref.3, bf16[256,1792]{1,0:T(8,128)(2,1)} %gate_ref.3, bf16[256,1792]{1,0:T(8,128)(2,1)} %grad_ref.3, f32[28,256]{1,0:T(8,128)} %bitcast.16, f32[1,28]{1,0:T(1,128)} %bitcast.18, ...), custom_call_target="tpu_custom_call" | custom-call | flops 8000000000 | bytes 4000000 | tf_op jit(solution)/shard_map/mixer_first/pallas_call | solution.py:243
  46.9 19.7 %all_to_all.15.parts_ref = bf16[32,64,128]{2,1,0:T(8,128)(2,1)S(1)} all-to-all(bf16[32,64,128]{2,1,0:T(8,128)(2,1)} %bitcast.11), channel_id=1, replica_groups=mesh['seq_0'=4,'seq_1'=2,'seq_2'=4,'head'=4] {'seq_0','seq_1','seq_2'}, dimensions={0} | all-to-all | bytes 1048576 | tf_op jit(solution)/shard_map/all_to_all | solution.py:726
  66.6 1.3 chain.1
  67.9 6.6 %all-to-all-start.1 = ((bf16[32,56,128]{2,1,0:T(8,128)(2,1)}), bf16[32,56,128]{2,1,0:T(8,128)(2,1)S(1)}, u32[]{:S(2)}, u32[]{:S(2)}) async-start(bf16[32,56,128]{2,1,0:T(8,128)(2,1)} %chain.1), calls=%async_computation.1 | async-start | bytes 917504 | tf_op jit(solution)/shard_map/all_to_all | solution.py:726
  74.5 1.0 copy-done.3
  75.5 8.9 %attention.1 = (bf16[4,224,256]{2,1,0:T(8,128)(2,1)}, f32[4,448,256]{2,1,0:T(8,128)}, bf16[4,448,256]{2,1,0:T(8,128)(2,1)}) custom-call(s32[64,128]{1,0:T(8,128)} %bitcast.14, bf16[1792,256]{1,0:T(8,128)(2,1)} %collective-permute-done.3.far_ref, bf16[896,256]{1,0:T(8,128)(2,1)S(1)} %copy-done.1, bf16[896,256]{1,0:T(8,128)(2,1)S(1)} %copy-done.3, ...), custom_call_target="tpu_custom_call" | custom-call | flops 12000000000 | bytes 8000000 | tf_op jit(solution)/shard_map/attention/pallas_call | solution.py:641
  84.4 1.5 collective-permute-start.4
  86.0 0.8 copy-done.10
  86.7 16.2 %mixer_second.1 = (bf16[256,1792]{1,0:T(8,128)(2,1)}, f32[8,1792]{1,0:T(8,128)}, f32[8,1792]{1,0:T(8,128)}, bf16[256,1792]{1,0:T(8,128)(2,1)}, f32[28,256]{1,0:T...) custom-call(bf16[256,1792]{1,0:T(8,128)(2,1)} %x_ref.3, bf16[8,1792]{1,0:T(8,128)(2,1)} %copy-done.12, ...), custom_call_target="tpu_custom_call" | custom-call | flops 17999998976 | bytes 8000000 | tf_op jit(solution)/shard_map/mixer_second/pallas_call | solution.py:464
  103.8 1.4 collective-permute-start.12
  105.2 1.3 collective-permute-start.9
  106.5 14.2 %all-to-all-start.2 = ((bf16[32,64,128]{2,1,0:T(8,128)(2,1)}), bf16[32,64,128]{2,1,0:T(8,128)(2,1)S(1)}, u32[]{:S(2)}, u32[]{:S(2)}) async-start(bf16[32,64,128]{2,1,0:T(8,128)(2,1)} %get-tuple-element.58), calls=%async_computation.2 | async-start | bytes 1048576 | tf_op jit(solution)/shard_map/all_to_all | solution.py:726
  120.8 3.0 %merge.1 = (bf16[672,256]{1,0:T(8,128)(2,1)}, bf16[672,256]{1,0:T(8,128)(2,1)}, bf16[672,256]{1,0:T(8,128)(2,1)}, bf16[672,256]{1,0:T(8,128)(2,1)}) custom-call(bf16[4,224,256]{2,1,0:T(8,128)(2,1)} %get-tuple-element.43.dq_ref, f32[4,448,256]{2,1,0:T(8,128)} %get-tuple-element.44.dkv_ref, bf16[4,448,256]{2,1,0:T(8,128)(2,1)S(1)} %collective-permute-done.4.back_ref), custom_call_target="tpu_custom_call" | custom-call | flops 3000000000 | bytes 4000000 | tf_op jit(solution)/shard_map/merge/pallas_call | solution.py:672
  123.7 1.8 %collective-permute-start.5 = (bf16[672,256]{1,0:T(8,128)(2,1)}, bf16[672,256]{1,0:T(8,128)(2,1)S(1)}, u32[]{:S(2)}, u32[]{:S(2)}) collective-permute-start(bf16[672,256]{1,0:T(8,128)(2,1)} %get-tuple-element.47), channel_id=1, source_target_pairs={{0,4},{4,8},{8,12},{12,0},{1,5},{5,9},{9,13},{13,1},{2,6},{6,10},{... | collective-permute-start | bytes 1032200 | tf_op jit(solution)/shard_map/ppermute | solution.py:716
  125.5 2.7 %collective-permute-start.6 = (bf16[672,256]{1,0:T(8,128)(2,1)}, bf16[672,256]{1,0:T(8,128)(2,1)S(1)}, u32[]{:S(2)}, u32[]{:S(2)}) collective-permute-start(bf16[672,256]{1,0:T(8,128)(2,1)} %get-tuple-element.48), channel_id=1, source_target_pairs={{0,8},{4,12},{8,0},{12,4},{1,9},{5,13},{9,1},{13,5},{2,10},{6,14},... | collective-permute-start | bytes 1032200 | tf_op jit(solution)/shard_map/ppermute | solution.py:716
  128.2 1.5 collective-permute-start.7
  130.3 3.9 %all-to-all-done.2.bundle_ref = bf16[32,64,128]{2,1,0:T(8,128)(2,1)S(1)} async-done(((bf16[32,64,128]{2,1,0:T(8,128)(2,1)}), bf16[32,64,128]{2,1,0:T(8,128)(2,1)S(1)}, u32[]{:S(2)}, u32[]{:S(2)}) %all-to-all-start.2) | async-done | bytes 524320 | tf_op jit(solution)/shard_map/all_to_all | solution.py:726
  134.2 0.9 finish.1
  135.0 2.8 %collective-permute-done.5.refs_1_ = bf16[672,256]{1,0:T(8,128)(2,1)S(1)} collective-permute-done((bf16[672,256]{1,0:T(8,128)(2,1)}, bf16[672,256]{1,0:T(8,128)(2,1)S(1)}, u32[]{:S(2)}, u32[]{:S(2)}) %collective-permute-start.5) | collective-permute-done | bytes 344096 | tf_op jit(solution)/shard_map/ppermute | solution.py:716
  137.9 6.3 %collective-permute-done.6.refs_2_ = bf16[672,256]{1,0:T(8,128)(2,1)S(1)} collective-permute-done((bf16[672,256]{1,0:T(8,128)(2,1)}, bf16[672,256]{1,0:T(8,128)(2,1)S(1)}, u32[]{:S(2)}, u32[]{:S(2)}) %collective-permute-start.6) | collective-permute-done | bytes 344096 | tf_op jit(solution)/shard_map/ppermute | solution.py:716
  144.2 1.0 copy-done.9
  145.2 1.4 unpack.1
  (36 shorter events, 3.0 us)
Async XLA Ops:
  4.0 13.6 %collective-permute-start = (bf16[896,256]{1,0:T(8,128)(2,1)}, bf16[896,256]{1,0:T(8,128)(2,1)S(1)}, u32[]{:S(2)}, u32[]{:S(2)}) collective-permute-start(bf16[896,256]{1,0:T(8,128)(2,1)} %get-tuple-element.40), channel_id=1, source_target_pairs={{0,4},{4,8},{8,12},{12,0},{1,5},{5,9},{9,13},{13,1},{2,6},{6,10},{... | collective-permute-start | bytes 1376264 | tf_op jit(solution)/shard_map/ppermute | solution.py:716
  5.6 23.4 %collective-permute-start.1 = (bf16[896,256]{1,0:T(8,128)(2,1)}, bf16[896,256]{1,0:T(8,128)(2,1)S(1)}, u32[]{:S(2)}, u32[]{:S(2)}) collective-permute-start(bf16[896,256]{1,0:T(8,128)(2,1)} %get-tuple-element.41), channel_id=1, source_target_pairs={{0,8},{4,12},{8,0},{12,4},{1,9},{5,13},{9,1},{13,5},{2,10},{6,14},... | collective-permute-start | bytes 1376264 | tf_op jit(solution)/shard_map/ppermute | solution.py:716
  8.3 20.6 %collective-permute-start.2 = (bf16[896,256]{1,0:T(8,128)(2,1)}, bf16[896,256]{1,0:T(8,128)(2,1)S(1)}, u32[]{:S(2)}, u32[]{:S(2)}) collective-permute-start(bf16[896,256]{1,0:T(8,128)(2,1)} %get-tuple-element.42), channel_id=1, source_target_pairs={{0,12},{4,0},{8,4},{12,8},{1,13},{5,1},{9,5},{13,9},{2,14},{6,2},{... | collective-permute-start | bytes 1376264 | tf_op jit(solution)/shard_map/ppermute | solution.py:716
  10.5 26.8 %collective-permute-start.8 = (bf16[8,1792]{1,0:T(8,128)(2,1)S(1)}, bf16[8,1792]{1,0:T(8,128)(2,1)S(1)}, u32[]{:S(2)}, u32[]{:S(2)}) collective-permute-start(bf16[8,1792]{1,0:T(8,128)(2,1)S(1)} %slice.3), channel_id=1, source_target_pairs={{0,4},{4,8},{8,12},{12,16},{16,20},{20,24},{24,28},{28,32},{32,36}... | collective-permute-start | bytes 86024 | tf_op jit(solution)/shard_map/ppermute | solution.py:710
  17.6 29.3 %copy-start.2 = (bf16[896,256]{1,0:T(8,128)(2,1)}, bf16[896,256]{1,0:T(8,128)(2,1)S(1)}, u32[]{:S(2)}) copy-start(bf16[896,256]{1,0:T(8,128)(2,1)S(1)} %collective-permute-done.refs_1_) | copy-start | bytes 1376260
  28.9 18.0 %copy-start.4 = (bf16[896,256]{1,0:T(8,128)(2,1)}, bf16[896,256]{1,0:T(8,128)(2,1)S(1)}, u32[]{:S(2)}) copy-start(bf16[896,256]{1,0:T(8,128)(2,1)S(1)} %collective-permute-done.1.refs_2_) | copy-start | bytes 1376260
  28.9 18.0 %copy-start.6 = (bf16[896,256]{1,0:T(8,128)(2,1)}, bf16[896,256]{1,0:T(8,128)(2,1)S(1)}, u32[]{:S(2)}) copy-start(bf16[896,256]{1,0:T(8,128)(2,1)S(1)} %collective-permute-done.2.refs_3_) | copy-start | bytes 1376260
  28.9 1.4 copy-start
  31.3 43.2 %collective-permute-start.3 = (bf16[1792,256]{1,0:T(8,128)(2,1)}, bf16[1792,256]{1,0:T(8,128)(2,1)}, u32[]{:S(2)}, u32[]{:S(2)}) collective-permute-start(bf16[1792,256]{1,0:T(8,128)(2,1)} %lend.1), channel_id=1, source_target_pairs={{0,16},{4,20},{8,24},{12,28},{16,32},{20,36},{24,40},{28,44},{32,4... | collective-permute-start | bytes 2752520 | tf_op jit(solution)/shard_map/ppermute | solution.py:710
  37.3 0.6 copy-start.12
  66.6 7.9 %copy-start.1 = (bf16[896,256]{1,0:T(8,128)(2,1)S(1)}, bf16[896,256]{1,0:T(8,128)(2,1)}, u32[]{:S(2)}) copy-start(bf16[896,256]{1,0:T(8,128)(2,1)} %get-tuple-element.39.refs_0_) | copy-start | bytes 1376260
  66.6 7.9 %copy-start.5 = (bf16[896,256]{1,0:T(8,128)(2,1)S(1)}, bf16[896,256]{1,0:T(8,128)(2,1)}, u32[]{:S(2)}) copy-start(bf16[896,256]{1,0:T(8,128)(2,1)} %copy-done.4) | copy-start | bytes 1376260
  66.6 7.9 %copy-start.7 = (bf16[896,256]{1,0:T(8,128)(2,1)S(1)}, bf16[896,256]{1,0:T(8,128)(2,1)}, u32[]{:S(2)}) copy-start(bf16[896,256]{1,0:T(8,128)(2,1)} %copy-done.6) | copy-start | bytes 1376260
  67.9 18.1 %all-to-all-start.1 = ((bf16[32,56,128]{2,1,0:T(8,128)(2,1)}), bf16[32,56,128]{2,1,0:T(8,128)(2,1)S(1)}, u32[]{:S(2)}, u32[]{:S(2)}) async-start(bf16[32,56,128]{2,1,0:T(8,128)(2,1)} %chain.1), calls=%async_computation.1 | async-start | bytes 917504 | tf_op jit(solution)/shard_map/all_to_all | solution.py:726
  74.5 1.0 copy-start.3
  84.4 36.3 %collective-permute-start.4 = (bf16[4,448,256]{2,1,0:T(8,128)(2,1)}, bf16[4,448,256]{2,1,0:T(8,128)(2,1)S(1)}, u32[]{:S(2)}, u32[]{:S(2)}) collective-permute-start(bf16[4,448,256]{2,1,0:T(8,128)(2,1)} %get-tuple-element.45), channel_id=1, source_target_pairs={{16,0},{20,4},{24,8},{28,12},{32,16},{36,20},{40,24},{44,28},{48,3... | collective-permute-start | bytes 2752520 | tf_op jit(solution)/shard_map/ppermute | solution.py:710
  86.0 0.8 copy-start.10
  103.0 25.2 %collective-permute-start.10 = (bf16[256,128]{1,0:T(8,128)(2,1)}, bf16[256,128]{1,0:T(8,128)(2,1)S(1)}, u32[]{:S(2)}, u32[]{:S(2)}) collective-permute-start(bf16[256,128]{1,0:T(8,128)(2,1)} %get-tuple-element.59.refs_0_), channel_id=1, source_target_pairs={{0,1},{1,2},{2,3},{3,0},{4,5},{5,6},{6,7},{7,4},{8,9},{9,10},{10,1... | collective-permute-start | bytes 196616 | tf_op jit(solution)/shard_map/ppermute | solution.py:716
  103.1 27.2 %collective-permute-start.11 = (bf16[256,128]{1,0:T(8,128)(2,1)}, bf16[256,128]{1,0:T(8,128)(2,1)S(1)}, u32[]{:S(2)}, u32[]{:S(2)}) collective-permute-start(bf16[256,128]{1,0:T(8,128)(2,1)} %get-tuple-element.59.refs_0_), channel_id=1, source_target_pairs={{0,2},{1,3},{2,0},{3,1},{4,6},{5,7},{6,4},{7,5},{8,10},{9,11},{10,... | collective-permute-start | bytes 196616 | tf_op jit(solution)/shard_map/ppermute | solution.py:716
  103.8 26.4 %collective-permute-start.12 = (bf16[256,128]{1,0:T(8,128)(2,1)}, bf16[256,128]{1,0:T(8,128)(2,1)S(1)}, u32[]{:S(2)}, u32[]{:S(2)}) collective-permute-start(bf16[256,128]{1,0:T(8,128)(2,1)} %get-tuple-element.59.refs_0_), channel_id=1, source_target_pairs={{0,3},{1,0},{2,1},{3,2},{4,7},{5,4},{6,5},{7,6},{8,11},{9,8},{10,9... | collective-permute-start | bytes 196616 | tf_op jit(solution)/shard_map/ppermute | solution.py:716
  105.2 20.3 %collective-permute-start.9 = (f32[8,1792]{1,0:T(8,128)}, f32[8,1792]{1,0:T(8,128)S(1)}, u32[]{:S(2)}, u32[]{:S(2)}) collective-permute-start(f32[8,1792]{1,0:T(8,128)} %get-tuple-element.55), channel_id=1, source_target_pairs={{4,0},{8,4},{12,8},{16,12},{20,16},{24,20},{28,24},{32,28},{36,32}... | collective-permute-start | bytes 172040 | tf_op jit(solution)/shard_map/ppermute | solution.py:710
  106.5 27.7 %all-to-all-start.2 = ((bf16[32,64,128]{2,1,0:T(8,128)(2,1)}), bf16[32,64,128]{2,1,0:T(8,128)(2,1)S(1)}, u32[]{:S(2)}, u32[]{:S(2)}) async-start(bf16[32,64,128]{2,1,0:T(8,128)(2,1)} %get-tuple-element.58), calls=%async_computation.2 | async-start | bytes 1048576 | tf_op jit(solution)/shard_map/all_to_all | solution.py:726
  120.7 8.9 %copy-start.11 = (f32[8,1792]{1,0:T(8,128)S(1)}, f32[8,1792]{1,0:T(8,128)}, u32[]{:S(2)}) copy-start(f32[8,1792]{1,0:T(8,128)} %get-tuple-element.54) | copy-start | bytes 172036
  120.7 13.4 %copy-start.8 = (bf16[256,128]{1,0:T(8,128)(2,1)S(1)}, bf16[256,128]{1,0:T(8,128)(2,1)}, u32[]{:S(2)}) copy-start(bf16[256,128]{1,0:T(8,128)(2,1)} %get-tuple-element.59.refs_0_) | copy-start | bytes 196612
  123.7 14.1 %collective-permute-start.5 = (bf16[672,256]{1,0:T(8,128)(2,1)}, bf16[672,256]{1,0:T(8,128)(2,1)S(1)}, u32[]{:S(2)}, u32[]{:S(2)}) collective-permute-start(bf16[672,256]{1,0:T(8,128)(2,1)} %get-tuple-element.47), channel_id=1, source_target_pairs={{0,4},{4,8},{8,12},{12,0},{1,5},{5,9},{9,13},{13,1},{2,6},{6,10},{... | collective-permute-start | bytes 1032200 | tf_op jit(solution)/shard_map/ppermute | solution.py:716
  125.5 18.7 %collective-permute-start.6 = (bf16[672,256]{1,0:T(8,128)(2,1)}, bf16[672,256]{1,0:T(8,128)(2,1)S(1)}, u32[]{:S(2)}, u32[]{:S(2)}) collective-permute-start(bf16[672,256]{1,0:T(8,128)(2,1)} %get-tuple-element.48), channel_id=1, source_target_pairs={{0,8},{4,12},{8,0},{12,4},{1,9},{5,13},{9,1},{13,5},{2,10},{6,14},... | collective-permute-start | bytes 1032200 | tf_op jit(solution)/shard_map/ppermute | solution.py:716
  128.2 16.0 %collective-permute-start.7 = (bf16[672,256]{1,0:T(8,128)(2,1)}, bf16[672,256]{1,0:T(8,128)(2,1)S(1)}, u32[]{:S(2)}, u32[]{:S(2)}) collective-permute-start(bf16[672,256]{1,0:T(8,128)(2,1)} %get-tuple-element.49), channel_id=1, source_target_pairs={{0,12},{4,0},{8,4},{12,8},{1,13},{5,1},{9,5},{13,9},{2,14},{6,2},{... | collective-permute-start | bytes 1032200 | tf_op jit(solution)/shard_map/ppermute | solution.py:716
  144.2 1.0 copy-start.9

commit v6 on v5

--- a/solution.py
+++ b/solution.py
@@ -68,8 +68,8 @@
     return pl.BlockSpec((rows, BLK), lambda c: (0, c))
 
 
-IN_SMEM = pl.BlockSpec(memory_space=pltpu.SMEM)
 IN_VMEM = pl.BlockSpec(memory_space=pltpu.VMEM)
+GRANT = pltpu.CompilerParams(vmem_limit_bytes=32 * 2**20)
 
 
 def seq_index():
@@ -252,6 +252,7 @@
             pltpu.VMEM((T, 128), BF16),
         ],
         cost_estimate=pl.CostEstimate(flops=8 * 10**9, bytes_accessed=4 * 10**6, transcendentals=0),
+        compiler_params=GRANT,
         name="mixer_first",
     )(*arrays)
 
@@ -281,9 +282,10 @@
         chain_kernel,
         in_specs=[IN_VMEM],
         out_specs=IN_VMEM,
-        out_shape=jax.ShapeDtypeStruct((SHARDS, ROWS, 128), BF16),
+        out_shape=pltpu.VMEM((SHARDS, ROWS, 128), BF16),
         scratch_shapes=[pltpu.VMEM((SHARDS, ROWS, 128), F32)],
         cost_estimate=pl.CostEstimate(flops=2 * 10**9, bytes_accessed=10**6, transcendentals=0),
+        compiler_params=GRANT,
         name="chain",
     )(parts)
 
@@ -492,6 +494,7 @@
             half, half, half, half,
         ],
         cost_estimate=pl.CostEstimate(flops=18 * 10**9, bytes_accessed=8 * 10**6, transcendentals=0),
+        compiler_params=GRANT,
         name="mixer_second",
     )(*arrays)
 
@@ -528,6 +531,7 @@
         out_specs=[IN_VMEM] * 6,
         out_shape=[jax.ShapeDtypeStruct((KERNEL, COLS), F32), small, small, small, wide, wide],
         scratch_shapes=[pltpu.VMEM((LOCAL_HEADS, T, 128), F32)],
+        compiler_params=GRANT,
         name="finish",
     )(bundle, *coeffs)
 
@@ -552,8 +556,9 @@
         pack_kernel,
         in_specs=[IN_VMEM] * 4,
         out_specs=[IN_VMEM] * ROW,
-        out_shape=[jax.ShapeDtypeStruct((4 * HEAD_DIM, T), BF16)] * ROW,
+        out_shape=[pltpu.VMEM((4 * HEAD_DIM, T), BF16)] * ROW,
         scratch_shapes=[pltpu.VMEM((LOCAL_HEADS, 4 * HEAD_DIM, T), BF16)],
+        compiler_params=GRANT,
         name="pack",
     )(keys, values, queries, grads)
 
@@ -568,7 +573,8 @@
         lend_kernel,
         in_specs=[IN_VMEM] * ROW,
         out_specs=IN_VMEM,
-        out_shape=jax.ShapeDtypeStruct((ROW * PAIR[0], T), BF16),
+        out_shape=pltpu.VMEM((ROW * PAIR[0], T), BF16),
+        compiler_params=GRANT,
         name="lend",
     )(*own)
 
@@ -643,9 +649,9 @@
         in_specs=[IN_VMEM] * (2 + ROW),
         out_specs=[IN_VMEM] * 3,
         out_shape=[
-            jax.ShapeDtypeStruct((ROW, HEAD_DIM, T), BF16),
-            jax.ShapeDtypeStruct(pairs, F32),
-            jax.ShapeDtypeStruct(pairs, BF16),
+            pltpu.VMEM((ROW, HEAD_DIM, T), BF16),
+            pltpu.VMEM(pairs, F32),
+            pltpu.VMEM(pairs, BF16),
         ],
         scratch_shapes=[
             pltpu.VMEM(pairs, F32),
@@ -653,6 +659,7 @@
             pltpu.VMEM((2 * ROW, *PAIR), BF16),
         ],
         cost_estimate=pl.CostEstimate(flops=12 * 10**9, bytes_accessed=8 * 10**6, transcendentals=0),
+        compiler_params=GRANT,
         name="attention",
     )(docs, far, *own)
 
@@ -673,8 +680,9 @@
         merge_kernel,
         in_specs=[IN_VMEM] * 3,
         out_specs=[IN_VMEM] * ROW,
-        out_shape=[jax.ShapeDtypeStruct((3 * HEAD_DIM, T), BF16)] * ROW,
+        out_shape=[pltpu.VMEM((3 * HEAD_DIM, T), BF16)] * ROW,
         cost_estimate=pl.CostEstimate(flops=3 * 10**9, bytes_accessed=4 * 10**6, transcendentals=0),
+        compiler_params=GRANT,
         name="merge",
     )(dq, dkv, back)
 
@@ -700,6 +708,7 @@
         out_shape=[wide] * 3,
         scratch_shapes=[pltpu.VMEM((3, LOCAL_HEADS, HEAD_DIM, T), BF16)],
         cost_estimate=pl.CostEstimate(flops=2 * 10**9, bytes_accessed=3 * 10**6, transcendentals=0),
+        compiler_params=GRANT,
         name="unpack",
     )(*parts)
 
@@ -750,7 +759,7 @@
     dq, dkv, back = attention(docs, near(far), own)
     returned = passed_along(back, SEQ, -ROW)
     dx, tail, spill, dgate, dstep, coeff, bundle = mixer_second(*mixer_args, entering)
-    leaving = merge(dq, dkv, near(returned))
+    leaving = merge(near(dq), near(dkv), near(returned))
     swapped = turns(leaving, "seq_2")
     spilled = passed_along(spill, SEQ, -1)
     bundles = exchange(bundle, SEQ)

time: 147 us -> 148 us (level)
  Pallas kernels: 44.9 us -> 34.1 us
  local copies, waits for them, and re-layouts: 5.5 us -> 13.9 us
  blocking collectives: 19.7 us -> 21.8 us
    unnamed x26 -> x48, local copies, waits for them, and re-layouts: 4.75 us -> 13.9 us
    pallas_call x1, Pallas kernels: 2.96 us -> 0.19 us  [merge(): pl.pallas_call(merge_kernel, in_specs=[IN_VMEM] * 3, out_specs=[IN_VMEM]...]
    pallas_call x1, Pallas kernels: 3.32 us -> 0.66 us  [pack(): pl.pallas_call(pack_kernel, in_specs=[IN_VMEM] * 4, out_specs=[IN_VMEM] *...]
    pallas_call x1, Pallas kernels: 9.02 us -> 6.4 us  [mixer_first(): pl.pallas_call(mixer_first_kernel, grid=(STEPS,), in_specs=mixer_specs(he...]
    all_to_all x1, blocking collectives: 19.7 us -> 21.8 us  [exchange(): return lax.all_to_all(array, axis, split_axis=0, concat_axis=0, tiled=True)]
  transfers between devices with their start and end apart: 15 -> 15, of which waited for: 6 -> 5; matrix products, arithmetic and copies ran while one was open for 1% -> 0% of each run, Pallas kernels for 27% -> 22%
where the time goes in v6:
time: 148 us
  starting transfers between devices  47 us (32%)
  Pallas kernels  34.1 us (23%)
  waiting for transfers between devices  29.1 us (20%)
  blocking collectives  21.8 us (15%)
  local copies, waits for them, and re-layouts  13.9 us (9%)
    ppermute x9, waiting for transfers between devices, turns(): lax.ppermute(part, axis, [(n, (n + turn) % count) for n in range(count)])  25.9 us
    all_to_all x2, starting transfers between devices, exchange(): return lax.all_to_all(array, axis, split_axis=0, concat_axis=0, tiled=True)  21.9 us
    all_to_all x1, blocking collectives, exchange(): return lax.all_to_all(array, axis, split_axis=0, concat_axis=0, tiled=True)  21.8 us
    pallas_call x1, Pallas kernels, mixer_second(): pl.pallas_call(mixer_second_kernel, grid=(STEPS,), in_specs=mixer_specs(h...  15 us
    unnamed x48, local copies, waits for them, and re-layouts  13.9 us
    ppermute x9, starting transfers between devices, turns(): lax.ppermute(part, axis, [(n, (n + turn) % count) for n in range(count)])  13.9 us
    ppermute x4, starting transfers between devices, passed_along(): lax.ppermute(value, axis, [(source, source + steps) for source in range(i...  11.3 us
    pallas_call x1, Pallas kernels, attention(): pl.pallas_call(attention_kernel, in_specs=[IN_VMEM] * (2 + ROW), out_spec...  8.35 us
  transfers between devices with their start and end apart: 15, of which 5 were waited for; matrix products, arithmetic and copies ran while one was open for 0% of the time, Pallas kernels for 22%

profile of v6, /device:TPU:0, one launch (start us, length us, event | category | flops | bytes accessed | tf_op | source)
XLA Modules:
  0.0 147.5 jit_solution(11526673982557940819)
XLA Ops:
  1.7 1.0 copy-done.1
  2.7 1.0 copy-done.2
  3.7 1.0 copy-done.3
  5.5 1.7 %collective-permute-start = (bf16[896,256]{1,0:T(8,128)(2,1)S(1)}, bf16[896,256]{1,0:T(8,128)(2,1)S(1)}, u32[]{:S(2)}, u32[]{:S(2)}) collective-permute-start(bf16[896,256]{1,0:T(8,128)(2,1)S(1)} %get-tuple-element.40), channel_id=1, source_target_pairs={{0,4},{4,8},{8,12},{12,0},{1,5},{5,9},{9,13},{13,1},{2,6},{6,10},{... | collective-permute-start | bytes 1376264 | tf_op jit(solution)/shard_map/ppermute | solution.py:725
  7.2 2.7 %collective-permute-start.1 = (bf16[896,256]{1,0:T(8,128)(2,1)S(1)}, bf16[896,256]{1,0:T(8,128)(2,1)S(1)}, u32[]{:S(2)}, u32[]{:S(2)}) collective-permute-start(bf16[896,256]{1,0:T(8,128)(2,1)S(1)} %get-tuple-element.41), channel_id=1, source_target_pairs={{0,8},{4,12},{8,0},{12,4},{1,9},{5,13},{9,1},{13,5},{2,10},{6,14},... | collective-permute-start | bytes 1376264 | tf_op jit(solution)/shard_map/ppermute | solution.py:725
  9.9 1.4 collective-permute-start.2
  11.4 2.5 %collective-permute-start.8 = (bf16[8,1792]{1,0:T(8,128)(2,1)S(1)}, bf16[8,1792]{1,0:T(8,128)(2,1)S(1)}, u32[]{:S(2)}, u32[]{:S(2)}) collective-permute-start(bf16[8,1792]{1,0:T(8,128)(2,1)S(1)} %slice.3), channel_id=1, source_target_pairs={{0,4},{4,8},{8,12},{12,16},{16,20},{20,24},{24,28},{28,32},{32,36}... | collective-permute-start | bytes 86024 | tf_op jit(solution)/shard_map/ppermute | solution.py:719
  13.9 5.7 %collective-permute-done.refs_1_ = bf16[896,256]{1,0:T(8,128)(2,1)S(1)} collective-permute-done((bf16[896,256]{1,0:T(8,128)(2,1)S(1)}, bf16[896,256]{1,0:T(8,128)(2,1)S(1)}, u32[]{:S(2)}, u32[]{:S(2)}) %collective-permute-start) | collective-permute-done | bytes 458784 | tf_op jit(solution)/shard_map/ppermute | solution.py:725
  19.5 10.8 %collective-permute-done.1.refs_2_ = bf16[896,256]{1,0:T(8,128)(2,1)S(1)} collective-permute-done((bf16[896,256]{1,0:T(8,128)(2,1)S(1)}, bf16[896,256]{1,0:T(8,128)(2,1)S(1)}, u32[]{:S(2)}, u32[]{:S(2)}) %collective-permute-start.1) | collective-permute-done | bytes 458784 | tf_op jit(solution)/shard_map/ppermute | solution.py:725
  30.4 6.0 %collective-permute-start.3 = (bf16[1792,256]{1,0:T(8,128)(2,1)S(1)}, bf16[1792,256]{1,0:T(8,128)(2,1)}, u32[]{:S(2)}, u32[]{:S(2)}) collective-permute-start(bf16[1792,256]{1,0:T(8,128)(2,1)S(1)} %lend.1), channel_id=1, source_target_pairs={{0,16},{4,20},{8,24},{12,28},{16,32},{20,36},{24,40},{28,44},{32,4... | collective-permute-start | bytes 2752520 | tf_op jit(solution)/shard_map/ppermute | solution.py:719
  36.5 6.4 %mixer_first.1 = bf16[2048,128]{1,0:T(8,128)(2,1)S(1)} custom-call(bf16[256,1792]{1,0:T(8,128)(2,1)S(1)} %copy-done.4, bf16[8,1792]{1,0:T(8,128)(2,1)S(1)} %collective-permute-done.8.halo_ref, f32[4,1792]{1,0:T(4,128)S(1)} %copy-done.14, bf16[256,1792]{1,0:T(8,128)(2,1)S(1)} %copy-done.6, bf16[256,1792]{1,0:T(8,128)(2,1)S(1)} %copy-done.8, ...), custom_call_target="tpu_custom_call" | custom-call | flops 8000000000 | bytes 4000000 | tf_op jit(solution)/shard_map/mixer_first/pallas_call | solution.py:243
  42.9 21.8 %all_to_all.15.parts_ref = bf16[32,64,128]{2,1,0:T(8,128)(2,1)S(1)} all-to-all(bf16[32,64,128]{2,1,0:T(8,128)(2,1)S(1)} %bitcast.11), channel_id=1, replica_groups=mesh['seq_0'=4,'seq_1'=2,'seq_2'=4,'head'=4] {'seq_0','seq_1','seq_2'}, dimensions={0} | all-to-all | bytes 1048576 | tf_op jit(solution)/shard_map/all_to_all | solution.py:735
  64.7 1.3 chain.1
  65.9 7.6 %all-to-all-start.1 = ((bf16[32,56,128]{2,1,0:T(8,128)(2,1)}), bf16[32,56,128]{2,1,0:T(8,128)(2,1)S(1)}, u32[]{:S(2)}, u32[]{:S(2)}) async-start(bf16[32,56,128]{2,1,0:T(8,128)(2,1)} %chain.1), calls=%async_computation.1 | async-start | bytes 917504 | tf_op jit(solution)/shard_map/all_to_all | solution.py:735
  73.5 8.4 %attention.1 = (bf16[4,224,256]{2,1,0:T(8,128)(2,1)S(1)}, f32[4,448,256]{2,1,0:T(8,128)S(1)}, bf16[4,448,256]{2,1,0:T(8,128)(2,1)}) custom-call(s32[64,128]{1,0:T(8,128)S(1)} %bitcast.14, bf16[1792,256]{1,0:T(8,128)(2,1)} %collective-permute-done.3.far_ref, bf16[896,256]{1,0:T(8,128)(2,1)S(1)} %get-tuple-element.39.refs_0_, ...), custom_call_target="tpu_custom_call" | custom-call | flops 12000000000 | bytes 8000000 | tf_op jit(solution)/shard_map/attention/pallas_call | solution.py:647
  81.9 1.3 copy-done.18
  83.9 1.5 collective-permute-start.4
  85.4 1.2 copy-done.5
  86.6 1.2 copy-done.7
  87.8 1.2 copy-done.9
  89.0 15.0 %mixer_second.1 = (bf16[256,1792]{1,0:T(8,128)(2,1)}, f32[8,1792]{1,0:T(8,128)S(1)}, f32[8,1792]{1,0:T(8,128)S(1)}, bf16[256,1792]{1,0:T(8,128)(2,1)}, f32[28,25...) custom-call(bf16[256,1792]{1,0:T(8,128)(2,1)S(1)} %copy-done.5, ...), custom_call_target="tpu_custom_call" | custom-call | flops 17999998976 | bytes 8000000 | tf_op jit(solution)/shard_map/mixer_second/pallas_call | solution.py:466
  104.7 1.4 collective-permute-start.12
  106.1 1.3 collective-permute-start.9
  107.4 14.3 %all-to-all-start.2 = ((bf16[32,64,128]{2,1,0:T(8,128)(2,1)}), bf16[32,64,128]{2,1,0:T(8,128)(2,1)S(1)}, u32[]{:S(2)}, u32[]{:S(2)}) async-start(bf16[32,64,128]{2,1,0:T(8,128)(2,1)} %get-tuple-element.58), calls=%async_computation.2 | async-start | bytes 1048576 | tf_op jit(solution)/shard_map/all_to_all | solution.py:735
  121.7 1.5 %copy-done.19 = f32[4,448,256]{2,1,0:T(8,128)S(1)} copy-done((f32[4,448,256]{2,1,0:T(8,128)S(1)}, f32[4,448,256]{2,1,0:T(8,128)}, u32[]{:S(2)}) %copy-start.19) | copy-done | bytes 1835032
  125.1 1.8 %collective-permute-start.5 = (bf16[672,256]{1,0:T(8,128)(2,1)S(1)}, bf16[672,256]{1,0:T(8,128)(2,1)S(1)}, u32[]{:S(2)}, u32[]{:S(2)}) collective-permute-start(bf16[672,256]{1,0:T(8,128)(2,1)S(1)} %get-tuple-element.47), channel_id=1, source_target_pairs={{0,4},{4,8},{8,12},{12,0},{1,5},{5,9},{9,13},{13,1},{2,6},{6,10},{... | collective-permute-start | bytes 1032200 | tf_op jit(solution)/shard_map/ppermute | solution.py:725
  126.9 2.7 %collective-permute-start.6 = (bf16[672,256]{1,0:T(8,128)(2,1)S(1)}, bf16[672,256]{1,0:T(8,128)(2,1)S(1)}, u32[]{:S(2)}, u32[]{:S(2)}) collective-permute-start(bf16[672,256]{1,0:T(8,128)(2,1)S(1)} %get-tuple-element.48), channel_id=1, source_target_pairs={{0,8},{4,12},{8,0},{12,4},{1,9},{5,13},{9,1},{13,5},{2,10},{6,14},... | collective-permute-start | bytes 1032200 | tf_op jit(solution)/shard_map/ppermute | solution.py:725
  129.6 1.5 collective-permute-start.7
  131.7 3.2 %all-to-all-done.2.bundle_ref = bf16[32,64,128]{2,1,0:T(8,128)(2,1)S(1)} async-done(((bf16[32,64,128]{2,1,0:T(8,128)(2,1)}), bf16[32,64,128]{2,1,0:T(8,128)(2,1)S(1)}, u32[]{:S(2)}, u32[]{:S(2)}) %all-to-all-start.2) | async-done | bytes 524320 | tf_op jit(solution)/shard_map/all_to_all | solution.py:735
  135.7 2.8 %collective-permute-done.5.refs_1_ = bf16[672,256]{1,0:T(8,128)(2,1)S(1)} collective-permute-done((bf16[672,256]{1,0:T(8,128)(2,1)S(1)}, bf16[672,256]{1,0:T(8,128)(2,1)S(1)}, u32[]{:S(2)}, u32[]{:S(2)}) %collective-permute-start.5) | collective-permute-done | bytes 344096 | tf_op jit(solution)/shard_map/ppermute | solution.py:725
  138.6 6.6 %collective-permute-done.6.refs_2_ = bf16[672,256]{1,0:T(8,128)(2,1)S(1)} collective-permute-done((bf16[672,256]{1,0:T(8,128)(2,1)S(1)}, bf16[672,256]{1,0:T(8,128)(2,1)S(1)}, u32[]{:S(2)}, u32[]{:S(2)}) %collective-permute-start.6) | collective-permute-done | bytes 344096 | tf_op jit(solution)/shard_map/ppermute | solution.py:725
  146.1 1.4 unpack.1
  (58 shorter events, 7.8 us)
Async XLA Ops:
  0.6 1.0 copy-start
  4.7 6.6 %copy-start.4 = (bf16[256,1792]{1,0:T(8,128)(2,1)S(1)}, bf16[256,1792]{1,0:T(8,128)(2,1)}, u32[]{:S(2)}) copy-start(bf16[256,1792]{1,0:T(8,128)(2,1)} %x_ref.3) | copy-start | bytes 2752516
  5.4 31.0 %copy-start.6 = (bf16[256,1792]{1,0:T(8,128)(2,1)S(1)}, bf16[256,1792]{1,0:T(8,128)(2,1)}, u32[]{:S(2)}) copy-start(bf16[256,1792]{1,0:T(8,128)(2,1)} %gate_ref.3) | copy-start | bytes 2752516
  5.4 31.0 %copy-start.8 = (bf16[256,1792]{1,0:T(8,128)(2,1)S(1)}, bf16[256,1792]{1,0:T(8,128)(2,1)}, u32[]{:S(2)}) copy-start(bf16[256,1792]{1,0:T(8,128)(2,1)} %grad_ref.3) | copy-start | bytes 2752516
  5.4 31.0 %copy-start.10 = (bf16[256,128]{1,0:T(8,128)(2,1)S(1)}, bf16[256,128]{1,0:T(8,128)(2,1)}, u32[]{:S(2)}) copy-start(bf16[256,128]{1,0:T(8,128)(2,1)} %in_ref.3) | copy-start | bytes 196612
  5.4 31.0 %copy-start.11 = (bf16[256,128]{1,0:T(8,128)(2,1)S(1)}, bf16[256,128]{1,0:T(8,128)(2,1)}, u32[]{:S(2)}) copy-start(bf16[256,128]{1,0:T(8,128)(2,1)} %out_ref.3) | copy-start | bytes 196612
  5.4 31.0 %copy-start.12 = (s32[8192]{0:T(1024)S(1)}, s32[8192]{0:T(1024)}, u32[]{:S(2)}) copy-start(s32[8192]{0:T(1024)} %param.19) | copy-start | bytes 98308
  5.5 31.0 %copy-start.13 = (f32[256,28]{0,1:T(8,128)S(1)}, f32[256,28]{0,1:T(8,128)}, u32[]{:S(2)}) copy-start(f32[256,28]{0,1:T(8,128)} %param.22) | copy-start | bytes 86020
  5.5 31.0 %copy-start.14 = (f32[4,1792]{1,0:T(4,128)S(1)}, f32[4,1792]{1,0:T(4,128)}, u32[]{:S(2)}) copy-start(f32[4,1792]{1,0:T(4,128)} %weight_ref.3) | copy-start | bytes 86020
  5.5 31.0 %copy-start.15 = (f32[28]{0:T(128)S(1)}, f32[28]{0:T(128)}, u32[]{:S(2)}) copy-start(f32[28]{0:T(128)} %param.23) | copy-start | bytes 340
  5.5 31.0 %copy-start.16 = (f32[28]{0:T(128)S(1)}, f32[28]{0:T(128)}, u32[]{:S(2)}) copy-start(f32[28]{0:T(128)} %param.24) | copy-start | bytes 340
  5.5 31.0 %copy-start.17 = (f32[28]{0:T(128)S(1)}, f32[28]{0:T(128)}, u32[]{:S(2)}) copy-start(f32[28]{0:T(128)} %param.25) | copy-start | bytes 340
  5.5 14.0 %collective-permute-start = (bf16[896,256]{1,0:T(8,128)(2,1)S(1)}, bf16[896,256]{1,0:T(8,128)(2,1)S(1)}, u32[]{:S(2)}, u32[]{:S(2)}) collective-permute-start(bf16[896,256]{1,0:T(8,128)(2,1)S(1)} %get-tuple-element.40), channel_id=1, source_target_pairs={{0,4},{4,8},{8,12},{12,0},{1,5},{5,9},{9,13},{13,1},{2,6},{6,10},{... | collective-permute-start | bytes 1376264 | tf_op jit(solution)/shard_map/ppermute | solution.py:725
  7.2 23.1 %collective-permute-start.1 = (bf16[896,256]{1,0:T(8,128)(2,1)S(1)}, bf16[896,256]{1,0:T(8,128)(2,1)S(1)}, u32[]{:S(2)}, u32[]{:S(2)}) collective-permute-start(bf16[896,256]{1,0:T(8,128)(2,1)S(1)} %get-tuple-element.41), channel_id=1, source_target_pairs={{0,8},{4,12},{8,0},{12,4},{1,9},{5,13},{9,1},{13,5},{2,10},{6,14},... | collective-permute-start | bytes 1376264 | tf_op jit(solution)/shard_map/ppermute | solution.py:725
  9.9 20.4 %collective-permute-start.2 = (bf16[896,256]{1,0:T(8,128)(2,1)S(1)}, bf16[896,256]{1,0:T(8,128)(2,1)S(1)}, u32[]{:S(2)}, u32[]{:S(2)}) collective-permute-start(bf16[896,256]{1,0:T(8,128)(2,1)S(1)} %get-tuple-element.42), channel_id=1, source_target_pairs={{0,12},{4,0},{8,4},{12,8},{1,13},{5,1},{9,5},{13,9},{2,14},{6,2},{... | collective-permute-start | bytes 1376264 | tf_op jit(solution)/shard_map/ppermute | solution.py:725
  11.4 25.0 %collective-permute-start.8 = (bf16[8,1792]{1,0:T(8,128)(2,1)S(1)}, bf16[8,1792]{1,0:T(8,128)(2,1)S(1)}, u32[]{:S(2)}, u32[]{:S(2)}) collective-permute-start(bf16[8,1792]{1,0:T(8,128)(2,1)S(1)} %slice.3), channel_id=1, source_target_pairs={{0,4},{4,8},{8,12},{12,16},{16,20},{20,24},{24,28},{28,32},{32,36}... | collective-permute-start | bytes 86024 | tf_op jit(solution)/shard_map/ppermute | solution.py:719
  30.4 43.2 %collective-permute-start.3 = (bf16[1792,256]{1,0:T(8,128)(2,1)S(1)}, bf16[1792,256]{1,0:T(8,128)(2,1)}, u32[]{:S(2)}, u32[]{:S(2)}) collective-permute-start(bf16[1792,256]{1,0:T(8,128)(2,1)S(1)} %lend.1), channel_id=1, source_target_pairs={{0,16},{4,20},{8,24},{12,28},{16,32},{20,36},{24,40},{28,44},{32,4... | collective-permute-start | bytes 2752520 | tf_op jit(solution)/shard_map/ppermute | solution.py:719
  65.9 19.5 %all-to-all-start.1 = ((bf16[32,56,128]{2,1,0:T(8,128)(2,1)}), bf16[32,56,128]{2,1,0:T(8,128)(2,1)S(1)}, u32[]{:S(2)}, u32[]{:S(2)}) async-start(bf16[32,56,128]{2,1,0:T(8,128)(2,1)} %chain.1), calls=%async_computation.1 | async-start | bytes 917504 | tf_op jit(solution)/shard_map/all_to_all | solution.py:735
  81.9 1.3 copy-start.18
  83.9 37.7 %collective-permute-start.4 = (bf16[4,448,256]{2,1,0:T(8,128)(2,1)}, bf16[4,448,256]{2,1,0:T(8,128)(2,1)S(1)}, u32[]{:S(2)}, u32[]{:S(2)}) collective-permute-start(bf16[4,448,256]{2,1,0:T(8,128)(2,1)} %get-tuple-element.45), channel_id=1, source_target_pairs={{16,0},{20,4},{24,8},{28,12},{32,16},{36,20},{40,24},{44,28},{48,3... | collective-permute-start | bytes 2752520 | tf_op jit(solution)/shard_map/ppermute | solution.py:719
  85.4 1.2 copy-start.5
  86.6 1.2 copy-start.7
  87.8 1.2 copy-start.9
  103.9 25.7 %collective-permute-start.10 = (bf16[256,128]{1,0:T(8,128)(2,1)S(1)}, bf16[256,128]{1,0:T(8,128)(2,1)S(1)}, u32[]{:S(2)}, u32[]{:S(2)}) collective-permute-start(bf16[256,128]{1,0:T(8,128)(2,1)S(1)} %get-tuple-element.59.refs_0_), channel_id=1, source_target_pairs={{0,1},{1,2},{2,3},{3,0},{4,5},{5,6},{6,7},{7,4},{8,9},{9,10},{10,1... | collective-permute-start | bytes 196616 | tf_op jit(solution)/shard_map/ppermute | solution.py:725
  104.0 27.7 %collective-permute-start.11 = (bf16[256,128]{1,0:T(8,128)(2,1)S(1)}, bf16[256,128]{1,0:T(8,128)(2,1)S(1)}, u32[]{:S(2)}, u32[]{:S(2)}) collective-permute-start(bf16[256,128]{1,0:T(8,128)(2,1)S(1)} %get-tuple-element.59.refs_0_), channel_id=1, source_target_pairs={{0,2},{1,3},{2,0},{3,1},{4,6},{5,7},{6,4},{7,5},{8,10},{9,11},{10,... | collective-permute-start | bytes 196616 | tf_op jit(solution)/shard_map/ppermute | solution.py:725
  104.7 27.0 %collective-permute-start.12 = (bf16[256,128]{1,0:T(8,128)(2,1)S(1)}, bf16[256,128]{1,0:T(8,128)(2,1)S(1)}, u32[]{:S(2)}, u32[]{:S(2)}) collective-permute-start(bf16[256,128]{1,0:T(8,128)(2,1)S(1)} %get-tuple-element.59.refs_0_), channel_id=1, source_target_pairs={{0,3},{1,0},{2,1},{3,2},{4,7},{5,4},{6,5},{7,6},{8,11},{9,8},{10,9... | collective-permute-start | bytes 196616 | tf_op jit(solution)/shard_map/ppermute | solution.py:725
  106.1 20.8 %collective-permute-start.9 = (f32[8,1792]{1,0:T(8,128)S(1)}, f32[8,1792]{1,0:T(8,128)S(1)}, u32[]{:S(2)}, u32[]{:S(2)}) collective-permute-start(f32[8,1792]{1,0:T(8,128)S(1)} %get-tuple-element.55), channel_id=1, source_target_pairs={{4,0},{8,4},{12,8},{16,12},{20,16},{24,20},{28,24},{32,28},{36,32}... | collective-permute-start | bytes 172040 | tf_op jit(solution)/shard_map/ppermute | solution.py:719
  107.4 27.5 %all-to-all-start.2 = ((bf16[32,64,128]{2,1,0:T(8,128)(2,1)}), bf16[32,64,128]{2,1,0:T(8,128)(2,1)S(1)}, u32[]{:S(2)}, u32[]{:S(2)}) async-start(bf16[32,64,128]{2,1,0:T(8,128)(2,1)} %get-tuple-element.58), calls=%async_computation.2 | async-start | bytes 1048576 | tf_op jit(solution)/shard_map/all_to_all | solution.py:735
  121.7 1.5 %copy-start.19 = (f32[4,448,256]{2,1,0:T(8,128)S(1)}, f32[4,448,256]{2,1,0:T(8,128)}, u32[]{:S(2)}) copy-start(f32[4,448,256]{2,1,0:T(8,128)} %copy-done.18) | copy-start | bytes 5505028
  125.1 13.4 %collective-permute-start.5 = (bf16[672,256]{1,0:T(8,128)(2,1)S(1)}, bf16[672,256]{1,0:T(8,128)(2,1)S(1)}, u32[]{:S(2)}, u32[]{:S(2)}) collective-permute-start(bf16[672,256]{1,0:T(8,128)(2,1)S(1)} %get-tuple-element.47), channel_id=1, source_target_pairs={{0,4},{4,8},{8,12},{12,0},{1,5},{5,9},{9,13},{13,1},{2,6},{6,10},{... | collective-permute-start | bytes 1032200 | tf_op jit(solution)/shard_map/ppermute | solution.py:725
  126.9 18.2 %collective-permute-start.6 = (bf16[672,256]{1,0:T(8,128)(2,1)S(1)}, bf16[672,256]{1,0:T(8,128)(2,1)S(1)}, u32[]{:S(2)}, u32[]{:S(2)}) collective-permute-start(bf16[672,256]{1,0:T(8,128)(2,1)S(1)} %get-tuple-element.48), channel_id=1, source_target_pairs={{0,8},{4,12},{8,0},{12,4},{1,9},{5,13},{9,1},{13,5},{2,10},{6,14},... | collective-permute-start | bytes 1032200 | tf_op jit(solution)/shard_map/ppermute | solution.py:725
  129.6 15.6 %collective-permute-start.7 = (bf16[672,256]{1,0:T(8,128)(2,1)S(1)}, bf16[672,256]{1,0:T(8,128)(2,1)S(1)}, u32[]{:S(2)}, u32[]{:S(2)}) collective-permute-start(bf16[672,256]{1,0:T(8,128)(2,1)S(1)} %get-tuple-element.49), channel_id=1, source_target_pairs={{0,12},{4,0},{8,4},{12,8},{1,13},{5,1},{9,5},{13,9},{2,14},{6,2},{... | collective-permute-start | bytes 1032200 | tf_op jit(solution)/shard_map/ppermute | solution.py:725
  (7 other events, 6.6 us)

commit v7 on v6

--- a/solution.py
+++ b/solution.py
@@ -252,7 +252,6 @@
             pltpu.VMEM((T, 128), BF16),
         ],
         cost_estimate=pl.CostEstimate(flops=8 * 10**9, bytes_accessed=4 * 10**6, transcendentals=0),
-        compiler_params=GRANT,
         name="mixer_first",
     )(*arrays)
 
@@ -494,7 +493,6 @@
             half, half, half, half,
         ],
         cost_estimate=pl.CostEstimate(flops=18 * 10**9, bytes_accessed=8 * 10**6, transcendentals=0),
-        compiler_params=GRANT,
         name="mixer_second",
     )(*arrays)
 
@@ -558,7 +556,6 @@
         out_specs=[IN_VMEM] * ROW,
         out_shape=[pltpu.VMEM((4 * HEAD_DIM, T), BF16)] * ROW,
         scratch_shapes=[pltpu.VMEM((LOCAL_HEADS, 4 * HEAD_DIM, T), BF16)],
-        compiler_params=GRANT,
         name="pack",
     )(keys, values, queries, grads)
 
@@ -649,9 +646,9 @@
         in_specs=[IN_VMEM] * (2 + ROW),
         out_specs=[IN_VMEM] * 3,
         out_shape=[
-            pltpu.VMEM((ROW, HEAD_DIM, T), BF16),
-            pltpu.VMEM(pairs, F32),
-            pltpu.VMEM(pairs, BF16),
+            jax.ShapeDtypeStruct((ROW, HEAD_DIM, T), BF16),
+            jax.ShapeDtypeStruct(pairs, F32),
+            jax.ShapeDtypeStruct(pairs, BF16),
         ],
         scratch_shapes=[
             pltpu.VMEM(pairs, F32),
@@ -659,7 +656,6 @@
             pltpu.VMEM((2 * ROW, *PAIR), BF16),
         ],
         cost_estimate=pl.CostEstimate(flops=12 * 10**9, bytes_accessed=8 * 10**6, transcendentals=0),
-        compiler_params=GRANT,
         name="attention",
     )(docs, far, *own)
 

time: 148 us -> 142 us (0.959)
  local copies, waits for them, and re-layouts: 13.9 us -> 4.89 us
  Pallas kernels: 34.1 us -> 39.5 us
  starting transfers between devices: 47 us -> 44.6 us
    unnamed x48 -> x22, local copies, waits for them, and re-layouts: 13.9 us -> 4.14 us
    pallas_call x1, Pallas kernels: 6.4 us -> 9.02 us  [mixer_first(): pl.pallas_call(mixer_first_kernel, grid=(STEPS,), in_specs=mixer_specs(he...]
    all_to_all x2, starting transfers between devices: 21.9 us -> 20.2 us  [exchange(): return lax.all_to_all(array, axis, split_axis=0, concat_axis=0, tiled=True)]
    all_to_all x2, waiting for transfers between devices: 3.18 us -> 4.83 us  [exchange(): return lax.all_to_all(array, axis, split_axis=0, concat_axis=0, tiled=True)]
  transfers between devices with their start and end apart: 15 -> 15, of which waited for: 5 -> 6; matrix products, arithmetic and copies ran while one was open for 0% -> 1% of each run, Pallas kernels for 22% -> 26%
where the time goes in v7:
time: 142 us; the launch traced here: 141 us
  starting transfers between devices  44.6 us (31%)
  Pallas kernels  39.5 us (28%)
  waiting for transfers between devices  29.6 us (21%)
  blocking collectives  20.7 us (15%)
  local copies, waits for them, and re-layouts  4.89 us (3%)
    ppermute x9, waiting for transfers between devices, turns(): lax.ppermute(part, axis, [(n, (n + turn) % count) for n in range(count)])  24.7 us
    all_to_all x1, blocking collectives, exchange(): return lax.all_to_all(array, axis, split_axis=0, concat_axis=0, tiled=True)  20.7 us
    all_to_all x2, starting transfers between devices, exchange(): return lax.all_to_all(array, axis, split_axis=0, concat_axis=0, tiled=True)  20.2 us
    pallas_call x1, Pallas kernels, mixer_second(): pl.pallas_call(mixer_second_kernel, grid=(STEPS,), in_specs=mixer_specs(h...  16.2 us
    ppermute x9, starting transfers between devices, turns(): lax.ppermute(part, axis, [(n, (n + turn) % count) for n in range(count)])  14 us
    ppermute x4, starting transfers between devices, passed_along(): lax.ppermute(value, axis, [(source, source + steps) for source in range(i...  10.3 us
    pallas_call x1, Pallas kernels, mixer_first(): pl.pallas_call(mixer_first_kernel, grid=(STEPS,), in_specs=mixer_specs(he...  9.02 us
    pallas_call x1, Pallas kernels, attention(): pl.pallas_call(attention_kernel, in_specs=[IN_VMEM] * (2 + ROW), out_spec...  8.44 us
  transfers between devices with their start and end apart: 15, of which 6 were waited for; matrix products, arithmetic and copies ran while one was open for 1% of the time, Pallas kernels for 26%

profile of v7, /device:TPU:0, one launch (start us, length us, event | category | flops | bytes accessed | tf_op | source)
XLA Modules:
  0.0 140.7 jit_solution(17375548733462606022)
XLA Ops:
  0.6 2.1 %pack.1 = (bf16[896,256]{1,0:T(8,128)(2,1)S(1)}, bf16[896,256]{1,0:T(8,128)(2,1)S(1)}, bf16[896,256]{1,0:T(8,128)(2,1)S(1)}, bf16[896,256]{1,0:T(8,128)(2,1)S(1)}) custom-call(bf16[256,896]{1,0:T(8,128)(2,1)} %k_ref.1, bf16[256,896]{1,0:T(8,128)(2,1)} %v_ref.1, bf16[256,896]{1,0:T(8,128)(2,1)} %q_ref.1, bf16[256,896]{1,0:T(8,128)(2,1)} %g_ref.1), custom_call_target="tpu_custom_call" | custom-call | tf_op jit(solution)/shard_map/pack/pallas_call | solution.py:553
  2.8 1.7 %collective-permute-start = (bf16[896,256]{1,0:T(8,128)(2,1)S(1)}, bf16[896,256]{1,0:T(8,128)(2,1)S(1)}, u32[]{:S(2)}, u32[]{:S(2)}) collective-permute-start(bf16[896,256]{1,0:T(8,128)(2,1)S(1)} %get-tuple-element.40), channel_id=1, source_target_pairs={{0,4},{4,8},{8,12},{12,0},{1,5},{5,9},{9,13},{13,1},{2,6},{6,10},{... | collective-permute-start | bytes 1376264 | tf_op jit(solution)/shard_map/ppermute | solution.py:721
  4.4 2.7 %collective-permute-start.1 = (bf16[896,256]{1,0:T(8,128)(2,1)S(1)}, bf16[896,256]{1,0:T(8,128)(2,1)S(1)}, u32[]{:S(2)}, u32[]{:S(2)}) collective-permute-start(bf16[896,256]{1,0:T(8,128)(2,1)S(1)} %get-tuple-element.41), channel_id=1, source_target_pairs={{0,8},{4,12},{8,0},{12,4},{1,9},{5,13},{9,1},{13,5},{2,10},{6,14},... | collective-permute-start | bytes 1376264 | tf_op jit(solution)/shard_map/ppermute | solution.py:721
  7.2 1.4 %collective-permute-start.2 = (bf16[896,256]{1,0:T(8,128)(2,1)S(1)}, bf16[896,256]{1,0:T(8,128)(2,1)S(1)}, u32[]{:S(2)}, u32[]{:S(2)}) collective-permute-start(bf16[896,256]{1,0:T(8,128)(2,1)S(1)} %get-tuple-element.42), channel_id=1, source_target_pairs={{0,12},{4,0},{8,4},{12,8},{1,13},{5,1},{9,5},{13,9},{2,14},{6,2},{... | collective-permute-start | bytes 1376264 | tf_op jit(solution)/shard_map/ppermute | solution.py:721
  8.6 0.8 slice.3
  9.3 2.5 %collective-permute-start.8 = (bf16[8,1792]{1,0:T(8,128)(2,1)S(1)}, bf16[8,1792]{1,0:T(8,128)(2,1)S(1)}, u32[]{:S(2)}, u32[]{:S(2)}) collective-permute-start(bf16[8,1792]{1,0:T(8,128)(2,1)S(1)} %slice.3), channel_id=1, source_target_pairs={{0,4},{4,8},{8,12},{12,16},{16,20},{20,24},{24,28},{28,32},{32,36}... | collective-permute-start | bytes 86024 | tf_op jit(solution)/shard_map/ppermute | solution.py:715
  11.8 4.4 %collective-permute-done.refs_1_ = bf16[896,256]{1,0:T(8,128)(2,1)S(1)} collective-permute-done((bf16[896,256]{1,0:T(8,128)(2,1)S(1)}, bf16[896,256]{1,0:T(8,128)(2,1)S(1)}, u32[]{:S(2)}, u32[]{:S(2)}) %collective-permute-start) | collective-permute-done | bytes 458784 | tf_op jit(solution)/shard_map/ppermute | solution.py:721
  16.2 11.4 %collective-permute-done.1.refs_2_ = bf16[896,256]{1,0:T(8,128)(2,1)S(1)} collective-permute-done((bf16[896,256]{1,0:T(8,128)(2,1)S(1)}, bf16[896,256]{1,0:T(8,128)(2,1)S(1)}, u32[]{:S(2)}, u32[]{:S(2)}) %collective-permute-start.1) | collective-permute-done | bytes 458784 | tf_op jit(solution)/shard_map/ppermute | solution.py:721
  27.6 5.1 %collective-permute-start.3 = (bf16[1792,256]{1,0:T(8,128)(2,1)S(1)}, bf16[1792,256]{1,0:T(8,128)(2,1)S(1)}, u32[]{:S(2)}, u32[]{:S(2)}) collective-permute-start(bf16[1792,256]{1,0:T(8,128)(2,1)S(1)} %lend.1), channel_id=1, source_target_pairs={{0,16},{4,20},{8,24},{12,28},{16,32},{20,36},{24,40},{28,44},{32,4... | collective-permute-start | bytes 2752520 | tf_op jit(solution)/shard_map/ppermute | solution.py:715
  33.4 9.0 %mixer_first.1 = bf16[2048,128]{1,0:T(8,128)(2,1)} custom-call(bf16[256,1792]{1,0:T(8,128)(2,1)} %x_ref.3, bf16[8,1792]{1,0:T(8,128)(2,1)} %copy-done.10, f32[4,1792]{1,0:T(4,128)} %weight_ref.3, bf16[256,1792]{1,0:T(8,128)(2,1)} %gate_ref.3, bf16[256,1792]{1,0:T(8,128)(2,1)} %grad_ref.3, f32[28,256]{1,0:T(8,128)} %bitcast.15, f32[1,28]{1,0:T(1,128)} %bitcast.17, ...), custom_call_target="tpu_custom_call" | custom-call | flops 8000000000 | bytes 4000000 | tf_op jit(solution)/shard_map/mixer_first/pallas_call | solution.py:243
  42.4 20.7 %all_to_all.15.parts_ref = bf16[32,64,128]{2,1,0:T(8,128)(2,1)S(1)} all-to-all(bf16[32,64,128]{2,1,0:T(8,128)(2,1)} %bitcast.11), channel_id=1, replica_groups=mesh['seq_0'=4,'seq_1'=2,'seq_2'=4,'head'=4] {'seq_0','seq_1','seq_2'}, dimensions={0} | all-to-all | bytes 1048576 | tf_op jit(solution)/shard_map/all_to_all | solution.py:731
  63.1 1.3 chain.1
  64.4 6.5 %all-to-all-start.1 = ((bf16[32,56,128]{2,1,0:T(8,128)(2,1)}), bf16[32,56,128]{2,1,0:T(8,128)(2,1)}, u32[]{:S(2)}, u32[]{:S(2)}) async-start(bf16[32,56,128]{2,1,0:T(8,128)(2,1)} %chain.1), calls=%async_computation.1 | async-start | bytes 917504 | tf_op jit(solution)/shard_map/all_to_all | solution.py:731
  70.9 1.0 copy-done.1
  71.9 8.4 %attention.1 = (bf16[4,224,256]{2,1,0:T(8,128)(2,1)}, f32[4,448,256]{2,1,0:T(8,128)}, bf16[4,448,256]{2,1,0:T(8,128)(2,1)}) custom-call(s32[64,128]{1,0:T(8,128)} %bitcast.13, bf16[1792,256]{1,0:T(8,128)(2,1)S(1)} %collective-permute-done.3.far_ref, bf16[896,256]{1,0:T(8,128)(2,1)S(1)} %get-tuple-element.39.refs_0_, bf16[896,256]{1,0:T(8,128)(2,1)S(1)} %copy-done.1, ...), custom_call_target="tpu_custom_call" | custom-call | flops 12000000000 | bytes 8000000 | tf_op jit(solution)/shard_map/attention/pallas_call | solution.py:644
  80.4 1.5 %collective-permute-start.4 = (bf16[4,448,256]{2,1,0:T(8,128)(2,1)}, bf16[4,448,256]{2,1,0:T(8,128)(2,1)S(1)}, u32[]{:S(2)}, u32[]{:S(2)}) collective-permute-start(bf16[4,448,256]{2,1,0:T(8,128)(2,1)} %get-tuple-element.45), channel_id=1, source_target_pairs={{16,0},{20,4},{24,8},{28,12},{32,16},{36,20},{40,24},{44,28},{48,3... | collective-permute-start | bytes 2752520 | tf_op jit(solution)/shard_map/ppermute | solution.py:715
  82.4 16.2 %mixer_second.1 = (bf16[256,1792]{1,0:T(8,128)(2,1)}, f32[8,1792]{1,0:T(8,128)}, f32[8,1792]{1,0:T(8,128)}, bf16[256,1792]{1,0:T(8,128)(2,1)}, f32[28,256]{1,0:T...) custom-call(bf16[256,1792]{1,0:T(8,128)(2,1)} %x_ref.3, bf16[8,1792]{1,0:T(8,128)(2,1)} %copy-done.10, ...), custom_call_target="tpu_custom_call" | custom-call | flops 17999998976 | bytes 8000000 | tf_op jit(solution)/shard_map/mixer_second/pallas_call | solution.py:465
  98.7 0.8 collective-permute-start.11
  99.5 1.4 collective-permute-start.12
  100.9 1.3 collective-permute-start.9
  102.2 13.7 %all-to-all-start.2 = ((bf16[32,64,128]{2,1,0:T(8,128)(2,1)}), bf16[32,64,128]{2,1,0:T(8,128)(2,1)S(1)}, u32[]{:S(2)}, u32[]{:S(2)}) async-start(bf16[32,64,128]{2,1,0:T(8,128)(2,1)} %get-tuple-element.58), calls=%async_computation.2 | async-start | bytes 1048576 | tf_op jit(solution)/shard_map/all_to_all | solution.py:731
  115.9 1.5 %copy-done.7 = f32[4,448,256]{2,1,0:T(8,128)S(1)} copy-done((f32[4,448,256]{2,1,0:T(8,128)S(1)}, f32[4,448,256]{2,1,0:T(8,128)}, u32[]{:S(2)}) %copy-start.7) | copy-done | bytes 1835032
  117.4 1.0 copy-done.8
  118.6 1.9 %collective-permute-start.5 = (bf16[672,256]{1,0:T(8,128)(2,1)S(1)}, bf16[672,256]{1,0:T(8,128)(2,1)S(1)}, u32[]{:S(2)}, u32[]{:S(2)}) collective-permute-start(bf16[672,256]{1,0:T(8,128)(2,1)S(1)} %get-tuple-element.47), channel_id=1, source_target_pairs={{0,4},{4,8},{8,12},{12,0},{1,5},{5,9},{9,13},{13,1},{2,6},{6,10},{... | collective-permute-start | bytes 1032200 | tf_op jit(solution)/shard_map/ppermute | solution.py:721
  120.5 2.7 %collective-permute-start.6 = (bf16[672,256]{1,0:T(8,128)(2,1)S(1)}, bf16[672,256]{1,0:T(8,128)(2,1)S(1)}, u32[]{:S(2)}, u32[]{:S(2)}) collective-permute-start(bf16[672,256]{1,0:T(8,128)(2,1)S(1)} %get-tuple-element.48), channel_id=1, source_target_pairs={{0,8},{4,12},{8,0},{12,4},{1,9},{5,13},{9,1},{13,5},{2,10},{6,14},... | collective-permute-start | bytes 1032200 | tf_op jit(solution)/shard_map/ppermute | solution.py:721
  123.1 1.5 %collective-permute-start.7 = (bf16[672,256]{1,0:T(8,128)(2,1)S(1)}, bf16[672,256]{1,0:T(8,128)(2,1)S(1)}, u32[]{:S(2)}, u32[]{:S(2)}) collective-permute-start(bf16[672,256]{1,0:T(8,128)(2,1)S(1)} %get-tuple-element.49), channel_id=1, source_target_pairs={{0,12},{4,0},{8,4},{12,8},{1,13},{5,1},{9,5},{13,9},{2,14},{6,2},{... | collective-permute-start | bytes 1032200 | tf_op jit(solution)/shard_map/ppermute | solution.py:721
  124.6 0.6 fusion
  125.2 4.3 %all-to-all-done.2.bundle_ref = bf16[32,64,128]{2,1,0:T(8,128)(2,1)S(1)} async-done(((bf16[32,64,128]{2,1,0:T(8,128)(2,1)}), bf16[32,64,128]{2,1,0:T(8,128)(2,1)S(1)}, u32[]{:S(2)}, u32[]{:S(2)}) %all-to-all-start.2) | async-done | bytes 524320 | tf_op jit(solution)/shard_map/all_to_all | solution.py:731
  129.5 0.9 finish.1
  130.4 2.8 %collective-permute-done.5.refs_1_ = bf16[672,256]{1,0:T(8,128)(2,1)S(1)} collective-permute-done((bf16[672,256]{1,0:T(8,128)(2,1)S(1)}, bf16[672,256]{1,0:T(8,128)(2,1)S(1)}, u32[]{:S(2)}, u32[]{:S(2)}) %collective-permute-start.5) | collective-permute-done | bytes 344096 | tf_op jit(solution)/shard_map/ppermute | solution.py:721
  133.2 6.2 %collective-permute-done.6.refs_2_ = bf16[672,256]{1,0:T(8,128)(2,1)S(1)} collective-permute-done((bf16[672,256]{1,0:T(8,128)(2,1)S(1)}, bf16[672,256]{1,0:T(8,128)(2,1)S(1)}, u32[]{:S(2)}, u32[]{:S(2)}) %collective-permute-start.6) | collective-permute-done | bytes 344096 | tf_op jit(solution)/shard_map/ppermute | solution.py:721
  139.4 1.4 unpack.1
  (32 shorter events, 1.5 us)
Async XLA Ops:
  2.8 13.5 %collective-permute-start = (bf16[896,256]{1,0:T(8,128)(2,1)S(1)}, bf16[896,256]{1,0:T(8,128)(2,1)S(1)}, u32[]{:S(2)}, u32[]{:S(2)}) collective-permute-start(bf16[896,256]{1,0:T(8,128)(2,1)S(1)} %get-tuple-element.40), channel_id=1, source_target_pairs={{0,4},{4,8},{8,12},{12,0},{1,5},{5,9},{9,13},{13,1},{2,6},{6,10},{... | collective-permute-start | bytes 1376264 | tf_op jit(solution)/shard_map/ppermute | solution.py:721
  4.4 23.1 %collective-permute-start.1 = (bf16[896,256]{1,0:T(8,128)(2,1)S(1)}, bf16[896,256]{1,0:T(8,128)(2,1)S(1)}, u32[]{:S(2)}, u32[]{:S(2)}) collective-permute-start(bf16[896,256]{1,0:T(8,128)(2,1)S(1)} %get-tuple-element.41), channel_id=1, source_target_pairs={{0,8},{4,12},{8,0},{12,4},{1,9},{5,13},{9,1},{13,5},{2,10},{6,14},... | collective-permute-start | bytes 1376264 | tf_op jit(solution)/shard_map/ppermute | solution.py:721
  7.2 20.4 %collective-permute-start.2 = (bf16[896,256]{1,0:T(8,128)(2,1)S(1)}, bf16[896,256]{1,0:T(8,128)(2,1)S(1)}, u32[]{:S(2)}, u32[]{:S(2)}) collective-permute-start(bf16[896,256]{1,0:T(8,128)(2,1)S(1)} %get-tuple-element.42), channel_id=1, source_target_pairs={{0,12},{4,0},{8,4},{12,8},{1,13},{5,1},{9,5},{13,9},{2,14},{6,2},{... | collective-permute-start | bytes 1376264 | tf_op jit(solution)/shard_map/ppermute | solution.py:721
  9.3 23.4 %collective-permute-start.8 = (bf16[8,1792]{1,0:T(8,128)(2,1)S(1)}, bf16[8,1792]{1,0:T(8,128)(2,1)S(1)}, u32[]{:S(2)}, u32[]{:S(2)}) collective-permute-start(bf16[8,1792]{1,0:T(8,128)(2,1)S(1)} %slice.3), channel_id=1, source_target_pairs={{0,4},{4,8},{8,12},{12,16},{16,20},{20,24},{24,28},{28,32},{32,36}... | collective-permute-start | bytes 86024 | tf_op jit(solution)/shard_map/ppermute | solution.py:715
  16.2 16.6 %copy-start = (bf16[896,256]{1,0:T(8,128)(2,1)}, bf16[896,256]{1,0:T(8,128)(2,1)S(1)}, u32[]{:S(2)}) copy-start(bf16[896,256]{1,0:T(8,128)(2,1)S(1)} %collective-permute-done.refs_1_) | copy-start | bytes 1376260
  27.6 5.2 %copy-start.2 = (bf16[896,256]{1,0:T(8,128)(2,1)}, bf16[896,256]{1,0:T(8,128)(2,1)S(1)}, u32[]{:S(2)}) copy-start(bf16[896,256]{1,0:T(8,128)(2,1)S(1)} %collective-permute-done.1.refs_2_) | copy-start | bytes 1376260
  27.6 5.2 %copy-start.4 = (bf16[896,256]{1,0:T(8,128)(2,1)}, bf16[896,256]{1,0:T(8,128)(2,1)S(1)}, u32[]{:S(2)}) copy-start(bf16[896,256]{1,0:T(8,128)(2,1)S(1)} %collective-permute-done.2.refs_3_) | copy-start | bytes 1376260
  27.6 43.3 %collective-permute-start.3 = (bf16[1792,256]{1,0:T(8,128)(2,1)S(1)}, bf16[1792,256]{1,0:T(8,128)(2,1)S(1)}, u32[]{:S(2)}, u32[]{:S(2)}) collective-permute-start(bf16[1792,256]{1,0:T(8,128)(2,1)S(1)} %lend.1), channel_id=1, source_target_pairs={{0,16},{4,20},{8,24},{12,28},{16,32},{20,36},{24,40},{28,44},{32,4... | collective-permute-start | bytes 2752520 | tf_op jit(solution)/shard_map/ppermute | solution.py:715
  32.8 0.6 copy-start.10
  63.1 7.8 %copy-start.3 = (bf16[896,256]{1,0:T(8,128)(2,1)S(1)}, bf16[896,256]{1,0:T(8,128)(2,1)}, u32[]{:S(2)}) copy-start(bf16[896,256]{1,0:T(8,128)(2,1)} %copy-done.2) | copy-start | bytes 1376260
  63.1 7.8 %copy-start.5 = (bf16[896,256]{1,0:T(8,128)(2,1)S(1)}, bf16[896,256]{1,0:T(8,128)(2,1)}, u32[]{:S(2)}) copy-start(bf16[896,256]{1,0:T(8,128)(2,1)} %copy-done.4) | copy-start | bytes 1376260
  64.4 18.0 %all-to-all-start.1 = ((bf16[32,56,128]{2,1,0:T(8,128)(2,1)}), bf16[32,56,128]{2,1,0:T(8,128)(2,1)}, u32[]{:S(2)}, u32[]{:S(2)}) async-start(bf16[32,56,128]{2,1,0:T(8,128)(2,1)} %chain.1), calls=%async_computation.1 | async-start | bytes 917504 | tf_op jit(solution)/shard_map/all_to_all | solution.py:731
  70.9 1.0 copy-start.1
  80.4 35.5 %collective-permute-start.4 = (bf16[4,448,256]{2,1,0:T(8,128)(2,1)}, bf16[4,448,256]{2,1,0:T(8,128)(2,1)S(1)}, u32[]{:S(2)}, u32[]{:S(2)}) collective-permute-start(bf16[4,448,256]{2,1,0:T(8,128)(2,1)} %get-tuple-element.45), channel_id=1, source_target_pairs={{16,0},{20,4},{24,8},{28,12},{32,16},{36,20},{40,24},{44,28},{48,3... | collective-permute-start | bytes 2752520 | tf_op jit(solution)/shard_map/ppermute | solution.py:715
  98.6 24.5 %collective-permute-start.10 = (bf16[256,128]{1,0:T(8,128)(2,1)}, bf16[256,128]{1,0:T(8,128)(2,1)S(1)}, u32[]{:S(2)}, u32[]{:S(2)}) collective-permute-start(bf16[256,128]{1,0:T(8,128)(2,1)} %get-tuple-element.59.refs_0_), channel_id=1, source_target_pairs={{0,1},{1,2},{2,3},{3,0},{4,5},{5,6},{6,7},{7,4},{8,9},{9,10},{10,1... | collective-permute-start | bytes 196616 | tf_op jit(solution)/shard_map/ppermute | solution.py:721
  98.7 26.5 %collective-permute-start.11 = (bf16[256,128]{1,0:T(8,128)(2,1)}, bf16[256,128]{1,0:T(8,128)(2,1)S(1)}, u32[]{:S(2)}, u32[]{:S(2)}) collective-permute-start(bf16[256,128]{1,0:T(8,128)(2,1)} %get-tuple-element.59.refs_0_), channel_id=1, source_target_pairs={{0,2},{1,3},{2,0},{3,1},{4,6},{5,7},{6,4},{7,5},{8,10},{9,11},{10,... | collective-permute-start | bytes 196616 | tf_op jit(solution)/shard_map/ppermute | solution.py:721
  99.5 25.7 %collective-permute-start.12 = (bf16[256,128]{1,0:T(8,128)(2,1)}, bf16[256,128]{1,0:T(8,128)(2,1)S(1)}, u32[]{:S(2)}, u32[]{:S(2)}) collective-permute-start(bf16[256,128]{1,0:T(8,128)(2,1)} %get-tuple-element.59.refs_0_), channel_id=1, source_target_pairs={{0,3},{1,0},{2,1},{3,2},{4,7},{5,4},{6,5},{7,6},{8,11},{9,8},{10,9... | collective-permute-start | bytes 196616 | tf_op jit(solution)/shard_map/ppermute | solution.py:721
  100.9 19.6 %collective-permute-start.9 = (f32[8,1792]{1,0:T(8,128)}, f32[8,1792]{1,0:T(8,128)S(1)}, u32[]{:S(2)}, u32[]{:S(2)}) collective-permute-start(f32[8,1792]{1,0:T(8,128)} %get-tuple-element.55), channel_id=1, source_target_pairs={{4,0},{8,4},{12,8},{16,12},{20,16},{24,20},{28,24},{32,28},{36,32}... | collective-permute-start | bytes 172040 | tf_op jit(solution)/shard_map/ppermute | solution.py:715
  102.2 27.3 %all-to-all-start.2 = ((bf16[32,64,128]{2,1,0:T(8,128)(2,1)}), bf16[32,64,128]{2,1,0:T(8,128)(2,1)S(1)}, u32[]{:S(2)}, u32[]{:S(2)}) async-start(bf16[32,64,128]{2,1,0:T(8,128)(2,1)} %get-tuple-element.58), calls=%async_computation.2 | async-start | bytes 1048576 | tf_op jit(solution)/shard_map/all_to_all | solution.py:731
  115.9 1.5 %copy-start.7 = (f32[4,448,256]{2,1,0:T(8,128)S(1)}, f32[4,448,256]{2,1,0:T(8,128)}, u32[]{:S(2)}) copy-start(f32[4,448,256]{2,1,0:T(8,128)} %get-tuple-element.44.dkv_ref) | copy-start | bytes 5505028
  117.4 1.0 copy-start.8
  118.4 6.2 %copy-start.9 = (f32[8,1792]{1,0:T(8,128)S(1)}, f32[8,1792]{1,0:T(8,128)}, u32[]{:S(2)}) copy-start(f32[8,1792]{1,0:T(8,128)} %get-tuple-element.54) | copy-start | bytes 172036
  118.4 11.1 %copy-start.6 = (bf16[256,128]{1,0:T(8,128)(2,1)S(1)}, bf16[256,128]{1,0:T(8,128)(2,1)}, u32[]{:S(2)}) copy-start(bf16[256,128]{1,0:T(8,128)(2,1)} %get-tuple-element.59.refs_0_) | copy-start | bytes 196612
  118.6 14.6 %collective-permute-start.5 = (bf16[672,256]{1,0:T(8,128)(2,1)S(1)}, bf16[672,256]{1,0:T(8,128)(2,1)S(1)}, u32[]{:S(2)}, u32[]{:S(2)}) collective-permute-start(bf16[672,256]{1,0:T(8,128)(2,1)S(1)} %get-tuple-element.47), channel_id=1, source_target_pairs={{0,4},{4,8},{8,12},{12,0},{1,5},{5,9},{9,13},{13,1},{2,6},{6,10},{... | collective-permute-start | bytes 1032200 | tf_op jit(solution)/shard_map/ppermute | solution.py:721
  120.5 18.9 %collective-permute-start.6 = (bf16[672,256]{1,0:T(8,128)(2,1)S(1)}, bf16[672,256]{1,0:T(8,128)(2,1)S(1)}, u32[]{:S(2)}, u32[]{:S(2)}) collective-permute-start(bf16[672,256]{1,0:T(8,128)(2,1)S(1)} %get-tuple-element.48), channel_id=1, source_target_pairs={{0,8},{4,12},{8,0},{12,4},{1,9},{5,13},{9,1},{13,5},{2,10},{6,14},... | collective-permute-start | bytes 1032200 | tf_op jit(solution)/shard_map/ppermute | solution.py:721
  123.1 16.2 %collective-permute-start.7 = (bf16[672,256]{1,0:T(8,128)(2,1)S(1)}, bf16[672,256]{1,0:T(8,128)(2,1)S(1)}, u32[]{:S(2)}, u32[]{:S(2)}) collective-permute-start(bf16[672,256]{1,0:T(8,128)(2,1)S(1)} %get-tuple-element.49), channel_id=1, source_target_pairs={{0,12},{4,0},{8,4},{12,8},{1,13},{5,1},{9,5},{13,9},{2,14},{6,2},{... | collective-permute-start | bytes 1032200 | tf_op jit(solution)/shard_map/ppermute | solution.py:721

commit v8 on v5

--- a/solution.py
+++ b/solution.py
@@ -68,8 +68,8 @@
     return pl.BlockSpec((rows, BLK), lambda c: (0, c))
 
 
-IN_SMEM = pl.BlockSpec(memory_space=pltpu.SMEM)
 IN_VMEM = pl.BlockSpec(memory_space=pltpu.VMEM)
+GRANT = pltpu.CompilerParams(vmem_limit_bytes=32 * 2**20)
 
 
 def seq_index():
@@ -292,16 +292,14 @@
 LANES_BLK = BLK // 128
 
 
-def mixer_second_kernel(
+def mixer_inner_kernel(
     x_ref, halo_ref, weight_ref, gate_ref, grad_ref, step_ref, bias_ref, rate_ref,
-    skip_ref, docs_ref, in_ref, out_ref, state_ref,
-    dx_ref, tail_ref, spill_ref, dgate_ref, dstep_ref, coeff_ref, bundle_ref,
+    skip_ref, docs_ref, in_ref, out_ref,
+    inner_ref, dscaled_ref, dtop_ref, dbottom_ref,
     cum_s, step_s, mask_s, prev_s, end_s, params_s,
-    cumt_s, pair_s, causal_s, dtop_s, dbottom_s, coeff_s, row_s, dt_s, ends_s, bundle_s,
-    in_low_s, in_high_s, out_low_s, out_high_s,
+    cumt_s, pair_s, causal_s, dtop_s, dbottom_s,
 ):
     step_id = pl.program_id(0)
-    lane = iota((T, 128), 1)
 
     @pl.when(step_id == 0)
     def _():
@@ -312,31 +310,17 @@
         cumt_s[...] = jnp.transpose(cum)
         same = (own == own_row) & (iota((T, T), 0) >= iota((T, T), 1))
         causal_s[...] = jnp.where(same, 0.0, NEG)
-        in_low_s[...], in_high_s[...] = group_halves(in_ref)
-        out_low_s[...], out_high_s[...] = group_halves(out_ref)
-        pair_s[...] = dot(out_low_s[...], in_low_s[...], NT)
+        pair_s[...] = dot(group_halves(out_ref)[0], group_halves(in_ref)[0], NT)
         dtop_s[...] = jnp.zeros((HALF, HALF), F32)
         dbottom_s[...] = jnp.zeros((HALF, T), F32)
-        coeff_s[...] = jnp.zeros((T, 128), F32)
-        row_s[...] = jnp.zeros((T, 128), F32)
-        dt_s[...] = jnp.zeros((T, 128), F32)
-        ends_s[...] = jnp.zeros((8, 128), F32)
-
-    out_low = out_low_s[...]
-    in_high = in_high_s[...]
-    spread, cum, step, enter, to_end = block_gains(step_id, cum_s, step_s, prev_s, end_s)
-    skip = sum(dot(part, spread) for part in split(params_s[...], 3))[2:3]
-    weight = weight_ref[...]
-    pre, shifted = conv_pre(x_ref[...], halo_ref[...], weight, mask_s)
-    sig = sigmoid(pre)
-    act = pre * sig
+
+    spread = spread_of(step_id)
+    cum = dot(cum_s[0], spread) + dot(cum_s[1], spread) + dot(cum_s[2], spread)
+    step = dot(step_s[0], spread) + dot(step_s[1], spread)
+    pre, _ = conv_pre(x_ref[...], halo_ref[...], weight_ref[...], mask_s)
     gate = gate_ref[...].astype(F32)
-    gate_sig = sigmoid(gate)
-    mix_grad = grad_ref[...].astype(F32)
-    out_grad = mix_grad * gate * gate_sig
-    scaled = act * step
-    scaled_half = scaled.astype(BF16)
-    grad_half = out_grad.astype(BF16)
+    scaled_half = (pre * sigmoid(pre) * step).astype(BF16)
+    grad_half = (grad_ref[...].astype(F32) * gate * sigmoid(gate)).astype(BF16)
 
     block_head = iota((T, BLK), 1) // 64
     tops, bottoms, scaled_parts, grad_parts = [], [], [], []
@@ -363,7 +347,7 @@
     dtop_s[...] = dtop
     dbottom_s[...] = dbottom
     join = jnp.concatenate
-    inner = join(
+    inner_ref[...] = join(
         [
             dot(join(tops, axis=1), join([v[:HALF] for v in scaled_parts], axis=0)),
             dot(join(bottoms, axis=1), join(scaled_parts, axis=0)),
@@ -372,8 +356,77 @@
     )
     upper_part = dot(join(tops, axis=0), join([v[:HALF] for v in grad_parts], axis=0), TN)
     dscaled = dot(join(bottoms, axis=0), join([v[HALF:] for v in grad_parts], axis=0), TN)
-    dscaled = join([dscaled[:HALF] + upper_part, dscaled[HALF:]], axis=0)
-
+    dscaled_ref[...] = join([dscaled[:HALF] + upper_part, dscaled[HALF:]], axis=0)
+    dtop_ref[...] = dtop
+    dbottom_ref[...] = dbottom
+
+
+def mixer_inner(*arrays):
+    heads = arrays[5].shape[0]
+    return pl.pallas_call(
+        mixer_inner_kernel,
+        grid=(STEPS,),
+        in_specs=mixer_specs(heads),
+        out_specs=[column_block(T), column_block(T), whole((HALF, HALF)), whole((HALF, T))],
+        out_shape=[
+            jax.ShapeDtypeStruct((T, COLS), F32),
+            jax.ShapeDtypeStruct((T, COLS), F32),
+            jax.ShapeDtypeStruct((HALF, HALF), F32),
+            jax.ShapeDtypeStruct((HALF, T), F32),
+        ],
+        scratch_shapes=TOKEN_SCRATCH + [
+            pltpu.VMEM((128, T), F32),
+            pltpu.VMEM((T, T), F32),
+            pltpu.VMEM((T, T), F32),
+            pltpu.VMEM((HALF, HALF), F32),
+            pltpu.VMEM((HALF, T), F32),
+        ],
+        cost_estimate=pl.CostEstimate(flops=10**10, bytes_accessed=6 * 10**6, transcendentals=0),
+        name="mixer_inner",
+    )(*arrays)
+
+
+def mixer_second_kernel(
+    x_ref, halo_ref, weight_ref, gate_ref, grad_ref, step_ref, bias_ref, rate_ref,
+    skip_ref, docs_ref, in_ref, out_ref, inner_ref, dscaled_ref, dtop_ref, dbottom_ref,
+    state_ref,
+    dx_ref, tail_ref, spill_ref, dgate_ref, dstep_ref, coeff_ref, bundle_ref,
+    cum_s, step_s, mask_s, prev_s, end_s, params_s,
+    coeff_s, row_s, dt_s, ends_s, bundle_s,
+    in_low_s, in_high_s, out_low_s, out_high_s,
+):
+    step_id = pl.program_id(0)
+    lane = iota((T, 128), 1)
+
+    @pl.when(step_id == 0)
+    def _():
+        params = padded_params(bias_ref, rate_ref, skip_ref, params_s)
+        token_setup(docs_ref, step_ref, params, cum_s, step_s, mask_s, prev_s, end_s)
+        in_low_s[...], in_high_s[...] = group_halves(in_ref)
+        out_low_s[...], out_high_s[...] = group_halves(out_ref)
+        coeff_s[...] = jnp.zeros((T, 128), F32)
+        row_s[...] = jnp.zeros((T, 128), F32)
+        dt_s[...] = jnp.zeros((T, 128), F32)
+        ends_s[...] = jnp.zeros((8, 128), F32)
+
+    out_low = out_low_s[...]
+    in_high = in_high_s[...]
+    spread, _, step, enter, to_end = block_gains(step_id, cum_s, step_s, prev_s, end_s)
+    skip = sum(dot(part, spread) for part in split(params_s[...], 3))[2:3]
+    weight = weight_ref[...]
+    pre, shifted = conv_pre(x_ref[...], halo_ref[...], weight, mask_s)
+    sig = sigmoid(pre)
+    act = pre * sig
+    gate = gate_ref[...].astype(F32)
+    gate_sig = sigmoid(gate)
+    mix_grad = grad_ref[...].astype(F32)
+    out_grad = mix_grad * gate * gate_sig
+    scaled = act * step
+    scaled_half = scaled.astype(BF16)
+    grad_half = out_grad.astype(BF16)
+
+    join = jnp.concatenate
+    inner, dscaled = inner_ref[...], dscaled_ref[...]
     state = state_ref[...]
     carried = dot(out_low, state, NT) * enter
     from_end = dot(in_high, state, NT) * to_end
@@ -448,7 +501,7 @@
         bundle = bundle_s[...].astype(BF16)
         for shard in range(SHARDS):
             bundle_ref[shard] = bundle
-        top_half, bottom_half = dtop.astype(BF16), dbottom.astype(BF16)
+        top_half, bottom_half = dtop_ref[...].astype(BF16), dbottom_ref[...].astype(BF16)
         in_low, out_high = in_low_s[...], out_high_s[...]
         out_part = join([dot(top_half, in_low[:HALF]), dot(bottom_half, in_low)], axis=0)
         in_part = dot(bottom_half, out_high[HALF:], TN)
@@ -464,7 +517,10 @@
     return pl.pallas_call(
         mixer_second_kernel,
         grid=(STEPS,),
-        in_specs=mixer_specs(heads) + [pl.BlockSpec((BLK, 128), lambda c: (c, 0))],
+        in_specs=mixer_specs(heads) + [
+            column_block(T), column_block(T), whole((HALF, HALF)), whole((HALF, T)),
+            pl.BlockSpec((BLK, 128), lambda c: (c, 0)),
+        ],
         out_specs=[
             column_block(T), column_block(8), column_block(8), column_block(T),
             whole((heads, T)), whole((T, 128)), whole((SHARDS, BUNDLE + 8, 128)),
@@ -479,11 +535,6 @@
             jax.ShapeDtypeStruct((SHARDS, BUNDLE + 8, 128), BF16),
         ],
         scratch_shapes=TOKEN_SCRATCH + [
-            pltpu.VMEM((128, T), F32),
-            pltpu.VMEM((T, T), F32),
-            pltpu.VMEM((T, T), F32),
-            pltpu.VMEM((HALF, HALF), F32),
-            pltpu.VMEM((HALF, T), F32),
             pltpu.VMEM((T, 128), F32),
             pltpu.VMEM((T, 128), F32),
             pltpu.VMEM((T, 128), F32),
@@ -673,8 +724,9 @@
         merge_kernel,
         in_specs=[IN_VMEM] * 3,
         out_specs=[IN_VMEM] * ROW,
-        out_shape=[jax.ShapeDtypeStruct((3 * HEAD_DIM, T), BF16)] * ROW,
+        out_shape=[pltpu.VMEM((3 * HEAD_DIM, T), BF16)] * ROW,
         cost_estimate=pl.CostEstimate(flops=3 * 10**9, bytes_accessed=4 * 10**6, transcendentals=0),
+        compiler_params=GRANT,
         name="merge",
     )(dq, dkv, back)
 
@@ -747,10 +799,13 @@
     gathered = exchange(parts, SEQ)
     scanned = chain(near(gathered))
     entering = exchange(scanned, SEQ).reshape(COLS, 128)
+    inside = mixer_inner(*mixer_args)
     dq, dkv, back = attention(docs, near(far), own)
     returned = passed_along(back, SEQ, -ROW)
-    dx, tail, spill, dgate, dstep, coeff, bundle = mixer_second(*mixer_args, entering)
-    leaving = merge(dq, dkv, near(returned))
+    dx, tail, spill, dgate, dstep, coeff, bundle = mixer_second(
+        *mixer_args, *inside, entering
+    )
+    leaving = merge(near(dq), near(dkv), near(returned))
     swapped = turns(leaving, "seq_2")
     spilled = passed_along(spill, SEQ, -1)
     bundles = exchange(bundle, SEQ)

time: 147 us -> 132 us (0.90)
  blocking collectives: 19.7 us -> 0 us
  waiting for transfers between devices: 29.1 us -> 18.9 us
  starting transfers between devices: 45.9 us -> 55.4 us
  Pallas kernels: 44.9 us -> 50.1 us
    all_to_all x1 -> x0, blocking collectives: 19.7 us -> none  [exchange(): return lax.all_to_all(array, axis, split_axis=0, concat_axis=0, tiled=True)]
    pallas_call x0 -> x1, Pallas kernels: none -> 10.5 us  [mixer_inner(): pl.pallas_call(mixer_inner_kernel, grid=(STEPS,), in_specs=mixer_specs(he...]
    ppermute x9, waiting for transfers between devices: 25.1 us -> 15.2 us  [turns(): lax.ppermute(part, axis, [(n, (n + turn) % count) for n in range(count)])]
    all_to_all x2 -> x3, starting transfers between devices: 20.8 us -> 29.4 us  [exchange(): return lax.all_to_all(array, axis, split_axis=0, concat_axis=0, tiled=True)]
    pallas_call x1, Pallas kernels: 2.96 us -> 0.19 us  [merge(): pl.pallas_call(merge_kernel, in_specs=[IN_VMEM] * 3, out_specs=[IN_VMEM]...]
    pallas_call x1, Pallas kernels: 16.2 us -> 13.6 us  [mixer_second(): pl.pallas_call(mixer_second_kernel, grid=(STEPS,), in_specs=mixer_specs(h...]
    all_to_all x2 -> x3, waiting for transfers between devices: 3.97 us -> 1.84 us  [exchange(): return lax.all_to_all(array, axis, split_axis=0, concat_axis=0, tiled=True)]
    ppermute x4, waiting for transfers between devices: 0.01 us -> 1.77 us  [passed_along(): lax.ppermute(value, axis, [(source, source + steps) for source in range(i...]
  transfers between devices with their start and end apart: 15 -> 16, of which waited for: 6 -> 7; matrix products, arithmetic and copies ran while one was open for 1% -> 0% of each run, Pallas kernels for 27% -> 37%
where the time goes in v8:
time: 132 us; the launch traced here: 131 us
  starting transfers between devices  55.4 us (42%)
  Pallas kernels  50.1 us (38%)
  waiting for transfers between devices  18.9 us (14%)
  local copies, waits for them, and re-layouts  5.34 us (4%)
    all_to_all x3, starting transfers between devices, exchange(): return lax.all_to_all(array, axis, split_axis=0, concat_axis=0, tiled=True)  29.4 us
    ppermute x9, starting transfers between devices, turns(): lax.ppermute(part, axis, [(n, (n + turn) % count) for n in range(count)])  15.6 us
    ppermute x9, waiting for transfers between devices, turns(): lax.ppermute(part, axis, [(n, (n + turn) % count) for n in range(count)])  15.2 us
    pallas_call x1, Pallas kernels, mixer_second(): pl.pallas_call(mixer_second_kernel, grid=(STEPS,), in_specs=mixer_specs(h...  13.6 us
    pallas_call x1, Pallas kernels, mixer_inner(): pl.pallas_call(mixer_inner_kernel, grid=(STEPS,), in_specs=mixer_specs(he...  10.5 us
    ppermute x4, starting transfers between devices, passed_along(): lax.ppermute(value, axis, [(source, source + steps) for source in range(i...  10.4 us
    pallas_call x1, Pallas kernels, mixer_first(): pl.pallas_call(mixer_first_kernel, grid=(STEPS,), in_specs=mixer_specs(he...  9.07 us
    pallas_call x1, Pallas kernels, attention(): pl.pallas_call(attention_kernel, in_specs=[IN_VMEM] * (2 + ROW), out_spec...  8.94 us
  transfers between devices with their start and end apart: 16, of which 7 were waited for; matrix products, arithmetic and copies ran while one was open for 0% of the time, Pallas kernels for 37%

profile of v8, /device:TPU:0, one launch (start us, length us, event | category | flops | bytes accessed | tf_op | source)
XLA Modules:
  0.0 131.1 jit_solution(16686441952552907714)
XLA Ops:
  0.6 0.8 slice.3
  1.4 3.5 %collective-permute-start.8 = (bf16[8,1792]{1,0:T(8,128)(2,1)S(1)}, bf16[8,1792]{1,0:T(8,128)(2,1)S(1)}, u32[]{:S(2)}, u32[]{:S(2)}) collective-permute-start(bf16[8,1792]{1,0:T(8,128)(2,1)S(1)} %slice.3), channel_id=1, source_target_pairs={{0,4},{4,8},{8,12},{12,16},{16,20},{20,24},{24,28},{28,32},{32,36}... | collective-permute-start | bytes 86024 | tf_op jit(solution)/shard_map/ppermute | solution.py:762
  4.9 3.3 %pack.1 = (bf16[896,256]{1,0:T(8,128)(2,1)}, bf16[896,256]{1,0:T(8,128)(2,1)}, bf16[896,256]{1,0:T(8,128)(2,1)}, bf16[896,256]{1,0:T(8,128)(2,1)}) custom-call(bf16[256,896]{1,0:T(8,128)(2,1)} %k_ref.1, bf16[256,896]{1,0:T(8,128)(2,1)} %v_ref.1, bf16[256,896]{1,0:T(8,128)(2,1)} %q_ref.1, bf16[256,896]{1,0:T(8,128)(2,1)} %g_ref.1), custom_call_target="tpu_custom_call" | custom-call | tf_op jit(solution)/shard_map/pack/pallas_call | solution.py:602
  8.2 1.5 %collective-permute-start = (bf16[896,256]{1,0:T(8,128)(2,1)}, bf16[896,256]{1,0:T(8,128)(2,1)S(1)}, u32[]{:S(2)}, u32[]{:S(2)}) collective-permute-start(bf16[896,256]{1,0:T(8,128)(2,1)} %get-tuple-element.44), channel_id=1, source_target_pairs={{0,4},{4,8},{8,12},{12,0},{1,5},{5,9},{9,13},{13,1},{2,6},{6,10},{... | collective-permute-start | bytes 1376264 | tf_op jit(solution)/shard_map/ppermute | solution.py:768
  9.7 4.3 %collective-permute-start.1 = (bf16[896,256]{1,0:T(8,128)(2,1)}, bf16[896,256]{1,0:T(8,128)(2,1)S(1)}, u32[]{:S(2)}, u32[]{:S(2)}) collective-permute-start(bf16[896,256]{1,0:T(8,128)(2,1)} %get-tuple-element.45), channel_id=1, source_target_pairs={{0,8},{4,12},{8,0},{12,4},{1,9},{5,13},{9,1},{13,5},{2,10},{6,14},... | collective-permute-start | bytes 1376264 | tf_op jit(solution)/shard_map/ppermute | solution.py:768
  14.7 9.1 %mixer_first.1 = bf16[2048,128]{1,0:T(8,128)(2,1)} custom-call(bf16[256,1792]{1,0:T(8,128)(2,1)} %x_ref.5, bf16[8,1792]{1,0:T(8,128)(2,1)} %copy-done.8, f32[4,1792]{1,0:T(4,128)} %weight_ref.5, bf16[256,1792]{1,0:T(8,128)(2,1)} %gate_ref.5, bf16[256,1792]{1,0:T(8,128)(2,1)} %grad_ref.5, f32[28,256]{1,0:T(8,128)} %bitcast.17, f32[1,28]{1,0:T(1,128)} %bitcast.20, ...), custom_call_target="tpu_custom_call" | custom-call | flops 8000000000 | bytes 4000000 | tf_op jit(solution)/shard_map/mixer_first/pallas_call | solution.py:243
  23.8 8.1 %all-to-all-start = ((bf16[32,64,128]{2,1,0:T(8,128)(2,1)}), bf16[32,64,128]{2,1,0:T(8,128)(2,1)S(1)}, u32[]{:S(2)}, u32[]{:S(2)}) async-start(bf16[32,64,128]{2,1,0:T(8,128)(2,1)} %bitcast.11), calls=%async_computation | async-start | bytes 1048576 | tf_op jit(solution)/shard_map/all_to_all | solution.py:778
  31.9 2.2 %collective-permute-done.1.refs_2_ = bf16[896,256]{1,0:T(8,128)(2,1)S(1)} collective-permute-done((bf16[896,256]{1,0:T(8,128)(2,1)}, bf16[896,256]{1,0:T(8,128)(2,1)S(1)}, u32[]{:S(2)}, u32[]{:S(2)}) %collective-permute-start.1) | collective-permute-done | bytes 458784 | tf_op jit(solution)/shard_map/ppermute | solution.py:768
  34.3 1.0 lend.1
  35.2 4.3 %collective-permute-start.3 = (bf16[1792,256]{1,0:T(8,128)(2,1)}, bf16[1792,256]{1,0:T(8,128)(2,1)}, u32[]{:S(2)}, u32[]{:S(2)}) collective-permute-start(bf16[1792,256]{1,0:T(8,128)(2,1)} %lend.1), channel_id=1, source_target_pairs={{0,16},{4,20},{8,24},{12,28},{16,32},{20,36},{24,40},{28,44},{32,4... | collective-permute-start | bytes 2752520 | tf_op jit(solution)/shard_map/ppermute | solution.py:762
  39.6 10.5 %mixer_inner.1 = (f32[256,1792]{1,0:T(8,128)}, f32[256,1792]{1,0:T(8,128)}, f32[128,128]{1,0:T(8,128)}, f32[128,256]{1,0:T(8,128)}) custom-call(bf16[256,1792]{1,0:T(8,128)(2,1)} %x_ref.5, bf16[8,1792]{1,0:T(8,128)(2,1)} %copy-done.8, f32[4,1792]{1,0:T(4,128)} %weight_ref.5, bf16[256,1792]{1,0:T(8,128)(2,1)} %gate_ref.5, bf16[256,1792]{1,0:T(8,128)(2,1)} %grad_ref.5, ...), custom_call_target="tpu_custom_call" | custom-call | flops 10000000000 | bytes 6000000 | tf_op jit(solution)/shard_map/mixer_inner/pallas_call | solution.py:366
  50.0 1.3 chain.1
  51.3 9.2 %all-to-all-start.1 = ((bf16[32,56,128]{2,1,0:T(8,128)(2,1)}), bf16[32,56,128]{2,1,0:T(8,128)(2,1)S(1)}, u32[]{:S(2)}, u32[]{:S(2)}) async-start(bf16[32,56,128]{2,1,0:T(8,128)(2,1)} %chain.1), calls=%async_computation.1 | async-start | bytes 917504 | tf_op jit(solution)/shard_map/all_to_all | solution.py:778
  60.5 8.9 %attention.1 = (bf16[4,224,256]{2,1,0:T(8,128)(2,1)}, f32[4,448,256]{2,1,0:T(8,128)}, bf16[4,448,256]{2,1,0:T(8,128)(2,1)}) custom-call(s32[64,128]{1,0:T(8,128)} %bitcast.15, bf16[1792,256]{1,0:T(8,128)(2,1)} %collective-permute-done.3.far_ref, bf16[896,256]{1,0:T(8,128)(2,1)S(1)} %copy-done, bf16[896,256]{1,0:T(8,128)(2,1)S(1)} %collective-permute-done.refs_1_, ...), custom_call_target="tpu_custom_call" | custom-call | flops 12000000000 | bytes 8000000 | tf_op jit(solution)/shard_map/attention/pallas_call | solution.py:692
  69.4 1.3 collective-permute-start.4
  70.7 1.8 %all-to-all-done.1 = bf16[32,56,128]{2,1,0:T(8,128)(2,1)S(1)} async-done(((bf16[32,56,128]{2,1,0:T(8,128)(2,1)}), bf16[32,56,128]{2,1,0:T(8,128)(2,1)S(1)}, u32[]{:S(2)}, u32[]{:S(2)}) %all-to-all-start.1) | async-done | bytes 458784 | tf_op jit(solution)/shard_map/all_to_all | solution.py:778
  72.6 0.8 copy-done.6
  73.3 13.6 %mixer_second.1 = (bf16[256,1792]{1,0:T(8,128)(2,1)}, f32[8,1792]{1,0:T(8,128)}, f32[8,1792]{1,0:T(8,128)}, bf16[256,1792]{1,0:T(8,128)(2,1)}, f32[28,256]{1,0:T...) custom-call(bf16[256,1792]{1,0:T(8,128)(2,1)} %x_ref.5, bf16[8,1792]{1,0:T(8,128)(2,1)} %copy-done.8, ...), custom_call_target="tpu_custom_call" | custom-call | flops 17999998976 | bytes 8000000 | tf_op jit(solution)/shard_map/mixer_second/pallas_call | solution.py:517
  87.8 1.4 %collective-permute-start.12 = (bf16[256,128]{1,0:T(8,128)(2,1)}, bf16[256,128]{1,0:T(8,128)(2,1)S(1)}, u32[]{:S(2)}, u32[]{:S(2)}) collective-permute-start(bf16[256,128]{1,0:T(8,128)(2,1)} %get-tuple-element.67.refs_0_), channel_id=1, source_target_pairs={{0,3},{1,0},{2,1},{3,2},{4,7},{5,4},{6,5},{7,6},{8,11},{9,8},{10,9... | collective-permute-start | bytes 196616 | tf_op jit(solution)/shard_map/ppermute | solution.py:768
  89.2 12.1 %all-to-all-start.2 = ((bf16[32,64,128]{2,1,0:T(8,128)(2,1)}), bf16[32,64,128]{2,1,0:T(8,128)(2,1)S(1)}, u32[]{:S(2)}, u32[]{:S(2)}) async-start(bf16[32,64,128]{2,1,0:T(8,128)(2,1)} %get-tuple-element.66), calls=%async_computation.2 | async-start | bytes 1048576 | tf_op jit(solution)/shard_map/all_to_all | solution.py:778
  101.3 1.3 collective-permute-start.9
  102.6 1.5 %copy-done.2 = f32[4,448,256]{2,1,0:T(8,128)S(1)} copy-done((f32[4,448,256]{2,1,0:T(8,128)S(1)}, f32[4,448,256]{2,1,0:T(8,128)}, u32[]{:S(2)}) %copy-start.2) | copy-done | bytes 1835032
  105.1 2.6 %collective-permute-start.5 = (bf16[672,256]{1,0:T(8,128)(2,1)S(1)}, bf16[672,256]{1,0:T(8,128)(2,1)S(1)}, u32[]{:S(2)}, u32[]{:S(2)}) collective-permute-start(bf16[672,256]{1,0:T(8,128)(2,1)S(1)} %get-tuple-element.51), channel_id=1, source_target_pairs={{0,4},{4,8},{8,12},{12,0},{1,5},{5,9},{9,13},{13,1},{2,6},{6,10},{... | collective-permute-start | bytes 1032200 | tf_op jit(solution)/shard_map/ppermute | solution.py:768
  107.7 1.8 %collective-permute-done.9 = f32[8,1792]{1,0:T(8,128)S(1)} collective-permute-done((f32[8,1792]{1,0:T(8,128)}, f32[8,1792]{1,0:T(8,128)S(1)}, u32[]{:S(2)}, u32[]{:S(2)}) %collective-permute-start.9) | collective-permute-done | bytes 57376 | tf_op jit(solution)/shard_map/ppermute | solution.py:762
  109.5 2.7 %collective-permute-start.6 = (bf16[672,256]{1,0:T(8,128)(2,1)S(1)}, bf16[672,256]{1,0:T(8,128)(2,1)S(1)}, u32[]{:S(2)}, u32[]{:S(2)}) collective-permute-start(bf16[672,256]{1,0:T(8,128)(2,1)S(1)} %get-tuple-element.52), channel_id=1, source_target_pairs={{0,8},{4,12},{8,0},{12,4},{1,9},{5,13},{9,1},{13,5},{2,10},{6,14},... | collective-permute-start | bytes 1032200 | tf_op jit(solution)/shard_map/ppermute | solution.py:768
  112.2 2.2 %collective-permute-start.7 = (bf16[672,256]{1,0:T(8,128)(2,1)S(1)}, bf16[672,256]{1,0:T(8,128)(2,1)S(1)}, u32[]{:S(2)}, u32[]{:S(2)}) collective-permute-start(bf16[672,256]{1,0:T(8,128)(2,1)S(1)} %get-tuple-element.53), channel_id=1, source_target_pairs={{0,12},{4,0},{8,4},{12,8},{1,13},{5,1},{9,5},{13,9},{2,14},{6,2},{... | collective-permute-start | bytes 1032200 | tf_op jit(solution)/shard_map/ppermute | solution.py:768
  115.0 0.9 finish.1
  115.9 3.2 %collective-permute-done.5.refs_1_ = bf16[672,256]{1,0:T(8,128)(2,1)S(1)} collective-permute-done((bf16[672,256]{1,0:T(8,128)(2,1)S(1)}, bf16[672,256]{1,0:T(8,128)(2,1)S(1)}, u32[]{:S(2)}, u32[]{:S(2)}) %collective-permute-start.5) | collective-permute-done | bytes 344096 | tf_op jit(solution)/shard_map/ppermute | solution.py:768
  119.1 5.5 %collective-permute-done.6.refs_2_ = bf16[672,256]{1,0:T(8,128)(2,1)S(1)} collective-permute-done((bf16[672,256]{1,0:T(8,128)(2,1)S(1)}, bf16[672,256]{1,0:T(8,128)(2,1)S(1)}, u32[]{:S(2)}, u32[]{:S(2)}) %collective-permute-start.6) | collective-permute-done | bytes 344096 | tf_op jit(solution)/shard_map/ppermute | solution.py:768
  124.6 4.1 %collective-permute-done.7.refs_3_ = bf16[672,256]{1,0:T(8,128)(2,1)S(1)} collective-permute-done((bf16[672,256]{1,0:T(8,128)(2,1)S(1)}, bf16[672,256]{1,0:T(8,128)(2,1)S(1)}, u32[]{:S(2)}, u32[]{:S(2)}) %collective-permute-start.7) | collective-permute-done | bytes 344096 | tf_op jit(solution)/shard_map/ppermute | solution.py:768
  128.7 1.0 copy-done.4
  129.7 1.4 %unpack.1 = (bf16[256,896]{1,0:T(8,128)(2,1)}, bf16[256,896]{1,0:T(8,128)(2,1)}, bf16[256,896]{1,0:T(8,128)(2,1)}) custom-call(bf16[672,256]{1,0:T(8,128)(2,1)S(1)} %copy-done.4, bf16[672,256]{1,0:T(8,128)(2,1)S(1)} %collective-permute-done.5.refs_1_, bf16[672,256]{1,0:T(8,128)(2,1)S(1)} %collective-permute-done.6.refs_2_, ...), custom_call_target="tpu_custom_call" | custom-call | flops 2000000000 | bytes 3000000 | tf_op jit(solution)/shard_map/unpack/pallas_call | solution.py:748
  (30 shorter events, 3.2 us)
Async XLA Ops:
  1.4 12.7 %collective-permute-start.8 = (bf16[8,1792]{1,0:T(8,128)(2,1)S(1)}, bf16[8,1792]{1,0:T(8,128)(2,1)S(1)}, u32[]{:S(2)}, u32[]{:S(2)}) collective-permute-start(bf16[8,1792]{1,0:T(8,128)(2,1)S(1)} %slice.3), channel_id=1, source_target_pairs={{0,4},{4,8},{8,12},{12,16},{16,20},{20,24},{24,28},{28,32},{32,36}... | collective-permute-start | bytes 86024 | tf_op jit(solution)/shard_map/ppermute | solution.py:762
  8.2 23.6 %collective-permute-start = (bf16[896,256]{1,0:T(8,128)(2,1)}, bf16[896,256]{1,0:T(8,128)(2,1)S(1)}, u32[]{:S(2)}, u32[]{:S(2)}) collective-permute-start(bf16[896,256]{1,0:T(8,128)(2,1)} %get-tuple-element.44), channel_id=1, source_target_pairs={{0,4},{4,8},{8,12},{12,0},{1,5},{5,9},{9,13},{13,1},{2,6},{6,10},{... | collective-permute-start | bytes 1376264 | tf_op jit(solution)/shard_map/ppermute | solution.py:768
  9.7 24.3 %collective-permute-start.1 = (bf16[896,256]{1,0:T(8,128)(2,1)}, bf16[896,256]{1,0:T(8,128)(2,1)S(1)}, u32[]{:S(2)}, u32[]{:S(2)}) collective-permute-start(bf16[896,256]{1,0:T(8,128)(2,1)} %get-tuple-element.45), channel_id=1, source_target_pairs={{0,8},{4,12},{8,0},{12,4},{1,9},{5,13},{9,1},{13,5},{2,10},{6,14},... | collective-permute-start | bytes 1376264 | tf_op jit(solution)/shard_map/ppermute | solution.py:768
  14.1 20.2 %collective-permute-start.2 = (bf16[896,256]{1,0:T(8,128)(2,1)}, bf16[896,256]{1,0:T(8,128)(2,1)S(1)}, u32[]{:S(2)}, u32[]{:S(2)}) collective-permute-start(bf16[896,256]{1,0:T(8,128)(2,1)} %get-tuple-element.46), channel_id=1, source_target_pairs={{0,12},{4,0},{8,4},{12,8},{1,13},{5,1},{9,5},{13,9},{2,14},{6,2},{... | collective-permute-start | bytes 1376264 | tf_op jit(solution)/shard_map/ppermute | solution.py:768
  14.1 0.6 copy-start.8
  14.7 19.6 %copy-start = (bf16[896,256]{1,0:T(8,128)(2,1)S(1)}, bf16[896,256]{1,0:T(8,128)(2,1)}, u32[]{:S(2)}) copy-start(bf16[896,256]{1,0:T(8,128)(2,1)} %get-tuple-element.43.refs_0_) | copy-start | bytes 1376260
  23.8 26.3 %all-to-all-start = ((bf16[32,64,128]{2,1,0:T(8,128)(2,1)}), bf16[32,64,128]{2,1,0:T(8,128)(2,1)S(1)}, u32[]{:S(2)}, u32[]{:S(2)}) async-start(bf16[32,64,128]{2,1,0:T(8,128)(2,1)} %bitcast.11), calls=%async_computation | async-start | bytes 1048576 | tf_op jit(solution)/shard_map/all_to_all | solution.py:778
  35.2 25.2 %collective-permute-start.3 = (bf16[1792,256]{1,0:T(8,128)(2,1)}, bf16[1792,256]{1,0:T(8,128)(2,1)}, u32[]{:S(2)}, u32[]{:S(2)}) collective-permute-start(bf16[1792,256]{1,0:T(8,128)(2,1)} %lend.1), channel_id=1, source_target_pairs={{0,16},{4,20},{8,24},{12,28},{16,32},{20,36},{24,40},{28,44},{32,4... | collective-permute-start | bytes 2752520 | tf_op jit(solution)/shard_map/ppermute | solution.py:762
  51.3 21.3 %all-to-all-start.1 = ((bf16[32,56,128]{2,1,0:T(8,128)(2,1)}), bf16[32,56,128]{2,1,0:T(8,128)(2,1)S(1)}, u32[]{:S(2)}, u32[]{:S(2)}) async-start(bf16[32,56,128]{2,1,0:T(8,128)(2,1)} %chain.1), calls=%async_computation.1 | async-start | bytes 917504 | tf_op jit(solution)/shard_map/all_to_all | solution.py:778
  69.4 33.2 %collective-permute-start.4 = (bf16[4,448,256]{2,1,0:T(8,128)(2,1)}, bf16[4,448,256]{2,1,0:T(8,128)(2,1)S(1)}, u32[]{:S(2)}, u32[]{:S(2)}) collective-permute-start(bf16[4,448,256]{2,1,0:T(8,128)(2,1)} %get-tuple-element.49), channel_id=1, source_target_pairs={{16,0},{20,4},{24,8},{28,12},{32,16},{36,20},{40,24},{44,28},{48,3... | collective-permute-start | bytes 2752520 | tf_op jit(solution)/shard_map/ppermute | solution.py:762
  72.6 0.8 copy-start.6
  73.3 29.3 %copy-start.5 = (bf16[4,224,256]{2,1,0:T(8,128)(2,1)S(1)}, bf16[4,224,256]{2,1,0:T(8,128)(2,1)}, u32[]{:S(2)}) copy-start(bf16[4,224,256]{2,1,0:T(8,128)(2,1)} %get-tuple-element.47.dq_ref) | copy-start | bytes 1376260
  87.0 25.2 %collective-permute-start.10 = (bf16[256,128]{1,0:T(8,128)(2,1)}, bf16[256,128]{1,0:T(8,128)(2,1)S(1)}, u32[]{:S(2)}, u32[]{:S(2)}) collective-permute-start(bf16[256,128]{1,0:T(8,128)(2,1)} %get-tuple-element.67.refs_0_), channel_id=1, source_target_pairs={{0,1},{1,2},{2,3},{3,0},{4,5},{5,6},{6,7},{7,4},{8,9},{9,10},{10,1... | collective-permute-start | bytes 196616 | tf_op jit(solution)/shard_map/ppermute | solution.py:768
  87.1 28.0 %collective-permute-start.11 = (bf16[256,128]{1,0:T(8,128)(2,1)}, bf16[256,128]{1,0:T(8,128)(2,1)S(1)}, u32[]{:S(2)}, u32[]{:S(2)}) collective-permute-start(bf16[256,128]{1,0:T(8,128)(2,1)} %get-tuple-element.67.refs_0_), channel_id=1, source_target_pairs={{0,2},{1,3},{2,0},{3,1},{4,6},{5,7},{6,4},{7,5},{8,10},{9,11},{10,... | collective-permute-start | bytes 196616 | tf_op jit(solution)/shard_map/ppermute | solution.py:768
  87.8 27.2 %collective-permute-start.12 = (bf16[256,128]{1,0:T(8,128)(2,1)}, bf16[256,128]{1,0:T(8,128)(2,1)S(1)}, u32[]{:S(2)}, u32[]{:S(2)}) collective-permute-start(bf16[256,128]{1,0:T(8,128)(2,1)} %get-tuple-element.67.refs_0_), channel_id=1, source_target_pairs={{0,3},{1,0},{2,1},{3,2},{4,7},{5,4},{6,5},{7,6},{8,11},{9,8},{10,9... | collective-permute-start | bytes 196616 | tf_op jit(solution)/shard_map/ppermute | solution.py:768
  89.2 25.8 %all-to-all-start.2 = ((bf16[32,64,128]{2,1,0:T(8,128)(2,1)}), bf16[32,64,128]{2,1,0:T(8,128)(2,1)S(1)}, u32[]{:S(2)}, u32[]{:S(2)}) async-start(bf16[32,64,128]{2,1,0:T(8,128)(2,1)} %get-tuple-element.66), calls=%async_computation.2 | async-start | bytes 1048576 | tf_op jit(solution)/shard_map/all_to_all | solution.py:778
  101.3 8.2 %collective-permute-start.9 = (f32[8,1792]{1,0:T(8,128)}, f32[8,1792]{1,0:T(8,128)S(1)}, u32[]{:S(2)}, u32[]{:S(2)}) collective-permute-start(f32[8,1792]{1,0:T(8,128)} %get-tuple-element.63), channel_id=1, source_target_pairs={{4,0},{8,4},{12,8},{16,12},{20,16},{24,20},{28,24},{32,28},{36,32}... | collective-permute-start | bytes 172040 | tf_op jit(solution)/shard_map/ppermute | solution.py:762
  102.6 1.5 %copy-start.2 = (f32[4,448,256]{2,1,0:T(8,128)S(1)}, f32[4,448,256]{2,1,0:T(8,128)}, u32[]{:S(2)}) copy-start(f32[4,448,256]{2,1,0:T(8,128)} %get-tuple-element.48.dkv_ref) | copy-start | bytes 5505028
  104.1 10.2 %copy-start.7 = (f32[8,1792]{1,0:T(8,128)S(1)}, f32[8,1792]{1,0:T(8,128)}, u32[]{:S(2)}) copy-start(f32[8,1792]{1,0:T(8,128)} %get-tuple-element.62) | copy-start | bytes 172036
  104.1 10.9 %copy-start.1 = (bf16[256,128]{1,0:T(8,128)(2,1)S(1)}, bf16[256,128]{1,0:T(8,128)(2,1)}, u32[]{:S(2)}) copy-start(bf16[256,128]{1,0:T(8,128)(2,1)} %get-tuple-element.67.refs_0_) | copy-start | bytes 196612
  104.3 0.7 copy-start.3
  105.1 14.0 %collective-permute-start.5 = (bf16[672,256]{1,0:T(8,128)(2,1)S(1)}, bf16[672,256]{1,0:T(8,128)(2,1)S(1)}, u32[]{:S(2)}, u32[]{:S(2)}) collective-permute-start(bf16[672,256]{1,0:T(8,128)(2,1)S(1)} %get-tuple-element.51), channel_id=1, source_target_pairs={{0,4},{4,8},{8,12},{12,0},{1,5},{5,9},{9,13},{13,1},{2,6},{6,10},{... | collective-permute-start | bytes 1032200 | tf_op jit(solution)/shard_map/ppermute | solution.py:768
  109.5 15.1 %collective-permute-start.6 = (bf16[672,256]{1,0:T(8,128)(2,1)S(1)}, bf16[672,256]{1,0:T(8,128)(2,1)S(1)}, u32[]{:S(2)}, u32[]{:S(2)}) collective-permute-start(bf16[672,256]{1,0:T(8,128)(2,1)S(1)} %get-tuple-element.52), channel_id=1, source_target_pairs={{0,8},{4,12},{8,0},{12,4},{1,9},{5,13},{9,1},{13,5},{2,10},{6,14},... | collective-permute-start | bytes 1032200 | tf_op jit(solution)/shard_map/ppermute | solution.py:768
  112.2 16.6 %collective-permute-start.7 = (bf16[672,256]{1,0:T(8,128)(2,1)S(1)}, bf16[672,256]{1,0:T(8,128)(2,1)S(1)}, u32[]{:S(2)}, u32[]{:S(2)}) collective-permute-start(bf16[672,256]{1,0:T(8,128)(2,1)S(1)} %get-tuple-element.53), channel_id=1, source_target_pairs={{0,12},{4,0},{8,4},{12,8},{1,13},{5,1},{9,5},{13,9},{2,14},{6,2},{... | collective-permute-start | bytes 1032200 | tf_op jit(solution)/shard_map/ppermute | solution.py:768
  128.7 1.0 copy-start.4

commit v9 on v8

--- a/solution.py
+++ b/solution.py
@@ -69,7 +69,6 @@
 
 
 IN_VMEM = pl.BlockSpec(memory_space=pltpu.VMEM)
-GRANT = pltpu.CompilerParams(vmem_limit_bytes=32 * 2**20)
 
 
 def seq_index():
@@ -724,9 +723,8 @@
         merge_kernel,
         in_specs=[IN_VMEM] * 3,
         out_specs=[IN_VMEM] * ROW,
-        out_shape=[pltpu.VMEM((3 * HEAD_DIM, T), BF16)] * ROW,
+        out_shape=[jax.ShapeDtypeStruct((3 * HEAD_DIM, T), BF16)] * ROW,
         cost_estimate=pl.CostEstimate(flops=3 * 10**9, bytes_accessed=4 * 10**6, transcendentals=0),
-        compiler_params=GRANT,
         name="merge",
     )(dq, dkv, back)
 
@@ -805,14 +803,14 @@
     dx, tail, spill, dgate, dstep, coeff, bundle = mixer_second(
         *mixer_args, *inside, entering
     )
-    leaving = merge(near(dq), near(dkv), near(returned))
+    leaving = merge(dq, dkv, near(returned))
     swapped = turns(leaving, "seq_2")
     spilled = passed_along(spill, SEQ, -1)
     bundles = exchange(bundle, SEQ)
     coeffs = turns([coeff] * LOCAL_HEADS, "head")
-    dq, dk, dv = unpack([near(v) for v in swapped])
+    dq, dk, dv = unpack(swapped[:1] + [near(v) for v in swapped[1:]])
     grad_weight, grad_bias, grad_rate, grad_skip, sum_in, sum_out = finish(
-        near(bundles), [near(v) for v in coeffs], heads
+        near(bundles), coeffs[:1] + [near(v) for v in coeffs[1:]], heads
     )
     tail = (tail + spilled).astype(BF16)
     grad_conv = lax.dynamic_update_slice_in_dim(dx, tail, T - 8, 0)

time: 132 us -> 132 us (level)
  Pallas kernels: 50.1 us -> 54.6 us
  local copies, waits for them, and re-layouts: 5.34 us -> 2.14 us
    unnamed x18 -> x8, local copies, waits for them, and re-layouts: 4.58 us -> 1.38 us
    pallas_call x1, Pallas kernels: 0.19 us -> 2.89 us  [merge(): pl.pallas_call(merge_kernel, in_specs=[IN_VMEM] * 3, out_specs=[IN_VMEM]...]
  transfers between devices with their start and end apart: 16 -> 16, of which waited for: 7 -> 7; matrix products, arithmetic and copies ran while one was open for 0% -> 0% of each run, Pallas kernels for 37% -> 40%
where the time goes in v9:
time: 132 us; the launch traced here: 131 us
  starting transfers between devices  55.3 us (42%)
  Pallas kernels  54.6 us (41%)
  waiting for transfers between devices  17.8 us (13%)
  local copies, waits for them, and re-layouts  2.14 us (2%)
    all_to_all x3, starting transfers between devices, exchange(): return lax.all_to_all(array, axis, split_axis=0, concat_axis=0, tiled=True)  29.4 us
    ppermute x9, starting transfers between devices, turns(): lax.ppermute(part, axis, [(n, (n + turn) % count) for n in range(count)])  15.6 us
    ppermute x9, waiting for transfers between devices, turns(): lax.ppermute(part, axis, [(n, (n + turn) % count) for n in range(count)])  14.6 us
    pallas_call x1, Pallas kernels, mixer_second(): pl.pallas_call(mixer_second_kernel, grid=(STEPS,), in_specs=mixer_specs(h...  13.6 us
    pallas_call x1, Pallas kernels, mixer_inner(): pl.pallas_call(mixer_inner_kernel, grid=(STEPS,), in_specs=mixer_specs(he...  10.5 us
    ppermute x4, starting transfers between devices, passed_along(): lax.ppermute(value, axis, [(source, source + steps) for source in range(i...  10.4 us
    pallas_call x1, Pallas kernels, mixer_first(): pl.pallas_call(mixer_first_kernel, grid=(STEPS,), in_specs=mixer_specs(he...  9.07 us
    pallas_call x1, Pallas kernels, attention(): pl.pallas_call(attention_kernel, in_specs=[IN_VMEM] * (2 + ROW), out_spec...  8.93 us
  transfers between devices with their start and end apart: 16, of which 7 were waited for; matrix products, arithmetic and copies ran while one was open for 0% of the time, Pallas kernels for 40%

profile of v9, /device:TPU:0, one launch (start us, length us, event | category | flops | bytes accessed | tf_op | source)
XLA Modules:
  0.0 131.2 jit_solution(1766128923530839883)
XLA Ops:
  0.6 0.8 slice.3
  1.4 3.5 %collective-permute-start.8 = (bf16[8,1792]{1,0:T(8,128)(2,1)S(1)}, bf16[8,1792]{1,0:T(8,128)(2,1)S(1)}, u32[]{:S(2)}, u32[]{:S(2)}) collective-permute-start(bf16[8,1792]{1,0:T(8,128)(2,1)S(1)} %slice.3), channel_id=1, source_target_pairs={{0,4},{4,8},{8,12},{12,16},{16,20},{20,24},{24,28},{28,32},{32,36}... | collective-permute-start | bytes 86024 | tf_op jit(solution)/shard_map/ppermute | solution.py:760
  4.9 3.3 %pack.1 = (bf16[896,256]{1,0:T(8,128)(2,1)}, bf16[896,256]{1,0:T(8,128)(2,1)}, bf16[896,256]{1,0:T(8,128)(2,1)}, bf16[896,256]{1,0:T(8,128)(2,1)}) custom-call(bf16[256,896]{1,0:T(8,128)(2,1)} %k_ref.1, bf16[256,896]{1,0:T(8,128)(2,1)} %v_ref.1, bf16[256,896]{1,0:T(8,128)(2,1)} %q_ref.1, bf16[256,896]{1,0:T(8,128)(2,1)} %g_ref.1), custom_call_target="tpu_custom_call" | custom-call | tf_op jit(solution)/shard_map/pack/pallas_call | solution.py:601
  8.2 1.5 %collective-permute-start = (bf16[896,256]{1,0:T(8,128)(2,1)}, bf16[896,256]{1,0:T(8,128)(2,1)S(1)}, u32[]{:S(2)}, u32[]{:S(2)}) collective-permute-start(bf16[896,256]{1,0:T(8,128)(2,1)} %get-tuple-element.44), channel_id=1, source_target_pairs={{0,4},{4,8},{8,12},{12,0},{1,5},{5,9},{9,13},{13,1},{2,6},{6,10},{... | collective-permute-start | bytes 1376264 | tf_op jit(solution)/shard_map/ppermute | solution.py:766
  9.7 4.3 %collective-permute-start.1 = (bf16[896,256]{1,0:T(8,128)(2,1)}, bf16[896,256]{1,0:T(8,128)(2,1)S(1)}, u32[]{:S(2)}, u32[]{:S(2)}) collective-permute-start(bf16[896,256]{1,0:T(8,128)(2,1)} %get-tuple-element.45), channel_id=1, source_target_pairs={{0,8},{4,12},{8,0},{12,4},{1,9},{5,13},{9,1},{13,5},{2,10},{6,14},... | collective-permute-start | bytes 1376264 | tf_op jit(solution)/shard_map/ppermute | solution.py:766
  14.7 9.1 %mixer_first.1 = bf16[2048,128]{1,0:T(8,128)(2,1)} custom-call(bf16[256,1792]{1,0:T(8,128)(2,1)} %x_ref.5, bf16[8,1792]{1,0:T(8,128)(2,1)} %copy-done.3, f32[4,1792]{1,0:T(4,128)} %weight_ref.5, bf16[256,1792]{1,0:T(8,128)(2,1)} %gate_ref.5, bf16[256,1792]{1,0:T(8,128)(2,1)} %grad_ref.5, f32[28,256]{1,0:T(8,128)} %bitcast.17, f32[1,28]{1,0:T(1,128)} %bitcast.20, ...), custom_call_target="tpu_custom_call" | custom-call | flops 8000000000 | bytes 4000000 | tf_op jit(solution)/shard_map/mixer_first/pallas_call | solution.py:242
  23.8 8.1 %all-to-all-start = ((bf16[32,64,128]{2,1,0:T(8,128)(2,1)}), bf16[32,64,128]{2,1,0:T(8,128)(2,1)S(1)}, u32[]{:S(2)}, u32[]{:S(2)}) async-start(bf16[32,64,128]{2,1,0:T(8,128)(2,1)} %bitcast.11), calls=%async_computation | async-start | bytes 1048576 | tf_op jit(solution)/shard_map/all_to_all | solution.py:776
  31.9 2.2 %collective-permute-done.1.refs_2_ = bf16[896,256]{1,0:T(8,128)(2,1)S(1)} collective-permute-done((bf16[896,256]{1,0:T(8,128)(2,1)}, bf16[896,256]{1,0:T(8,128)(2,1)S(1)}, u32[]{:S(2)}, u32[]{:S(2)}) %collective-permute-start.1) | collective-permute-done | bytes 458784 | tf_op jit(solution)/shard_map/ppermute | solution.py:766
  34.3 1.0 lend.1
  35.2 4.3 %collective-permute-start.3 = (bf16[1792,256]{1,0:T(8,128)(2,1)}, bf16[1792,256]{1,0:T(8,128)(2,1)}, u32[]{:S(2)}, u32[]{:S(2)}) collective-permute-start(bf16[1792,256]{1,0:T(8,128)(2,1)} %lend.1), channel_id=1, source_target_pairs={{0,16},{4,20},{8,24},{12,28},{16,32},{20,36},{24,40},{28,44},{32,4... | collective-permute-start | bytes 2752520 | tf_op jit(solution)/shard_map/ppermute | solution.py:760
  39.6 10.5 %mixer_inner.1 = (f32[256,1792]{1,0:T(8,128)}, f32[256,1792]{1,0:T(8,128)}, f32[128,128]{1,0:T(8,128)}, f32[128,256]{1,0:T(8,128)}) custom-call(bf16[256,1792]{1,0:T(8,128)(2,1)} %x_ref.5, bf16[8,1792]{1,0:T(8,128)(2,1)} %copy-done.3, f32[4,1792]{1,0:T(4,128)} %weight_ref.5, bf16[256,1792]{1,0:T(8,128)(2,1)} %gate_ref.5, bf16[256,1792]{1,0:T(8,128)(2,1)} %grad_ref.5, ...), custom_call_target="tpu_custom_call" | custom-call | flops 10000000000 | bytes 6000000 | tf_op jit(solution)/shard_map/mixer_inner/pallas_call | solution.py:365
  50.1 1.3 chain.1
  51.3 9.2 %all-to-all-start.1 = ((bf16[32,56,128]{2,1,0:T(8,128)(2,1)}), bf16[32,56,128]{2,1,0:T(8,128)(2,1)S(1)}, u32[]{:S(2)}, u32[]{:S(2)}) async-start(bf16[32,56,128]{2,1,0:T(8,128)(2,1)} %chain.1), calls=%async_computation.1 | async-start | bytes 917504 | tf_op jit(solution)/shard_map/all_to_all | solution.py:776
  60.5 8.9 %attention.1 = (bf16[4,224,256]{2,1,0:T(8,128)(2,1)}, f32[4,448,256]{2,1,0:T(8,128)}, bf16[4,448,256]{2,1,0:T(8,128)(2,1)}) custom-call(s32[64,128]{1,0:T(8,128)} %bitcast.15, bf16[1792,256]{1,0:T(8,128)(2,1)} %collective-permute-done.3.far_ref, bf16[896,256]{1,0:T(8,128)(2,1)S(1)} %copy-done, bf16[896,256]{1,0:T(8,128)(2,1)S(1)} %collective-permute-done.refs_1_, ...), custom_call_target="tpu_custom_call" | custom-call | flops 12000000000 | bytes 8000000 | tf_op jit(solution)/shard_map/attention/pallas_call | solution.py:691
  69.5 1.3 collective-permute-start.4
  70.7 1.8 %all-to-all-done.1 = bf16[32,56,128]{2,1,0:T(8,128)(2,1)S(1)} async-done(((bf16[32,56,128]{2,1,0:T(8,128)(2,1)}), bf16[32,56,128]{2,1,0:T(8,128)(2,1)S(1)}, u32[]{:S(2)}, u32[]{:S(2)}) %all-to-all-start.1) | async-done | bytes 458784 | tf_op jit(solution)/shard_map/all_to_all | solution.py:776
  72.6 0.8 copy-done.1
  73.3 13.6 %mixer_second.1 = (bf16[256,1792]{1,0:T(8,128)(2,1)}, f32[8,1792]{1,0:T(8,128)}, f32[8,1792]{1,0:T(8,128)}, bf16[256,1792]{1,0:T(8,128)(2,1)}, f32[28,256]{1,0:T...) custom-call(bf16[256,1792]{1,0:T(8,128)(2,1)} %x_ref.5, bf16[8,1792]{1,0:T(8,128)(2,1)} %copy-done.3, ...), custom_call_target="tpu_custom_call" | custom-call | flops 17999998976 | bytes 8000000 | tf_op jit(solution)/shard_map/mixer_second/pallas_call | solution.py:516
  87.0 0.8 collective-permute-start.11
  87.8 1.4 %collective-permute-start.12 = (bf16[256,128]{1,0:T(8,128)(2,1)}, bf16[256,128]{1,0:T(8,128)(2,1)S(1)}, u32[]{:S(2)}, u32[]{:S(2)}) collective-permute-start(bf16[256,128]{1,0:T(8,128)(2,1)} %get-tuple-element.67.refs_0_), channel_id=1, source_target_pairs={{0,3},{1,0},{2,1},{3,2},{4,7},{5,4},{6,5},{7,6},{8,11},{9,8},{10,9... | collective-permute-start | bytes 196616 | tf_op jit(solution)/shard_map/ppermute | solution.py:766
  89.2 12.1 %all-to-all-start.2 = ((bf16[32,64,128]{2,1,0:T(8,128)(2,1)}), bf16[32,64,128]{2,1,0:T(8,128)(2,1)S(1)}, u32[]{:S(2)}, u32[]{:S(2)}) async-start(bf16[32,64,128]{2,1,0:T(8,128)(2,1)} %get-tuple-element.66), calls=%async_computation.2 | async-start | bytes 1048576 | tf_op jit(solution)/shard_map/all_to_all | solution.py:776
  101.3 1.3 collective-permute-start.9
  102.6 2.9 %merge.1 = (bf16[672,256]{1,0:T(8,128)(2,1)}, bf16[672,256]{1,0:T(8,128)(2,1)}, bf16[672,256]{1,0:T(8,128)(2,1)}, bf16[672,256]{1,0:T(8,128)(2,1)}) custom-call(bf16[4,224,256]{2,1,0:T(8,128)(2,1)} %get-tuple-element.47.dq_ref, f32[4,448,256]{2,1,0:T(8,128)} %get-tuple-element.48.dkv_ref, bf16[4,448,256]{2,1,0:T(8,128)(2,1)S(1)} %collective-permute-done.4.back_ref), custom_call_target="tpu_custom_call" | custom-call | flops 3000000000 | bytes 4000000 | tf_op jit(solution)/shard_map/merge/pallas_call | solution.py:722
  105.5 2.6 %collective-permute-start.5 = (bf16[672,256]{1,0:T(8,128)(2,1)}, bf16[672,256]{1,0:T(8,128)(2,1)S(1)}, u32[]{:S(2)}, u32[]{:S(2)}) collective-permute-start(bf16[672,256]{1,0:T(8,128)(2,1)} %get-tuple-element.51), channel_id=1, source_target_pairs={{0,4},{4,8},{8,12},{12,0},{1,5},{5,9},{9,13},{13,1},{2,6},{6,10},{... | collective-permute-start | bytes 1032200 | tf_op jit(solution)/shard_map/ppermute | solution.py:766
  108.1 1.3 collective-permute-done.9
  109.4 2.7 %collective-permute-start.6 = (bf16[672,256]{1,0:T(8,128)(2,1)}, bf16[672,256]{1,0:T(8,128)(2,1)S(1)}, u32[]{:S(2)}, u32[]{:S(2)}) collective-permute-start(bf16[672,256]{1,0:T(8,128)(2,1)} %get-tuple-element.52), channel_id=1, source_target_pairs={{0,8},{4,12},{8,0},{12,4},{1,9},{5,13},{9,1},{13,5},{2,10},{6,14},... | collective-permute-start | bytes 1032200 | tf_op jit(solution)/shard_map/ppermute | solution.py:766
  112.1 2.2 %collective-permute-start.7 = (bf16[672,256]{1,0:T(8,128)(2,1)}, bf16[672,256]{1,0:T(8,128)(2,1)S(1)}, u32[]{:S(2)}, u32[]{:S(2)}) collective-permute-start(bf16[672,256]{1,0:T(8,128)(2,1)} %get-tuple-element.53), channel_id=1, source_target_pairs={{0,12},{4,0},{8,4},{12,8},{1,13},{5,1},{9,5},{13,9},{2,14},{6,2},{... | collective-permute-start | bytes 1032200 | tf_op jit(solution)/shard_map/ppermute | solution.py:766
  115.0 1.7 %finish.1 = (f32[4,1792]{1,0:T(4,128)}, f32[1,28]{1,0:T(1,128)}, f32[1,28]{1,0:T(1,128)}, f32[1,28]{1,0:T(1,128)}, f32[256,128]{1,0:T(8,128)}, /*index=5*/f32[256,128]{1,0:T(8,128)}) custom-call(bf16[32,64,128]{2,1,0:T(8,128)(2,1)S(1)} %all-to-all-done.2.bundle_ref, bf16[256,128]{1,0:T(8,128)(2,1)} %get-tuple-element.67.refs_0_, ...), custom_call_target="tpu_custom_call" | custom-call | tf_op jit(solution)/shard_map/finish/pallas_call | solution.py:575
  116.7 1.8 %collective-permute-done.5.refs_1_ = bf16[672,256]{1,0:T(8,128)(2,1)S(1)} collective-permute-done((bf16[672,256]{1,0:T(8,128)(2,1)}, bf16[672,256]{1,0:T(8,128)(2,1)S(1)}, u32[]{:S(2)}, u32[]{:S(2)}) %collective-permute-start.5) | collective-permute-done | bytes 344096 | tf_op jit(solution)/shard_map/ppermute | solution.py:766
  118.5 6.7 %collective-permute-done.6.refs_2_ = bf16[672,256]{1,0:T(8,128)(2,1)S(1)} collective-permute-done((bf16[672,256]{1,0:T(8,128)(2,1)}, bf16[672,256]{1,0:T(8,128)(2,1)S(1)}, u32[]{:S(2)}, u32[]{:S(2)}) %collective-permute-start.6) | collective-permute-done | bytes 344096 | tf_op jit(solution)/shard_map/ppermute | solution.py:766
  125.2 3.7 %collective-permute-done.7.refs_3_ = bf16[672,256]{1,0:T(8,128)(2,1)S(1)} collective-permute-done((bf16[672,256]{1,0:T(8,128)(2,1)}, bf16[672,256]{1,0:T(8,128)(2,1)S(1)}, u32[]{:S(2)}, u32[]{:S(2)}) %collective-permute-start.7) | collective-permute-done | bytes 344096 | tf_op jit(solution)/shard_map/ppermute | solution.py:766
  128.9 2.3 %unpack.1 = (bf16[256,896]{1,0:T(8,128)(2,1)}, bf16[256,896]{1,0:T(8,128)(2,1)}, bf16[256,896]{1,0:T(8,128)(2,1)}) custom-call(bf16[672,256]{1,0:T(8,128)(2,1)} %get-tuple-element.50.refs_0_, bf16[672,256]{1,0:T(8,128)(2,1)S(1)} %collective-permute-done.5.refs_1_, bf16[672,256]{1,0:T(8,128)(2,1)S(1)} %collective-permute-done.6.refs_2_, ...), custom_call_target="tpu_custom_call" | custom-call | flops 2000000000 | bytes 3000000 | tf_op jit(solution)/shard_map/unpack/pallas_call | solution.py:746
  (20 shorter events, 1.5 us)
Async XLA Ops:
  1.4 12.7 %collective-permute-start.8 = (bf16[8,1792]{1,0:T(8,128)(2,1)S(1)}, bf16[8,1792]{1,0:T(8,128)(2,1)S(1)}, u32[]{:S(2)}, u32[]{:S(2)}) collective-permute-start(bf16[8,1792]{1,0:T(8,128)(2,1)S(1)} %slice.3), channel_id=1, source_target_pairs={{0,4},{4,8},{8,12},{12,16},{16,20},{20,24},{24,28},{28,32},{32,36}... | collective-permute-start | bytes 86024 | tf_op jit(solution)/shard_map/ppermute | solution.py:760
  8.2 23.6 %collective-permute-start = (bf16[896,256]{1,0:T(8,128)(2,1)}, bf16[896,256]{1,0:T(8,128)(2,1)S(1)}, u32[]{:S(2)}, u32[]{:S(2)}) collective-permute-start(bf16[896,256]{1,0:T(8,128)(2,1)} %get-tuple-element.44), channel_id=1, source_target_pairs={{0,4},{4,8},{8,12},{12,0},{1,5},{5,9},{9,13},{13,1},{2,6},{6,10},{... | collective-permute-start | bytes 1376264 | tf_op jit(solution)/shard_map/ppermute | solution.py:766
  9.7 24.3 %collective-permute-start.1 = (bf16[896,256]{1,0:T(8,128)(2,1)}, bf16[896,256]{1,0:T(8,128)(2,1)S(1)}, u32[]{:S(2)}, u32[]{:S(2)}) collective-permute-start(bf16[896,256]{1,0:T(8,128)(2,1)} %get-tuple-element.45), channel_id=1, source_target_pairs={{0,8},{4,12},{8,0},{12,4},{1,9},{5,13},{9,1},{13,5},{2,10},{6,14},... | collective-permute-start | bytes 1376264 | tf_op jit(solution)/shard_map/ppermute | solution.py:766
  14.1 20.2 %collective-permute-start.2 = (bf16[896,256]{1,0:T(8,128)(2,1)}, bf16[896,256]{1,0:T(8,128)(2,1)S(1)}, u32[]{:S(2)}, u32[]{:S(2)}) collective-permute-start(bf16[896,256]{1,0:T(8,128)(2,1)} %get-tuple-element.46), channel_id=1, source_target_pairs={{0,12},{4,0},{8,4},{12,8},{1,13},{5,1},{9,5},{13,9},{2,14},{6,2},{... | collective-permute-start | bytes 1376264 | tf_op jit(solution)/shard_map/ppermute | solution.py:766
  14.1 0.6 copy-start.3
  14.7 19.6 %copy-start = (bf16[896,256]{1,0:T(8,128)(2,1)S(1)}, bf16[896,256]{1,0:T(8,128)(2,1)}, u32[]{:S(2)}) copy-start(bf16[896,256]{1,0:T(8,128)(2,1)} %get-tuple-element.43.refs_0_) | copy-start | bytes 1376260
  23.8 26.3 %all-to-all-start = ((bf16[32,64,128]{2,1,0:T(8,128)(2,1)}), bf16[32,64,128]{2,1,0:T(8,128)(2,1)S(1)}, u32[]{:S(2)}, u32[]{:S(2)}) async-start(bf16[32,64,128]{2,1,0:T(8,128)(2,1)} %bitcast.11), calls=%async_computation | async-start | bytes 1048576 | tf_op jit(solution)/shard_map/all_to_all | solution.py:776
  35.2 25.3 %collective-permute-start.3 = (bf16[1792,256]{1,0:T(8,128)(2,1)}, bf16[1792,256]{1,0:T(8,128)(2,1)}, u32[]{:S(2)}, u32[]{:S(2)}) collective-permute-start(bf16[1792,256]{1,0:T(8,128)(2,1)} %lend.1), channel_id=1, source_target_pairs={{0,16},{4,20},{8,24},{12,28},{16,32},{20,36},{24,40},{28,44},{32,4... | collective-permute-start | bytes 2752520 | tf_op jit(solution)/shard_map/ppermute | solution.py:760
  51.3 21.3 %all-to-all-start.1 = ((bf16[32,56,128]{2,1,0:T(8,128)(2,1)}), bf16[32,56,128]{2,1,0:T(8,128)(2,1)S(1)}, u32[]{:S(2)}, u32[]{:S(2)}) async-start(bf16[32,56,128]{2,1,0:T(8,128)(2,1)} %chain.1), calls=%async_computation.1 | async-start | bytes 917504 | tf_op jit(solution)/shard_map/all_to_all | solution.py:776
  69.5 33.1 %collective-permute-start.4 = (bf16[4,448,256]{2,1,0:T(8,128)(2,1)}, bf16[4,448,256]{2,1,0:T(8,128)(2,1)S(1)}, u32[]{:S(2)}, u32[]{:S(2)}) collective-permute-start(bf16[4,448,256]{2,1,0:T(8,128)(2,1)} %get-tuple-element.49), channel_id=1, source_target_pairs={{16,0},{20,4},{24,8},{28,12},{32,16},{36,20},{40,24},{44,28},{48,3... | collective-permute-start | bytes 2752520 | tf_op jit(solution)/shard_map/ppermute | solution.py:760
  72.6 0.8 copy-start.1
  87.0 25.2 %collective-permute-start.10 = (bf16[256,128]{1,0:T(8,128)(2,1)}, bf16[256,128]{1,0:T(8,128)(2,1)S(1)}, u32[]{:S(2)}, u32[]{:S(2)}) collective-permute-start(bf16[256,128]{1,0:T(8,128)(2,1)} %get-tuple-element.67.refs_0_), channel_id=1, source_target_pairs={{0,1},{1,2},{2,3},{3,0},{4,5},{5,6},{6,7},{7,4},{8,9},{9,10},{10,1... | collective-permute-start | bytes 196616 | tf_op jit(solution)/shard_map/ppermute | solution.py:766
  87.0 27.9 %collective-permute-start.11 = (bf16[256,128]{1,0:T(8,128)(2,1)}, bf16[256,128]{1,0:T(8,128)(2,1)S(1)}, u32[]{:S(2)}, u32[]{:S(2)}) collective-permute-start(bf16[256,128]{1,0:T(8,128)(2,1)} %get-tuple-element.67.refs_0_), channel_id=1, source_target_pairs={{0,2},{1,3},{2,0},{3,1},{4,6},{5,7},{6,4},{7,5},{8,10},{9,11},{10,... | collective-permute-start | bytes 196616 | tf_op jit(solution)/shard_map/ppermute | solution.py:766
  87.8 27.2 %collective-permute-start.12 = (bf16[256,128]{1,0:T(8,128)(2,1)}, bf16[256,128]{1,0:T(8,128)(2,1)S(1)}, u32[]{:S(2)}, u32[]{:S(2)}) collective-permute-start(bf16[256,128]{1,0:T(8,128)(2,1)} %get-tuple-element.67.refs_0_), channel_id=1, source_target_pairs={{0,3},{1,0},{2,1},{3,2},{4,7},{5,4},{6,5},{7,6},{8,11},{9,8},{10,9... | collective-permute-start | bytes 196616 | tf_op jit(solution)/shard_map/ppermute | solution.py:766
  89.2 25.8 %all-to-all-start.2 = ((bf16[32,64,128]{2,1,0:T(8,128)(2,1)}), bf16[32,64,128]{2,1,0:T(8,128)(2,1)S(1)}, u32[]{:S(2)}, u32[]{:S(2)}) async-start(bf16[32,64,128]{2,1,0:T(8,128)(2,1)} %get-tuple-element.66), calls=%async_computation.2 | async-start | bytes 1048576 | tf_op jit(solution)/shard_map/all_to_all | solution.py:776
  101.3 8.2 %collective-permute-start.9 = (f32[8,1792]{1,0:T(8,128)}, f32[8,1792]{1,0:T(8,128)S(1)}, u32[]{:S(2)}, u32[]{:S(2)}) collective-permute-start(f32[8,1792]{1,0:T(8,128)} %get-tuple-element.63), channel_id=1, source_target_pairs={{4,0},{8,4},{12,8},{16,12},{20,16},{24,20},{28,24},{32,28},{36,32}... | collective-permute-start | bytes 172040 | tf_op jit(solution)/shard_map/ppermute | solution.py:760
  102.6 11.8 %copy-start.2 = (f32[8,1792]{1,0:T(8,128)S(1)}, f32[8,1792]{1,0:T(8,128)}, u32[]{:S(2)}) copy-start(f32[8,1792]{1,0:T(8,128)} %get-tuple-element.62) | copy-start | bytes 172036
  105.5 13.0 %collective-permute-start.5 = (bf16[672,256]{1,0:T(8,128)(2,1)}, bf16[672,256]{1,0:T(8,128)(2,1)S(1)}, u32[]{:S(2)}, u32[]{:S(2)}) collective-permute-start(bf16[672,256]{1,0:T(8,128)(2,1)} %get-tuple-element.51), channel_id=1, source_target_pairs={{0,4},{4,8},{8,12},{12,0},{1,5},{5,9},{9,13},{13,1},{2,6},{6,10},{... | collective-permute-start | bytes 1032200 | tf_op jit(solution)/shard_map/ppermute | solution.py:766
  109.4 15.8 %collective-permute-start.6 = (bf16[672,256]{1,0:T(8,128)(2,1)}, bf16[672,256]{1,0:T(8,128)(2,1)S(1)}, u32[]{:S(2)}, u32[]{:S(2)}) collective-permute-start(bf16[672,256]{1,0:T(8,128)(2,1)} %get-tuple-element.52), channel_id=1, source_target_pairs={{0,8},{4,12},{8,0},{12,4},{1,9},{5,13},{9,1},{13,5},{2,10},{6,14},... | collective-permute-start | bytes 1032200 | tf_op jit(solution)/shard_map/ppermute | solution.py:766
  112.1 16.8 %collective-permute-start.7 = (bf16[672,256]{1,0:T(8,128)(2,1)}, bf16[672,256]{1,0:T(8,128)(2,1)S(1)}, u32[]{:S(2)}, u32[]{:S(2)}) collective-permute-start(bf16[672,256]{1,0:T(8,128)(2,1)} %get-tuple-element.53), channel_id=1, source_target_pairs={{0,12},{4,0},{8,4},{12,8},{1,13},{5,1},{9,5},{13,9},{2,14},{6,2},{... | collective-permute-start | bytes 1032200 | tf_op jit(solution)/shard_map/ppermute | solution.py:766
